TPU v7x, 32 devices: a whole 2x2x4 slice. The times are simulated.
32 devices in a mesh: dp: 8 (over z, core), expert: 4 (over y, x).
Axes of the slice: x: 2, y: 2, z: 4, core: 2. Of those that a mesh axis runs over, the one named last changes fastest.
Arguments:
- tokens: bfloat16 [24576, 768], P(('dp', 'expert')), may hold values from -6 to 6
- cotangent: bfloat16 [24576, 768], P(('dp', 'expert')), may hold values from -6 to 6
- expert_ids: int32 [24576, 2], P(('dp', 'expert')), may hold values from 0 to 15, all different within a row
- route_gates: float32 [24576, 2], P(('dp', 'expert')), may hold values from 0.25 to 1
- slot_order: int32 [32, 1536], P(('dp', 'expert')), may hold values from 0 to 1535, each once within a row
- prefix_len: int32 [32], P(('dp', 'expert')), may hold values from 1 to 767
- attention_gain: float32 [768], replicated, may hold values from 0.1 to 1.9
- qkv_weight: bfloat16 [768, 2304], replicated, may hold values from -0.21875 to 0.21875
- output_weight: bfloat16 [768, 768], replicated, may hold values from -0.875 to 0.875
- feedforward_gain: float32 [768], replicated, may hold values from 0.1 to 1.9
- shared_gate: bfloat16 [768, 2048], replicated, may hold values from -0.21875 to 0.21875
- shared_up: bfloat16 [768, 2048], replicated, may hold values from -0.21875 to 0.21875
- shared_down: bfloat16 [2048, 768], replicated, may hold values from -0.125 to 0.125
- expert_gate: bfloat16 [16, 768, 2048], P('expert'), may hold values from -0.21875 to 0.21875
- expert_up: bfloat16 [16, 768, 2048], P('expert'), may hold values from -0.21875 to 0.21875
- expert_down: bfloat16 [16, 2048, 768], P('expert'), may hold values from -0.125 to 0.125
Outputs:
- block_out: bfloat16 [24576, 768], P(('dp', 'expert'))
- tokens_grad: bfloat16 [24576, 768], P(('dp', 'expert'))
- attention_gain_grad: float32 [768], P('dp')
- qkv_weight_grad: float32 [768, 2304], P('dp')
- output_weight_grad: float32 [768, 768], P('dp')
- feedforward_gain_grad: float32 [768], P('dp')
- shared_gate_grad: float32 [768, 2048], P('dp')
- shared_up_grad: float32 [768, 2048], P('dp')
- shared_down_grad: float32 [2048, 768], P('dp')
- expert_gate_grad: float32 [16, 768, 2048], P('expert', 'dp')
- expert_up_grad: float32 [16, 768, 2048], P('expert', 'dp')
- expert_down_grad: float32 [16, 2048, 768], P('expert', 'dp')
Inputs may be any that keep to these rules, and one draw needn't show every extreme that they name: `expert_ids`: each token names two different experts; every expert is named by some token. `slot_order`: each row is a permutation of its sequence's pair numbers 2 p + k.
All inputs are finite; a program needn't handle non-finite values.
Results may differ from a plain program's by a relative error of at most 0.023.
Values may be sent and summed in bfloat16 or wider, within the bound.
A program may use at most 320 MiB of HBM per device.

v0:
```python
import jax
import jax.numpy as jnp
from jax import lax
from jax.sharding import PartitionSpec as P

HEADS = 12
HEAD_DIM = 64
E = 16
CAP = 120


epsilon = 1e-06


def rms_forward(values, gain_vector):
    inverse = lax.rsqrt(jnp.mean(values * values, axis=-1, keepdims=True) + epsilon)
    normed = values * inverse
    return (normed * gain_vector, normed, inverse)


def rms_backward(upstream, gain_vector, normed, inverse):
    scaled = upstream * gain_vector
    gain_grad = jnp.sum(upstream * normed, axis=0)
    row_inner = jnp.mean(scaled * normed, axis=-1, keepdims=True)
    return (inverse * (scaled - normed * row_inner), gain_grad)


def rope_tables(length, head_size):
    positions = jnp.arange(length, dtype=jnp.float32)
    frequency = 10000.0 ** (-jnp.arange(head_size // 2, dtype=jnp.float32) * 2.0 / head_size)
    angles = positions[:, None] * frequency[None, :]
    return (jnp.cos(angles)[:, None, :], jnp.sin(angles)[:, None, :])


def rotate(values, cosine, sine_table):
    half_size = values.shape[-1] // 2
    first_half = values[..., :half_size]
    second = values[..., half_size:]
    return jnp.concatenate(
        [first_half * cosine - second * sine_table, second * cosine + first_half * sine_table],
        axis=-1,
    )


def contract_rows(left_side, right_side):
    return lax.dot_general(
        left_side, right_side, (((0,), (0,)), ((), ())), preferred_element_type=jnp.float32
    )


def contract_last(left_side, right_side):
    return lax.dot_general(
        left_side, right_side, (((1,), (1,)), ((), ())), preferred_element_type=jnp.float32
    )


def silu_slope(pre_values):
    sigmoid_gate = jax.nn.sigmoid(pre_values)
    return sigmoid_gate * (1.0 + pre_values * (1.0 - sigmoid_gate))


def shards(
    tokens,
    cotangent,
    expert_ids,
    route_gates,
    slot_order,
    prefix_len,
    attention_gain,
    qkv_weight,
    output_weight,
    feedforward_gain,
    shared_gate,
    shared_up,
    shared_down,
    expert_gate,
    expert_up,
    expert_down,
):
    length, features = tokens.shape
    local_experts = expert_gate.shape[0]
    groups = lax.axis_size("expert")
    pair_count = 2 * length
    score_scale = HEAD_DIM ** (-0.5)
    pair_expert = expert_ids.reshape(pair_count)
    order_row = slot_order[0]
    sorted_expert = pair_expert[order_row]
    onehot = (sorted_expert[:, None] == jnp.arange(E, dtype=jnp.int32)[None, :]).astype(jnp.int32)
    before = jnp.cumsum(onehot, axis=0) - onehot
    sorted_slot = jnp.sum(before * onehot, axis=1)
    position = jnp.zeros((pair_count,), jnp.int32).at[order_row].set(sorted_slot)
    slot_index = jnp.where(position < CAP, pair_expert * CAP + position, E * CAP)
    pair_table = (
        jnp.full((E * CAP + 1,), pair_count, jnp.int32)
        .at[slot_index]
        .set(jnp.arange(pair_count, dtype=jnp.int32))[: E * CAP]
    )
    token_table = pair_table // 2
    zero_row = jnp.zeros((1, features), jnp.bfloat16)
    resid = tokens.astype(jnp.float32)
    normed_one, unit_one, inverse_one = rms_forward(resid, attention_gain)
    normed_low = normed_one.astype(jnp.bfloat16)
    projected = jnp.dot(normed_low, qkv_weight, preferred_element_type=jnp.float32).reshape(
        length, 3, HEADS, HEAD_DIM
    )
    cosine, sine_table = rope_tables(length, HEAD_DIM)
    queries = rotate(projected[:, 0], cosine, sine_table).astype(jnp.bfloat16)
    key_rows = rotate(projected[:, 1], cosine, sine_table).astype(jnp.bfloat16)
    values = projected[:, 2].astype(jnp.bfloat16)
    row_ids = jnp.arange(length)[:, None]
    col_ids = jnp.arange(length)[None, :]
    visible = ((col_ids <= row_ids) | (col_ids < prefix_len[0]))[None]
    scores = (
        jnp.einsum("qhd,khd->hqk", queries, key_rows, preferred_element_type=jnp.float32)
        * score_scale
    )
    scores = jnp.where(visible, scores, -1e30)
    row_peak = jnp.max(scores, axis=-1, keepdims=True)
    exp_scores = jnp.exp(scores - row_peak)
    row_total = jnp.sum(exp_scores, axis=-1, keepdims=True)
    log_total = row_peak + jnp.log(row_total)
    soft_probs = (exp_scores / row_total).astype(jnp.bfloat16)
    attended = jnp.einsum("hqk,khd->qhd", soft_probs, values, preferred_element_type=jnp.float32)
    attended_low = attended.reshape(length, features).astype(jnp.bfloat16)
    attn_branch = jnp.dot(attended_low, output_weight, preferred_element_type=jnp.float32)
    state = resid + attn_branch
    normed_two, unit_two, inverse_two = rms_forward(state, feedforward_gain)
    normed_two_low = normed_two.astype(jnp.bfloat16)
    gate_pre = jnp.dot(normed_two_low, shared_gate, preferred_element_type=jnp.float32)
    up_pre = jnp.dot(normed_two_low, shared_up, preferred_element_type=jnp.float32)
    shared_hidden = (jax.nn.silu(gate_pre) * up_pre).astype(jnp.bfloat16)
    shared_branch = jnp.dot(shared_hidden, shared_down, preferred_element_type=jnp.float32)
    padded_rows = jnp.concatenate([normed_two_low, zero_row], axis=0)
    outgoing = padded_rows[token_table].reshape(groups, local_experts, CAP, features)
    arrived = lax.all_to_all(outgoing, "expert", split_axis=0, concat_axis=0, tiled=True)
    expert_gate_pre = jnp.einsum(
        "slcd,ldf->slcf", arrived, expert_gate, preferred_element_type=jnp.float32
    )
    expert_up_pre = jnp.einsum(
        "slcd,ldf->slcf", arrived, expert_up, preferred_element_type=jnp.float32
    )
    expert_hidden = (jax.nn.silu(expert_gate_pre) * expert_up_pre).astype(jnp.bfloat16)
    expert_result = jnp.einsum(
        "slcf,lfd->slcd", expert_hidden, expert_down, preferred_element_type=jnp.float32
    ).astype(jnp.bfloat16)
    returned = lax.all_to_all(expert_result, "expert", split_axis=0, concat_axis=0, tiled=True)
    returned_pad = jnp.concatenate([returned.reshape(E * CAP, features), zero_row], axis=0)
    picked = returned_pad[slot_index].astype(jnp.float32).reshape(length, 2, features)
    mixture = jnp.sum(picked * route_gates[:, :, None], axis=1)
    block_out = (state + shared_branch + mixture).astype(jnp.bfloat16)
    upstream = cotangent.astype(jnp.float32)
    pair_grad = (route_gates[:, :, None] * upstream[:, None, :]).reshape(pair_count, features)
    pair_grad_pad = jnp.concatenate([pair_grad, jnp.zeros((1, features), jnp.float32)], axis=0)
    slot_grad = (
        pair_grad_pad[pair_table].astype(jnp.bfloat16).reshape(groups, local_experts, CAP, features)
    )
    slot_grad_in = lax.all_to_all(slot_grad, "expert", split_axis=0, concat_axis=0, tiled=True)
    down_w_grad = jnp.einsum(
        "slcf,slcd->lfd", expert_hidden, slot_grad_in, preferred_element_type=jnp.float32
    )
    expert_hidden_grad = jnp.einsum(
        "slcd,lfd->slcf", slot_grad_in, expert_down, preferred_element_type=jnp.float32
    )
    expert_gate_back = (expert_hidden_grad * expert_up_pre * silu_slope(expert_gate_pre)).astype(
        jnp.bfloat16
    )
    expert_up_back = (expert_hidden_grad * jax.nn.silu(expert_gate_pre)).astype(jnp.bfloat16)
    gate_w_grad = jnp.einsum(
        "slcd,slcf->ldf", arrived, expert_gate_back, preferred_element_type=jnp.float32
    )
    up_w_grad = jnp.einsum(
        "slcd,slcf->ldf", arrived, expert_up_back, preferred_element_type=jnp.float32
    )
    dispatched_grad = jnp.einsum(
        "slcf,ldf->slcd", expert_gate_back, expert_gate, preferred_element_type=jnp.float32
    )
    dispatched_grad = dispatched_grad + jnp.einsum(
        "slcf,ldf->slcd", expert_up_back, expert_up, preferred_element_type=jnp.float32
    )
    sent_back = lax.all_to_all(
        dispatched_grad.astype(jnp.bfloat16), "expert", split_axis=0, concat_axis=0, tiled=True
    )
    expert_sums = (
        lax.psum_scatter(
            gate_w_grad.astype(jnp.bfloat16), "dp", scatter_dimension=1, tiled=True
        ).astype(jnp.float32),
        lax.psum_scatter(
            up_w_grad.astype(jnp.bfloat16), "dp", scatter_dimension=1, tiled=True
        ).astype(jnp.float32),
        lax.psum_scatter(
            down_w_grad.astype(jnp.bfloat16), "dp", scatter_dimension=1, tiled=True
        ).astype(jnp.float32),
    )
    back_pad = jnp.concatenate([sent_back.reshape(E * CAP, features), zero_row], axis=0)
    from_experts = jnp.sum(
        back_pad[slot_index].astype(jnp.float32).reshape(length, 2, features), axis=1
    )
    shared_down_grad = contract_rows(shared_hidden, cotangent)
    shared_hidden_grad = contract_last(cotangent, shared_down)
    gate_back = (shared_hidden_grad * up_pre * silu_slope(gate_pre)).astype(jnp.bfloat16)
    up_back = (shared_hidden_grad * jax.nn.silu(gate_pre)).astype(jnp.bfloat16)
    shared_gate_grad = contract_rows(normed_two_low, gate_back)
    shared_up_grad = contract_rows(normed_two_low, up_back)
    normed_two_grad = (
        contract_last(gate_back, shared_gate) + contract_last(up_back, shared_up) + from_experts
    )
    state_norm_grad, feedforward_gain_grad = rms_backward(
        normed_two_grad, feedforward_gain, unit_two, inverse_two
    )
    state_grad = upstream + state_norm_grad
    branch_grad = state_grad.astype(jnp.bfloat16)
    output_weight_grad = contract_rows(attended_low, branch_grad)
    attended_grad = (
        contract_last(branch_grad, output_weight)
        .astype(jnp.bfloat16)
        .reshape(length, HEADS, HEAD_DIM)
    )
    scores_again = (
        jnp.einsum("qhd,khd->hqk", queries, key_rows, preferred_element_type=jnp.float32)
        * score_scale
    )
    probs_again = jnp.exp(jnp.where(visible, scores_again, -1e30) - log_total)
    values_grad = jnp.einsum(
        "hqk,qhd->khd",
        probs_again.astype(jnp.bfloat16),
        attended_grad,
        preferred_element_type=jnp.float32,
    )
    prob_grad = jnp.einsum(
        "qhd,khd->hqk", attended_grad, values, preferred_element_type=jnp.float32
    )
    row_inner = jnp.sum(prob_grad * probs_again, axis=-1, keepdims=True)
    score_grad = (probs_again * (prob_grad - row_inner)).astype(jnp.bfloat16)
    queries_grad = (
        jnp.einsum("hqk,khd->qhd", score_grad, key_rows, preferred_element_type=jnp.float32)
        * score_scale
    )
    keys_grad = (
        jnp.einsum("hqk,qhd->khd", score_grad, queries, preferred_element_type=jnp.float32)
        * score_scale
    )
    queries_grad = rotate(queries_grad, cosine, -sine_table)
    keys_grad = rotate(keys_grad, cosine, -sine_table)
    projected_grad = (
        jnp.stack([queries_grad, keys_grad, values_grad], axis=1)
        .reshape(length, 3 * features)
        .astype(jnp.bfloat16)
    )
    qkv_weight_grad = contract_rows(normed_low, projected_grad)
    normed_one_grad = contract_last(projected_grad, qkv_weight)
    tokens_norm_grad, attention_gain_grad = rms_backward(
        normed_one_grad, attention_gain, unit_one, inverse_one
    )
    tokens_grad = (state_grad + tokens_norm_grad).astype(jnp.bfloat16)
    partial_sums = (
        lax.psum_scatter(
            attention_gain_grad.astype(jnp.bfloat16), "dp", scatter_dimension=0, tiled=True
        ).astype(jnp.float32),
        lax.psum_scatter(
            qkv_weight_grad.astype(jnp.bfloat16), "dp", scatter_dimension=0, tiled=True
        ).astype(jnp.float32),
        lax.psum_scatter(
            output_weight_grad.astype(jnp.bfloat16), "dp", scatter_dimension=0, tiled=True
        ).astype(jnp.float32),
        lax.psum_scatter(
            feedforward_gain_grad.astype(jnp.bfloat16), "dp", scatter_dimension=0, tiled=True
        ).astype(jnp.float32),
        lax.psum_scatter(
            shared_gate_grad.astype(jnp.bfloat16), "dp", scatter_dimension=0, tiled=True
        ).astype(jnp.float32),
        lax.psum_scatter(
            shared_up_grad.astype(jnp.bfloat16), "dp", scatter_dimension=0, tiled=True
        ).astype(jnp.float32),
        lax.psum_scatter(
            shared_down_grad.astype(jnp.bfloat16), "dp", scatter_dimension=0, tiled=True
        ).astype(jnp.float32),
    )
    dense_sums = (
        lax.psum(partial_sums[0].astype(jnp.bfloat16), "expert").astype(jnp.float32),
        lax.psum(partial_sums[1].astype(jnp.bfloat16), "expert").astype(jnp.float32),
        lax.psum(partial_sums[2].astype(jnp.bfloat16), "expert").astype(jnp.float32),
        lax.psum(partial_sums[3].astype(jnp.bfloat16), "expert").astype(jnp.float32),
        lax.psum(partial_sums[4].astype(jnp.bfloat16), "expert").astype(jnp.float32),
        lax.psum(partial_sums[5].astype(jnp.bfloat16), "expert").astype(jnp.float32),
        lax.psum(partial_sums[6].astype(jnp.bfloat16), "expert").astype(jnp.float32),
    )
    return (
        block_out,
        tokens_grad,
        dense_sums[0],
        dense_sums[1],
        dense_sums[2],
        dense_sums[3],
        dense_sums[4],
        dense_sums[5],
        dense_sums[6],
        expert_sums[0],
        expert_sums[1],
        expert_sums[2],
    )


def solution(mesh):
    return jax.shard_map(
        shards,
        mesh=mesh,
        in_specs=(
            P(("dp", "expert"), None),
            P(("dp", "expert"), None),
            P(("dp", "expert"), None),
            P(("dp", "expert"), None),
            P(("dp", "expert"), None),
            P(("dp", "expert")),
            P(),
            P(),
            P(),
            P(),
            P(),
            P(),
            P(),
            P("expert", None, None),
            P("expert", None, None),
            P("expert", None, None),
        ),
        out_specs=(
            P(("dp", "expert"), None),
            P(("dp", "expert"), None),
            P("dp"),
            P("dp", None),
            P("dp", None),
            P("dp"),
            P("dp", None),
            P("dp", None),
            P("dp", None),
            P("expert", "dp", None),
            P("expert", "dp", None),
            P("expert", "dp", None),
        ),
        check_vma=False,
    )
```

profile of v0, /device:TPU:0, one launch (start us, length us, event | category | flops | bytes accessed | tf_op | source)
XLA Modules:
  0.0 993.5 jit_solution(16320943424098945938)
XLA Ops:
  16.8 12.3 %fusion.85 = (f32[12,768]{1,0:T(8,128)S(1)}, f32[12,768,768]{1,2,0:T(8,128)}) fusion(bf16[768,12,32]{0,2,1:T(8,128)(2,1)S(1)} %get-tuple-element.43, bf16[768,12,32]{0,2,1:T(8,128)(2,1)S(1)} %get-tuple-element.44, bf16[768,12,32]{0,2,1:T(8,128)(2,1)S(1)} %get-tuple-element.38, bf16[768,12,32]{0,2,1:T(8,128)(2,1)S(1)} %get-tuple-element.37, ...), kind=kOutput, calls=%fused_computation.163 | convolution fusion | flops 931912704 | bytes 31297536 | tf_op jit(solution)/shard_map/qhd,khd->hqk/dot_general | solution.py:114
  29.1 11.6 %fusion = f32[12,768]{1,0:T(8,128)S(1)} fusion(f32[12,768,768]{1,2,0:T(8,128)} %get-tuple-element.51, f32[12,768]{1,0:T(8,128)S(1)} %get-tuple-element.50), kind=kLoop, calls=%fused_computation.16 | loop fusion | flops 14146560 | bytes 28385280 | tf_op jit(solution)/shard_map/reduce_sum | solution.py:120
  40.8 12.8 %fusion.55 = bf16[12,64,768]{2,1,0:T(8,128)(2,1)} fusion(f32[12,768,768]{1,2,0:T(8,128)} %get-tuple-element.51, f32[12,768]{1,0:T(8,128)S(1)} %fusion, f32[12,768]{1,0:T(8,128)S(1)} %get-tuple-element.50, f32[768,3,12,64]{0,3,2,1:T(8,128)S(1)} %bitcast.173), kind=kOutput, calls=%fused_computation.101 | convolution fusion | flops 927793152 | bytes 30769152 | tf_op jit(solution)/shard_map/hqk,khd->qhd/dot_general | solution.py:123
  64.2 7.5 multiply_convert_fusion.1
  71.7 6.0 convolution_convert_fusion.3
  81.9 8.5 gather_fusion
  91.0 9.4 reduce-window.6
  105.5 6.9 scatter_custom_fusion
  116.1 6.3 scatter_custom_fusion.1
  122.5 9.9 gather_fusion.1
  137.7 6.6 convolution_convert_fusion.2
  151.7 6.9 mul.474
  163.0 10.5 %gather_fusion.3 = bf16[1920,768]{1,0:T(8,128)(2,1)} fusion(bf16[1537,768]{1,0:T(8,128)(2,1)} %concatenate.32, s32[2048]{0:T(1024)S(1)} %get-tuple-element.58), kind=kCustom, calls=%fused_computation.3 | custom fusion | bytes 5905920 | tf_op jit(solution)/shard_map/gather | solution.py:155
  178.6 14.8 %fusion.17 = f32[4,4,120,2048]{3,2,1,0:T(8,128)} fusion(bf16[4,768,2048]{2,1,0:T(8,128)(2,1)} %param.30, bf16[4,4,120,768]{3,2,1,0:T(8,128)(2,1)} %all-to-all-done), kind=kOutput, calls=%fused_computation.38 | convolution fusion | flops 6039797760 | bytes 31260672 | tf_op jit(solution)/shard_map/slcd,ldf->slcf/dot_general | solution.py:139
  193.4 14.7 %fusion.21 = f32[4,4,120,2048]{3,2,1,0:T(8,128)} fusion(bf16[4,768,2048]{2,1,0:T(8,128)(2,1)} %param.29, bf16[4,4,120,768]{3,2,1,0:T(8,128)(2,1)} %all-to-all-done), kind=kOutput, calls=%fused_computation.42 | convolution fusion | flops 6039797760 | bytes 31260672 | tf_op jit(solution)/shard_map/slcd,ldf->slcf/dot_general | solution.py:136
  208.1 5.7 all-to-all-done.2
  213.8 25.5 %fusion.3 = (bf16[4,4,120,2048]{3,2,0,1:T(8,128)(2,1)}, bf16[4,4,120,2048]{3,2,0,1:T(8,128)(2,1)}, bf16[4,4,120,2048]{3,2,0,1:T(8,128)(2,1)}) fusion(f32[4,4,120,2048]{3,2,1,0:T(8,128)} %fusion.17, f32[4,4,120,2048]{3,2,1,0:T(8,128)} %fusion.21, bf16[4,2048,768]{2,1,0:T(8,128)(2,1)} %param.31, bf16[4,4,120,768]{3,2,1,0:T(8,128)(2,1)} %all-to-all-done.2), kind=kOutput, calls=%fused_computation.21 | convolution fusion | flops 6098780160 | bytes 70582272 | tf_op jit(solution)/shard_map/slcd,lfd->slcf/dot_general | solution.py:161
  239.3 14.3 %fusion.15 = f32[4,4,120,768]{3,2,1,0:T(8,128)} fusion(bf16[4,4,120,2048]{3,2,0,1:T(8,128)(2,1)} %get-tuple-element.27, bf16[4,768,2048]{2,1,0:T(8,128)(2,1)} %param.30), kind=kOutput, calls=%fused_computation.36 | convolution fusion | flops 6039797760 | bytes 26345472 | tf_op jit(solution)/shard_map/slcf,ldf->slcd/dot_general | solution.py:177
  253.6 14.9 %fusion.34 = bf16[4,4,120,768]{3,2,0,1:T(8,128)(2,1)} fusion(f32[4,4,120,768]{3,2,1,0:T(8,128)} %fusion.15, bf16[4,4,120,2048]{3,2,0,1:T(8,128)(2,1)} %get-tuple-element.25, bf16[4,768,2048]{2,1,0:T(8,128)(2,1)} %param.29), kind=kOutput, calls=%fused_computation.69 | convolution fusion | flops 6042746880 | bytes 29294592 | tf_op jit(solution)/shard_map/slcf,ldf->slcd/dot_general | solution.py:174
  276.7 6.5 convolution_convert_fusion.1
  285.4 6.9 fusion.88
  292.3 18.3 %all-to-all-done.3 = bf16[4,4,120,768]{3,2,1,0:T(8,128)(2,1)} async-done(((bf16[4,4,120,768]{3,2,1,0:T(8,128)(2,1)}), bf16[4,4,120,768]{3,2,1,0:T(8,128)(2,1)}, u32[]{:S(2)}, u32[]{:S(2)}) %all-to-all-start.3) | async-done | bytes 2949152 | tf_op jit(solution)/shard_map/all_to_all | solution.py:180
  314.3 8.9 gather_fusion.4
  323.2 6.4 reshape.241
  329.7 9.4 reduce_sum.104
  339.0 8.6 multiply_reduce_fusion.2
  355.0 23.3 %multiply_reduce_fusion = (f32[12,768]{1,0:T(8,128)}, f32[12,768,768]{1,2,0:T(8,128)}) fusion(f32[12,768,768]{1,2,0:T(8,128)} %get-tuple-element.51, f32[12,768]{1,0:T(8,128)S(1)} %copy-done.20, bf16[768,12,64]{0,2,1:T(8,128)(2,1)S(1)} %bitcast.175, f32[768,3,12,64]{0,3,2,1:T(8,128)} %bitcast.174), kind=kOutput, calls=%fused_computation.8 | convolution fusion | flops 927194112 | bytes 59056128 | tf_op jit(solution)/shard_map/qhd,khd->hqk/dot_general | solution.py:229
  378.3 23.3 %multiply_convert_fusion = bf16[12,768,768]{1,2,0:T(8,128)(2,1)} fusion(f32[12,768,768]{1,2,0:T(8,128)} %get-tuple-element.56, f32[12,768,768]{1,2,0:T(8,128)} %get-tuple-element.51, f32[12,768]{1,0:T(8,128)} %get-tuple-element.55, f32[12,768]{1,0:T(8,128)} %log_add_fusion), kind=kLoop, calls=%fused_computation.7 | loop fusion | flops 28311552 | bytes 70852608 | tf_op jit(solution)/shard_map/convert_element_type | solution.py:233
  401.6 11.2 %multiply_bitcast_fusion = f32[768,12,64]{0,2,1:T(8,128)} fusion(bf16[12,768,768]{1,2,0:T(8,128)(2,1)} %multiply_convert_fusion, bf16[768,12,32]{0,2,1:T(8,128)(2,1)} %copy-done.18, bf16[768,12,32]{0,2,1:T(8,128)(2,1)} %copy-done.17), kind=kOutput, calls=%fused_computation.87 | convolution fusion | flops 908918784 | bytes 17694720 | tf_op jit(solution)/shard_map/hqk,qhd->khd/dot_general | solution.py:239
  412.9 9.0 multiply_bitcast_fusion.1
  426.3 11.8 %fusion.56 = bf16[768,1,12,64]{0,3,2,1:T(8,128)(2,1)S(1)} fusion(bf16[768,12,64]{0,2,1:T(8,128)(2,1)S(1)} %bitcast.176, f32[12,768,768]{1,2,0:T(8,128)} %get-tuple-element.51, f32[12,768]{1,0:T(8,128)S(1)} %copy-done.21), kind=kOutput, calls=%fused_computation.102 | convolution fusion | flops 920715264 | bytes 30707712 | tf_op jit(solution)/shard_map/hqk,qhd->khd/dot_general | solution.py:223
  445.3 9.6 reduce-scatter.11.cloned.1.call-done
  454.9 44.3 %reduce-scatter.9.cloned.1.call-done = bf16[96,2304]{1,0:T(8,128)(2,1)} async-done(((bf16[768,2304]{1,0:T(8,128)(2,1)}), bf16[96,2304]{1,0:T(8,128)(2,1)}) %reduce-scatter.9.cloned.1.call-update) | async-done | bytes 442384 | tf_op jit(solution)/shard_map/reduce_scatter | solution.py:259
  499.3 12.9 %bitcast_convert_fusion = bf16[4,2048,768]{2,1,0:T(8,128)(2,1)} fusion(bf16[4,4,120,2048]{3,2,0,1:T(8,128)(2,1)} %get-tuple-element.26, bf16[4,4,120,768]{3,2,1,0:T(8,128)(2,1)} %all-to-all-done.2), kind=kOutput, calls=%fused_computation.13 | convolution fusion | flops 6046089216 | bytes 23396352 | tf_op jit(solution)/shard_map/slcf,slcd->lfd/dot_general | solution.py:158
  512.3 12.7 %bitcast_convert_fusion.2 = bf16[4,768,2048]{2,1,0:T(8,128)(2,1)} fusion(bf16[4,4,120,768]{3,2,1,0:T(8,128)(2,1)} %all-to-all-done, bf16[4,4,120,2048]{3,2,0,1:T(8,128)(2,1)} %get-tuple-element.25), kind=kOutput, calls=%fused_computation.15 | convolution fusion | flops 6046089216 | bytes 23396352 | tf_op jit(solution)/shard_map/slcd,slcf->ldf/dot_general | solution.py:168
  525.1 13.0 %bitcast_convert_fusion.1 = bf16[4,768,2048]{2,1,0:T(8,128)(2,1)} fusion(bf16[4,4,120,768]{3,2,1,0:T(8,128)(2,1)} %all-to-all-done, bf16[4,4,120,2048]{3,2,0,1:T(8,128)(2,1)} %get-tuple-element.27), kind=kOutput, calls=%fused_computation.14 | convolution fusion | flops 6046089216 | bytes 23396352 | tf_op jit(solution)/shard_map/slcd,slcf->ldf/dot_general | solution.py:171
  538.1 12.7 %convert_bitcast_fusion = bf16[4,4,120,768]{3,2,0,1:T(8,128)(2,1)S(1)} fusion(bf16[4,4,120,2048]{3,2,0,1:T(8,128)(2,1)} %get-tuple-element.26, bf16[4,2048,768]{2,1,0:T(8,128)(2,1)} %param.31), kind=kOutput, calls=%fused_computation.70 | convolution fusion | flops 6041272320 | bytes 23396352 | tf_op jit(solution)/shard_map/slcf,lfd->slcd/dot_general | solution.py:143
  559.4 38.8 %all-to-all-done.1 = bf16[4,4,120,768]{3,2,1,0:T(8,128)(2,1)} async-done(((bf16[4,4,120,768]{3,2,1,0:T(8,128)(2,1)}), bf16[4,4,120,768]{3,2,1,0:T(8,128)(2,1)}, u32[]{:S(2)}, u32[]{:S(2)}) %all-to-all-start.1) | async-done | bytes 2949152 | tf_op jit(solution)/shard_map/all_to_all | solution.py:146
  602.4 8.9 gather_fusion.2
  611.3 6.2 reshape.240
  617.5 7.7 fusion.47
  625.2 17.9 %all-reduce.6 = (bf16[768]{0:T(1024)(128)(2,1)}, bf16[768]{0:T(1024)(128)(2,1)}) all-reduce(bf16[768]{0:T(1024)(128)(2,1)} %get-tuple-element.14, bf16[768]{0:T(1024)(128)(2,1)S(1)} %copy-done.39), channel_id=2, replica_groups=mesh['dp'=8,'expert'=4] {'dp'}, use_global_device_ids=true, to_apply=%region_15.16.clone | all-reduce | flops 1536 | bytes 6144
  645.1 10.1 %all-reduce.7 = (bf16[96]{0:T(256)(128)(2,1)}, bf16[96]{0:T(256)(128)(2,1)}) all-reduce(bf16[96]{0:T(256)(128)(2,1)S(1)} %dynamic-slice.1, bf16[96]{0:T(256)(128)(2,1)} %dynamic-slice.3), channel_id=1, replica_groups=mesh['dp'=8,'expert'=4] {'expert'}, use_global_device_ids=true, to_apply=%region_16.17 | all-reduce | flops 192 | bytes 768 | tf_op jit(solution)/shard_map/psum | solution.py:279
  662.0 9.6 multiply_reduce_fusion.1
  671.6 7.9 add_convert_fusion.1
  687.1 36.1 %reduce-scatter.23.cloned.1.call-done = bf16[4,256,768]{2,1,0:T(8,128)(2,1)} async-done(((bf16[4,2048,768]{2,1,0:T(8,128)(2,1)}), bf16[4,256,768]{2,1,0:T(8,128)(2,1)}) %reduce-scatter.23.cloned.1.call-update) | async-done | bytes 1572880 | tf_op jit(solution)/shard_map/reduce_scatter | solution.py:190
  726.5 126.7 %reduce-scatter.19.cloned.1.call-done = bf16[4,96,2048]{2,1,0:T(8,128)(2,1)} async-done(((bf16[4,768,2048]{2,1,0:T(8,128)(2,1)}), bf16[4,96,2048]{2,1,0:T(8,128)(2,1)}) %reduce-scatter.19.cloned.1.call-update) | async-done | bytes 1572880 | tf_op jit(solution)/shard_map/reduce_scatter | solution.py:184
  856.6 126.6 %reduce-scatter.21.cloned.1.call-done = bf16[4,96,2048]{2,1,0:T(8,128)(2,1)} async-done(((bf16[4,768,2048]{2,1,0:T(8,128)(2,1)}), bf16[4,96,2048]{2,1,0:T(8,128)(2,1)}) %reduce-scatter.21.cloned.1.call-update) | async-done | bytes 1572880 | tf_op jit(solution)/shard_map/reduce_scatter | solution.py:187
  (180 shorter events, 126.8 us)
Async XLA Ops:
  7.2 4.0 copy-start
  7.2 438.1 %reduce-scatter.13.cloned.1.call-start = ((), (), s32[]{:S(2)}) async-start(), calls=%async_computation.14 | async-start | bytes 3538944 | tf_op jit(solution)/shard_map/reduce_scatter | solution.py:268
  9.8 5.7 copy-start.33
  10.9 5.1 copy-start.19
  15.5 25.2 %copy-start.4 = (f32[768,2304]{0,1:T(8,128)}, f32[768,2304]{0,1:T(8,128)S(1)}, u32[]{:S(2)}) copy-start(f32[768,2304]{0,1:T(8,128)S(1)} %fusion.66) | copy-start | bytes 21233668
  16.7 12.4 %copy-start.13 = (bf16[768,12,32]{0,2,1:T(8,128)(2,1)}, bf16[768,12,32]{0,2,1:T(8,128)(2,1)S(1)}, u32[]{:S(2)}) copy-start(bf16[768,12,32]{0,2,1:T(8,128)(2,1)S(1)} %get-tuple-element.43) | copy-start | bytes 1769476
  16.7 12.4 %copy-start.15 = (bf16[768,12,32]{0,2,1:T(8,128)(2,1)}, bf16[768,12,32]{0,2,1:T(8,128)(2,1)S(1)}, u32[]{:S(2)}) copy-start(bf16[768,12,32]{0,2,1:T(8,128)(2,1)S(1)} %get-tuple-element.44) | copy-start | bytes 1769476
  16.8 12.4 %copy-start.17 = (bf16[768,12,32]{0,2,1:T(8,128)(2,1)}, bf16[768,12,32]{0,2,1:T(8,128)(2,1)S(1)}, u32[]{:S(2)}) copy-start(bf16[768,12,32]{0,2,1:T(8,128)(2,1)S(1)} %get-tuple-element.37) | copy-start | bytes 1769476
  16.8 12.4 %copy-start.18 = (bf16[768,12,32]{0,2,1:T(8,128)(2,1)}, bf16[768,12,32]{0,2,1:T(8,128)(2,1)S(1)}, u32[]{:S(2)}) copy-start(bf16[768,12,32]{0,2,1:T(8,128)(2,1)S(1)} %get-tuple-element.38) | copy-start | bytes 1769476
  29.1 11.6 %copy-start.24 = (f32[12,768]{1,0:T(8,128)}, f32[12,768]{1,0:T(8,128)S(1)}, u32[]{:S(2)}) copy-start(f32[12,768]{1,0:T(8,128)S(1)} %get-tuple-element.50) | copy-start | bytes 110596
  40.7 12.9 %copy-start.25 = (f32[12,768]{1,0:T(8,128)}, f32[12,768]{1,0:T(8,128)S(1)}, u32[]{:S(2)}) copy-start(f32[12,768]{1,0:T(8,128)S(1)} %fusion) | copy-start | bytes 110596
  40.7 12.9 %copy-start.8 = (bf16[768,768]{1,0:T(8,128)(2,1)S(1)}, bf16[768,768]{1,0:T(8,128)(2,1)}, u32[]{:S(2)}) copy-start(bf16[768,768]{1,0:T(8,128)(2,1)} %param.16) | copy-start | bytes 3538948
  40.8 12.9 %copy-start.43 = (bf16[768,768]{1,0:T(8,128)(2,1)S(1)}, bf16[768,768]{1,0:T(8,128)(2,1)}, u32[]{:S(2)}) copy-start(bf16[768,768]{1,0:T(8,128)(2,1)} %param.24) | copy-start | bytes 3538948
  53.6 4.0 copy-start.31
  56.2 2.7 copy-start.41
  56.2 5.3 copy-start.26
  59.0 12.8 %copy-start.7 = (bf16[768,768]{1,0:T(8,128)(2,1)}, bf16[768,768]{1,0:T(8,128)(2,1)S(1)}, u32[]{:S(2)}) copy-start(bf16[768,768]{1,0:T(8,128)(2,1)S(1)} %multiply_convert_fusion.4) | copy-start | bytes 3538948
  59.0 2.6 copy-start.40
  61.6 2.6 copy-start.5
  61.6 2.6 copy-start.42
  77.8 2.9 copy-start.35
  115.5 7.0 copy-start.28
  132.4 41.1 %all-to-all-start = ((bf16[4,4,120,768]{3,2,1,0:T(8,128)(2,1)}), bf16[4,4,120,768]{3,2,1,0:T(8,128)(2,1)}, u32[]{:S(2)}, u32[]{:S(2)}) async-start(bf16[4,4,120,768]{3,2,1,0:T(8,128)(2,1)} %bitcast.170), calls=%async_computation | async-start | bytes 5898240 | tf_op jit(solution)/shard_map/all_to_all | solution.py:135
  137.5 307.8 %reduce-scatter.15.cloned.1.call-start = ((), (), s32[]{:S(2)}) async-start(), calls=%async_computation.15 | async-start | bytes 3538944 | tf_op jit(solution)/shard_map/reduce_scatter | solution.py:271
  173.5 40.3 %all-to-all-start.2 = ((bf16[4,4,120,768]{3,2,1,0:T(8,128)(2,1)}), bf16[4,4,120,768]{3,2,1,0:T(8,128)(2,1)}, u32[]{:S(2)}, u32[]{:S(2)}) async-start(bf16[4,4,120,768]{3,2,1,0:T(8,128)(2,1)} %bitcast.171), calls=%async_computation.2 | async-start | bytes 5898240 | tf_op jit(solution)/shard_map/all_to_all | solution.py:157
  272.1 38.5 %all-to-all-start.3 = ((bf16[4,4,120,768]{3,2,1,0:T(8,128)(2,1)}), bf16[4,4,120,768]{3,2,1,0:T(8,128)(2,1)}, u32[]{:S(2)}, u32[]{:S(2)}) async-start(bf16[4,4,120,768]{3,2,1,0:T(8,128)(2,1)} %copy.57), calls=%async_computation.3 | async-start | bytes 5898240 | tf_op jit(solution)/shard_map/all_to_all | solution.py:180
  276.7 168.6 %reduce-scatter.17.cloned.1.call-start = ((), (), s32[]{:S(2)}) async-start(), calls=%async_computation.16 | async-start | bytes 3538944 | tf_op jit(solution)/shard_map/reduce_scatter | solution.py:274
  283.3 171.7 %reduce-scatter.11.cloned.1.call-start = ((), (), s32[]{:S(2)}) async-start(), calls=%async_computation.13 | async-start | bytes 1327104 | tf_op jit(solution)/shard_map/reduce_scatter | solution.py:262
  329.6 9.4 copy-start.27
  329.7 9.4 copy-start.32
  339.0 8.6 copy-start.2
  339.0 8.6 copy-start.6
  351.9 3.1 copy-start.20
  355.0 23.3 %copy-start.10 = (bf16[768,768]{0,1:T(8,128)(2,1)}, bf16[768,768]{0,1:T(8,128)(2,1)S(1)}, u32[]{:S(2)}) copy-start(bf16[768,768]{0,1:T(8,128)(2,1)S(1)} %convolution_convert_fusion.5) | copy-start | bytes 3538948
  401.6 11.2 %copy-start.14 = (bf16[768,12,32]{0,2,1:T(8,128)(2,1)S(1)}, bf16[768,12,32]{0,2,1:T(8,128)(2,1)}, u32[]{:S(2)}) copy-start(bf16[768,12,32]{0,2,1:T(8,128)(2,1)} %copy-done.13) | copy-start | bytes 1769476
  401.6 11.2 %copy-start.16 = (bf16[768,12,32]{0,2,1:T(8,128)(2,1)S(1)}, bf16[768,12,32]{0,2,1:T(8,128)(2,1)}, u32[]{:S(2)}) copy-start(bf16[768,12,32]{0,2,1:T(8,128)(2,1)} %copy-done.15) | copy-start | bytes 1769476
  421.9 77.3 %reduce-scatter.9.cloned.1.call-start = ((), (), s32[]{:S(2)}) async-start(), calls=%async_computation.12 | async-start | bytes 3981312 | tf_op jit(solution)/shard_map/reduce_scatter | solution.py:259
  438.1 2.2 copy-start.9
  438.1 2.2 copy-start.34
  438.1 2.2 copy-start.38
  445.2 234.4 %all-reduce.11.cloned.1.call-start = ((), (), s32[]{:S(2)}) async-start(), calls=%async_computation.20 | async-start | bytes 3538944 | tf_op jit(solution)/shard_map/psum | solution.py:280
  499.3 223.9 %reduce-scatter.23.cloned.1.call-start = ((), (), s32[]{:S(2)}) async-start(), calls=%async_computation.19 | async-start | bytes 14155776 | tf_op jit(solution)/shard_map/reduce_scatter | solution.py:190
  512.2 341.0 %reduce-scatter.19.cloned.1.call-start = ((), (), s32[]{:S(2)}) async-start(), calls=%async_computation.17 | async-start | bytes 14155776 | tf_op jit(solution)/shard_map/reduce_scatter | solution.py:184
  525.0 458.2 %reduce-scatter.21.cloned.1.call-start = ((), (), s32[]{:S(2)}) async-start(), calls=%async_computation.18 | async-start | bytes 14155776 | tf_op jit(solution)/shard_map/reduce_scatter | solution.py:187
  552.6 45.6 %all-to-all-start.1 = ((bf16[4,4,120,768]{3,2,1,0:T(8,128)(2,1)}), bf16[4,4,120,768]{3,2,1,0:T(8,128)(2,1)}, u32[]{:S(2)}, u32[]{:S(2)}) async-start(bf16[4,4,120,768]{3,2,1,0:T(8,128)(2,1)} %copy.53), calls=%async_computation.1 | async-start | bytes 5898240 | tf_op jit(solution)/shard_map/all_to_all | solution.py:146
  617.5 7.7 copy-start.39
  679.5 5.7 copy-start.23
  679.5 6.6 copy-start.22
  (10 other events, 11.9 us)
Sparse Core Ops, SparseCore 0:
  77.9 43.0 reduce-scatter.12
  144.4 42.9 reduce-scatter.14
  283.4 42.1 reduce-scatter.16
  422.0 32.8 reduce-scatter.10
  457.1 42.0 reduce-scatter.8
  503.2 87.7 all-reduce.10
  593.4 129.6 reduce-scatter.22
  725.6 127.5 reduce-scatter.18
  855.6 127.5 reduce-scatter.20
where the time goes:
time: 1000 us; the launch traced here: 993 us
  waiting for transfers between devices  406 us (41%)
  matrix products  296 us (30%)
  local copies, waits for them, and re-layouts  121 us (12%)
  other arithmetic  105 us (10%)
  blocking collectives  28 us (3%)
  starting transfers between devices  20.3 us (2%)
  between operations  16.3 us (2%)
    reduce_scatter x1, waiting for transfers between devices, shards(): lax.psum_scatter(gate_w_grad.astype(jnp.bfloat16), 'dp', scatter_dimensio...  127 us
    reduce_scatter x1, waiting for transfers between devices, shards(): lax.psum_scatter(up_w_grad.astype(jnp.bfloat16), 'dp', scatter_dimension=...  127 us
    reduce_scatter x1, waiting for transfers between devices, shards(): lax.psum_scatter(qkv_weight_grad.astype(jnp.bfloat16), 'dp', scatter_dime...  44.3 us
    all_to_all x1, waiting for transfers between devices, shards(): lax.all_to_all(expert_result, 'expert', split_axis=0, concat_axis=0, tile...  38.8 us
    reduce_scatter x1, waiting for transfers between devices, shards(): lax.psum_scatter(down_w_grad.astype(jnp.bfloat16), 'dp', scatter_dimensio...  36.1 us
    dot_general x5, matrix products, contract_last(): lax.dot_general(left_side, right_side, (((1,), (1,)), ((), ())), preferre...  33.8 us
    dot_general x5, matrix products, contract_rows(): lax.dot_general(left_side, right_side, (((0,), (0,)), ((), ())), preferre...  26.1 us
    dot_general x1, matrix products, shards(): jnp.einsum('slcd,lfd->slcf', slot_grad_in, expert_down, preferred_element...  25.5 us
  transfers between devices with their start and end apart: 13, of which 8 were waited for; matrix products, arithmetic and copies ran while one was open for 45% of the time, Pallas kernels for 0%

commit v1 on v0

v1 whole, which is shorter than its diff:
```python
import jax
import jax.numpy as jnp
from jax import lax
from jax.experimental import pallas as pl
from jax.experimental.pallas import tpu as pltpu
from jax.sharding import PartitionSpec as P

f32=jnp.float32; bf16=jnp.bfloat16
def nn(a,b): return lax.dot_general(a,b,(((1,),(0,)),((),())),preferred_element_type=f32)
def nt(a,b): return lax.dot_general(a,b,(((1,),(1,)),((),())),preferred_element_type=f32)
def tn(a,b): return lax.dot_general(a,b,(((0,),(0,)),((),())),preferred_element_type=f32)
EPS=1e-6
HD=64; GH=4; GW=GH*HD; QC=256
def lane_head(shape):
    return lax.broadcasted_iota(jnp.int32,shape,1)//HD
def swap_half(x):
    w=x.shape[1]
    first=(lax.broadcasted_iota(jnp.int32,x.shape,1)%HD)<HD//2
    return jnp.where(first,pltpu.roll(x,w-HD//2,1),pltpu.roll(x,HD//2,1))
def wide(t):
    return jnp.concatenate([t,t],axis=1)
def inv_rms(v):
    return lax.rsqrt(jnp.mean(v*v,axis=1,keepdims=True)+EPS)

def attn_fwd(tokens, prefix, again, wqkv, wo, fgain, cosw, sinw):
    T,D=tokens.shape
    ng=D//GW; nq=T//QC
    def kernel(pre,tok,ag,fg,wq,wk,wv,wor,cw,sw,qo,ko,vo,atto,lseo,stateo,ntwoo,normed,bias,q4,k4,vT,OT,acc):
        g=pl.program_id(0)
        @pl.when(g==0)
        def _():
            for c in range(nq):
                r=slice(c*QC,(c+1)*QC)
                x=tok[r,:].astype(f32)
                normed[r,:]=(x*inv_rms(x)*ag[...]).astype(bf16)
                j=lax.broadcasted_iota(jnp.int32,(T,QC),0)
                i=lax.broadcasted_iota(jnp.int32,(T,QC),1)+c*QC
                bias[c]=jnp.where((j<=i)|(j<pre[0]),0.0,-1e30)
        for c in range(nq):
            r=slice(c*QC,(c+1)*QC)
            n=normed[r,:]
            C=wide(cw[r,:]); S=wide(sw[r,:])
            q=nn(n,wq[...]); k=nn(n,wk[...]); v=nn(n,wv[...])
            qb=((q*C+swap_half(q)*S).astype(bf16)).astype(f32)*(HD**-0.5)
            qb=qb.astype(bf16)
            kb=(k*C+swap_half(k)*S).astype(bf16)
            q4[r,:]=qb; qo[r,:]=qb
            k4[r,:]=kb; ko[r,:]=kb
            vo[r,:]=v.astype(bf16)
            vT[:,r]=v.T.astype(bf16)
        lh=lane_head((QC,GW))
        @pl.loop(0,GH)
        def _(h):
            hr=pl.ds(pl.multiple_of(h*HD,HD),HD)
            for c in range(nq):
                r=slice(c*QC,(c+1)*QC)
                qm=jnp.where(lh==h,q4[r,:],jnp.zeros((),bf16))
                st=nt(k4[...],qm)+bias[c]
                m=jnp.max(st,axis=0,keepdims=True)
                p=jnp.exp(st-m)
                l=jnp.sum(p,axis=0,keepdims=True)
                ot=nn(vT[hr,:],p.astype(bf16))
                OT[c,hr,:]=ot*(1.0/l)
                lseo[0,pl.ds(h,1),r]=m+jnp.log(l)
        for c in range(nq):
            r=slice(c*QC,(c+1)*QC)
            a=OT[c].T.astype(bf16)
            atto[r,:]=a
            o=nn(a,wor[...])
            @pl.when(g==0)
            def _(): acc[r,:]=o+tok[r,:].astype(f32)
            @pl.when(g>0)
            def _(): acc[r,:]+=o
        @pl.when(g==ng-1)
        def _():
            for c in range(nq):
                r=slice(c*QC,(c+1)*QC)
                st=acc[r,:]
                stateo[r,:]=st
                ntwoo[r,:]=(st*inv_rms(st)*fg[...]).astype(bf16)
    full=lambda s: pl.BlockSpec(s,lambda g:(0,)*len(s))
    col=lambda off: pl.BlockSpec((D,GW),lambda g,off=off:(0,g+off))
    tcol=pl.BlockSpec((T,GW),lambda g:(0,g))
    return pl.pallas_call(kernel,grid=(ng,),
      in_specs=[pl.BlockSpec(memory_space=pltpu.SMEM),full((T,D)),full((1,D)),full((1,D)),col(0),col(ng),col(2*ng),pl.BlockSpec((GW,D),lambda g:(g,0)),full((T,128)),full((T,128))],
      out_specs=[tcol,tcol,tcol,tcol,pl.BlockSpec((1,8,T),lambda g:(g,0,0)),full((T,D)),full((T,D))],
      out_shape=[jax.ShapeDtypeStruct((T,D),bf16)]*4+[jax.ShapeDtypeStruct((ng,8,T),f32),jax.ShapeDtypeStruct((T,D),f32),jax.ShapeDtypeStruct((T,D),bf16)],
      scratch_shapes=[pltpu.VMEM((T,D),bf16),pltpu.VMEM((nq,T,QC),f32),pltpu.VMEM((T,GW),bf16),pltpu.VMEM((T,GW),bf16),pltpu.VMEM((GW,T),bf16),pltpu.VMEM((nq,GW,QC),f32),pltpu.VMEM((T,D),f32)],
      compiler_params=pltpu.CompilerParams(vmem_limit_bytes=56<<20,dimension_semantics=("arbitrary",)),
      cost_estimate=pl.CostEstimate(flops=2*T*D*4*D+4*T*T*D,bytes_accessed=16<<20,transcendentals=12*T*T),
      name="attn_fwd")(prefix,tokens,again[None],fgain[None],wqkv,wqkv,wqkv,wo,cosw,sinw)

def attn_bwd(sgrad, prefix, tokens, again, wqkv, wo, cosw, sinw, q, k, v, att, lse):
    T,D=tokens.shape
    ng=D//GW; nq=T//QC
    def kernel(pre,sg,tok,ag,wq,wk,wv,wor,cw,sw,qr,kr,vr,attr,lser,tgo,ggo,gq,gk,gv,gwo,normed,normedT,bg,bias,dO,kT,PB,DS,dv,dk,dqT,drow,acc):
        g=pl.program_id(0)
        @pl.when(g==0)
        def _():
            for c in range(nq):
                r=slice(c*QC,(c+1)*QC)
                x=tok[r,:].astype(f32)
                n=x*inv_rms(x)*ag[...]
                normedT[:,r]=n.T.astype(bf16)
                bg[r,:]=sg[r,:].astype(bf16)
                j=lax.broadcasted_iota(jnp.int32,(T,QC),0)
                i=lax.broadcasted_iota(jnp.int32,(T,QC),1)+c*QC
                bias[c]=jnp.where((j<=i)|(j<pre[0]),0.0,-1e30)
        hmask=(lax.broadcasted_iota(jnp.int32,(8,GW),0)==lane_head((8,GW))).astype(f32)
        for c in range(nq):
            r=slice(c*QC,(c+1)*QC)
            d=nt(bg[r,:],wor[...]).astype(bf16)
            dO[r,:]=d
            a=attr[r,:].astype(f32)
            drow[:,r]=lax.dot_general(hmask,d.astype(f32)*a,(((1,),(1,)),((),())),preferred_element_type=f32,precision=lax.Precision.HIGHEST)
            kT[:,r]=kr[r,:].astype(f32).T.astype(bf16)
        gwo[...]=tn(attr[...],bg[...]).astype(bf16)
        dv[...]=jnp.zeros_like(dv); dk[...]=jnp.zeros_like(dk)
        lh=lane_head((QC,GW)); lhT=lane_head((T,GW))
        @pl.loop(0,GH)
        def _(h):
            hr=pl.ds(pl.multiple_of(h*HD,HD),HD)
            zero=jnp.zeros((),bf16)
            for c in range(nq):
                r=slice(c*QC,(c+1)*QC)
                qm=jnp.where(lh==h,qr[r,:],zero)
                dOm=jnp.where(lh==h,dO[r,:],zero)
                st=nt(kr[...],qm)+bias[c]
                p=jnp.exp(st-lser[0,pl.ds(h,1),r])
                PB[:,r]=p.astype(bf16)
                dp=nt(vr[...],dOm)
                DS[:,r]=(p*(dp-drow[pl.ds(h,1),r])).astype(bf16)
            dv[...]+=nn(PB[...],jnp.where(lhT==h,dO[...],zero))
            dk[...]+=nn(DS[...],jnp.where(lhT==h,qr[...],zero))
            dqT[hr,:]=nn(kT[hr,:],DS[...])
        for c in range(nq):
            r=slice(c*QC,(c+1)*QC)
            C=wide(cw[r,:]); S=wide(sw[r,:])
            dq=dqT[:,r].T*(HD**-0.5)
            dq=dq*C-swap_half(dq)*S
            dkk=dk[r,:]
            dkk=dkk*C-swap_half(dkk)*S
            a=dq.astype(bf16); b=dkk.astype(bf16); e=dv[r,:].astype(bf16)
            PB[r,0:GW]=a; PB[r,GW:2*GW]=b; PB[r,2*GW:3*GW]=e
            o=nt(a,wq[...])+nt(b,wk[...])+nt(e,wv[...])
            @pl.when(g==0)
            def _(): acc[r,:]=o
            @pl.when(g>0)
            def _(): acc[r,:]+=o
        gq[...]=nn(normedT[...],PB[:,0:GW]).astype(bf16)
        gk[...]=nn(normedT[...],PB[:,GW:2*GW]).astype(bf16)
        gv[...]=nn(normedT[...],PB[:,2*GW:3*GW]).astype(bf16)
        @pl.when(g==ng-1)
        def _():
            gg=jnp.zeros((1,D),f32)
            for c in range(nq):
                r=slice(c*QC,(c+1)*QC)
                x=tok[r,:].astype(f32)
                inv=inv_rms(x); u=x*inv
                ngd=acc[r,:]
                gg=gg+jnp.sum(ngd*u,axis=0,keepdims=True)
                w=ngd*ag[...]
                tgo[r,:]=(sg[r,:]+inv*(w-u*jnp.mean(w*u,axis=1,keepdims=True))).astype(bf16)
            ggo[...]=jnp.broadcast_to(gg,(8,D))
    full=lambda s: pl.BlockSpec(s,lambda g:(0,)*len(s))
    col=lambda off: pl.BlockSpec((D,GW),lambda g,off=off:(0,g+off))
    tcol=pl.BlockSpec((T,GW),lambda g:(0,g))
    rowb=pl.BlockSpec((GW,D),lambda g:(g,0))
    return pl.pallas_call(kernel,grid=(ng,),
      in_specs=[pl.BlockSpec(memory_space=pltpu.SMEM),full((T,D)),full((T,D)),full((1,D)),col(0),col(ng),col(2*ng),rowb,full((T,128)),full((T,128)),tcol,tcol,tcol,tcol,pl.BlockSpec((1,8,T),lambda g:(g,0,0))],
      out_specs=[full((T,D)),full((8,D)),tcol,tcol,tcol,rowb],
      out_shape=[jax.ShapeDtypeStruct((T,D),bf16),jax.ShapeDtypeStruct((8,D),f32)]+[jax.ShapeDtypeStruct((D,D),bf16)]*4,
      scratch_shapes=[pltpu.VMEM((T,D),bf16),pltpu.VMEM((D,T),bf16),pltpu.VMEM((T,D),bf16),pltpu.VMEM((nq,T,QC),f32),pltpu.VMEM((T,GW),bf16),pltpu.VMEM((GW,T),bf16),
        pltpu.VMEM((T,T),bf16),pltpu.VMEM((T,T),bf16),pltpu.VMEM((T,GW),f32),pltpu.VMEM((T,GW),f32),pltpu.VMEM((GW,T),f32),pltpu.VMEM((8,T),f32),pltpu.VMEM((T,D),f32)],
      compiler_params=pltpu.CompilerParams(vmem_limit_bytes=60<<20,dimension_semantics=("arbitrary",)),
      cost_estimate=pl.CostEstimate(flops=2*T*D*8*D+10*T*T*D,bytes_accessed=24<<20,transcendentals=12*T*T),
      name="attn_bwd")(prefix,sgrad,tokens,again[None],wqkv,wqkv,wqkv,wo,cosw,sinw,q,k,v,att,lse)


def make_ffn(parts, G, L, cap, D, FF, FB, chunk, out_dt):
    R=parts*G*cap
    nf=FF//FB
    def kernel(*refs):
        xs=refs[:parts]; ss=refs[parts:2*parts]
        wg,wu,wd=refs[2*parts:2*parts+3]
        o=2*parts+3
        res=refs[o:o+parts]; dgr=refs[o+parts:o+2*parts]
        gG,gU,gD=refs[o+2*parts:o+2*parts+3]
        X,S,H,GB,UB,AR,AD=refs[o+2*parts+3:]
        f=pl.program_id(1)
        @pl.when(f==0)
        def _():
            for p in range(parts):
                for g in range(G):
                    r=(p*G+g)*cap
                    X[r:r+cap,:]=xs[p][g,0]
                    S[r:r+cap,:]=ss[p][g,0]
        @pl.loop(0,R//chunk)
        def _(i):
            rows=pl.ds(pl.multiple_of(i*chunk,chunk),chunk)
            x=X[rows,:]; s=S[rows,:]
            gate=nn(x,wg[0]); up=nn(x,wu[0]); hg=nt(s,wd[0])
            sig=1.0/(1.0+jnp.exp(-gate))
            sil=gate*sig
            h=(sil*up).astype(bf16)
            gb=(hg*up*(sig*(1.0+gate*(1.0-sig)))).astype(bf16)
            ub=(hg*sil).astype(bf16)
            H[rows,:]=h; GB[rows,:]=gb; UB[rows,:]=ub
            r=nn(h,wd[0]); d=nt(gb,wg[0])+nt(ub,wu[0])
            @pl.when(f==0)
            def _():
                AR[rows,:]=r; AD[rows,:]=d
            @pl.when(f>0)
            def _():
                AR[rows,:]+=r; AD[rows,:]+=d
        gG[0]=tn(X[...],GB[...]).astype(bf16)
        gU[0]=tn(X[...],UB[...]).astype(bf16)
        gD[0]=tn(H[...],S[...]).astype(bf16)
        @pl.when(f==nf-1)
        def _():
            for p in range(parts):
                for g in range(G):
                    r=(p*G+g)*cap
                    res[p][g,0]=AR[r:r+cap,:].astype(out_dt)
                    dgr[p][g,0]=AD[r:r+cap,:].astype(out_dt)
    rowspec=pl.BlockSpec((G,1,cap,D),lambda l,f:(0,l,0,0))
    wspec=pl.BlockSpec((1,D,FB),lambda l,f:(l,0,f))
    wdspec=pl.BlockSpec((1,FB,D),lambda l,f:(l,f,0))
    call=pl.pallas_call(kernel,
      out_shape=[jax.ShapeDtypeStruct((G,L,cap,D),out_dt)]*(2*parts)+[jax.ShapeDtypeStruct((L,D,FF),bf16)]*2+[jax.ShapeDtypeStruct((L,FF,D),bf16)],
      grid=(L,nf),
      in_specs=[rowspec]*(2*parts)+[wspec,wspec,wdspec],
      out_specs=[rowspec]*(2*parts)+[wspec,wspec,wdspec],
      scratch_shapes=[pltpu.VMEM((R,D),bf16)]*2+[pltpu.VMEM((R,FB),bf16)]*3+[pltpu.VMEM((R,D),f32)]*2,
      compiler_params=pltpu.CompilerParams(vmem_limit_bytes=60<<20,dimension_semantics=("arbitrary","arbitrary")),
      cost_estimate=pl.CostEstimate(flops=2*9*R*D*FF*L,bytes_accessed=L*(6*D*FF*2+4*R*D*2),transcendentals=R*FF*L),
      name="ffn")
    return call

E=16; CAP=120

def route(order, expert_ids, gates, cot, core, G, L, parts):
    T,D=cot.shape; P2=2*T
    LP=L//parts; S=G*LP*CAP
    big=E*CAP
    CH=480 if S%480==0 else CAP*4
    def kernel(core_ref,orow,ids,gts,ct,rowo,colo,*rest):
        sgs=rest[:parts]; PT,PG=rest[parts:]
        lane=lax.broadcasted_iota(jnp.int32,(T,128),1)
        e0=ids[:,0:1].astype(f32); e1=ids[:,1:2].astype(f32)
        er=jnp.where(lane==0,e0,jnp.where(lane==1,e1,0.0)).T[0:8,:]
        ecat=jnp.concatenate([er[0:1,:],er[1:2,:]],axis=1)
        eoh=(lax.broadcasted_iota(jnp.int32,(E,P2),0).astype(f32)==ecat)
        eohb=jnp.where(eoh,1.0,0.0).astype(bf16)
        o=orow[...]
        oj=(o&1)*T+(o>>1)
        CB=256
        for c in range(P2//CB):
            jj=lax.broadcasted_iota(jnp.int32,(CB,P2),0)+c*CB
            PT[c*CB:(c+1)*CB,:]=jnp.where(jj==oj,1.0,0.0).astype(bf16)
        soh=nn(eohb,PT[...])
        sohb=soh.astype(bf16)
        tri=jnp.where(lax.broadcasted_iota(jnp.int32,(CB,CB),0)<lax.broadcasted_iota(jnp.int32,(CB,CB),1),1.0,0.0).astype(bf16)
        run=jnp.zeros((E,1),f32)
        pos=[]
        for c in range(P2//CB):
            blk=soh[:,c*CB:(c+1)*CB]
            before=nn(sohb[:,c*CB:(c+1)*CB],tri)+run
            run=run+jnp.sum(blk,axis=1,keepdims=True)
            pos.append(jnp.sum(before*blk,axis=0,keepdims=True))
        posr=jnp.minimum(jnp.concatenate(pos,axis=1),127.0)
        posj=nt(jnp.broadcast_to(posr,(16,P2)).astype(bf16),PT[...])[0:1,:]
        e=ecat.astype(jnp.int32)
        l=lax.rem(e,L); j=lax.div(e,L)
        if parts==2:
            cc=lax.rem(lax.div(l,LP)+core_ref[0],2)
            base=((cc*G+j)*LP+lax.rem(l,LP))*CAP
        else:
            base=e*CAP
        p=posj.astype(jnp.int32)
        slot=jnp.where(p<CAP,base+p,big)
        s0=slot[:,0:T]; s1=slot[:,T:P2]
        r8=lax.broadcasted_iota(jnp.int32,(8,T),0)
        rows=jnp.where(r8==0,s0,jnp.where(r8==1,s1,big))
        rowo[...]=rows
        rep=jnp.concatenate([rows.astype(f32)]*16,axis=0).T
        colo[...]=rep[:,0:8].astype(jnp.int32)
        ctf=ct[...].astype(f32)
        PG[0:T,:]=(gts[:,0:1]*ctf).astype(bf16)
        PG[T:P2,:]=(gts[:,1:2]*ctf).astype(bf16)
        for pi in range(parts):
            @pl.loop(0,S//CH)
            def _(i):
                si=lax.broadcasted_iota(jnp.int32,(CH,T),0)+(i*CH+pi*S)
                d0=jnp.where(si==rowo[0:1,:],1.0,0.0).astype(bf16)
                d1=jnp.where(si==rowo[1:2,:],1.0,0.0).astype(bf16)
                sgs[pi][pl.ds(pl.multiple_of(i*CH,CH),CH),:]=(nn(d0,PG[0:T,:])+nn(d1,PG[T:P2,:])).astype(bf16)
    vm=pl.BlockSpec(memory_space=pltpu.VMEM)
    out=pl.pallas_call(kernel,
      in_specs=[pl.BlockSpec(memory_space=pltpu.SMEM)]+[vm]*4,out_specs=[vm]*(2+parts),
      out_shape=[jax.ShapeDtypeStruct((8,T),jnp.int32),jax.ShapeDtypeStruct((T,8),jnp.int32)]+[jax.ShapeDtypeStruct((S,D),bf16)]*parts,
      scratch_shapes=[pltpu.VMEM((P2,P2),bf16),pltpu.VMEM((P2,D),bf16)],
      compiler_params=pltpu.CompilerParams(vmem_limit_bytes=50<<20),
      cost_estimate=pl.CostEstimate(flops=4*S*parts*T*D+4*P2*P2*16,bytes_accessed=8<<20,transcendentals=0),
      name="route")(core,order,expert_ids,gates,cot)
    return out[0],out[1],out[2:]

def dispatch(rows, x, parts):
    T,D=x.shape; S=E*CAP//parts; CH=480
    def kernel(rowr,xr,*outs):
        for pi in range(parts):
            @pl.loop(0,S//CH)
            def _(i):
                si=lax.broadcasted_iota(jnp.int32,(CH,T),0)+(i*CH+pi*S)
                d=jnp.where((si==rowr[0:1,:])|(si==rowr[1:2,:]),1.0,0.0).astype(bf16)
                outs[pi][pl.ds(pl.multiple_of(i*CH,CH),CH),:]=nn(d,xr[...]).astype(bf16)
    vm=pl.BlockSpec(memory_space=pltpu.VMEM)
    return pl.pallas_call(kernel,in_specs=[vm]*2,out_specs=[vm]*parts,out_shape=[jax.ShapeDtypeStruct((S,D),bf16)]*parts,
      compiler_params=pltpu.CompilerParams(vmem_limit_bytes=50<<20),
      cost_estimate=pl.CostEstimate(flops=2*S*parts*T*D,bytes_accessed=6<<20,transcendentals=0),name="dispatch")(rows,x)

def combine(cols, gates, ret, state, shared):
    parts=len(ret); T,D=state.shape; S=ret[0].shape[0]
    def kernel(colr,g,*refs):
        rs=refs[:parts]; st,sh,out=refs[parts:]
        @pl.loop(0,T//QC)
        def _(i):
            r=pl.ds(pl.multiple_of(i*QC,QC),QC)
            acc=st[r,:]+sh[r,:]
            for k in range(2):
                pk=None
                for pi in range(parts):
                    si=lax.broadcasted_iota(jnp.int32,(QC,S),1)+pi*S
                    d=jnp.where(si==colr[r,k:k+1],1.0,0.0).astype(bf16)
                    q=nn(d,rs[pi][...])
                    pk=q if pk is None else pk+q
                acc=acc+g[r,k:k+1]*pk
            out[r,:]=acc.astype(bf16)
    vm=pl.BlockSpec(memory_space=pltpu.VMEM)
    return pl.pallas_call(kernel,in_specs=[vm]*(4+parts),out_specs=vm,out_shape=jax.ShapeDtypeStruct((T,D),bf16),
      compiler_params=pltpu.CompilerParams(vmem_limit_bytes=50<<20),
      cost_estimate=pl.CostEstimate(flops=4*S*parts*T*D,bytes_accessed=9<<20,transcendentals=0),name="combine")(cols,gates,*ret,state,shared)

def mid_bwd(cols, back, dsh, state, fgain, cot):
    parts=len(back); T,D=state.shape; S=back[0].shape[0]
    def kernel(colr,*refs):
        bs=refs[:parts]; ds,st,fg,ct,sgo,fgo=refs[parts:]
        fgo[...]=jnp.zeros_like(fgo)
        @pl.loop(0,T//QC)
        def _(i):
            r=pl.ds(pl.multiple_of(i*QC,QC),QC)
            n=ds[r,:]
            for pi in range(parts):
                si=lax.broadcasted_iota(jnp.int32,(QC,S),1)+pi*S
                d=jnp.where((si==colr[r,0:1])|(si==colr[r,1:2]),1.0,0.0).astype(bf16)
                n=n+nn(d,bs[pi][...])
            x=st[r,:]; inv=inv_rms(x); u=x*inv
            fgo[...]+=jnp.broadcast_to(jnp.sum(n*u,axis=0,keepdims=True),(8,D))
            w=n*fg[...]
            sgo[r,:]=ct[r,:].astype(f32)+inv*(w-u*jnp.mean(w*u,axis=1,keepdims=True))
    vm=pl.BlockSpec(memory_space=pltpu.VMEM)
    return pl.pallas_call(kernel,in_specs=[vm]*(5+parts),out_specs=[vm]*2,out_shape=[jax.ShapeDtypeStruct((T,D),f32),jax.ShapeDtypeStruct((8,D),f32)],
      compiler_params=pltpu.CompilerParams(vmem_limit_bytes=50<<20),
      cost_estimate=pl.CostEstimate(flops=2*S*parts*T*D,bytes_accessed=12<<20,transcendentals=0),name="mid_bwd")(cols,*back,dsh,state,fgain[None],cot)

HEADS = 12
HEAD_DIM = 64


def rope_wide(length):
    positions = jnp.arange(length, dtype=f32)
    frequency = 10000.0 ** (-jnp.arange(HEAD_DIM // 2, dtype=f32) * 2.0 / HEAD_DIM)
    angles = positions[:, None] * frequency[None, :]
    c = jnp.cos(angles)
    s = jnp.sin(angles)
    return jnp.concatenate([c, c, c, c], axis=1), jnp.concatenate([-s, s, -s, s], axis=1)


def shards(tokens, cotangent, expert_ids, route_gates, slot_order, prefix_len, attention_gain, qkv_weight,
           output_weight, feedforward_gain, shared_gate, shared_up, shared_down, expert_gate, expert_up, expert_down):
    T, D = tokens.shape
    L, _, FF = expert_gate.shape
    G = lax.axis_size("expert")
    DP = lax.axis_size("dp")
    Z = DP // 2
    parts = 2 if L % 2 == 0 else 1
    LP = L // parts
    dpi = lax.axis_index("dp")
    core = lax.rem(dpi, 2)
    swap_perm = [(i, i ^ 1) for i in range(DP)]
    zgroups = [[2 * z + c for z in range(Z)] for c in range(2)]

    def swap(x):
        return lax.ppermute(x, "dp", swap_perm)

    def a2a(x):
        return lax.all_to_all(x, "expert", split_axis=0, concat_axis=0, tiled=True)

    def to_experts(arrs):
        arrs = [a.reshape(G, LP, CAP, D) for a in arrs]
        if parts == 2:
            arrs = [arrs[0], swap(arrs[1])]
        return [a2a(a) for a in arrs]

    def from_experts(arrs):
        arrs = [a2a(a) for a in arrs]
        if parts == 2:
            arrs = [arrs[0], swap(arrs[1])]
        return [a.reshape(G * LP * CAP, D) for a in arrs]

    cosw, sinw = rope_wide(T)
    rows, cols, sgs = route(slot_order, expert_ids, route_gates, cotangent, core[None].astype(jnp.int32), G, L, parts)
    slot_in = to_experts(sgs)
    q, k, v, att, lse, state, ntwo = attn_fwd(tokens, prefix_len, attention_gain, qkv_weight, output_weight,
                                              feedforward_gain, cosw, sinw)
    xs = dispatch(rows, ntwo, parts)
    x_in = to_experts(xs)
    sh = make_ffn(1, 1, 1, T, D, FF, 512, T // 2, f32)(
        ntwo[None, None], cotangent[None, None], shared_gate[None], shared_up[None], shared_down[None])
    shared_branch = sh[0].reshape(T, D)
    dshared = sh[1].reshape(T, D)
    dense_shared = [sh[2][0], sh[3][0], sh[4][0]]

    res, dgr, eg = [], [], []
    one = make_ffn(parts, G, 1, CAP, D, FF, 512, parts * G * CAP // 2, bf16)
    for l in range(LP):
        o = one(*[a[:, l:l + 1] for a in x_in], *[a[:, l:l + 1] for a in slot_in],
                *[lax.dynamic_slice_in_dim(w, (core * LP if parts == 2 else 0) + l, 1, 0)
                  for w in (expert_gate, expert_up, expert_down)])
        res.append(o[:parts])
        dgr.append(o[parts:2 * parts])
        eg.append(o[2 * parts:])
    cat = lambda xs_: jnp.concatenate(xs_, axis=1) if len(xs_) > 1 else xs_[0]
    res = [cat([r[p] for r in res]) for p in range(parts)]
    dgr = [cat([r[p] for r in dgr]) for p in range(parts)]

    egr = []
    for l in range(LP):
        if parts == 2:
            egr.append([lax.psum_scatter(g[0], "dp", scatter_dimension=0, tiled=True, axis_index_groups=zgroups)
                        for g in eg[l]])
        else:
            egr.append([lax.psum_scatter(g[0], "dp", scatter_dimension=0, tiled=True) for g in eg[l]])

    back = from_experts(dgr)
    ret = from_experts(res)
    sgrad, fgg = mid_bwd(cols, back, dshared, state, feedforward_gain, cotangent)
    tokens_grad, agg, gq, gk, gv, gwo = attn_bwd(sgrad, prefix_len, tokens, attention_gain, qkv_weight, output_weight,
                                                 cosw, sinw, q, k, v, att, lse)
    block_out = combine(cols, route_gates, ret, state, shared_branch)

    def dense(g):
        r = g.shape[0] // DP
        h = g.reshape(Z, 2, r, g.shape[1])
        mine = lax.dynamic_index_in_dim(h, core, 1, keepdims=False)
        other = lax.dynamic_index_in_dim(h, 1 - core, 1, keepdims=False)
        s = (mine.astype(f32) + swap(other).astype(f32)).astype(bf16)
        quarter = s.reshape(Z, G, r // G, g.shape[1])
        quarter = jnp.swapaxes(quarter, 0, 1)
        got = lax.all_to_all(quarter, "expert", split_axis=0, concat_axis=0, tiled=True)
        s = jnp.sum(got.astype(f32), axis=0).astype(bf16)
        zs = lax.psum_scatter(s, "dp", scatter_dimension=0, tiled=True, axis_index_groups=zgroups)
        return lax.all_gather(zs[0], "expert", axis=0, tiled=True).astype(f32)

    def dense_simple(g):
        p = lax.psum_scatter(g, "dp", scatter_dimension=0, tiled=True)
        return lax.psum(p, "expert").astype(f32)

    if (qkv_weight.shape[0] // DP) % (8 * G) == 0 and parts == 2:
        dn = dense
    else:
        dn = dense_simple
    dsh = [dn(g) for g in dense_shared]
    dq, dk, dv, dwo = [dn(g) for g in (gq, gk, gv, gwo)]
    gains = lax.psum(jnp.stack([agg[0], fgg[0]]), ("dp", "expert"))
    gs = D // DP
    gains = lax.dynamic_slice_in_dim(gains, dpi * gs, gs, 1)

    def finish(t):
        a = [egr[l][t] for l in range(LP)]
        if parts == 1:
            return jnp.stack(a).astype(f32)
        b = jnp.stack(a)
        h = b.reshape(LP, 2, b.shape[1] // 2, b.shape[2])
        mine = lax.dynamic_index_in_dim(h, core, 1, keepdims=False)
        other = swap(lax.dynamic_index_in_dim(h, 1 - core, 1, keepdims=False))
        return jnp.concatenate([jnp.where(core == 0, mine, other), jnp.where(core == 0, other, mine)], axis=0).astype(f32)

    return (block_out, tokens_grad, gains[0], jnp.concatenate([dq, dk, dv], axis=1), dwo, gains[1],
            dsh[0], dsh[1], dsh[2], finish(0), finish(1), finish(2))


def solution(mesh):
    row = P(("dp", "expert"), None)
    return jax.shard_map(
        shards,
        mesh=mesh,
        in_specs=(row, row, row, row, row, P(("dp", "expert")), P(), P(), P(), P(), P(), P(), P(),
                  P("expert", None, None), P("expert", None, None), P("expert", None, None)),
        out_specs=(row, row, P("dp"), P("dp", None), P("dp", None), P("dp"), P("dp", None), P("dp", None),
                   P("dp", None), P("expert", "dp", None), P("expert", "dp", None), P("expert", "dp", None)),
        check_vma=False,
    )
```

time: 1000 us -> 885 us (0.89)
  matrix products: 296 us -> 0 us
  Pallas kernels: 0 us -> 217 us
  blocking collectives: 28 us -> 133 us
  local copies, waits for them, and re-layouts: 121 us -> 49.7 us
  other arithmetic: 105 us -> 43 us
  waiting for transfers between devices: 406 us -> 360 us
  starting transfers between devices: 20.3 us -> 59.1 us
    dot_general x30 -> x0, matrix products: 296 us -> none  [the longest x5 33.8 us: contract_last(): lax.dot_general(left_side, right_side, (((1,), (1,)), ((), ())), preferre...]
    pallas_call x0 -> x9, Pallas kernels: none -> 217 us  [the longest x2 77 us: shards(): one(*[a[:, l:l + 1] for a in x_in], *[a[:, l:l + 1] for a in slot_in], *[...]
    all_gather x0 -> x7, blocking collectives: none -> 74.9 us  [dense(): return lax.all_gather(zs[0], 'expert', axis=0, tiled=True).astype(f32)]
    reduce_scatter x8 -> x13, waiting for transfers between devices: 343 us -> 269 us  [the longest x6 250 us: shards(): lax.psum_scatter(g[0], 'dp', scatter_dimension=0, tiled=True, axis_index_...]
    gather x5 -> x0, local copies, waits for them, and re-layouts: 46.7 us -> none  [the longest x1 10.5 us: shards(): pair_grad_pad[pair_table].astype(jnp.bfloat16)]
    all_to_all x4 -> x14, starting transfers between devices: 19.8 us -> 56 us  [the longest x8 33.1 us: a2a(): return lax.all_to_all(x, 'expert', split_axis=0, concat_axis=0, tiled=True)]
    psum x1, blocking collectives: 10.1 us -> 46.2 us  [shards(): gains = lax.psum(jnp.stack([agg[0], fgg[0]]), ('dp', 'expert'))]
    convert_element_type x14, other arithmetic: 48.8 us -> 18.9 us  [the longest x7 9.74 us: dense(): s = (mine.astype(f32) + swap(other).astype(f32)).astype(bf16)]
  transfers between devices with their start and end apart: 13 -> 41, of which waited for: 8 -> 16; matrix products, arithmetic and copies ran while one was open for 45% -> 9% of each run, Pallas kernels for 0% -> 20%
where the time goes in v1:
time: 885 us; the launch traced here: 878 us
  waiting for transfers between devices  360 us (41%)
  Pallas kernels  217 us (25%)
  blocking collectives  133 us (15%)
  starting transfers between devices  59.1 us (7%)
  local copies, waits for them, and re-layouts  49.7 us (6%)
  other arithmetic  43 us (5%)
  between operations  15.7 us (2%)
    reduce_scatter x6, waiting for transfers between devices, shards(): lax.psum_scatter(g[0], 'dp', scatter_dimension=0, tiled=True, axis_index_...  250 us
    pallas_call x2, Pallas kernels, shards(): one(*[a[:, l:l + 1] for a in x_in], *[a[:, l:l + 1] for a in slot_in], *[...  77 us
    all_gather x7, blocking collectives, dense(): return lax.all_gather(zs[0], 'expert', axis=0, tiled=True).astype(f32)  74.9 us
    all_to_all x8, waiting for transfers between devices, a2a(): return lax.all_to_all(x, 'expert', split_axis=0, concat_axis=0, tiled=True)  53.6 us
    psum x1, blocking collectives, shards(): gains = lax.psum(jnp.stack([agg[0], fgg[0]]), ('dp', 'expert'))  46.2 us
    pallas_call x1, Pallas kernels, attn_bwd(): pl.pallas_call(kernel, grid=(ng,), in_specs=[pl.BlockSpec(memory_space=pl...  44.5 us
    all_to_all x8, starting transfers between devices, a2a(): return lax.all_to_all(x, 'expert', split_axis=0, concat_axis=0, tiled=True)  33.1 us
    pallas_call x1, Pallas kernels, shards(): make_ffn(1, 1, 1, T, D, FF, 512, T // 2, f32)  32.5 us
  transfers between devices with their start and end apart: 41, of which 16 were waited for; matrix products, arithmetic and copies ran while one was open for 9% of the time, Pallas kernels for 20%

profile of v1, /device:TPU:0, one launch (start us, length us, event | category | flops | bytes accessed | tf_op | source)
XLA Modules:
  0.0 878.4 jit_solution(14391663264291167790)
XLA Ops:
  14.0 9.5 %route.1 = (s32[8,768]{1,0:T(8,128)S(1)}, s32[768,8]{1,0:T(8,128)S(1)}, bf16[960,768]{1,0:T(8,128)(2,1)}, bf16[960,768]{1,0:T(8,128)(2,1)}) custom-call(s32[1]{0:T(128)} %bitcast.core_ref, s32[1,1536]{1,0:T(1,128)S(1)} %copy-done.5, s32[768,2]{1,0:T(8,128)S(1)} %copy.34.ids, f32[768,2]{1,0:T(8,128)S(1)} %copy.35.gts.g, bf16[768,768]{1,0:T(8,128)(2,1)S(1)} %copy-done), custom_call_target="tpu_custom_call" | custom-call | flops 4680843264 | bytes 8388608 | tf_op jit(solution)/shard_map/route/pallas_call | solution.py:299
  23.5 31.2 %attn_fwd.1 = (bf16[768,768]{1,0:T(8,128)(2,1)}, bf16[768,768]{1,0:T(8,128)(2,1)}, bf16[768,768]{1,0:T(8,128)(2,1)}, bf16[768,768]{1,0:T(8,128)(2,1)}, f32[3,8,7...) custom-call(s32[1]{0:T(128)S(6)} %copy.58.pre, bf16[768,768]{1,0:T(8,128)(2,1)} %tok.3, ...), custom_call_target="tpu_custom_call" | custom-call | flops 5435817984 | bytes 16777216 | tf_op jit(solution)/shard_map/attn_fwd/pallas_call | solution.py:84
  56.0 4.4 dispatch.1
  60.4 5.2 all-to-all-start
  66.1 17.7 %all-to-all-done = bf16[4,2,120,768]{3,2,1,0:T(8,128)(2,1)S(1)} async-done(((bf16[4,2,120,768]{3,2,1,0:T(8,128)(2,1)}), bf16[4,2,120,768]{3,2,1,0:T(8,128)(2,1)S(1)}, u32[]{:S(2)}, u32[]{:S(2)}) %all-to-all-start) | async-done | bytes 1474592 | tf_op jit(solution)/shard_map/all_to_all | solution.py:397
  83.8 4.1 all-to-all-start.2
  87.8 32.5 %ffn.5 = (f32[1,1,768,768]{3,2,1,0:T(8,128)}, f32[1,1,768,768]{3,2,1,0:T(8,128)}, bf16[1,768,2048]{2,1,0:T(8,128)(2,1)}, bf16[1,768,2048]{2,1,0:T(8,128)(2,1)}, bf16[1,2048,768]{2,1,0:T(8,128)(2,1)}) custom-call(bf16[1,1,768,768]{3,2,1,0:T(8,128)(2,1)} %bitcast.151, bf16[1,1,768,768]{3,2,1,0:T(8,128)(2,1)} %bitcast.150, bf16[1,768,2048]{2,1,0:T(8,128)(2,1)} %bitcast.195, ...), custom_call_target="tpu_custom_call" | custom-call | flops 21743271936 | bytes 23592960 | tf_op jit(solution)/shard_map/ffn/pallas_call | solution.py:418
  123.0 4.3 all-to-all-start.1
  130.6 5.9 constant_dynamic-slice_fusion.4
  136.5 9.3 %constant_dynamic-slice_fusion.5 = (bf16[1,768,2048]{2,1,0:T(8,128)(2,1)}, bf16[1,768,2048]{2,1,0:T(8,128)(2,1)}, bf16[1,768,2048]{2,1,0:T(8,128)(2,1)}, bf16[1,768,2048]{2,1,0:T(8,128)(2,1)}) fusion(bf16[4,768,2048]{2,1,0:T(8,128)(2,1)} %param.30, s32[]{:T(128)S(6)} %select_n.74, s32[]{:T(128)S(6)} %select_n.75, bf16[4,768,2048]{2,1,0:T(8,128)(2,1)} %param.29), kind=kLoop, calls=%fused_computation.74 | loop fusion | bytes 25165832 | tf_op jit(solution)/shard_map/dynamic_slice | solution.py:428
  146.9 4.4 all-to-all-start.3
  159.8 10.1 %all-to-all-done.3 = bf16[4,2,120,768]{3,2,1,0:T(8,128)(2,1)} async-done(((bf16[4,2,120,768]{3,2,1,0:T(8,128)(2,1)}), bf16[4,2,120,768]{3,2,1,0:T(8,128)(2,1)}, u32[]{:S(2)}, u32[]{:S(2)}) %all-to-all-start.3) | async-done | bytes 1474592 | tf_op jit(solution)/shard_map/all_to_all | solution.py:397
  169.9 3.7 all-to-all-start.14
  176.2 38.5 %ffn.3 = (bf16[4,1,120,768]{3,2,1,0:T(8,128)(2,1)}, bf16[4,1,120,768]{3,2,1,0:T(8,128)(2,1)}, bf16[4,1,120,768]{3,2,1,0:T(8,128)(2,1)}, bf16[4,1,120,768]{3,2,1,...) custom-call(bf16[4,1,120,768]{3,2,1,0:T(8,128)(2,1)} %get-tuple-element, ...), custom_call_target="tpu_custom_call" | custom-call | flops 27179089920 | bytes 24772608 | tf_op jit(solution)/shard_map/ffn/pallas_call | solution.py:427
  214.7 38.6 %ffn.4 = (bf16[4,1,120,768]{3,2,1,0:T(8,128)(2,1)}, bf16[4,1,120,768]{3,2,1,0:T(8,128)(2,1)}, bf16[4,1,120,768]{3,2,1,0:T(8,128)(2,1)}, bf16[4,1,120,768]{3,2,1,...) custom-call(bf16[4,1,120,768]{3,2,1,0:T(8,128)(2,1)} %get-tuple-element, ...), custom_call_target="tpu_custom_call" | custom-call | flops 27179089920 | bytes 24772608 | tf_op jit(solution)/shard_map/ffn/pallas_call | solution.py:427
  255.6 4.3 all-to-all-start.7
  263.7 14.0 %all-to-all-done.7 = bf16[4,2,120,768]{3,2,1,0:T(8,128)(2,1)} async-done(((bf16[4,2,120,768]{3,2,1,0:T(8,128)(2,1)}), bf16[4,2,120,768]{3,2,1,0:T(8,128)(2,1)}, u32[]{:S(2)}, u32[]{:S(2)}) %all-to-all-start.7) | async-done | bytes 1474592 | tf_op jit(solution)/shard_map/all_to_all | solution.py:397
  277.8 3.8 all-to-all-start.13
  286.2 14.1 %all-to-all-done.13 = bf16[4,4,24,2048]{3,2,1,0:T(8,128)(2,1)S(1)} async-done(((bf16[4,4,24,2048]{3,2,1,0:T(8,128)(2,1)}), bf16[4,4,24,2048]{3,2,1,0:T(8,128)(2,1)S(1)}, u32[]{:S(2)}, u32[]{:S(2)}) %all-to-all-start.13) | async-done | bytes 1572896 | tf_op jit(solution)/shard_map/all_to_all | solution.py:460
  301.4 3.6 all-to-all-start.6
  311.9 10.7 %all-to-all-done.6 = bf16[4,2,120,768]{3,2,1,0:T(8,128)(2,1)S(1)} async-done(((bf16[4,2,120,768]{3,2,1,0:T(8,128)(2,1)}), bf16[4,2,120,768]{3,2,1,0:T(8,128)(2,1)S(1)}, u32[]{:S(2)}, u32[]{:S(2)}) %all-to-all-start.6) | async-done | bytes 1474592 | tf_op jit(solution)/shard_map/all_to_all | solution.py:397
  322.6 4.3 all-to-all-start.12
  327.0 8.1 mid_bwd.1
  335.1 44.5 %attn_bwd.1 = (bf16[768,768]{1,0:T(8,128)(2,1)}, f32[8,768]{1,0:T(8,128)}, bf16[768,768]{1,0:T(8,128)(2,1)}, bf16[768,768]{1,0:T(8,128)(2,1)}, bf16[768,768]{1,0:T(8,128)(2,1)}, /*index=5*/bf16[768,768]{1,0:T(8,128)(2,1)}) custom-call(s32[1]{0:T(128)S(6)} %copy.58.pre, f32[768,768]{1,0:T(8,128)} %get-tuple-element.70.sg, bf16[768,768]{1,0:T(8,128)(2,1)} %tok.3, ...), custom_call_target="tpu_custom_call" | custom-call | flops 11777605632 | bytes 25165824 | tf_op jit(solution)/shard_map/attn_bwd/pallas_call | solution.py:169
  385.2 4.1 all-to-all-start.8
  392.3 6.0 all-to-all-done.8
  398.3 3.5 all-to-all-start.9
  404.7 5.4 all-to-all-done.9
  410.1 3.5 all-to-all-start.10
  414.5 6.6 all-to-all-done.10
  426.3 12.4 %all_to_all.75 = bf16[4,4,24,768]{3,2,1,0:T(8,128)(2,1)S(1)} all-to-all(bf16[4,4,24,768]{3,2,1,0:T(8,128)(2,1)S(1)} %copy.44), channel_id=1, replica_groups=mesh['dp'=8,'expert'=4] {'expert'}, dimensions={0} | all-to-all | bytes 1179648 | tf_op jit(solution)/shard_map/all_to_all | solution.py:460
  444.0 3.7 all-to-all-start.5
  449.0 21.9 %all-gather.6 = bf16[1,256,768]{2,1,0:T(8,128)(2,1)S(1)} all-gather(bf16[1,64,768]{2,1,0:T(8,128)(2,1)} %reduce-scatter.26.cloned.1.call-done), channel_id=8, replica_groups=mesh['dp'=8,'expert'=4] {'expert'}, dimensions={1}, use_global_device_ids=true | all-gather | bytes 491520 | tf_op jit(solution)/shard_map/all_gather | solution.py:463
  470.9 9.2 %all-gather.5 = bf16[1,96,2048]{2,1,0:T(8,128)(2,1)S(1)} all-gather(bf16[1,24,2048]{2,1,0:T(8,128)(2,1)} %reduce-scatter.24.cloned.1.call-done), channel_id=7, replica_groups=mesh['dp'=8,'expert'=4] {'expert'}, dimensions={1}, use_global_device_ids=true | all-gather | bytes 491520 | tf_op jit(solution)/shard_map/all_gather | solution.py:463
  480.1 9.3 %all-gather.4 = bf16[1,96,2048]{2,1,0:T(8,128)(2,1)S(1)} all-gather(bf16[1,24,2048]{2,1,0:T(8,128)(2,1)} %reduce-scatter.22.cloned.1.call-done), channel_id=6, replica_groups=mesh['dp'=8,'expert'=4] {'expert'}, dimensions={1}, use_global_device_ids=true | all-gather | bytes 491520 | tf_op jit(solution)/shard_map/all_gather | solution.py:463
  490.6 3.6 all-to-all-start.4
  497.8 46.2 %psum.7 = f32[2,768]{1,0:T(2,128)S(1)} all-reduce(f32[2,768]{1,0:T(2,128)S(1)} %pad_maximum_fusion.6), channel_id=1, replica_groups=mesh['dp'=8,'expert'=4] {'dp','expert'}, use_global_device_ids=true, to_apply=%region_0.0 | all-reduce | flops 1536 | bytes 12288 | tf_op jit(solution)/shard_map/psum | solution.py:475
  544.6 9.6 %combine.1 = bf16[768,768]{1,0:T(8,128)(2,1)} custom-call(s32[768,8]{1,0:T(8,128)S(1)} %get-tuple-element.52.colr, f32[768,2]{1,0:T(8,128)S(1)} %copy-done.3, bf16[960,768]{1,0:T(8,128)(2,1)S(1)} %bitcast.149, bf16[960,768]{1,0:T(8,128)(2,1)} %bitcast.6.refs_1_, f32[768,768]{1,0:T(8,128)} %get-tuple-element.63.refs_2_.refs_3_, f32[768,768]{1,0:T(8,128)} %bitcast.198), custom_call_target="tpu_custom_call" | custom-call | flops 4529848320 | bytes 9437184 | tf_op jit(solution)/shard_map/combine/pallas_call | solution.py:340
  554.2 9.6 %all-gather = bf16[1,96,768]{2,1,0:T(8,128)(2,1)S(1)} all-gather(bf16[1,24,768]{2,1,0:T(8,128)(2,1)} %reduce-scatter.14.cloned.1.call-done), channel_id=2, replica_groups=mesh['dp'=8,'expert'=4] {'expert'}, dimensions={1}, use_global_device_ids=true | all-gather | bytes 184320 | tf_op jit(solution)/shard_map/all_gather | solution.py:463
  563.7 7.8 all-gather.1
  571.6 8.4 all-gather.2
  579.9 10.9 %reduce-scatter.38.cloned.1.call-done = bf16[512,768]{1,0:T(8,128)(2,1)} async-done(((bf16[2048,768]{1,0:T(8,128)(2,1)}), bf16[512,768]{1,0:T(8,128)(2,1)}) %reduce-scatter.38.cloned.1.call-update) | async-done | bytes 786448 | tf_op jit(solution)/shard_map/reduce_scatter | solution.py:440
  593.1 19.3 %reduce-scatter.20.cloned.1.call-done = bf16[1,24,768]{2,1,0:T(8,128)(2,1)} async-done(((bf16[4,24,768]{2,1,0:T(8,128)(2,1)}), bf16[1,24,768]{2,1,0:T(8,128)(2,1)}) %reduce-scatter.20.cloned.1.call-update) | async-done | bytes 36880 | tf_op jit(solution)/shard_map/reduce_scatter | solution.py:462
  612.4 8.7 all-gather.3
  621.1 52.0 %reduce-scatter.32.cloned.1.call-done = bf16[192,2048]{1,0:T(8,128)(2,1)} async-done(((bf16[768,2048]{1,0:T(8,128)(2,1)}), bf16[192,2048]{1,0:T(8,128)(2,1)}) %reduce-scatter.32.cloned.1.call-update) | async-done | bytes 786448 | tf_op jit(solution)/shard_map/reduce_scatter | solution.py:440
  673.2 62.7 %reduce-scatter.34.cloned.1.call-done = bf16[192,2048]{1,0:T(8,128)(2,1)} async-done(((bf16[768,2048]{1,0:T(8,128)(2,1)}), bf16[192,2048]{1,0:T(8,128)(2,1)}) %reduce-scatter.34.cloned.1.call-update) | async-done | bytes 786448 | tf_op jit(solution)/shard_map/reduce_scatter | solution.py:440
  737.9 60.5 %reduce-scatter.28.cloned.1.call-done = bf16[192,2048]{1,0:T(8,128)(2,1)} async-done(((bf16[768,2048]{1,0:T(8,128)(2,1)}), bf16[192,2048]{1,0:T(8,128)(2,1)}) %reduce-scatter.28.cloned.1.call-update) | async-done | bytes 786448 | tf_op jit(solution)/shard_map/reduce_scatter | solution.py:440
  798.5 63.3 %reduce-scatter.30.cloned.1.call-done = bf16[192,2048]{1,0:T(8,128)(2,1)} async-done(((bf16[768,2048]{1,0:T(8,128)(2,1)}), bf16[192,2048]{1,0:T(8,128)(2,1)}) %reduce-scatter.30.cloned.1.call-update) | async-done | bytes 786448 | tf_op jit(solution)/shard_map/reduce_scatter | solution.py:440
  (189 shorter events, 87.7 us)
Async XLA Ops:
  8.1 5.8 copy-start.2
  60.4 23.4 %all-to-all-start = ((bf16[4,2,120,768]{3,2,1,0:T(8,128)(2,1)}), bf16[4,2,120,768]{3,2,1,0:T(8,128)(2,1)S(1)}, u32[]{:S(2)}, u32[]{:S(2)}) async-start(bf16[4,2,120,768]{3,2,1,0:T(8,128)(2,1)} %bitcast.1), calls=%async_computation | async-start | bytes 2949120 | tf_op jit(solution)/shard_map/all_to_all | solution.py:397
  65.6 57.5 %collective-permute-start = (bf16[4,2,120,768]{3,2,1,0:T(8,128)(2,1)}, bf16[4,2,120,768]{3,2,1,0:T(8,128)(2,1)}, u32[]{:S(2)}, u32[]{:S(2)}) collective-permute-start(bf16[4,2,120,768]{3,2,1,0:T(8,128)(2,1)} %bitcast.2), channel_id=1, source_target_pairs={{0,4},{4,0},{8,12},{12,8},{16,20},{20,16},{24,28},{28,24},{1,5},{5... | collective-permute-start | bytes 4423688 | tf_op jit(solution)/shard_map/ppermute | solution.py:394
  65.6 80.3 %collective-permute-start.1 = (bf16[4,2,120,768]{3,2,1,0:T(8,128)(2,1)}, bf16[4,2,120,768]{3,2,1,0:T(8,128)(2,1)}, u32[]{:S(2)}, u32[]{:S(2)}) collective-permute-start(bf16[4,2,120,768]{3,2,1,0:T(8,128)(2,1)} %bitcast.4), channel_id=1, source_target_pairs={{0,4},{4,0},{8,12},{12,8},{16,20},{20,16},{24,28},{28,24},{1,5},{5... | collective-permute-start | bytes 4423688 | tf_op jit(solution)/shard_map/ppermute | solution.py:394
  83.8 39.3 %all-to-all-start.2 = ((bf16[4,2,120,768]{3,2,1,0:T(8,128)(2,1)}), bf16[4,2,120,768]{3,2,1,0:T(8,128)(2,1)S(1)}, u32[]{:S(2)}, u32[]{:S(2)}) async-start(bf16[4,2,120,768]{3,2,1,0:T(8,128)(2,1)} %bitcast.3), calls=%async_computation.2 | async-start | bytes 2949120 | tf_op jit(solution)/shard_map/all_to_all | solution.py:397
  123.0 30.7 %collective-permute-start.10 = (bf16[4,256,768]{2,1,0:T(8,128)(2,1)}, bf16[4,256,768]{2,1,0:T(8,128)(2,1)}, u32[]{:S(2)}, u32[]{:S(2)}) collective-permute-start(bf16[4,256,768]{2,1,0:T(8,128)(2,1)} %dynamic-slice_bitcast_fusion), channel_id=1, source_target_pairs={{0,4},{4,0},{8,12},{12,8},{16,20},{20,16},{24,28},{28,24},{1,5},{5... | collective-permute-start | bytes 4718600 | tf_op jit(solution)/shard_map/ppermute | solution.py:394
  123.0 23.8 %all-to-all-start.1 = ((bf16[4,2,120,768]{3,2,1,0:T(8,128)(2,1)}), bf16[4,2,120,768]{3,2,1,0:T(8,128)(2,1)}, u32[]{:S(2)}, u32[]{:S(2)}) async-start(bf16[4,2,120,768]{3,2,1,0:T(8,128)(2,1)} %collective-permute-done), calls=%async_computation.1 | async-start | bytes 2949120 | tf_op jit(solution)/shard_map/all_to_all | solution.py:397
  130.1 129.8 %collective-permute-start.9 = (bf16[4,96,2048]{2,1,0:T(8,128)(2,1)}, bf16[4,96,2048]{2,1,0:T(8,128)(2,1)}, u32[]{:S(2)}, u32[]{:S(2)}) collective-permute-start(bf16[4,96,2048]{2,1,0:T(8,128)(2,1)} %dynamic-slice_bitcast_fusion.1), channel_id=1, source_target_pairs={{0,4},{4,0},{8,12},{12,8},{16,20},{20,16},{24,28},{28,24},{1,5},{5... | collective-permute-start | bytes 4718600 | tf_op jit(solution)/shard_map/ppermute | solution.py:394
  146.9 23.0 %all-to-all-start.3 = ((bf16[4,2,120,768]{3,2,1,0:T(8,128)(2,1)}), bf16[4,2,120,768]{3,2,1,0:T(8,128)(2,1)}, u32[]{:S(2)}, u32[]{:S(2)}) async-start(bf16[4,2,120,768]{3,2,1,0:T(8,128)(2,1)} %collective-permute-done.1), calls=%async_computation.3 | async-start | bytes 2949120 | tf_op jit(solution)/shard_map/all_to_all | solution.py:397
  169.9 85.7 %all-to-all-start.14 = ((bf16[4,4,64,768]{3,2,1,0:T(8,128)(2,1)}), bf16[4,4,64,768]{3,2,1,0:T(8,128)(2,1)S(1)}, u32[]{:S(2)}, u32[]{:S(2)}) async-start(bf16[4,4,64,768]{3,2,1,0:T(8,128)(2,1)} %copy.50), calls=%async_computation.20 | async-start | bytes 3145728 | tf_op jit(solution)/shard_map/all_to_all | solution.py:460
  214.7 38.6 %copy-start.27 = (bf16[4,1,120,768]{3,2,1,0:T(8,128)(2,1)S(1)}, bf16[4,1,120,768]{3,2,1,0:T(8,128)(2,1)}, u32[]{:S(2)}) copy-start(bf16[4,1,120,768]{3,2,1,0:T(8,128)(2,1)} %get-tuple-element.67) | copy-start | bytes 2211844
  255.6 22.1 %all-to-all-start.7 = ((bf16[4,2,120,768]{3,2,1,0:T(8,128)(2,1)}), bf16[4,2,120,768]{3,2,1,0:T(8,128)(2,1)}, u32[]{:S(2)}, u32[]{:S(2)}) async-start(bf16[4,2,120,768]{3,2,1,0:T(8,128)(2,1)} %pad_maximum_fusion.3), calls=%async_computation.7 | async-start | bytes 2949120 | tf_op jit(solution)/shard_map/all_to_all | solution.py:397
  277.8 22.5 %all-to-all-start.13 = ((bf16[4,4,24,2048]{3,2,1,0:T(8,128)(2,1)}), bf16[4,4,24,2048]{3,2,1,0:T(8,128)(2,1)S(1)}, u32[]{:S(2)}, u32[]{:S(2)}) async-start(bf16[4,4,24,2048]{3,2,1,0:T(8,128)(2,1)} %copy.48), calls=%async_computation.18 | async-start | bytes 3145728 | tf_op jit(solution)/shard_map/all_to_all | solution.py:460
  284.4 21.8 %collective-permute-start.8 = (bf16[4,96,2048]{2,1,0:T(8,128)(2,1)}, bf16[4,96,2048]{2,1,0:T(8,128)(2,1)}, u32[]{:S(2)}, u32[]{:S(2)}) collective-permute-start(bf16[4,96,2048]{2,1,0:T(8,128)(2,1)} %dynamic-slice_bitcast_fusion.2), channel_id=1, source_target_pairs={{0,4},{4,0},{8,12},{12,8},{16,20},{20,16},{24,28},{28,24},{1,5},{5... | collective-permute-start | bytes 4718600 | tf_op jit(solution)/shard_map/ppermute | solution.py:394
  284.4 42.6 %collective-permute-start.3 = (bf16[4,2,120,768]{3,2,1,0:T(8,128)(2,1)}, bf16[4,2,120,768]{3,2,1,0:T(8,128)(2,1)}, u32[]{:S(2)}, u32[]{:S(2)}) collective-permute-start(bf16[4,2,120,768]{3,2,1,0:T(8,128)(2,1)} %all-to-all-done.7), channel_id=1, source_target_pairs={{0,4},{4,0},{8,12},{12,8},{16,20},{20,16},{24,28},{28,24},{1,5},{5... | collective-permute-start | bytes 4423688 | tf_op jit(solution)/shard_map/ppermute | solution.py:394
  301.4 21.2 %all-to-all-start.6 = ((bf16[4,2,120,768]{3,2,1,0:T(8,128)(2,1)}), bf16[4,2,120,768]{3,2,1,0:T(8,128)(2,1)S(1)}, u32[]{:S(2)}, u32[]{:S(2)}) async-start(bf16[4,2,120,768]{3,2,1,0:T(8,128)(2,1)} %pad_maximum_fusion.2), calls=%async_computation.6 | async-start | bytes 2949120 | tf_op jit(solution)/shard_map/all_to_all | solution.py:397
  305.0 144.0 %reduce-scatter.26.cloned.1.call-start = ((), (), s32[]{:S(2)}) async-start(), calls=%async_computation.34 | async-start | bytes 491520 | tf_op jit(solution)/shard_map/reduce_scatter | solution.py:462
  306.2 164.7 %reduce-scatter.24.cloned.1.call-start = ((), (), s32[]{:S(2)}) async-start(), calls=%async_computation.33 | async-start | bytes 491520 | tf_op jit(solution)/shard_map/reduce_scatter | solution.py:462
  311.8 15.2 %copy-start.1 = (bf16[768,768]{1,0:T(8,128)(2,1)S(1)}, bf16[768,768]{1,0:T(8,128)(2,1)}, u32[]{:S(2)}) copy-start(bf16[768,768]{1,0:T(8,128)(2,1)} %refs_5_.1) | copy-start | bytes 3538948
  311.9 15.2 %copy-start.4 = (f32[1,768]{1,0:T(1,128)S(1)}, f32[1,768]{1,0:T(1,128)}, u32[]{:S(2)}) copy-start(f32[1,768]{1,0:T(1,128)} %broadcast_in_dim.30.fg.refs_4_) | copy-start | bytes 9220
  322.6 59.0 %all-to-all-start.12 = ((bf16[4,4,24,2048]{3,2,1,0:T(8,128)(2,1)}), bf16[4,4,24,2048]{3,2,1,0:T(8,128)(2,1)}, u32[]{:S(2)}, u32[]{:S(2)}) async-start(bf16[4,4,24,2048]{3,2,1,0:T(8,128)(2,1)} %copy.46), calls=%async_computation.16 | async-start | bytes 3145728 | tf_op jit(solution)/shard_map/all_to_all | solution.py:460
  326.9 153.2 %reduce-scatter.22.cloned.1.call-start = ((), (), s32[]{:S(2)}) async-start(), calls=%async_computation.32 | async-start | bytes 491520 | tf_op jit(solution)/shard_map/reduce_scatter | solution.py:462
  380.8 3.3 collective-permute-start.4
  381.1 9.0 %collective-permute-start.5 = (bf16[4,96,768]{2,1,0:T(8,128)(2,1)S(1)}, bf16[4,96,768]{2,1,0:T(8,128)(2,1)}, u32[]{:S(2)}, u32[]{:S(2)}) collective-permute-start(bf16[4,96,768]{2,1,0:T(8,128)(2,1)S(1)} %dynamic-slice_bitcast_fusion.5), channel_id=1, source_target_pairs={{0,4},{4,0},{8,12},{12,8},{16,20},{20,16},{24,28},{28,24},{1,5},{5... | collective-permute-start | bytes 1769480 | tf_op jit(solution)/shard_map/ppermute | solution.py:394
  385.2 13.2 %all-to-all-start.8 = ((bf16[4,4,24,768]{3,2,1,0:T(8,128)(2,1)}), bf16[4,4,24,768]{3,2,1,0:T(8,128)(2,1)S(1)}, u32[]{:S(2)}, u32[]{:S(2)}) async-start(bf16[4,4,24,768]{3,2,1,0:T(8,128)(2,1)} %copy.38), calls=%async_computation.8 | async-start | bytes 1179648 | tf_op jit(solution)/shard_map/all_to_all | solution.py:460
  390.1 12.6 %collective-permute-start.6 = (bf16[4,96,768]{2,1,0:T(8,128)(2,1)}, bf16[4,96,768]{2,1,0:T(8,128)(2,1)}, u32[]{:S(2)}, u32[]{:S(2)}) collective-permute-start(bf16[4,96,768]{2,1,0:T(8,128)(2,1)} %dynamic-slice_bitcast_fusion.4), channel_id=1, source_target_pairs={{0,4},{4,0},{8,12},{12,8},{16,20},{20,16},{24,28},{28,24},{1,5},{5... | collective-permute-start | bytes 1769480 | tf_op jit(solution)/shard_map/ppermute | solution.py:394
  398.3 11.8 %all-to-all-start.9 = ((bf16[4,4,24,768]{3,2,1,0:T(8,128)(2,1)}), bf16[4,4,24,768]{3,2,1,0:T(8,128)(2,1)S(1)}, u32[]{:S(2)}, u32[]{:S(2)}) async-start(bf16[4,4,24,768]{3,2,1,0:T(8,128)(2,1)} %copy.40), calls=%async_computation.10 | async-start | bytes 1179648 | tf_op jit(solution)/shard_map/all_to_all | solution.py:460
  401.8 152.4 %reduce-scatter.14.cloned.1.call-start = ((), (), s32[]{:S(2)}) async-start(), calls=%async_computation.28 | async-start | bytes 184320 | tf_op jit(solution)/shard_map/reduce_scatter | solution.py:462
  410.1 11.0 %all-to-all-start.10 = ((bf16[4,4,24,768]{3,2,1,0:T(8,128)(2,1)}), bf16[4,4,24,768]{3,2,1,0:T(8,128)(2,1)S(1)}, u32[]{:S(2)}, u32[]{:S(2)}) async-start(bf16[4,4,24,768]{3,2,1,0:T(8,128)(2,1)} %copy.42), calls=%async_computation.12 | async-start | bytes 1179648 | tf_op jit(solution)/shard_map/all_to_all | solution.py:460
  413.6 150.1 %reduce-scatter.16.cloned.1.call-start = ((), (), s32[]{:S(2)}) async-start(), calls=%async_computation.29 | async-start | bytes 184320 | tf_op jit(solution)/shard_map/reduce_scatter | solution.py:462
  414.5 157.1 %reduce-scatter.18.cloned.1.call-start = ((), (), s32[]{:S(2)}) async-start(), calls=%async_computation.30 | async-start | bytes 184320 | tf_op jit(solution)/shard_map/reduce_scatter | solution.py:462
  421.9 158.0 %reduce-scatter.36.cloned.1.call-start = ((), (), s32[]{:S(2)}) async-start(), calls=%async_computation.39 | async-start | bytes 3932160 | tf_op jit(solution)/shard_map/reduce_scatter | solution.py:440
  422.7 168.2 %reduce-scatter.38.cloned.1.call-start = ((), (), s32[]{:S(2)}) async-start(), calls=%async_computation.40 | async-start | bytes 3932160 | tf_op jit(solution)/shard_map/reduce_scatter | solution.py:440
  423.4 189.0 %reduce-scatter.20.cloned.1.call-start = ((), (), s32[]{:S(2)}) async-start(), calls=%async_computation.31 | async-start | bytes 184320 | tf_op jit(solution)/shard_map/reduce_scatter | solution.py:462
  424.1 2.1 collective-permute-start.7
  439.5 233.7 %reduce-scatter.32.cloned.1.call-start = ((), (), s32[]{:S(2)}) async-start(), calls=%async_computation.37 | async-start | bytes 3932160 | tf_op jit(solution)/shard_map/reduce_scatter | solution.py:440
  440.1 295.8 %reduce-scatter.34.cloned.1.call-start = ((), (), s32[]{:S(2)}) async-start(), calls=%async_computation.38 | async-start | bytes 3932160 | tf_op jit(solution)/shard_map/reduce_scatter | solution.py:440
  440.8 357.7 %reduce-scatter.28.cloned.1.call-start = ((), (), s32[]{:S(2)}) async-start(), calls=%async_computation.35 | async-start | bytes 3932160 | tf_op jit(solution)/shard_map/reduce_scatter | solution.py:440
  441.4 420.4 %reduce-scatter.30.cloned.1.call-start = ((), (), s32[]{:S(2)}) async-start(), calls=%async_computation.36 | async-start | bytes 3932160 | tf_op jit(solution)/shard_map/reduce_scatter | solution.py:440
  444.0 45.4 %all-to-all-start.5 = ((bf16[4,2,120,768]{3,2,1,0:T(8,128)(2,1)}), bf16[4,2,120,768]{3,2,1,0:T(8,128)(2,1)S(1)}, u32[]{:S(2)}, u32[]{:S(2)}) async-start(bf16[4,2,120,768]{3,2,1,0:T(8,128)(2,1)} %pad_maximum_fusion.1), calls=%async_computation.5 | async-start | bytes 2949120 | tf_op jit(solution)/shard_map/all_to_all | solution.py:397
  490.6 54.0 %all-to-all-start.4 = ((bf16[4,2,120,768]{3,2,1,0:T(8,128)(2,1)}), bf16[4,2,120,768]{3,2,1,0:T(8,128)(2,1)S(1)}, u32[]{:S(2)}, u32[]{:S(2)}) async-start(bf16[4,2,120,768]{3,2,1,0:T(8,128)(2,1)} %pad_maximum_fusion), calls=%async_computation.4 | async-start | bytes 2949120 | tf_op jit(solution)/shard_map/all_to_all | solution.py:397
  494.1 50.4 %copy-start.3 = (f32[768,2]{1,0:T(8,128)S(1)}, f32[768,2]{1,0:T(8,128)}, u32[]{:S(2)}) copy-start(f32[768,2]{1,0:T(8,128)} %copy-done.2) | copy-start | bytes 18436
  494.1 50.4 %collective-permute-start.2 = (bf16[4,2,120,768]{3,2,1,0:T(8,128)(2,1)}, bf16[4,2,120,768]{3,2,1,0:T(8,128)(2,1)}, u32[]{:S(2)}, u32[]{:S(2)}) collective-permute-start(bf16[4,2,120,768]{3,2,1,0:T(8,128)(2,1)} %copy-done.16), channel_id=1, source_target_pairs={{0,4},{4,0},{8,12},{12,8},{16,20},{20,16},{24,28},{28,24},{1,5},{5... | collective-permute-start | bytes 4423688 | tf_op jit(solution)/shard_map/ppermute | solution.py:394
  592.1 271.0 %collective-permute-start.13 = (bf16[2,256,768]{2,1,0:T(8,128)(2,1)S(1)}, bf16[2,256,768]{2,1,0:T(8,128)(2,1)}, u32[]{:S(2)}, u32[]{:S(2)}) collective-permute-start(bf16[2,256,768]{2,1,0:T(8,128)(2,1)S(1)} %fusion.8), channel_id=1, source_target_pairs={{0,4},{4,0},{8,12},{12,8},{16,20},{20,16},{24,28},{28,24},{1,5},{5... | collective-permute-start | bytes 2359304 | tf_op jit(solution)/shard_map/ppermute | solution.py:394
  737.1 126.0 %copy-start.10 = (bf16[512,768]{1,0:T(8,128)(2,1)S(1)}, bf16[512,768]{1,0:T(8,128)(2,1)}, u32[]{:S(2)}) copy-start(bf16[512,768]{1,0:T(8,128)(2,1)} %reduce-scatter.36.cloned.1.call-done) | copy-start | bytes 2359300
  737.1 126.0 %copy-start.11 = (bf16[512,768]{1,0:T(8,128)(2,1)S(1)}, bf16[512,768]{1,0:T(8,128)(2,1)}, u32[]{:S(2)}) copy-start(bf16[512,768]{1,0:T(8,128)(2,1)} %reduce-scatter.38.cloned.1.call-done) | copy-start | bytes 2359300
  737.1 129.1 %collective-permute-start.12 = (bf16[2,96,2048]{2,1,0:T(8,128)(2,1)S(1)}, bf16[2,96,2048]{2,1,0:T(8,128)(2,1)}, u32[]{:S(2)}, u32[]{:S(2)}) collective-permute-start(bf16[2,96,2048]{2,1,0:T(8,128)(2,1)S(1)} %fusion.12), channel_id=1, source_target_pairs={{0,4},{4,0},{8,12},{12,8},{16,20},{20,16},{24,28},{28,24},{1,5},{5... | collective-permute-start | bytes 2359304 | tf_op jit(solution)/shard_map/ppermute | solution.py:394
  862.9 6.4 collective-permute-start.11
  (23 other events, 60.5 us)
Sparse Core Ops, SparseCore 0:
  308.1 22.3 reduce-scatter.25
  332.8 18.8 reduce-scatter.23
  384.2 22.2 reduce-scatter.21
  408.7 17.5 reduce-scatter.13
  429.0 17.4 reduce-scatter.15
  449.2 17.4 reduce-scatter.17
  469.0 59.1 reduce-scatter.35
  530.5 60.3 reduce-scatter.37
  593.1 19.2 reduce-scatter.19
  614.7 58.4 reduce-scatter.31
  675.6 60.2 reduce-scatter.33
  738.2 60.2 reduce-scatter.27
  801.4 60.2 reduce-scatter.29

commit v2 on v1

--- a/solution.py
+++ b/solution.py
@@ -10,6 +10,7 @@
 def nt(a,b): return lax.dot_general(a,b,(((1,),(1,)),((),())),preferred_element_type=f32)
 def tn(a,b): return lax.dot_general(a,b,(((0,),(0,)),((),())),preferred_element_type=f32)
 EPS=1e-6
+E=16; CAP=120
 HD=64; GH=4; GW=GH*HD; QC=256
 def lane_head(shape):
     return lax.broadcasted_iota(jnp.int32,shape,1)//HD
@@ -22,13 +23,50 @@
 def inv_rms(v):
     return lax.rsqrt(jnp.mean(v*v,axis=1,keepdims=True)+EPS)
 
-def attn_fwd(tokens, prefix, again, wqkv, wo, fgain, cosw, sinw):
+def plane_copies(src, dst, local_sem, send_sem, recv_sem):
+    d=lax.axis_index("dp"); e=lax.axis_index("expert")
+    c=lax.rem(d,2); z2=d-c; me=c*4+e
+    own=pltpu.make_async_copy(src.at[me],dst.at[me],local_sem)
+    out=[]
+    for kk in range(1,8):
+        pc=lax.rem(c+(kk>>2),2)
+        pe=xor4(e,kk&3)
+        out.append(pltpu.make_async_remote_copy(src_ref=src.at[pc*4+pe],dst_ref=dst.at[me],send_sem=send_sem.at[kk-1],recv_sem=recv_sem.at[kk-1],
+            device_id=(z2+pc,pe),device_id_type=pl.DeviceIdType.MESH))
+    return own,out
+
+def xor4(e,k):
+    lo=lax.rem(e,2); hi=lax.div(e,2)
+    if k&1: lo=1-lo
+    if k&2: hi=1-hi
+    return hi*2+lo
+
+def plane_barrier():
+    d=lax.axis_index("dp"); e=lax.axis_index("expert")
+    c=lax.rem(d,2); z2=d-c
+    b=pltpu.get_barrier_semaphore()
+    for kk in range(1,8):
+        pl.semaphore_signal(b,inc=1,device_id=(z2+lax.rem(c+(kk>>2),2),xor4(e,kk&3)),device_id_type=pl.DeviceIdType.MESH)
+    pl.semaphore_wait(b,7)
+
+def attn_fwd(tokens, prefix, again, wqkv, wo, fgain, cosw, sinw, rows=None, sout=None):
     T,D=tokens.shape
     ng=D//GW; nq=T//QC
-    def kernel(pre,tok,ag,fg,wq,wk,wv,wor,cw,sw,qo,ko,vo,atto,lseo,stateo,ntwoo,normed,bias,q4,k4,vT,OT,acc):
+    fused=rows is not None
+    NS=E*CAP; CH=480
+    def kernel(pre,tok,ag,fg,wq,wk,wv,wor,cw,sw,*rest):
+        if fused:
+            rowr,so,qo,ko,vo,atto,lseo,stateo,ntwoo,xo,sino,normed,bias,q4,k4,vT,OT,acc,lsem,ssem,rsem=rest
+        else:
+            qo,ko,vo,atto,lseo,stateo,ntwoo,normed,bias,q4,k4,vT,OT,acc=rest
         g=pl.program_id(0)
         @pl.when(g==0)
         def _():
+            if fused:
+                plane_barrier()
+                own,others=plane_copies(so,sino,lsem.at[0],ssem,rsem)
+                own.start()
+                for cpy in others: cpy.start()
             for c in range(nq):
                 r=slice(c*QC,(c+1)*QC)
                 x=tok[r,:].astype(f32)
@@ -78,22 +116,38 @@
                 st=acc[r,:]
                 stateo[r,:]=st
                 ntwoo[r,:]=(st*inv_rms(st)*fg[...]).astype(bf16)
+            if fused:
+                for i in range(NS//CH):
+                    si=lax.broadcasted_iota(jnp.int32,(CH,T),0)+i*CH
+                    d=jnp.where((si==rowr[0:1,:])|(si==rowr[1:2,:]),1.0,0.0).astype(bf16)
+                    xo[i*CH:(i+1)*CH,:]=nn(d,ntwoo[...]).astype(bf16)
+                own,others=plane_copies(so,sino,lsem.at[0],ssem,rsem)
+                own.wait()
+                for cpy in others: cpy.wait()
     full=lambda s: pl.BlockSpec(s,lambda g:(0,)*len(s))
     col=lambda off: pl.BlockSpec((D,GW),lambda g,off=off:(0,g+off))
     tcol=pl.BlockSpec((T,GW),lambda g:(0,g))
     return pl.pallas_call(kernel,grid=(ng,),
-      in_specs=[pl.BlockSpec(memory_space=pltpu.SMEM),full((T,D)),full((1,D)),full((1,D)),col(0),col(ng),col(2*ng),pl.BlockSpec((GW,D),lambda g:(g,0)),full((T,128)),full((T,128))],
-      out_specs=[tcol,tcol,tcol,tcol,pl.BlockSpec((1,8,T),lambda g:(g,0,0)),full((T,D)),full((T,D))],
-      out_shape=[jax.ShapeDtypeStruct((T,D),bf16)]*4+[jax.ShapeDtypeStruct((ng,8,T),f32),jax.ShapeDtypeStruct((T,D),f32),jax.ShapeDtypeStruct((T,D),bf16)],
-      scratch_shapes=[pltpu.VMEM((T,D),bf16),pltpu.VMEM((nq,T,QC),f32),pltpu.VMEM((T,GW),bf16),pltpu.VMEM((T,GW),bf16),pltpu.VMEM((GW,T),bf16),pltpu.VMEM((nq,GW,QC),f32),pltpu.VMEM((T,D),f32)],
-      compiler_params=pltpu.CompilerParams(vmem_limit_bytes=56<<20,dimension_semantics=("arbitrary",)),
+      in_specs=[pl.BlockSpec(memory_space=pltpu.SMEM),full((T,D)),full((1,D)),full((1,D)),col(0),col(ng),col(2*ng),pl.BlockSpec((GW,D),lambda g:(g,0)),full((T,128)),full((T,128))]+([full((8,T)),pl.BlockSpec(memory_space=pl.ANY)] if fused else []),
+      out_specs=[tcol,tcol,tcol,tcol,pl.BlockSpec((1,8,T),lambda g:(g,0,0)),full((T,D)),full((T,D))]+([full((NS,D)),pl.BlockSpec(memory_space=pl.ANY)] if fused else []),
+      out_shape=[jax.ShapeDtypeStruct((T,D),bf16)]*4+[jax.ShapeDtypeStruct((ng,8,T),f32),jax.ShapeDtypeStruct((T,D),f32),jax.ShapeDtypeStruct((T,D),bf16)]+([jax.ShapeDtypeStruct((NS,D),bf16),jax.ShapeDtypeStruct((8,2*CAP,D),bf16)] if fused else []),
+      scratch_shapes=[pltpu.VMEM((T,D),bf16),pltpu.VMEM((nq,T,QC),f32),pltpu.VMEM((T,GW),bf16),pltpu.VMEM((T,GW),bf16),pltpu.VMEM((GW,T),bf16),pltpu.VMEM((nq,GW,QC),f32),pltpu.VMEM((T,D),f32)]+([pltpu.SemaphoreType.DMA((1,)),pltpu.SemaphoreType.DMA((7,)),pltpu.SemaphoreType.DMA((7,))] if fused else []),
+      compiler_params=pltpu.CompilerParams(vmem_limit_bytes=56<<20,dimension_semantics=("arbitrary",),**(dict(collective_id=0,has_side_effects=True) if fused else {})),
       cost_estimate=pl.CostEstimate(flops=2*T*D*4*D+4*T*T*D,bytes_accessed=16<<20,transcendentals=12*T*T),
-      name="attn_fwd")(prefix,tokens,again[None],fgain[None],wqkv,wqkv,wqkv,wo,cosw,sinw)
-
-def attn_bwd(sgrad, prefix, tokens, again, wqkv, wo, cosw, sinw, q, k, v, att, lse):
+      name="attn_fwd")(prefix,tokens,again[None],fgain[None],wqkv,wqkv,wqkv,wo,cosw,sinw,*([rows,sout] if fused else []))
+
+def attn_bwd(sgrad, prefix, tokens, again, wqkv, wo, cosw, sinw, q, k, v, att, lse, place=None):
     T,D=tokens.shape
     ng=D//GW; nq=T//QC
-    def kernel(pre,sg,tok,ag,wq,wk,wv,wor,cw,sw,qr,kr,vr,attr,lser,tgo,ggo,gq,gk,gv,gwo,normed,normedT,bg,bias,dO,kT,PB,DS,dv,dk,dqT,drow,acc):
+    fast=place is not None
+    if not fast:
+        place=jnp.zeros((8,),jnp.int32)
+    SH=D//8
+    def kernel(pre,plc,sg,tok,ag,wq,wk,wv,wor,cw,sw,qr,kr,vr,attr,lser,tgo,ggo,*rest):
+        if fast:
+            at0,at1,normed,normedT,bg,bias,dO,kT,PB,DS,dv,dk,dqT,drow,acc,GS=rest
+        else:
+            gq,gk,gv,gwo,normed,normedT,bg,bias,dO,kT,PB,DS,dv,dk,dqT,drow,acc=rest
         g=pl.program_id(0)
         @pl.when(g==0)
         def _():
@@ -114,7 +168,11 @@
             a=attr[r,:].astype(f32)
             drow[:,r]=lax.dot_general(hmask,d.astype(f32)*a,(((1,),(1,)),((),())),preferred_element_type=f32,precision=lax.Precision.HIGHEST)
             kT[:,r]=kr[r,:].astype(f32).T.astype(bf16)
-        gwo[...]=tn(attr[...],bg[...]).astype(bf16)
+        gwv=tn(attr[...],bg[...]).astype(bf16)
+        if fast:
+            GS[3,pl.ds(pl.multiple_of(g*GW,GW),GW),:]=gwv
+        else:
+            gwo[...]=gwv
         dv[...]=jnp.zeros_like(dv); dk[...]=jnp.zeros_like(dk)
         lh=lane_head((QC,GW)); lhT=lane_head((T,GW))
         @pl.loop(0,GH)
@@ -147,9 +205,12 @@
             def _(): acc[r,:]=o
             @pl.when(g>0)
             def _(): acc[r,:]+=o
-        gq[...]=nn(normedT[...],PB[:,0:GW]).astype(bf16)
-        gk[...]=nn(normedT[...],PB[:,GW:2*GW]).astype(bf16)
-        gv[...]=nn(normedT[...],PB[:,2*GW:3*GW]).astype(bf16)
+        for i in range(3):
+            gval=nn(normedT[...],PB[:,i*GW:(i+1)*GW]).astype(bf16)
+            if fast:
+                GS[i,:,pl.ds(pl.multiple_of(g*GW,GW),GW)]=gval
+            else:
+                (gq,gk,gv)[i][...]=gval
         @pl.when(g==ng-1)
         def _():
             gg=jnp.zeros((1,D),f32)
@@ -162,19 +223,33 @@
                 w=ngd*ag[...]
                 tgo[r,:]=(sg[r,:]+inv*(w-u*jnp.mean(w*u,axis=1,keepdims=True))).astype(bf16)
             ggo[...]=jnp.broadcast_to(gg,(8,D))
+            if fast:
+                for i in range(4):
+                    for zr in range(4):
+                        for cp in range(2):
+                            src=pl.multiple_of(2*SH*plc[1+zr]+SH*((plc[0]+cp)&1),SH)
+                            (at0,at1)[cp][i,zr]=GS[i,pl.ds(src,SH),:]
     full=lambda s: pl.BlockSpec(s,lambda g:(0,)*len(s))
     col=lambda off: pl.BlockSpec((D,GW),lambda g,off=off:(0,g+off))
     tcol=pl.BlockSpec((T,GW),lambda g:(0,g))
+    if fast:
+        outs=[full((4,4,SH,D))]*2
+        oshape=[jax.ShapeDtypeStruct((4,4,SH,D),bf16)]*2
+        extra=[pltpu.VMEM((4,D,D),bf16)]
+    else:
+        outs=[tcol,tcol,tcol,pl.BlockSpec((GW,D),lambda g:(g,0))]
+        oshape=[jax.ShapeDtypeStruct((D,D),bf16)]*4
+        extra=[]
     rowb=pl.BlockSpec((GW,D),lambda g:(g,0))
     return pl.pallas_call(kernel,grid=(ng,),
-      in_specs=[pl.BlockSpec(memory_space=pltpu.SMEM),full((T,D)),full((T,D)),full((1,D)),col(0),col(ng),col(2*ng),rowb,full((T,128)),full((T,128)),tcol,tcol,tcol,tcol,pl.BlockSpec((1,8,T),lambda g:(g,0,0))],
-      out_specs=[full((T,D)),full((8,D)),tcol,tcol,tcol,rowb],
-      out_shape=[jax.ShapeDtypeStruct((T,D),bf16),jax.ShapeDtypeStruct((8,D),f32)]+[jax.ShapeDtypeStruct((D,D),bf16)]*4,
+      in_specs=[pl.BlockSpec(memory_space=pltpu.SMEM)]*2+[full((T,D)),full((T,D)),full((1,D)),col(0),col(ng),col(2*ng),rowb,full((T,128)),full((T,128)),tcol,tcol,tcol,tcol,pl.BlockSpec((1,8,T),lambda g:(g,0,0))],
+      out_specs=[full((T,D)),full((8,D))]+outs,
+      out_shape=[jax.ShapeDtypeStruct((T,D),bf16),jax.ShapeDtypeStruct((8,D),f32)]+oshape,
       scratch_shapes=[pltpu.VMEM((T,D),bf16),pltpu.VMEM((D,T),bf16),pltpu.VMEM((T,D),bf16),pltpu.VMEM((nq,T,QC),f32),pltpu.VMEM((T,GW),bf16),pltpu.VMEM((GW,T),bf16),
-        pltpu.VMEM((T,T),bf16),pltpu.VMEM((T,T),bf16),pltpu.VMEM((T,GW),f32),pltpu.VMEM((T,GW),f32),pltpu.VMEM((GW,T),f32),pltpu.VMEM((8,T),f32),pltpu.VMEM((T,D),f32)],
+        pltpu.VMEM((T,T),bf16),pltpu.VMEM((T,T),bf16),pltpu.VMEM((T,GW),f32),pltpu.VMEM((T,GW),f32),pltpu.VMEM((GW,T),f32),pltpu.VMEM((8,T),f32),pltpu.VMEM((T,D),f32)]+extra,
       compiler_params=pltpu.CompilerParams(vmem_limit_bytes=60<<20,dimension_semantics=("arbitrary",)),
       cost_estimate=pl.CostEstimate(flops=2*T*D*8*D+10*T*T*D,bytes_accessed=24<<20,transcendentals=12*T*T),
-      name="attn_bwd")(prefix,sgrad,tokens,again[None],wqkv,wqkv,wqkv,wo,cosw,sinw,q,k,v,att,lse)
+      name="attn_bwd")(prefix,place,sgrad,tokens,again[None],wqkv,wqkv,wqkv,wo,cosw,sinw,q,k,v,att,lse)
 
 
 def make_ffn(parts, G, L, cap, D, FF, FB, chunk, out_dt):
@@ -237,9 +312,127 @@
       name="ffn")
     return call
 
-E=16; CAP=120
-
-def route(order, expert_ids, gates, cot, core, G, L, parts):
+
+def ffn_rows(x,s,wg,wu,wd,H,GB,UB,rows):
+    gate=nn(x,wg); up=nn(x,wu); hg=nt(s,wd)
+    sig=1.0/(1.0+jnp.exp(-gate))
+    sil=gate*sig
+    h=(sil*up).astype(bf16)
+    gb=(hg*up*(sig*(1.0+gate*(1.0-sig)))).astype(bf16)
+    ub=(hg*sil).astype(bf16)
+    H[rows,:]=h; GB[rows,:]=gb; UB[rows,:]=ub
+    return nn(h,wd),nt(gb,wg)+nt(ub,wu)
+
+def expert_ffn(place, xs, ss, wg, wu, wd, half, prev=(), FB=512, chunk=480):
+    n=len(xs); RG,D=xs[0].shape; FF=wg.shape[2]; R=n*RG; nf=2; HB=nf*FB
+    SR=D//4; np_=len(prev)
+    def kernel(plc,*refs):
+        xr=refs[:n]; sr=refs[n:2*n]; wgr,wur,wdr=refs[2*n:2*n+3]; o=2*n+3
+        pv=refs[o:o+np_]; o+=np_
+        res=refs[o:o+n]; dgr=refs[o+n:o+2*n]; o+=2*n
+        gf,gi,go,dw,tok,XT,XN,H,GB,UB,AR,AD=refs[o:]
+        f=pl.program_id(0)
+        tok[...]=jnp.zeros_like(tok)
+        @pl.when(f==0)
+        def _():
+            for a in range(n):
+                for b in range(RG//chunk):
+                    XN[...]=xr[a][b*chunk:(b+1)*chunk,:].astype(f32).T.astype(bf16)
+                    for q in range(4):
+                        XT[a*(RG//chunk)+b,q*SR:(q+1)*SR,:]=XN[pl.ds(pl.multiple_of(plc[1+q]*SR,SR),SR),:]
+        for a in range(n):
+            @pl.loop(0,RG//chunk)
+            def _(i):
+                src=pl.ds(pl.multiple_of(i*chunk,chunk),chunk)
+                rows=pl.ds(pl.multiple_of(a*RG+i*chunk,chunk),chunk)
+                r,d=ffn_rows(xr[a][src,:],sr[a][src,:],wgr[0],wur[0],wdr[0],H,GB,UB,rows)
+                @pl.when(f==0)
+                def _():
+                    if np_:
+                        AR[rows,:]=r+pv[a][src,:].astype(f32); AD[rows,:]=d+pv[n+a][src,:].astype(f32)
+                    else:
+                        AR[rows,:]=r; AD[rows,:]=d
+                @pl.when(f>0)
+                def _():
+                    res[a][src,:]=(AR[rows,:]+r).astype(bf16); dgr[a][src,:]=(AD[rows,:]+d).astype(bf16)
+        for t,Y in enumerate((GB,UB)):
+            gv=None
+            for b in range(R//chunk):
+                p=nn(XT[b],Y[b*chunk:(b+1)*chunk,:])
+                gv=p if gv is None else gv+p
+            gv=gv.astype(bf16)
+            cols=pl.ds(pl.multiple_of(t*HB+f*FB,FB),FB)
+            gf[:,cols]=gv[0:2*SR]; gi[:,cols]=gv[2*SR:3*SR]; go[:,cols]=gv[3*SR:4*SR]
+        dv=None
+        for a in range(n):
+            t=tn(H[a*RG:(a+1)*RG,:],sr[a][...])
+            dv=t if dv is None else dv+t
+        dw[...]=dv.astype(bf16)
+    one=pl.Buffered(1)
+    rowspec=pl.BlockSpec((RG,D),lambda f,p:(0,0),pipeline_mode=one)
+    wspec=pl.BlockSpec((1,D,FB),lambda f,p:(p[5],0,f+nf*half))
+    wdspec=pl.BlockSpec((1,FB,D),lambda f,p:(p[5],f+nf*half,0))
+    full=lambda r,c: pl.BlockSpec((r,c),lambda f,p:(0,0),pipeline_mode=one)
+    out=pl.pallas_call(kernel,
+      grid_spec=pltpu.PrefetchScalarGridSpec(num_scalar_prefetch=1,grid=(nf,),
+        in_specs=[rowspec]*(2*n)+[wspec,wspec,wdspec]+[rowspec]*np_,
+        out_specs=[rowspec]*(2*n)+[full(2*SR,2*HB),full(SR,2*HB),full(SR,2*HB),pl.BlockSpec((FB,D),lambda f,p:((1-f) if half else f,0)),full(8,128)],
+        scratch_shapes=[pltpu.VMEM((R//chunk,D,chunk),bf16),pltpu.VMEM((D,chunk),bf16)]+[pltpu.VMEM((R,FB),bf16)]*3+[pltpu.VMEM((R,D),f32)]*2),
+      out_shape=[jax.ShapeDtypeStruct((RG,D),bf16)]*(2*n)+[jax.ShapeDtypeStruct((2*SR,2*HB),bf16)]+[jax.ShapeDtypeStruct((SR,2*HB),bf16)]*2+[jax.ShapeDtypeStruct((HB,D),bf16),jax.ShapeDtypeStruct((8,128),f32)],
+      compiler_params=pltpu.CompilerParams(vmem_limit_bytes=62<<20,dimension_semantics=("arbitrary",)),
+      cost_estimate=pl.CostEstimate(flops=9*R*D*FF,bytes_accessed=3*D*FF*2+4*R*D*2,transcendentals=R*FF//2),
+      name=f"expert_ffn{n}_{half}")(place,*xs,*ss,wg,wu,wd,*prev)
+    return out[:2*n],out[2*n:2*n+3],out[2*n+3],out[2*n+4]
+
+def shared_ffn(place, x, s, wg, wu, wd, FB=512):
+    T,D=x.shape; FF=wg.shape[1]; nf=FF//FB; chunk=T//2
+    SG=D//8; SD=FB//8
+    NR=2*SG*(FB//128)+SD*(D//128)
+    def kernel(plc,xr,sr,wgr,wur,wdr,res,dgr,o0,o1,tok,XT,H,GB,UB,VG,VD):
+        f=pl.program_id(0)
+        tok[...]=jnp.zeros_like(tok)
+        @pl.when(f==0)
+        def _():
+            for b in range(2):
+                XT[:,b*chunk:(b+1)*chunk]=xr[b*chunk:(b+1)*chunk,:].astype(f32).T.astype(bf16)
+        @pl.loop(0,T//chunk)
+        def _(i):
+            rows=pl.ds(pl.multiple_of(i*chunk,chunk),chunk)
+            r,d=ffn_rows(xr[rows,:],sr[rows,:],wgr[...],wur[...],wdr[...],H,GB,UB,rows)
+            @pl.when(f==0)
+            def _():
+                res[rows,:]=r; dgr[rows,:]=d
+            @pl.when(f>0)
+            def _():
+                res[rows,:]+=r; dgr[rows,:]+=d
+        for t,Y in enumerate((GB,UB)):
+            VG[...]=nn(XT[...],Y[...]).astype(bf16)
+            for zr in range(4):
+                for cp in range(2):
+                    src=pl.ds(pl.multiple_of(2*SG*plc[1+zr]+SG*((plc[0]+cp)&1),SG),SG)
+                    for b in range(FB//128):
+                        off=(t*(FB//128)+b)*SG
+                        (o0,o1)[cp][f,zr,off:off+SG,:]=VG[src,b*128:(b+1)*128]
+        VD[...]=tn(H[...],sr[...]).astype(bf16)
+        zr=jnp.where(plc[1]==f,0,jnp.where(plc[2]==f,1,jnp.where(plc[3]==f,2,3)))
+        for cp in range(2):
+            for e in range(4):
+                src=pl.ds(pl.multiple_of(((plc[0]+cp)&1)*4*SD+e*SD,SD),SD)
+                for b in range(D//128):
+                    off=2*SG*(FB//128)+b*SD
+                    (o0,o1)[cp][e,zr,off:off+SD,:]=VD[src,b*128:(b+1)*128]
+    full=lambda sh: pl.BlockSpec(sh,lambda f:(0,)*len(sh))
+    return pl.pallas_call(kernel,grid=(nf,),
+      in_specs=[pl.BlockSpec(memory_space=pltpu.SMEM),full((T,D)),full((T,D)),pl.BlockSpec((D,FB),lambda f:(0,f)),pl.BlockSpec((D,FB),lambda f:(0,f)),pl.BlockSpec((FB,D),lambda f:(f,0))],
+      out_specs=[full((T,D)),full((T,D)),full((4,4,NR,128)),full((4,4,NR,128)),full((8,128))],
+      out_shape=[jax.ShapeDtypeStruct((T,D),f32)]*2+[jax.ShapeDtypeStruct((4,4,NR,128),bf16)]*2+[jax.ShapeDtypeStruct((8,128),f32)],
+      scratch_shapes=[pltpu.VMEM((D,T),bf16)]+[pltpu.VMEM((T,FB),bf16)]*3+[pltpu.VMEM((D,FB),bf16),pltpu.VMEM((FB,D),bf16)],
+      compiler_params=pltpu.CompilerParams(vmem_limit_bytes=62<<20,dimension_semantics=("arbitrary",)),
+      cost_estimate=pl.CostEstimate(flops=2*9*T*D*FF,bytes_accessed=6*D*FF*2+8*T*D*2,transcendentals=T*FF),
+      name="shared_ffn")(place,x,s,wg,wu,wd)
+
+
+def route(order, expert_ids, gates, cot, core, G, L, parts, plane=False):
     T,D=cot.shape; P2=2*T
     LP=L//parts; S=G*LP*CAP
     big=E*CAP
@@ -272,7 +465,9 @@
         posj=nt(jnp.broadcast_to(posr,(16,P2)).astype(bf16),PT[...])[0:1,:]
         e=ecat.astype(jnp.int32)
         l=lax.rem(e,L); j=lax.div(e,L)
-        if parts==2:
+        if plane:
+            base=((lax.div(l,2)*G+j)*2+lax.rem(l,2))*CAP
+        elif parts==2:
             cc=lax.rem(lax.div(l,LP)+core_ref[0],2)
             base=((cc*G+j)*LP+lax.rem(l,LP))*CAP
         else:
@@ -376,7 +571,7 @@
     return jnp.concatenate([c, c, c, c], axis=1), jnp.concatenate([-s, s, -s, s], axis=1)
 
 
-def shards(tokens, cotangent, expert_ids, route_gates, slot_order, prefix_len, attention_gain, qkv_weight,
+def shards_any(tokens, cotangent, expert_ids, route_gates, slot_order, prefix_len, attention_gain, qkv_weight,
            output_weight, feedforward_gain, shared_gate, shared_up, shared_down, expert_gate, expert_up, expert_down):
     T, D = tokens.shape
     L, _, FF = expert_gate.shape
@@ -490,6 +685,165 @@
             dsh[0], dsh[1], dsh[2], finish(0), finish(1), finish(2))
 
 
+def shards_fast(tokens, cotangent, expert_ids, route_gates, slot_order, prefix_len, attention_gain, qkv_weight,
+                output_weight, feedforward_gain, shared_gate, shared_up, shared_down, expert_gate, expert_up, expert_down):
+    T, D = tokens.shape
+    FF = expert_gate.shape[2]
+    i32 = jnp.int32
+    dpi = lax.axis_index("dp").astype(i32)
+    ei = lax.axis_index("expert").astype(i32)
+    core = lax.rem(dpi, 2)
+    zi = lax.div(dpi, 2)
+    outer = (zi == 0) | (zi == 3)
+    low = zi < 2
+    pick = lambda a, b: jnp.where(low, a, b).astype(i32)
+    place = jnp.stack([core, pick(3, 0), pick(2, 1), pick(1, 2), pick(0, 3)])
+    place_a = jnp.concatenate([place, (2 * core)[None]])
+    place_b = jnp.concatenate([place, (2 * core + 1)[None]])
+    plane = [[(2 * z + c) * 4 + e for c in range(2) for e in range(4)] for z in range(4)]
+
+    def swap(x):
+        return lax.ppermute(x, "dp", [(i, i ^ 1) for i in range(8)])
+
+    def inward(x):
+        return lax.ppermute(x, "dp", [(0, 2), (1, 3), (6, 4), (7, 5)])
+
+    def outward(x):
+        return lax.ppermute(x, "dp", [(2, 0), (3, 1), (4, 6), (5, 7)])
+
+    def across(x):
+        return lax.ppermute(x, "dp", [(2, 4), (3, 5), (4, 2), (5, 3)])
+
+    def a2a(x):
+        return lax.all_to_all(x.reshape(8, 2 * CAP, D), ("dp", "expert"), split_axis=0, concat_axis=0,
+                              axis_index_groups=plane, tiled=True)
+
+    def add(*xs):
+        t = xs[0].astype(f32)
+        for x in xs[1:]:
+            t = t + x.astype(f32)
+        return t.astype(bf16)
+
+    def tie(x, token):
+        return lax.optimization_barrier((x, token))[0]
+
+    def zdense(far, inner, out):
+        r = far.shape[0] // 2
+        m = across(add(far, inward(far)))
+        rin = inward(inner)
+        ro = outward(add(out, m[:r]))
+        return jnp.where(outer, add(out, ro), add(inner, m[r:], rin))
+
+    cosw, sinw = rope_wide(T)
+    rows, cols, (s_out,) = route(slot_order, expert_ids, route_gates, cotangent, core[None], 4, 4, 1, True)
+    q, k, v, att, lse, state, ntwo, x_out, sab = attn_fwd(tokens, prefix_len, attention_gain, qkv_weight, output_weight,
+                                                     feedforward_gain, cosw, sinw, rows,
+                                                          s_out.reshape(8, 2 * CAP, D))
+    xab = a2a(x_out)
+    half_rows = lambda y, l: y.reshape(8, 2, CAP, D)[:, l].reshape(8 * CAP, D)
+    sa, sb = half_rows(sab, 0), half_rows(sab, 1)
+    sx = inward(sa)
+    shared_branch, dshared, sh0, sh1, t_sh = shared_ffn(place, ntwo, cotangent, shared_gate, shared_up, shared_down)
+    xa, xb = half_rows(xab, 0), half_rows(xab, 1)
+    xx = inward(xa)
+    ws = (expert_gate, expert_up, expert_down)
+    p0, gb0, wb0, t_b0 = expert_ffn(tie(place_b, t_sh), [xb], [sb], *ws, 0)
+    (rb, db), gb1, wb1, t_b1 = expert_ffn(place_b, [xb], [sb], *ws, 1, p0)
+    rf0 = inward(gb0[0])
+    p0, ga0, wa0, t_a0 = expert_ffn(tie(place_a, t_b1), [xa, xx], [sa, sx], *ws, 0)
+    bs0 = add(gb0[0], tie(rf0, t_a0))
+    (ra, rx, da, dx), ga1, wa1, t_a1 = expert_ffn(tie(place_a, bs0), [xa, xx], [sa, sx], *ws, 1, p0)
+
+    far_w = lambda w0, w1: jnp.where(low, w1, w0)
+    near_w = lambda w0, w1: jnp.where(low, w0, w1)
+    hw = FF // 4
+    bfar = [gb0[0], gb1[0], far_w(wb0, wb1)]
+    bin_ = [gb0[1], gb1[1], near_w(wb0[hw:], wb1[hw:])]
+    bout = [gb0[2], gb1[2], near_w(wb0[:hw], wb1[:hw])]
+    afar = [ga0[0], ga1[0], far_w(wa0, wa1)]
+    ain = [ga0[1], ga1[1], near_w(wa0[hw:], wa1[hw:])]
+    aout = [ga0[2], ga1[2], near_w(wa0[:hw], wa1[:hw])]
+
+    rf = [tie(inward(x), t_a1) for x in bfar[1:]]
+    bm = [across(bs0)] + [across(add(x, r)) for x, r in zip(bfar[1:], rf)]
+    am = [across(x) for x in afar]
+    rin = [inward(x) for x in bin_]
+
+    def both(b, a):
+        return jnp.concatenate([b.reshape(8, 1, CAP, D), a.reshape(8, 1, CAP, D)], axis=1)
+
+    da = jnp.where(outer, outward(dx), da)
+    dback = a2a(both(da, db)).reshape(16 * CAP, D)
+    sgrad, fgg = mid_bwd(cols, [dback], dshared, state, feedforward_gain, cotangent)
+    tokens_grad, agg, at0, at1 = attn_bwd(sgrad, prefix_len, tokens, attention_gain, qkv_weight, output_weight,
+                                          cosw, sinw, q, k, v, att, lse, place)
+    ra = jnp.where(outer, outward(rx), ra)
+    rback = a2a(both(ra, rb)).reshape(16 * CAP, D)
+    block_out = combine(tie(cols, agg), route_gates, [rback], state, shared_branch)
+
+    def last(m, inner, out, r=None):
+        h = m.shape[0] // 2
+        m = tie(m, agg)
+        ro = outward(add(out, m[:h]))
+        if r is None:
+            return jnp.where(outer, ro, add(inner, m[h:]))
+        return jnp.where(outer, add(out, ro), add(inner, m[h:], r))
+
+    eb = [last(m, i, o, r) for m, i, o, r in zip(bm, bin_, bout, rin)]
+    ea = [last(m, i, o) for m, i, o in zip(am, ain, aout)]
+
+    def dense(mine, other):
+        s = add(mine, swap(other))
+        s = lax.all_to_all(s, "expert", split_axis=0, concat_axis=0, tiled=True)
+        s = add(s[0], s[1], s[2], s[3])
+        s = zdense(s[0:2].reshape(-1, s.shape[2]), s[2], s[3])
+        p = [s] + [lax.ppermute(s, "expert", [(e, e ^ kk) for e in range(4)]) for kk in (1, 2, 3)]
+        odd = lax.rem(ei, 2) == 1
+        p = [jnp.where(odd, p[kk ^ 1], p[kk]) for kk in range(4)]
+        return [jnp.where(ei >= 2, p[kk ^ 2], p[kk]) for kk in range(4)]
+
+    shd = jnp.stack(dense(sh0, sh1))
+    nb = FF // 4 // 128
+    sg = D // 8
+    sd = FF // 32
+    cut = nb * sg
+
+    def columns(x):
+        return x.reshape(4, nb, sg, 128).transpose(2, 0, 1, 3).reshape(sg, FF).astype(f32)
+
+    d_gate = columns(shd[:, :cut])
+    d_up = columns(shd[:, cut:2 * cut])
+    d_down = shd[:, 2 * cut:].reshape(4, D // 128, sd, 128).transpose(0, 2, 1, 3).reshape(4 * sd, D).astype(f32)
+    dq, dk, dv, dwo = dense(at0, at1)
+
+    gains = jnp.concatenate([agg[0:1], fgg[0:1]], axis=0)
+    for kk in (1, 2, 4):
+        gains = gains + lax.ppermute(gains, "dp", [(i, i ^ kk) for i in range(8)])
+    for kk in (1, 2):
+        gains = gains + lax.ppermute(gains, "expert", [(i, i ^ kk) for i in range(4)])
+    gains = lax.dynamic_slice_in_dim(gains, dpi * sg, sg, 1)
+
+    def finish(a, b):
+        h = jnp.stack([a, b]).reshape(2, 2, a.shape[0] // 2, a.shape[1])
+        mine = lax.dynamic_index_in_dim(h, core, 1, keepdims=False)
+        other = swap(lax.dynamic_index_in_dim(h, 1 - core, 1, keepdims=False))
+        return jnp.concatenate([jnp.where(core == 0, mine, other), jnp.where(core == 0, other, mine)], axis=0).astype(f32)
+
+    full = [finish(a, b) for a, b in zip(ea, eb)]
+    hc = FF // 2
+    outs = [jnp.concatenate([full[0][:, :, :hc], full[1][:, :, :hc]], axis=2),
+            jnp.concatenate([full[0][:, :, hc:], full[1][:, :, hc:]], axis=2), full[2]]
+    return (block_out, tokens_grad, gains[0], jnp.concatenate([dq, dk, dv], axis=1).astype(f32), dwo.astype(f32), gains[1],
+            d_gate, d_up, d_down, *outs)
+
+
+def shards(*args):
+    local = args[13].shape[0]
+    if lax.axis_size("dp") == 8 and lax.axis_size("expert") == 4 and local == 4:
+        return shards_fast(*args)
+    return shards_any(*args)
+
+
 def solution(mesh):
     row = P(("dp", "expert"), None)
     return jax.shard_map(

time: 885 us -> 729 us (0.82)
  waiting for transfers between devices: 360 us -> 199 us
  blocking collectives: 133 us -> 0 us
  starting transfers between devices: 59.1 us -> 139 us
  Pallas kernels: 217 us -> 275 us
  other arithmetic: 43 us -> 76.9 us
  local copies, waits for them, and re-layouts: 49.7 us -> 29.5 us
  between operations: 15.7 us -> 2.57 us
    reduce_scatter x13 -> x0, waiting for transfers between devices: 269 us -> none  [the longest x6 250 us: shards(): lax.psum_scatter(g[0], 'dp', scatter_dimension=0, tiled=True, axis_index_...]
    ppermute x14 -> x46, waiting for transfers between devices: 2.02 us -> 159 us  [the longest x10 74.6 us: outward(): return lax.ppermute(x, 'dp', [(2, 0), (3, 1), (4, 6), (5, 7)])]
    ppermute x14 -> x46, starting transfers between devices: 2.36 us -> 118 us  [the longest x12 67.4 us: inward(): return lax.ppermute(x, 'dp', [(0, 2), (1, 3), (6, 4), (7, 5)])]
    all_gather x7 -> x0, blocking collectives: 74.9 us -> none  [dense(): return lax.all_gather(zs[0], 'expert', axis=0, tiled=True).astype(f32)]
    pallas_call x4 -> x5, Pallas kernels: 114 us -> 160 us  [the longest x4 124 us: expert_ffn(): pl.pallas_call(kernel, grid_spec=pltpu.PrefetchScalarGridSpec(num_scalar_...]
    psum x1 -> x0, blocking collectives: 46.2 us -> none  [shards(): gains = lax.psum(jnp.stack([agg[0], fgg[0]]), ('dp', 'expert'))]
    all_to_all x14 -> x5, waiting for transfers between devices: 85.7 us -> 40.1 us  [the longest x3 26.4 us: a2a(): lax.all_to_all(x.reshape(8, 2 * CAP, D), ('dp', 'expert'), split_axis=0,...]
    all_to_all x14 -> x5, starting transfers between devices: 56 us -> 21.5 us  [the longest x3 11.7 us: a2a(): lax.all_to_all(x.reshape(8, 2 * CAP, D), ('dp', 'expert'), split_axis=0,...]
  transfers between devices with their start and end apart: 41 -> 51, of which waited for: 16 -> 18; matrix products, arithmetic and copies ran while one was open for 9% -> 12% of each run, Pallas kernels for 20% -> 31%
where the time goes in v2:
time: 729 us; the launch traced here: 723 us
  Pallas kernels  275 us (38%)
  waiting for transfers between devices  199 us (27%)
  starting transfers between devices  139 us (19%)
  other arithmetic  76.9 us (11%)
  local copies, waits for them, and re-layouts  29.5 us (4%)
    pallas_call x4, Pallas kernels, expert_ffn(): pl.pallas_call(kernel, grid_spec=pltpu.PrefetchScalarGridSpec(num_scalar_...  124 us
    ppermute x10, waiting for transfers between devices, outward(): return lax.ppermute(x, 'dp', [(2, 0), (3, 1), (4, 6), (5, 7)])  74.6 us
    ppermute x12, starting transfers between devices, inward(): return lax.ppermute(x, 'dp', [(0, 2), (1, 3), (6, 4), (7, 5)])  67.4 us
    ppermute x12, waiting for transfers between devices, inward(): return lax.ppermute(x, 'dp', [(0, 2), (1, 3), (6, 4), (7, 5)])  53.9 us
    pallas_call x1, Pallas kernels, attn_bwd(): pl.pallas_call(kernel, grid=(ng,), in_specs=[pl.BlockSpec(memory_space=pl...  45.8 us
    pallas_call x1, Pallas kernels, attn_fwd(): pl.pallas_call(kernel, grid=(ng,), in_specs=[pl.BlockSpec(memory_space=pl...  42.4 us
    pallas_call x1, Pallas kernels, shared_ffn(): pl.pallas_call(kernel, grid=(nf,), in_specs=[pl.BlockSpec(memory_space=pl...  35.8 us
    convert_element_type x15, other arithmetic, add(): return t.astype(bf16)  31.9 us
  transfers between devices with their start and end apart: 51, of which 18 were waited for; matrix products, arithmetic and copies ran while one was open for 12% of the time, Pallas kernels for 31%

profile of v2, /device:TPU:0, one launch (start us, length us, event | category | flops | bytes accessed | tf_op | source)
XLA Modules:
  0.0 722.8 jit_solution(896091557822758862)
XLA Ops:
  8.7 10.0 %route.1 = (s32[8,768]{1,0:T(8,128)S(1)}, s32[768,8]{1,0:T(8,128)S(1)}, bf16[1920,768]{1,0:T(8,128)(2,1)}) custom-call(s32[1]{0:T(128)} %bitcast.core_ref, s32[1,1536]{1,0:T(1,128)S(1)} %copy-done.7, s32[768,2]{1,0:T(8,128)S(1)} %copy.38.ids, f32[768,2]{1,0:T(8,128)S(1)} %copy.39.gts.g, bf16[768,768]{1,0:T(8,128)(2,1)S(1)} %copy-done.1), custom_call_target="tpu_custom_call" | custom-call | flops 4680843264 | bytes 8388608 | tf_op jit(solution)/shard_map/route/pallas_call | solution.py:494
  19.2 42.4 %attn_fwd.1 = (bf16[768,768]{1,0:T(8,128)(2,1)}, bf16[768,768]{1,0:T(8,128)(2,1)}, bf16[768,768]{1,0:T(8,128)(2,1)}, bf16[768,768]{1,0:T(8,128)(2,1)}, f32[3,8,7...) custom-call(s32[1]{0:T(128)S(6)} %copy.53.pre, ...), custom_call_target="tpu_custom_call" | custom-call | flops 5435817984 | bytes 16777216 | tf_op jit(solution)/shard_map/attn_fwd/pallas_call | solution.py:130
  61.7 3.7 all-to-all-start
  65.4 3.6 fusion.37
  69.0 4.6 collective-permute-start.2
  74.2 26.4 %all-to-all-done = bf16[8,240,768]{2,1,0:T(8,128)(2,1)S(1)} async-done(((bf16[8,240,768]{2,1,0:T(8,128)(2,1)}), bf16[8,240,768]{2,1,0:T(8,128)(2,1)S(1)}, u32[]{:S(2)}, u32[]{:S(2)}) %all-to-all-start) | async-done | bytes 2949152 | tf_op jit(solution)/shard_map/all_to_all | solution.py:718
  102.4 4.6 collective-permute-start.1
  107.0 35.8 %shared_ffn.1 = (f32[768,768]{1,0:T(8,128)}, f32[768,768]{1,0:T(8,128)}, bf16[4,4,1152,128]{3,2,1,0:T(8,128)(2,1)}, bf16[4,4,1152,128]{3,2,1,0:T(8,128)(2,1)}, f32[8,128]{1,0:T(8,128)}) custom-call(s32[5]{0:T(128)} %stack.62.plc, bf16[768,768]{1,0:T(8,128)(2,1)} %get-tuple-element.89.xr, bf16[768,768]{1,0:T(8,128)(2,1)} %refs_4_.9, bf16[768,2048]{1,0:T(8,128)(2,1)} %wgr.1, ...), custom_call_target="tpu_custom_call" | custom-call | flops 21743271936 | bytes 28311552 | tf_op jit(solution)/shard_map/shared_ffn/pallas_call | solution.py:425
  144.1 21.9 %expert_ffn1_0.1 = (bf16[960,768]{1,0:T(8,128)(2,1)}, bf16[960,768]{1,0:T(8,128)(2,1)}, bf16[384,2048]{1,0:T(8,128)(2,1)}, bf16[192,2048]{1,0:T(8,128)(2,1)}, bf...) custom-call(s32[6]{0:T(128)} %concatenate.45.plc, bf16[960,768]{1,0:T(8,128)(2,1)} %bitcast.139, ...), custom_call_target="tpu_custom_call" | custom-call | flops 13589544960 | bytes 15335424 | tf_op jit(solution)/shard_map/expert_ffn1_0/pallas_call | solution.py:376
  166.0 2.6 collective-permute-start
  168.7 39.1 %expert_ffn2_0.1 = (bf16[960,768]{1,0:T(8,128)(2,1)}, bf16[960,768]{1,0:T(8,128)(2,1)}, bf16[960,768]{1,0:T(8,128)(2,1)}, bf16[960,768]{1,0:T(8,128)(2,1)}, bf16...) custom-call(s32[6]{0:T(128)} %concatenate.44.plc, ...), custom_call_target="tpu_custom_call" | custom-call | flops 27179089920 | bytes 21233664 | tf_op jit(solution)/shard_map/expert_ffn2_0/pallas_call | solution.py:376
  207.8 3.3 add_convert_fusion.4
  211.1 40.3 %expert_ffn2_1.1 = (bf16[960,768]{1,0:T(8,128)(2,1)}, bf16[960,768]{1,0:T(8,128)(2,1)}, bf16[960,768]{1,0:T(8,128)(2,1)}, bf16[960,768]{1,0:T(8,128)(2,1)}, bf16...) custom-call(s32[6]{0:T(128)} %concatenate.44.plc, ...), custom_call_target="tpu_custom_call" | custom-call | flops 27179089920 | bytes 21233664 | tf_op jit(solution)/shard_map/expert_ffn2_1/pallas_call | solution.py:376
  252.7 23.1 %expert_ffn1_1.1 = (bf16[960,768]{1,0:T(8,128)(2,1)}, bf16[960,768]{1,0:T(8,128)(2,1)}, bf16[384,2048]{1,0:T(8,128)(2,1)}, bf16[192,2048]{1,0:T(8,128)(2,1)}, bf...) custom-call(s32[6]{0:T(128)} %concatenate.45.plc, bf16[960,768]{1,0:T(8,128)(2,1)} %bitcast.140, ...), custom_call_target="tpu_custom_call" | custom-call | flops 13589544960 | bytes 15335424 | tf_op jit(solution)/shard_map/expert_ffn1_1/pallas_call | solution.py:376
  275.8 6.8 collective-permute-start.34
  282.6 2.9 broadcast_select_fusion
  292.2 3.6 all-to-all-start.1
  297.1 6.6 collective-permute-start.37
  306.1 10.4 %collective-permute-done.34 = bf16[384,2048]{1,0:T(8,128)(2,1)} collective-permute-done((bf16[384,2048]{1,0:T(8,128)(2,1)}, bf16[384,2048]{1,0:T(8,128)(2,1)}, u32[]{:S(2)}, u32[]{:S(2)}) %collective-permute-start.34) | collective-permute-done | bytes 1572896 | tf_op jit(solution)/shard_map/ppermute | solution.py:709
  318.4 31.8 %collective-permute-done.41 = bf16[1024,768]{1,0:T(8,128)(2,1)} collective-permute-done((bf16[1024,768]{1,0:T(8,128)(2,1)}, bf16[1024,768]{1,0:T(8,128)(2,1)}, u32[]{:S(2)}, u32[]{:S(2)}) %collective-permute-start.41) | collective-permute-done | bytes 1572896 | tf_op jit(solution)/shard_map/ppermute | solution.py:709
  352.0 3.5 add_convert_fusion.2
  355.5 3.3 add_convert_fusion.3
  366.1 4.4 all-to-all-start.2
  372.9 7.3 %add_convert_fusion = bf16[4,4,1152,128]{3,2,1,0:T(8,128)(2,1)} fusion(bf16[4,4,1152,128]{3,2,1,0:T(8,128)(2,1)} %collective-permute-done.18, bf16[4,4,1152,128]{3,2,1,0:T(8,128)(2,1)} %get-tuple-element.108), kind=kLoop, calls=%fused_computation | loop fusion | flops 9437184 | bytes 14155776 | tf_op jit(solution)/shard_map/convert_element_type | solution.py:725
  380.2 7.5 %mid_bwd.1 = (f32[768,768]{1,0:T(8,128)S(1)}, f32[8,768]{1,0:T(8,128)S(1)}) custom-call(s32[768,8]{1,0:T(8,128)S(1)} %get-tuple-element.99.colr, bf16[1920,768]{1,0:T(8,128)(2,1)} %bitcast.111, f32[768,768]{1,0:T(8,128)} %get-tuple-element.90.refs_1_, f32[768,768]{1,0:T(8,128)} %get-tuple-element.91.refs_2_.refs_1_, f32[1,768]{1,0:T(1,128)S(1)} %copy-done.5, ...), custom_call_target="tpu_custom_call" | custom-call | flops 2264924160 | bytes 12582912 | tf_op jit(solution)/shard_map/mid_bwd/pallas_call | solution.py:557
  389.1 45.8 %attn_bwd.1 = (bf16[768,768]{1,0:T(8,128)(2,1)}, f32[8,768]{1,0:T(8,128)}, bf16[4,4,96,768]{3,2,1,0:T(8,128)(2,1)}, bf16[4,4,96,768]{3,2,1,0:T(8,128)(2,1)}) custom-call(s32[1]{0:T(128)S(6)} %copy.53.pre, s32[5]{0:T(128)} %stack.62.plc, f32[768,768]{1,0:T(8,128)} %copy-done.6, bf16[768,768]{1,0:T(8,128)(2,1)} %tok.3, f32[1,768]{1,0:T(1,128)} %broadcast_in_dim.22.ag, ...), custom_call_target="tpu_custom_call" | custom-call | flops 11777605632 | bytes 25165824 | tf_op jit(solution)/shard_map/attn_bwd/pallas_call | solution.py:244
  436.3 9.8 %collective-permute-start.30 = (bf16[192,2048]{1,0:T(8,128)(2,1)}, bf16[192,2048]{1,0:T(8,128)(2,1)}, u32[]{:S(2)}, u32[]{:S(2)}) collective-permute-start(bf16[192,2048]{1,0:T(8,128)(2,1)} %get-tuple-element.116), channel_id=1, source_target_pairs={{0,8},{4,12},{24,16},{28,20},{1,9},{5,13},{25,17},{29,21},{2,10},{... | collective-permute-start | bytes 2359304 | tf_op jit(solution)/shard_map/ppermute | solution.py:709
  447.9 5.0 all-to-all-start.4
  452.9 2.6 add_convert_fusion.11
  460.0 14.5 %collective-permute-start.6 = (f32[2,768]{1,0:T(2,128)S(1)}, f32[2,768]{1,0:T(2,128)S(1)}, u32[]{:S(2)}, u32[]{:S(2)}) collective-permute-start(f32[2,768]{1,0:T(2,128)S(1)} %fusion.34), channel_id=1, source_target_pairs={{0,8},{4,12},{8,0},{12,4},{16,24},{20,28},{24,16},{28,20},{1,9},{5... | collective-permute-start | bytes 18440 | tf_op jit(solution)/shard_map/ppermute | solution.py:821
  479.4 9.4 %combine.1 = bf16[768,768]{1,0:T(8,128)(2,1)} custom-call(s32[768,8]{1,0:T(8,128)S(1)} %get-tuple-element.99.colr, f32[768,2]{1,0:T(8,128)S(1)} %copy-done.4, bf16[1920,768]{1,0:T(8,128)(2,1)} %bitcast.22.refs_0_, f32[768,768]{1,0:T(8,128)S(1)} %copy-done, f32[768,768]{1,0:T(8,128)} %get-tuple-element.103.refs_2_), custom_call_target="tpu_custom_call" | custom-call | flops 4529848320 | bytes 9437184 | tf_op jit(solution)/shard_map/combine/pallas_call | solution.py:535
  488.8 10.7 %collective-permute-start.44 = (bf16[512,768]{1,0:T(8,128)(2,1)}, bf16[512,768]{1,0:T(8,128)(2,1)}, u32[]{:S(2)}, u32[]{:S(2)}) collective-permute-start(bf16[512,768]{1,0:T(8,128)(2,1)} %slice_select_fusion), channel_id=1, source_target_pairs={{0,8},{4,12},{24,16},{28,20},{1,9},{5,13},{25,17},{29,21},{2,10},{... | collective-permute-start | bytes 2359304 | tf_op jit(solution)/shard_map/ppermute | solution.py:709
  499.5 27.2 %collective-permute-done.7 = f32[2,768]{1,0:T(2,128)S(1)} collective-permute-done((f32[2,768]{1,0:T(2,128)S(1)}, f32[2,768]{1,0:T(2,128)S(1)}, u32[]{:S(2)}, u32[]{:S(2)}) %collective-permute-start.7) | collective-permute-done | bytes 6176 | tf_op jit(solution)/shard_map/ppermute | solution.py:821
  535.3 3.1 add_convert_fusion.5
  538.5 5.7 collective-permute-start.19
  544.8 7.2 collective-permute-done.19
  557.1 17.3 %collective-permute-done.33 = bf16[192,2048]{1,0:T(8,128)(2,1)S(1)} collective-permute-done((bf16[192,2048]{1,0:T(8,128)(2,1)S(1)}, bf16[192,2048]{1,0:T(8,128)(2,1)S(1)}, u32[]{:S(2)}, u32[]{:S(2)}) %collective-permute-start.33) | collective-permute-done | bytes 786464 | tf_op jit(solution)/shard_map/ppermute | solution.py:712
  577.3 13.9 %collective-permute-done.27 = bf16[192,2048]{1,0:T(8,128)(2,1)S(1)} collective-permute-done((bf16[192,2048]{1,0:T(8,128)(2,1)S(1)}, bf16[192,2048]{1,0:T(8,128)(2,1)S(1)}, u32[]{:S(2)}, u32[]{:S(2)}) %collective-permute-start.27) | collective-permute-done | bytes 786464 | tf_op jit(solution)/shard_map/ppermute | solution.py:712
  596.6 11.5 %collective-permute-done.29 = bf16[192,2048]{1,0:T(8,128)(2,1)S(1)} collective-permute-done((bf16[192,2048]{1,0:T(8,128)(2,1)S(1)}, bf16[192,2048]{1,0:T(8,128)(2,1)S(1)}, u32[]{:S(2)}, u32[]{:S(2)}) %collective-permute-start.29) | collective-permute-done | bytes 786464 | tf_op jit(solution)/shard_map/ppermute | solution.py:712
  612.3 12.6 %collective-permute-done.43 = bf16[512,768]{1,0:T(8,128)(2,1)S(1)} collective-permute-done((bf16[512,768]{1,0:T(8,128)(2,1)S(1)}, bf16[512,768]{1,0:T(8,128)(2,1)S(1)}, u32[]{:S(2)}, u32[]{:S(2)}) %collective-permute-start.43) | collective-permute-done | bytes 786464 | tf_op jit(solution)/shard_map/ppermute | solution.py:712
  627.7 9.3 %collective-permute-done.40 = bf16[512,768]{1,0:T(8,128)(2,1)S(1)} collective-permute-done((bf16[512,768]{1,0:T(8,128)(2,1)S(1)}, bf16[512,768]{1,0:T(8,128)(2,1)S(1)}, u32[]{:S(2)}, u32[]{:S(2)}) %collective-permute-start.40) | collective-permute-done | bytes 786464 | tf_op jit(solution)/shard_map/ppermute | solution.py:712
  641.0 4.6 collective-permute-done.21
  654.8 4.7 all-to-all-start.3
  669.6 13.7 %all-to-all-done.3 = bf16[4,4,96,768]{3,2,1,0:T(8,128)(2,1)} async-done(((bf16[4,4,96,768]{3,2,1,0:T(8,128)(2,1)}), bf16[4,4,96,768]{3,2,1,0:T(8,128)(2,1)}, u32[]{:S(2)}, u32[]{:S(2)}) %all-to-all-start.3) | async-done | bytes 2359328 | tf_op jit(solution)/shard_map/all_to_all | solution.py:797
  685.2 4.6 collective-permute-start.11
  691.2 4.5 collective-permute-done.11
  696.7 7.5 %collective-permute-start.14 = (bf16[96,768]{1,0:T(8,128)(2,1)S(1)}, bf16[96,768]{1,0:T(8,128)(2,1)S(1)}, u32[]{:S(2)}, u32[]{:S(2)}) collective-permute-start(bf16[96,768]{1,0:T(8,128)(2,1)S(1)} %slice_bitcast_fusion.2), channel_id=1, source_target_pairs={{0,8},{4,12},{24,16},{28,20},{1,9},{5,13},{25,17},{29,21},{2,10},{... | collective-permute-start | bytes 442376 | tf_op jit(solution)/shard_map/ppermute | solution.py:709
  707.3 5.1 collective-permute-done.13
  (247 shorter events, 120.4 us)
Async XLA Ops:
  61.7 38.9 %all-to-all-start = ((bf16[8,240,768]{2,1,0:T(8,128)(2,1)}), bf16[8,240,768]{2,1,0:T(8,128)(2,1)S(1)}, u32[]{:S(2)}, u32[]{:S(2)}) async-start(bf16[8,240,768]{2,1,0:T(8,128)(2,1)} %bitcast.130), calls=%async_computation | async-start | bytes 5898240 | tf_op jit(solution)/shard_map/all_to_all | solution.py:718
  69.0 99.7 %collective-permute-start.2 = (bf16[960,768]{1,0:T(8,128)(2,1)}, bf16[960,768]{1,0:T(8,128)(2,1)}, u32[]{:S(2)}, u32[]{:S(2)}) collective-permute-start(bf16[960,768]{1,0:T(8,128)(2,1)} %bitcast.14.refs_2_), channel_id=1, source_target_pairs={{0,8},{4,12},{24,16},{28,20},{1,9},{5,13},{25,17},{29,21},{2,10},{... | collective-permute-start | bytes 4423688 | tf_op jit(solution)/shard_map/ppermute | solution.py:709
  102.4 66.2 %collective-permute-start.1 = (bf16[960,768]{1,0:T(8,128)(2,1)}, bf16[960,768]{1,0:T(8,128)(2,1)}, u32[]{:S(2)}, u32[]{:S(2)}) collective-permute-start(bf16[960,768]{1,0:T(8,128)(2,1)} %bitcast.13.refs_0_), channel_id=1, source_target_pairs={{0,8},{4,12},{24,16},{28,20},{1,9},{5,13},{25,17},{29,21},{2,10},{... | collective-permute-start | bytes 4423688 | tf_op jit(solution)/shard_map/ppermute | solution.py:709
  142.8 229.3 %collective-permute-start.18 = (bf16[4,4,1152,128]{3,2,1,0:T(8,128)(2,1)}, bf16[4,4,1152,128]{3,2,1,0:T(8,128)(2,1)}, u32[]{:S(2)}, u32[]{:S(2)}) collective-permute-start(bf16[4,4,1152,128]{3,2,1,0:T(8,128)(2,1)} %get-tuple-element.109), channel_id=1, source_target_pairs={{0,4},{4,0},{8,12},{12,8},{16,20},{20,16},{24,28},{28,24},{1,5},{5... | collective-permute-start | bytes 14155784 | tf_op jit(solution)/shard_map/ppermute | solution.py:706
  166.0 41.8 %collective-permute-start = (bf16[384,2048]{1,0:T(8,128)(2,1)}, bf16[384,2048]{1,0:T(8,128)(2,1)}, u32[]{:S(2)}, u32[]{:S(2)}) collective-permute-start(bf16[384,2048]{1,0:T(8,128)(2,1)} %get-tuple-element.78), channel_id=1, source_target_pairs={{0,8},{4,12},{24,16},{28,20},{1,9},{5,13},{25,17},{29,21},{2,10},{... | collective-permute-start | bytes 4718600 | tf_op jit(solution)/shard_map/ppermute | solution.py:709
  251.4 36.9 %collective-permute-start.3 = (bf16[960,768]{1,0:T(8,128)(2,1)}, bf16[960,768]{1,0:T(8,128)(2,1)}, u32[]{:S(2)}, u32[]{:S(2)}) collective-permute-start(bf16[960,768]{1,0:T(8,128)(2,1)} %get-tuple-element.84), channel_id=1, source_target_pairs={{8,0},{12,4},{16,24},{20,28},{9,1},{13,5},{17,25},{21,29},{10,2},{... | collective-permute-start | bytes 4423688 | tf_op jit(solution)/shard_map/ppermute | solution.py:712
  275.8 40.7 %collective-permute-start.34 = (bf16[384,2048]{1,0:T(8,128)(2,1)}, bf16[384,2048]{1,0:T(8,128)(2,1)}, u32[]{:S(2)}, u32[]{:S(2)}) collective-permute-start(bf16[384,2048]{1,0:T(8,128)(2,1)} %get-tuple-element.122), channel_id=1, source_target_pairs={{0,8},{4,12},{24,16},{28,20},{1,9},{5,13},{25,17},{29,21},{2,10},{... | collective-permute-start | bytes 4718600 | tf_op jit(solution)/shard_map/ppermute | solution.py:709
  285.5 64.7 %collective-permute-start.41 = (bf16[1024,768]{1,0:T(8,128)(2,1)}, bf16[1024,768]{1,0:T(8,128)(2,1)}, u32[]{:S(2)}, u32[]{:S(2)}) collective-permute-start(bf16[1024,768]{1,0:T(8,128)(2,1)} %broadcast_select_fusion), channel_id=1, source_target_pairs={{0,8},{4,12},{24,16},{28,20},{1,9},{5,13},{25,17},{29,21},{2,10},{... | collective-permute-start | bytes 4718600 | tf_op jit(solution)/shard_map/ppermute | solution.py:709
  292.2 72.3 %all-to-all-start.1 = ((bf16[8,240,768]{2,1,0:T(8,128)(2,1)}), bf16[8,240,768]{2,1,0:T(8,128)(2,1)S(1)}, u32[]{:S(2)}, u32[]{:S(2)}) async-start(bf16[8,240,768]{2,1,0:T(8,128)(2,1)} %bitcast.112), calls=%async_computation.1 | async-start | bytes 5898240 | tf_op jit(solution)/shard_map/all_to_all | solution.py:718
  295.8 62.9 %collective-permute-start.4 = (bf16[960,768]{1,0:T(8,128)(2,1)}, bf16[960,768]{1,0:T(8,128)(2,1)}, u32[]{:S(2)}, u32[]{:S(2)}) collective-permute-start(bf16[960,768]{1,0:T(8,128)(2,1)} %get-tuple-element.100), channel_id=1, source_target_pairs={{8,0},{12,4},{16,24},{20,28},{9,1},{13,5},{17,25},{21,29},{10,2},{... | collective-permute-start | bytes 4423688 | tf_op jit(solution)/shard_map/ppermute | solution.py:712
  297.1 256.3 %collective-permute-start.37 = (bf16[192,2048]{1,0:T(8,128)(2,1)}, bf16[192,2048]{1,0:T(8,128)(2,1)}, u32[]{:S(2)}, u32[]{:S(2)}) collective-permute-start(bf16[192,2048]{1,0:T(8,128)(2,1)} %get-tuple-element.126), channel_id=1, source_target_pairs={{0,8},{4,12},{24,16},{28,20},{1,9},{5,13},{25,17},{29,21},{2,10},{... | collective-permute-start | bytes 2359304 | tf_op jit(solution)/shard_map/ppermute | solution.py:709
  316.5 131.4 %collective-permute-start.26 = (bf16[384,2048]{1,0:T(8,128)(2,1)}, bf16[384,2048]{1,0:T(8,128)(2,1)}, u32[]{:S(2)}, u32[]{:S(2)}) collective-permute-start(bf16[384,2048]{1,0:T(8,128)(2,1)} %get-tuple-element.111), channel_id=1, source_target_pairs={{8,16},{12,20},{16,8},{20,12},{9,17},{13,21},{17,9},{21,13},{10,18... | collective-permute-start | bytes 4718600 | tf_op jit(solution)/shard_map/ppermute | solution.py:715
  350.2 108.9 %collective-permute-start.28 = (bf16[384,2048]{1,0:T(8,128)(2,1)}, bf16[384,2048]{1,0:T(8,128)(2,1)}, u32[]{:S(2)}, u32[]{:S(2)}) collective-permute-start(bf16[384,2048]{1,0:T(8,128)(2,1)} %add_convert_fusion.4), channel_id=1, source_target_pairs={{8,16},{12,20},{16,8},{20,12},{9,17},{13,21},{17,9},{21,13},{10,18... | collective-permute-start | bytes 4718600 | tf_op jit(solution)/shard_map/ppermute | solution.py:715
  358.8 77.5 %collective-permute-start.32 = (bf16[384,2048]{1,0:T(8,128)(2,1)}, bf16[384,2048]{1,0:T(8,128)(2,1)}, u32[]{:S(2)}, u32[]{:S(2)}) collective-permute-start(bf16[384,2048]{1,0:T(8,128)(2,1)} %get-tuple-element.118), channel_id=1, source_target_pairs={{8,16},{12,20},{16,8},{20,12},{9,17},{13,21},{17,9},{21,13},{10,18... | collective-permute-start | bytes 4718600 | tf_op jit(solution)/shard_map/ppermute | solution.py:715
  366.1 81.9 %all-to-all-start.2 = ((bf16[8,240,768]{2,1,0:T(8,128)(2,1)}), bf16[8,240,768]{2,1,0:T(8,128)(2,1)}, u32[]{:S(2)}, u32[]{:S(2)}) async-start(bf16[8,240,768]{2,1,0:T(8,128)(2,1)} %bitcast.113), calls=%async_computation.2 | async-start | bytes 5898240 | tf_op jit(solution)/shard_map/all_to_all | solution.py:718
  372.1 74.0 %collective-permute-start.35 = (bf16[384,2048]{1,0:T(8,128)(2,1)}, bf16[384,2048]{1,0:T(8,128)(2,1)S(1)}, u32[]{:S(2)}, u32[]{:S(2)}) collective-permute-start(bf16[384,2048]{1,0:T(8,128)(2,1)} %add_convert_fusion.3), channel_id=1, source_target_pairs={{8,16},{12,20},{16,8},{20,12},{9,17},{13,21},{17,9},{21,13},{10,18... | collective-permute-start | bytes 4718600 | tf_op jit(solution)/shard_map/ppermute | solution.py:715
  436.3 157.9 %collective-permute-start.30 = (bf16[192,2048]{1,0:T(8,128)(2,1)}, bf16[192,2048]{1,0:T(8,128)(2,1)}, u32[]{:S(2)}, u32[]{:S(2)}) collective-permute-start(bf16[192,2048]{1,0:T(8,128)(2,1)} %get-tuple-element.116), channel_id=1, source_target_pairs={{0,8},{4,12},{24,16},{28,20},{1,9},{5,13},{25,17},{29,21},{2,10},{... | collective-permute-start | bytes 2359304 | tf_op jit(solution)/shard_map/ppermute | solution.py:709
  446.1 42.7 %collective-permute-start.39 = (bf16[1024,768]{1,0:T(8,128)(2,1)S(1)}, bf16[1024,768]{1,0:T(8,128)(2,1)}, u32[]{:S(2)}, u32[]{:S(2)}) collective-permute-start(bf16[1024,768]{1,0:T(8,128)(2,1)S(1)} %broadcast_select_fusion.1), channel_id=1, source_target_pairs={{8,16},{12,20},{16,8},{20,12},{9,17},{13,21},{17,9},{21,13},{10,18... | collective-permute-start | bytes 4718600 | tf_op jit(solution)/shard_map/ppermute | solution.py:715
  447.9 12.1 %collective-permute-start.5 = (f32[2,768]{1,0:T(2,128)}, f32[2,768]{1,0:T(2,128)S(1)}, u32[]{:S(2)}, u32[]{:S(2)}) collective-permute-start(f32[2,768]{1,0:T(2,128)} %pad_maximum_fusion.7), channel_id=1, source_target_pairs={{0,4},{4,0},{8,12},{12,8},{16,20},{20,16},{24,28},{28,24},{1,5},{5... | collective-permute-start | bytes 18440 | tf_op jit(solution)/shard_map/ppermute | solution.py:821
  447.9 87.4 %all-to-all-start.4 = ((bf16[4,4,1152,128]{3,2,1,0:T(8,128)(2,1)}), bf16[4,4,1152,128]{3,2,1,0:T(8,128)(2,1)}, u32[]{:S(2)}, u32[]{:S(2)}) async-start(bf16[4,4,1152,128]{3,2,1,0:T(8,128)(2,1)} %add_convert_fusion), calls=%async_computation.4 | async-start | bytes 9437184 | tf_op jit(solution)/shard_map/all_to_all | solution.py:797
  459.1 71.1 %collective-permute-start.42 = (bf16[1024,768]{1,0:T(8,128)(2,1)S(1)}, bf16[1024,768]{1,0:T(8,128)(2,1)S(1)}, u32[]{:S(2)}, u32[]{:S(2)}) collective-permute-start(bf16[1024,768]{1,0:T(8,128)(2,1)S(1)} %copy-done.27), channel_id=1, source_target_pairs={{8,16},{12,20},{16,8},{20,12},{9,17},{13,21},{17,9},{21,13},{10,18... | collective-permute-start | bytes 4718600 | tf_op jit(solution)/shard_map/ppermute | solution.py:715
  460.0 16.8 %collective-permute-start.6 = (f32[2,768]{1,0:T(2,128)S(1)}, f32[2,768]{1,0:T(2,128)S(1)}, u32[]{:S(2)}, u32[]{:S(2)}) collective-permute-start(f32[2,768]{1,0:T(2,128)S(1)} %fusion.34), channel_id=1, source_target_pairs={{0,8},{4,12},{8,0},{12,4},{16,24},{20,28},{24,16},{28,20},{1,9},{5... | collective-permute-start | bytes 18440 | tf_op jit(solution)/shard_map/ppermute | solution.py:821
  476.9 49.9 %collective-permute-start.7 = (f32[2,768]{1,0:T(2,128)S(1)}, f32[2,768]{1,0:T(2,128)S(1)}, u32[]{:S(2)}, u32[]{:S(2)}) collective-permute-start(f32[2,768]{1,0:T(2,128)S(1)} %fusion.40), channel_id=1, source_target_pairs={{0,16},{4,20},{8,24},{12,28},{16,0},{20,4},{24,8},{28,12},{1,17},{... | collective-permute-start | bytes 18440 | tf_op jit(solution)/shard_map/ppermute | solution.py:821
  488.8 122.8 %collective-permute-start.44 = (bf16[512,768]{1,0:T(8,128)(2,1)}, bf16[512,768]{1,0:T(8,128)(2,1)}, u32[]{:S(2)}, u32[]{:S(2)}) collective-permute-start(bf16[512,768]{1,0:T(8,128)(2,1)} %slice_select_fusion), channel_id=1, source_target_pairs={{0,8},{4,12},{24,16},{28,20},{1,9},{5,13},{25,17},{29,21},{2,10},{... | collective-permute-start | bytes 2359304 | tf_op jit(solution)/shard_map/ppermute | solution.py:709
  530.2 23.4 %collective-permute-start.36 = (bf16[192,2048]{1,0:T(8,128)(2,1)}, bf16[192,2048]{1,0:T(8,128)(2,1)}, u32[]{:S(2)}, u32[]{:S(2)}) collective-permute-start(bf16[192,2048]{1,0:T(8,128)(2,1)} %fusion.2), channel_id=1, source_target_pairs={{8,0},{12,4},{16,24},{20,28},{9,1},{13,5},{17,25},{21,29},{10,2},{... | collective-permute-start | bytes 2359304 | tf_op jit(solution)/shard_map/ppermute | solution.py:712
  538.5 13.5 %collective-permute-start.19 = (bf16[2304,128]{1,0:T(8,128)(2,1)S(1)}, bf16[2304,128]{1,0:T(8,128)(2,1)S(1)}, u32[]{:S(2)}, u32[]{:S(2)}) collective-permute-start(bf16[2304,128]{1,0:T(8,128)(2,1)S(1)} %bitcast.132), channel_id=1, source_target_pairs={{0,8},{4,12},{24,16},{28,20},{1,9},{5,13},{25,17},{29,21},{2,10},{... | collective-permute-start | bytes 1769480 | tf_op jit(solution)/shard_map/ppermute | solution.py:709
  552.0 22.4 %collective-permute-start.33 = (bf16[192,2048]{1,0:T(8,128)(2,1)S(1)}, bf16[192,2048]{1,0:T(8,128)(2,1)S(1)}, u32[]{:S(2)}, u32[]{:S(2)}) collective-permute-start(bf16[192,2048]{1,0:T(8,128)(2,1)S(1)} %copy-done.43), channel_id=1, source_target_pairs={{8,0},{12,4},{16,24},{20,28},{9,1},{13,5},{17,25},{21,29},{10,2},{... | collective-permute-start | bytes 2359304 | tf_op jit(solution)/shard_map/ppermute | solution.py:712
  553.5 98.2 %collective-permute-start.10 = (bf16[4,4,96,768]{3,2,1,0:T(8,128)(2,1)S(1)}, bf16[4,4,96,768]{3,2,1,0:T(8,128)(2,1)S(1)}, u32[]{:S(2)}, u32[]{:S(2)}) collective-permute-start(bf16[4,4,96,768]{3,2,1,0:T(8,128)(2,1)S(1)} %copy-done.48), channel_id=1, source_target_pairs={{0,4},{4,0},{8,12},{12,8},{16,20},{20,16},{24,28},{28,24},{1,5},{5... | collective-permute-start | bytes 7077896 | tf_op jit(solution)/shard_map/ppermute | solution.py:706
  553.6 37.6 %collective-permute-start.27 = (bf16[192,2048]{1,0:T(8,128)(2,1)S(1)}, bf16[192,2048]{1,0:T(8,128)(2,1)S(1)}, u32[]{:S(2)}, u32[]{:S(2)}) collective-permute-start(bf16[192,2048]{1,0:T(8,128)(2,1)S(1)} %copy-done.42), channel_id=1, source_target_pairs={{8,0},{12,4},{16,24},{20,28},{9,1},{13,5},{17,25},{21,29},{10,2},{... | collective-permute-start | bytes 2359304 | tf_op jit(solution)/shard_map/ppermute | solution.py:712
  574.4 33.7 %collective-permute-start.29 = (bf16[192,2048]{1,0:T(8,128)(2,1)S(1)}, bf16[192,2048]{1,0:T(8,128)(2,1)S(1)}, u32[]{:S(2)}, u32[]{:S(2)}) collective-permute-start(bf16[192,2048]{1,0:T(8,128)(2,1)S(1)} %copy-done.41), channel_id=1, source_target_pairs={{8,0},{12,4},{16,24},{20,28},{9,1},{13,5},{17,25},{21,29},{10,2},{... | collective-permute-start | bytes 2359304 | tf_op jit(solution)/shard_map/ppermute | solution.py:712
  591.2 33.7 %collective-permute-start.43 = (bf16[512,768]{1,0:T(8,128)(2,1)S(1)}, bf16[512,768]{1,0:T(8,128)(2,1)S(1)}, u32[]{:S(2)}, u32[]{:S(2)}) collective-permute-start(bf16[512,768]{1,0:T(8,128)(2,1)S(1)} %copy-done.47), channel_id=1, source_target_pairs={{8,0},{12,4},{16,24},{20,28},{9,1},{13,5},{17,25},{21,29},{10,2},{... | collective-permute-start | bytes 2359304 | tf_op jit(solution)/shard_map/ppermute | solution.py:712
  595.2 41.8 %collective-permute-start.40 = (bf16[512,768]{1,0:T(8,128)(2,1)S(1)}, bf16[512,768]{1,0:T(8,128)(2,1)S(1)}, u32[]{:S(2)}, u32[]{:S(2)}) collective-permute-start(bf16[512,768]{1,0:T(8,128)(2,1)S(1)} %copy-done.46), channel_id=1, source_target_pairs={{8,0},{12,4},{16,24},{20,28},{9,1},{13,5},{17,25},{21,29},{10,2},{... | collective-permute-start | bytes 2359304 | tf_op jit(solution)/shard_map/ppermute | solution.py:712
  608.1 32.9 %collective-permute-start.22 = (bf16[1152,128]{1,0:T(8,128)(2,1)S(1)}, bf16[1152,128]{1,0:T(8,128)(2,1)S(1)}, u32[]{:S(2)}, u32[]{:S(2)}) collective-permute-start(bf16[1152,128]{1,0:T(8,128)(2,1)S(1)} %slice_bitcast_fusion), channel_id=1, source_target_pairs={{0,8},{4,12},{24,16},{28,20},{1,9},{5,13},{25,17},{29,21},{2,10},{... | collective-permute-start | bytes 884744 | tf_op jit(solution)/shard_map/ppermute | solution.py:709
  611.6 15.5 %collective-permute-start.20 = (bf16[2304,128]{1,0:T(8,128)(2,1)S(1)}, bf16[2304,128]{1,0:T(8,128)(2,1)S(1)}, u32[]{:S(2)}, u32[]{:S(2)}) collective-permute-start(bf16[2304,128]{1,0:T(8,128)(2,1)S(1)} %add_convert_fusion.15), channel_id=1, source_target_pairs={{8,16},{12,20},{16,8},{20,12},{9,17},{13,21},{17,9},{21,13},{10,18... | collective-permute-start | bytes 1769480 | tf_op jit(solution)/shard_map/ppermute | solution.py:715
  624.9 22.5 %collective-permute-start.38 = (bf16[2,96,2048]{2,1,0:T(8,128)(2,1)S(1)}, bf16[2,96,2048]{2,1,0:T(8,128)(2,1)S(1)}, u32[]{:S(2)}, u32[]{:S(2)}) collective-permute-start(bf16[2,96,2048]{2,1,0:T(8,128)(2,1)S(1)} %fusion.17), channel_id=1, source_target_pairs={{0,4},{4,0},{8,12},{12,8},{16,20},{20,16},{24,28},{28,24},{1,5},{5... | collective-permute-start | bytes 2359304 | tf_op jit(solution)/shard_map/ppermute | solution.py:706
  627.0 21.7 %collective-permute-start.31 = (bf16[2,96,2048]{2,1,0:T(8,128)(2,1)S(1)}, bf16[2,96,2048]{2,1,0:T(8,128)(2,1)S(1)}, u32[]{:S(2)}, u32[]{:S(2)}) collective-permute-start(bf16[2,96,2048]{2,1,0:T(8,128)(2,1)S(1)} %fusion.21), channel_id=1, source_target_pairs={{0,4},{4,0},{8,12},{12,8},{16,20},{20,16},{24,28},{28,24},{1,5},{5... | collective-permute-start | bytes 2359304 | tf_op jit(solution)/shard_map/ppermute | solution.py:706
  637.0 8.6 %collective-permute-start.21 = (bf16[1152,128]{1,0:T(8,128)(2,1)S(1)}, bf16[1152,128]{1,0:T(8,128)(2,1)S(1)}, u32[]{:S(2)}, u32[]{:S(2)}) collective-permute-start(bf16[1152,128]{1,0:T(8,128)(2,1)S(1)} %fusion.24), channel_id=1, source_target_pairs={{8,0},{12,4},{16,24},{20,28},{9,1},{13,5},{17,25},{21,29},{10,2},{... | collective-permute-start | bytes 884744 | tf_op jit(solution)/shard_map/ppermute | solution.py:712
  641.0 18.6 %collective-permute-start.45 = (bf16[2,256,768]{2,1,0:T(8,128)(2,1)}, bf16[2,256,768]{2,1,0:T(8,128)(2,1)}, u32[]{:S(2)}, u32[]{:S(2)}) collective-permute-start(bf16[2,256,768]{2,1,0:T(8,128)(2,1)} %fusion.13), channel_id=1, source_target_pairs={{0,4},{4,0},{8,12},{12,8},{16,20},{20,16},{24,28},{28,24},{1,5},{5... | collective-permute-start | bytes 2359304 | tf_op jit(solution)/shard_map/ppermute | solution.py:706
  645.8 44.0 %collective-permute-start.23 = (bf16[1152,128]{1,0:T(8,128)(2,1)S(1)}, bf16[1152,128]{1,0:T(8,128)(2,1)}, u32[]{:S(2)}, u32[]{:S(2)}) collective-permute-start(bf16[1152,128]{1,0:T(8,128)(2,1)S(1)} %fusion.30), channel_id=1, source_target_pairs={{0,3},{1,2},{2,1},{3,0},{4,7},{5,6},{6,5},{7,4},{8,11},{9,10},{10,... | collective-permute-start | bytes 884744 | tf_op jit(solution)/shard_map/ppermute | solution.py:800
  647.4 42.4 %collective-permute-start.24 = (bf16[1152,128]{1,0:T(8,128)(2,1)S(1)}, bf16[1152,128]{1,0:T(8,128)(2,1)}, u32[]{:S(2)}, u32[]{:S(2)}) collective-permute-start(bf16[1152,128]{1,0:T(8,128)(2,1)S(1)} %fusion.30), channel_id=1, source_target_pairs={{0,2},{1,3},{2,0},{3,1},{4,6},{5,7},{6,4},{7,5},{8,10},{9,11},{10,... | collective-permute-start | bytes 884744 | tf_op jit(solution)/shard_map/ppermute | solution.py:800
  648.7 41.1 %collective-permute-start.25 = (bf16[1152,128]{1,0:T(8,128)(2,1)S(1)}, bf16[1152,128]{1,0:T(8,128)(2,1)}, u32[]{:S(2)}, u32[]{:S(2)}) collective-permute-start(bf16[1152,128]{1,0:T(8,128)(2,1)S(1)} %fusion.30), channel_id=1, source_target_pairs={{0,1},{1,0},{2,3},{3,2},{4,5},{5,4},{6,7},{7,6},{8,9},{9,8},{10,11... | collective-permute-start | bytes 884744 | tf_op jit(solution)/shard_map/ppermute | solution.py:800
  654.8 28.5 %all-to-all-start.3 = ((bf16[4,4,96,768]{3,2,1,0:T(8,128)(2,1)}), bf16[4,4,96,768]{3,2,1,0:T(8,128)(2,1)}, u32[]{:S(2)}, u32[]{:S(2)}) async-start(bf16[4,4,96,768]{3,2,1,0:T(8,128)(2,1)} %add_convert_fusion.1), calls=%async_computation.3 | async-start | bytes 4718592 | tf_op jit(solution)/shard_map/all_to_all | solution.py:797
  685.2 10.6 %collective-permute-start.11 = (bf16[192,768]{1,0:T(8,128)(2,1)S(1)}, bf16[192,768]{1,0:T(8,128)(2,1)S(1)}, u32[]{:S(2)}, u32[]{:S(2)}) collective-permute-start(bf16[192,768]{1,0:T(8,128)(2,1)S(1)} %bitcast.142), channel_id=1, source_target_pairs={{0,8},{4,12},{24,16},{28,20},{1,9},{5,13},{25,17},{29,21},{2,10},{... | collective-permute-start | bytes 884744 | tf_op jit(solution)/shard_map/ppermute | solution.py:709
  695.9 8.3 %collective-permute-start.12 = (bf16[192,768]{1,0:T(8,128)(2,1)S(1)}, bf16[192,768]{1,0:T(8,128)(2,1)S(1)}, u32[]{:S(2)}, u32[]{:S(2)}) collective-permute-start(bf16[192,768]{1,0:T(8,128)(2,1)S(1)} %add_convert_fusion.18), channel_id=1, source_target_pairs={{8,16},{12,20},{16,8},{20,12},{9,17},{13,21},{17,9},{21,13},{10,18... | collective-permute-start | bytes 884744 | tf_op jit(solution)/shard_map/ppermute | solution.py:715
  696.7 10.7 %collective-permute-start.14 = (bf16[96,768]{1,0:T(8,128)(2,1)S(1)}, bf16[96,768]{1,0:T(8,128)(2,1)S(1)}, u32[]{:S(2)}, u32[]{:S(2)}) collective-permute-start(bf16[96,768]{1,0:T(8,128)(2,1)S(1)} %slice_bitcast_fusion.2), channel_id=1, source_target_pairs={{0,8},{4,12},{24,16},{28,20},{1,9},{5,13},{25,17},{29,21},{2,10},{... | collective-permute-start | bytes 442376 | tf_op jit(solution)/shard_map/ppermute | solution.py:709
  704.3 8.2 %collective-permute-start.13 = (bf16[96,768]{1,0:T(8,128)(2,1)S(1)}, bf16[96,768]{1,0:T(8,128)(2,1)S(1)}, u32[]{:S(2)}, u32[]{:S(2)}) collective-permute-start(bf16[96,768]{1,0:T(8,128)(2,1)S(1)} %fusion.28), channel_id=1, source_target_pairs={{8,0},{12,4},{16,24},{20,28},{9,1},{13,5},{17,25},{21,29},{10,2},{... | collective-permute-start | bytes 442376 | tf_op jit(solution)/shard_map/ppermute | solution.py:712
  712.5 6.6 collective-permute-start.16
  713.9 6.9 collective-permute-start.17
  (52 other events, 670.8 us)

commit v3 on v2

--- a/solution.py
+++ b/solution.py
@@ -4,6 +4,405 @@
 from jax.experimental import pallas as pl
 from jax.experimental.pallas import tpu as pltpu
 from jax.sharding import PartitionSpec as P
+
+
+MESH_ID = pl.DeviceIdType.MESH
+
+def xor4(e,k):
+    lo=lax.rem(e,2); hi=lax.div(e,2)
+    if k&1: lo=1-lo
+    if k&2: hi=1-hi
+    return hi*2+lo
+
+def spot():
+    d=lax.axis_index("dp"); e=lax.axis_index("expert")
+    c=lax.rem(d,2)
+    return c,lax.div(d,2),e
+
+def shard_of(q):
+    c,z,e=spot()
+    return jnp.where(z<2,3-q,q).astype(jnp.int32)
+
+def peer(z,kk):
+    c,_,e=spot()
+    return (2*z+lax.rem(c+(kk>>2),2),xor4(e,kk&3))
+
+def block_of(kk):
+    c,_,e=spot()
+    return lax.rem(c+(kk>>2),2)*4+xor4(e,kk&3)
+
+def plane_sems(n):
+    return [pltpu.SemaphoreType.DMA((n,)),pltpu.SemaphoreType.DMA((n,7)),pltpu.SemaphoreType.DMA((n,7))]
+
+def plane_barrier():
+    c,z,e=spot()
+    b=pltpu.get_barrier_semaphore()
+    for kk in range(1,8):
+        pl.semaphore_signal(b,inc=1,device_id=peer(z,kk),device_id_type=MESH_ID)
+    pl.semaphore_wait(b,7)
+
+def plane_copies(pairs, sems):
+    local,send,recv=sems
+    c,z,e=spot()
+    me=block_of(0)
+    out=[]
+    for i,(src,dst) in enumerate(pairs):
+        out.append(pltpu.make_async_copy(src.at[me],dst.at[me],local.at[i]))
+        for kk in range(1,8):
+            out.append(pltpu.make_async_remote_copy(src_ref=src.at[block_of(kk)],dst_ref=dst.at[me],send_sem=send.at[i,kk-1],
+                recv_sem=recv.at[i,kk-1],device_id=peer(z,kk),device_id_type=MESH_ID))
+    return out
+
+def home_sems():
+    return [pltpu.SemaphoreType.DMA((1,)),pltpu.SemaphoreType.DMA((8,)),pltpu.SemaphoreType.DMA((8,)),pltpu.SemaphoreType.DMA((8,))]
+
+def home_barrier():
+    c,z,e=spot()
+    b=pltpu.get_barrier_semaphore()
+    inner=(z==1)|(z==2)
+    zo=jnp.where(z<2,0,3); zi=jnp.where(z<2,1,2)
+    @pl.when(inner)
+    def _():
+        for kk in range(8):
+            pl.semaphore_signal(b,inc=1,device_id=peer(zo,kk),device_id_type=MESH_ID)
+            if kk:
+                pl.semaphore_signal(b,inc=1,device_id=peer(z,kk),device_id_type=MESH_ID)
+        pl.semaphore_wait(b,15)
+    @pl.when(jnp.logical_not(inner))
+    def _():
+        for kk in range(8):
+            pl.semaphore_signal(b,inc=1,device_id=peer(zi,kk),device_id_type=MESH_ID)
+        pl.semaphore_wait(b,8)
+
+def home_run(own, ext, dst, sems, start):
+    local,send,send2,recv=sems
+    c,z,e=spot()
+    inner=(z==1)|(z==2)
+    zo=jnp.where(z<2,0,3); zi=jnp.where(z<2,1,2)
+    me=block_of(0)
+    def remote(src,kk,zz,s):
+        return pltpu.make_async_remote_copy(src_ref=src.at[block_of(kk)],dst_ref=dst.at[me],send_sem=s.at[kk],recv_sem=recv.at[kk],
+            device_id=peer(zz,kk),device_id_type=MESH_ID)
+    @pl.when(inner)
+    def _():
+        lc=pltpu.make_async_copy(own.at[me],dst.at[me],local.at[0])
+        if start:
+            lc.start()
+            for kk in range(8):
+                remote(ext,kk,zo,send2).start()
+                if kk: remote(own,kk,z,send).start()
+        else:
+            lc.wait()
+            for kk in range(8):
+                remote(ext,kk,zo,send2).wait_send()
+                if kk:
+                    remote(own,kk,z,send).wait()
+    if not start:
+        @pl.when(jnp.logical_not(inner))
+        def _():
+            for kk in range(8):
+                remote(own,kk,zi,send).wait_recv()
+
+
+def addb(*refs):
+    t=refs[0].astype(f32)
+    for r in refs[1:]: t=t+r.astype(f32)
+    return t.astype(bf16)
+
+class Tail:
+    KIND=("g","g","g","g","w","w")
+    L2=(1,0,1,0,0,1)
+    H=(0,0,1,1,0,0)
+    def __init__(self, arrays, T, D, FF):
+        self.names=list(arrays); self.arrays=[arrays[n] for n in self.names]
+        self.T,self.D,self.FF=T,D,FF
+        SG=D//8; self.SG=SG; self.SD=FF//32
+        R2=2*SG; self.R2=R2; HW=FF//4
+        self.gs=(R2,FF); self.ws=(HW,D)
+        self.NR=arrays["msh"].shape[1]
+        an=pl.BlockSpec(memory_space=pl.ANY)
+        S=jax.ShapeDtypeStruct
+        outs={"gate":S((4,SG,FF),f32),"up":S((4,SG,FF),f32),"down":S((4,FF//8,D),f32),
+              "dgate":S((SG,FF),f32),"dup":S((SG,FF),f32),"ddown":S((FF//8,D),f32),
+              "dqkv":S((SG,3*D),f32),"dwo":S((SG,D),f32),"gains":S((8,D),f32),
+              "ra":S((8,CAP,D),bf16)}
+        for i in range(2,6):
+            outs[f"m{i}"]=S((2*R2,FF) if self.KIND[i]=="g" else (2*HW,D),bf16)
+        for i in range(6):
+            outs[f"ro{i}"]=S(self.shape(i),bf16)
+        self.onames=list(outs); self.oshape=[outs[n] for n in self.onames]
+        self.in_specs=[an]*len(self.names); self.out_specs=[an]*len(self.onames)
+        V=pltpu.VMEM; DM=pltpu.SemaphoreType.DMA
+        scr={"ga":V((3,)+self.gs,bf16),"wa":V((3,)+self.ws,bf16),
+             "gto":V((2,)+self.gs,bf16),"wto":V((2,)+self.ws,bf16),
+             "gfin":V((2,)+self.gs,bf16),"wfin":V((2,)+self.ws,bf16),
+             "gfs":V((2,SG,FF),f32),"wfs":V((2,FF//8,D),f32),
+             "gsw":V((4,SG,FF),bf16),"wsw":V((2,FF//8,D),bf16),
+             "atr":V((4,4,SG,D),bf16),"sv":V((4,4,SG,D),bf16),"xr":V((3,4,SG,D),bf16),
+             "za":V((4,SG,D),bf16),"zb":V((4,self.NR,128),bf16),
+             "gn":V((8,8,D),f32),
+             "s_x":DM((4,)),"r_x":DM((4,)),"s_o":DM((6,)),"r_o":DM((6,)),"s_w":DM((6,)),"r_w":DM((6,)),
+             "ld":DM((3,)),"st":DM((8,)),"s_at":DM((16,)),"r_at":DM((16,)),"s_xr":DM((3,)),"r_xr":DM((3,)),
+             "s_gn":DM((7,)),"r_gn":DM((7,)),"st2":DM((4,))}
+        for nm,sh in (("a",(SG,D)),("b",(self.NR,128))):
+            scr.update({"zr"+nm:V((2,)+sh,bf16),"zs"+nm:V((2,)+sh,bf16),"zm"+nm:V((2,)+sh,bf16),"zi"+nm:V(sh,bf16),"zt"+nm:V(sh,bf16),
+                "zo"+nm:V(sh,bf16),"fi"+nm:V(sh,bf16),"ag"+nm:V((3,)+sh,bf16),
+                "s_z"+nm:DM((4,)),"r_z"+nm:DM((4,)),"s_ag"+nm:DM((3,)),"r_ag"+nm:DM((3,))})
+        scr.update({"oa":V((2,SG,D),f32),"og":V((2,SG,FF//4),f32),"od":V((self.SD,D),f32)})
+        self.snames=list(scr)+[f"home{i}" for i in range(4)]
+        self.scratch=[scr[n] for n in scr]+home_sems()
+    def shape(self,i): return self.gs if self.KIND[i]=="g" else self.ws
+    def bind(self,ins,outs,scr):
+        self.r=dict(zip(self.names,ins)); self.r.update(zip(self.onames,outs)); self.r.update(zip(self.snames,scr))
+        c,z,e=spot()
+        self.c,self.z,self.e=c,z,e
+        self.inner=(z==1)|(z==2); self.outer=jnp.logical_not(self.inner); self.low=z<2
+        self.zo=jnp.where(z<2,0,3); self.zi=jnp.where(z<2,1,2); self.zx=3-z
+        self.home=[self.r[f"home{i}"] for i in range(4)]
+    def rcopy(self,src,dst,s,r,dev):
+        return pltpu.make_async_remote_copy(src_ref=src,dst_ref=dst,send_sem=s,recv_sem=r,device_id=dev,device_id_type=MESH_ID)
+    def barrier(self):
+        b=pltpu.get_barrier_semaphore()
+        def sig(dev): pl.semaphore_signal(b,inc=1,device_id=dev,device_id_type=MESH_ID)
+        for kk in range(1,8): sig(peer(self.z,kk))
+        @pl.when(self.inner)
+        def _():
+            for kk in range(8): sig(peer(self.zo,kk))
+            sig(peer(self.zx,0))
+            pl.semaphore_wait(b,16)
+        @pl.when(self.outer)
+        def _():
+            for kk in range(8): sig(peer(self.zi,kk))
+            pl.semaphore_wait(b,15)
+    def far_src(self,i):
+        return self.r[f"far{i}"]
+    def across(self,i):
+        return self.rcopy(self.far_src(i),self.r[f"m{i}"],self.r["s_x"].at[i-2],self.r["r_x"].at[i-2],peer(self.zx,0))
+    def start(self):
+        self.barrier()
+        home_run(self.r["hown"],self.r["hext"],self.r["ra"],self.home,True)
+        ld=pltpu.make_async_copy(self.r["msh"],self.r["zb"],self.r["st2"].at[0])
+        ld.start(); ld.wait()
+        self.z_inward("b")
+        @pl.when(self.inner)
+        def _():
+            for i in (2,3): self.across(i).start()
+    def load(self,pairs):
+        cs=[pltpu.make_async_copy(s,d,self.r["ld"].at[k]) for k,(s,d) in enumerate(pairs)]
+        for c in cs: c.start()
+        for c in cs: c.wait()
+    def near(self,i,which):
+        if self.KIND[i]=="g":
+            return self.r[f"n{which}{i}"]
+        n=self.ws[0]
+        return self.r[f"nw{i}"].at[pl.ds(0 if which=="o" else n,n)]
+    def piece(self,i):
+        g=self.KIND[i]=="g"; k="g" if g else "w"
+        buf=self.r[k+"a"]; to=self.r[k+"to"]; fin=self.r[k+"fin"]; fs=self.r[k+"fs"]; sw=self.r[k+"sw"]
+        n=self.shape(i)[0]; hn=n//2; b=self.L2[i]==1
+        idx=i if g else i-4
+        slot=idx%2
+        o=self.rcopy(to.at[slot],self.r[f"ro{i}"],self.r["s_o"].at[i],self.r["r_o"].at[i],peer(self.zo,0))
+        @pl.when(self.inner)
+        def _():
+            if i>=2: self.across(i).wait()
+            m=self.r[f"m{i}"]
+            self.load([(m.at[pl.ds(0,n)],buf.at[0]),(self.near(i,"o"),buf.at[1])])
+            if g and idx>=2:
+                self.rcopy(to.at[slot],self.r[f"ro{i-2}"],self.r["s_o"].at[i-2],self.r["r_o"].at[i-2],peer(self.zo,0)).wait_send()
+            to[slot]=addb(buf[0],buf[1])
+            o.start()
+            self.load([(m.at[pl.ds(n,n)],buf.at[0]),(self.near(i,"i"),buf.at[1])]+([(self.r[f"rin{i}"],buf.at[2])] if b else []))
+        @pl.when(self.outer)
+        def _():
+            self.rcopy(to.at[slot],self.r[f"ro{i}"],self.r["s_o"].at[i],self.r["r_o"].at[i],peer(self.zi,0)).wait_recv()
+            self.load([(self.r[f"ro{i}"],buf.at[0])]+([(self.near(i,"o"),buf.at[1])] if b else []))
+        if g and idx>=2:
+            self.swap(i-2,fin,sw).wait_send()
+        @pl.when(self.inner)
+        def _():
+            fin[slot]=addb(buf[0],buf[1],buf[2]) if b else addb(buf[0],buf[1])
+        @pl.when(self.outer)
+        def _():
+            fin[slot]=addb(buf[0],buf[1]) if b else buf[0]
+        self.swap(i,fin,sw).start()
+        fs[slot]=fin[slot,pl.ds(pl.multiple_of(self.c*hn,hn),hn),:].astype(f32)
+        for cp in self.store(i,fs,slot,self.c): cp.start()
+    def swap(self,i,fin,sw):
+        g=self.KIND[i]=="g"; n=self.shape(i)[0]; hn=n//2; idx=i if g else i-4
+        return self.rcopy(fin.at[idx%2,pl.ds(pl.multiple_of((1-self.c)*hn,hn),hn)],sw.at[idx],self.r["s_w"].at[i],self.r["r_w"].at[i],peer(self.z,4))
+    def store(self,i,fs,slot,core):
+        ex=2*core+self.L2[i]; base=0 if self.KIND[i]=="g" else 4
+        if self.KIND[i]=="g":
+            hc=self.FF//2; h=self.H[i]
+            return [pltpu.make_async_copy(fs.at[slot,:,pl.ds(t*hc,hc)],self.r[nm].at[ex,:,pl.ds(h*hc,hc)],self.r["st"].at[base+2*slot+t])
+                    for t,nm in enumerate(("gate","up"))]
+        return [pltpu.make_async_copy(fs.at[slot],self.r["down"].at[ex],self.r["st"].at[base+slot])]
+    def store_wait(self,i,fs):
+        idx=i if self.KIND[i]=="g" else i-4
+        for cp in self.store(i,fs,idx%2,self.c): cp.wait()
+    def other_half(self,i):
+        g=self.KIND[i]=="g"; k="g" if g else "w"
+        fin=self.r[k+"fin"]; sw=self.r[k+"sw"]; fs=self.r[k+"fs"]; idx=i if g else i-4; slot=idx%2
+        self.store_wait(i,fs)
+        self.swap(i,fin,sw).wait_recv()
+        fs[slot]=sw[idx].astype(f32)
+        for cp in self.store(i,fs,slot,1-self.c): cp.start()
+        for cp in self.store(i,fs,slot,1-self.c): cp.wait()
+    def zsem(self,nm,k): return self.r["s_z"+nm].at[k],self.r["r_z"+nm].at[k]
+    def zc(self,nm,k):
+        r=self.r; M=r["z"+nm]
+        src,dst,dev={0:(M.at[pl.ds(0,2)],r["zr"+nm],peer(self.zi,0)),1:(M.at[2],r["zi"+nm],peer(self.zi,0)),
+            2:(r["zs"+nm],r["zm"+nm],peer(self.zx,0)),3:(r["zt"+nm],r["zo"+nm],peer(self.zo,0))}[k]
+        s,v=self.zsem(nm,k)
+        return self.rcopy(src,dst,s,v,dev)
+    def z_inward(self,nm):
+        @pl.when(self.outer)
+        def _():
+            self.zc(nm,0).start(); self.zc(nm,1).start()
+    def z_across(self,nm):
+        r=self.r
+        @pl.when(self.inner)
+        def _():
+            self.zrecv(nm,0)
+            r["zs"+nm][...]=addb(r["z"+nm][0:2],r["zr"+nm][...])
+            self.zc(nm,2).start()
+    def zrecv(self,nm,k):
+        r=self.r; M=r["z"+nm]
+        dst={0:r["zr"+nm],1:r["zi"+nm],2:r["zm"+nm],3:r["zo"+nm]}[k]
+        src={0:M.at[pl.ds(0,2)],1:M.at[2],2:r["zs"+nm],3:r["zt"+nm]}[k]
+        s,v=self.zsem(nm,k)
+        dev={0:peer(self.zo,0),1:peer(self.zo,0),2:peer(self.zx,0),3:peer(self.zi,0)}[k]
+        self.rcopy(src,dst,s,v,dev).wait_recv()
+    def z_last(self,nm):
+        r=self.r; M=r["z"+nm]
+        @pl.when(self.inner)
+        def _():
+            self.zrecv(nm,2)
+            r["zt"+nm][...]=addb(M[3],r["zm"+nm][0])
+            self.zc(nm,3).start()
+            self.zrecv(nm,1)
+            r["fi"+nm][...]=addb(M[2],r["zm"+nm][1],r["zi"+nm][...])
+            self.zc(nm,2).wait_send()
+        @pl.when(self.outer)
+        def _():
+            self.zrecv(nm,3)
+            r["fi"+nm][...]=addb(M[3],r["zo"+nm][...])
+            self.zc(nm,0).wait_send(); self.zc(nm,1).wait_send()
+        for kk in (1,2,3): self.agc(nm,kk).start()
+    def agc(self,nm,kk):
+        r=self.r
+        return self.rcopy(r["fi"+nm],r["ag"+nm].at[kk-1],r["s_ag"+nm].at[kk-1],r["r_ag"+nm].at[kk-1],peer(self.z,kk))
+    def z_out(self,nm):
+        r=self.r
+        for kk in range(4):
+            if kk: self.agc(nm,kk).wait()
+            a=xor4(self.e,kk)
+            v=(r["fi"+nm][...] if kk==0 else r["ag"+nm][kk-1]).astype(f32)
+            if nm=="a":
+                oa=r["oa"].at[kk%2]
+                oa[...]=v
+                cols=pl.ds(pl.multiple_of(jnp.minimum(a,2)*self.D,self.D),self.D)
+                @pl.when(a<3)
+                def _():
+                    cp=pltpu.make_async_copy(oa,r["dqkv"].at[:,cols],r["st2"].at[0]); cp.start(); cp.wait()
+                @pl.when(a==3)
+                def _():
+                    cp=pltpu.make_async_copy(oa,r["dwo"],r["st2"].at[0]); cp.start(); cp.wait()
+            else:
+                SG,SD,Q=self.SG,self.SD,self.FF//4; nb=Q//128
+                for t in range(2):
+                    for b in range(nb):
+                        r["og"][t,:,b*128:(b+1)*128]=v[(t*nb+b)*SG:(t*nb+b+1)*SG,:]
+                off=2*nb*SG
+                for b in range(self.D//128):
+                    r["od"][:,b*128:(b+1)*128]=v[off+b*SD:off+(b+1)*SD,:]
+                cols=pl.ds(pl.multiple_of(a*Q,Q),Q)
+                cps=[pltpu.make_async_copy(r["og"].at[0],r["dgate"].at[:,cols],r["st2"].at[0]),
+                     pltpu.make_async_copy(r["og"].at[1],r["dup"].at[:,cols],r["st2"].at[1]),
+                     pltpu.make_async_copy(r["od"],r["ddown"].at[pl.ds(pl.multiple_of(a*SD,SD),SD),:],r["st2"].at[2])]
+                for cp in cps: cp.start()
+                for cp in cps: cp.wait()
+    def rows_of(self,core,zr):
+        return pl.ds(pl.multiple_of(2*self.SG*shard_of(zr)+self.SG*core,self.SG),self.SG)
+    def at_swap(self,GS):
+        return [self.rcopy(GS.at[i,self.rows_of(1-self.c,zr)],self.r["atr"].at[i,zr],self.r["s_at"].at[4*i+zr],self.r["r_at"].at[4*i+zr],peer(self.z,4))
+                for i in range(4) for zr in range(4)]
+    def at_xy(self,kk):
+        return self.rcopy(self.r["sv"].at[xor4(self.e,kk)],self.r["xr"].at[kk-1],self.r["s_xr"].at[kk-1],self.r["r_xr"].at[kk-1],peer(self.z,kk))
+    def gcopy(self,k,dev):
+        return self.rcopy(self.r["gn"].at[0] ,self.r["gn"].at[k+1],self.r["s_gn"].at[k],self.r["r_gn"].at[k],dev)
+    def finish(self,GS,gg):
+        r=self.r; gn=r["gn"]
+        sw=self.at_swap(GS)
+        for cp in sw: cp.start()
+        row=lax.broadcasted_iota(jnp.int32,(8,self.D),0)
+        ld=pltpu.make_async_copy(r["fgg"],gn.at[7],r["st2"].at[1]); ld.start(); ld.wait()
+        gn[0]=jnp.where(row==0,gg,jnp.where(row==1,gn[7],0.0))
+        self.gcopy(0,peer(self.z,4)).start()
+        @pl.when(self.inner)
+        def _(): self.across(4).start()
+        self.z_across("b")
+        self.piece(0)
+        self.piece(1)
+        self.gcopy(0,peer(self.z,4)).wait()
+        gn[0]=gn[0]+gn[1]
+        for kk in (1,2,3): self.gcopy(kk,peer(self.z,kk)).start()
+        for cp in sw: cp.wait()
+        for i in range(4):
+            for zr in range(4):
+                r["sv"][i,zr]=addb(GS[i,self.rows_of(self.c,zr),:],r["atr"][i,zr])
+        for kk in (1,2,3): self.at_xy(kk).start()
+        self.z_last("b")
+        self.other_half(0)
+        self.other_half(1)
+        self.piece(2)
+        for kk in (1,2,3): self.gcopy(kk,peer(self.z,kk)).wait()
+        gn[0]=(gn[0]+gn[2])+(gn[3]+gn[4])
+        @pl.when(self.outer)
+        def _(): self.gcopy(4,peer(self.zi,0)).start()
+        for kk in (1,2,3): self.at_xy(kk).wait()
+        r["za"][...]=addb(r["sv"][self.e],r["xr"][0],r["xr"][1],r["xr"][2])
+        self.z_inward("a")
+        self.z_out("b")
+        @pl.when(self.inner)
+        def _():
+            self.gcopy(4,peer(self.zo,0)).wait_recv()
+            gn[0]=gn[0]+gn[5]
+            self.gcopy(5,peer(self.zx,0)).start()
+        self.piece(3)
+        self.z_across("a")
+        @pl.when(self.inner)
+        def _():
+            self.across(5).start()
+            self.gcopy(5,peer(self.zx,0)).wait()
+            gn[0]=gn[0]+gn[6]
+            self.gcopy(6,peer(self.zo,0)).start()
+        @pl.when(self.outer)
+        def _():
+            self.gcopy(4,peer(self.zi,0)).wait_send()
+            self.gcopy(6,peer(self.zi,0)).wait_recv()
+            gn[0]=gn[7]
+        self.other_half(2)
+        self.piece(4)
+        self.z_last("a")
+        self.other_half(3)
+        self.z_out("a")
+        self.piece(5)
+        @pl.when(self.inner)
+        def _(): self.gcopy(6,peer(self.zo,0)).wait_send()
+        gcp=pltpu.make_async_copy(gn.at[0],r["gains"],r["st2"].at[1]); gcp.start()
+        self.other_half(4); self.other_half(5)
+        for i in (2,3): self.swap(i,r["gfin"],r["gsw"]).wait_send()
+        for i in (4,5): self.swap(i,r["wfin"],r["wsw"]).wait_send()
+        @pl.when(self.inner)
+        def _():
+            for i in (2,3,4,5):
+                k="g" if self.KIND[i]=="g" else "w"; idx=i if k=="g" else i-4
+                self.rcopy(r[k+"to"].at[idx%2],r[f"ro{i}"],r["s_o"].at[i],r["r_o"].at[i],peer(self.zo,0)).wait_send()
+            self.zc("a",3).wait_send(); self.zc("b",3).wait_send()
+        gcp.wait()
+        home_run(r["hown"],r["hext"],r["ra"],self.home,False)
 
 f32=jnp.float32; bf16=jnp.bfloat16
 def nn(a,b): return lax.dot_general(a,b,(((1,),(0,)),((),())),preferred_element_type=f32)
@@ -23,32 +422,6 @@
 def inv_rms(v):
     return lax.rsqrt(jnp.mean(v*v,axis=1,keepdims=True)+EPS)
 
-def plane_copies(src, dst, local_sem, send_sem, recv_sem):
-    d=lax.axis_index("dp"); e=lax.axis_index("expert")
-    c=lax.rem(d,2); z2=d-c; me=c*4+e
-    own=pltpu.make_async_copy(src.at[me],dst.at[me],local_sem)
-    out=[]
-    for kk in range(1,8):
-        pc=lax.rem(c+(kk>>2),2)
-        pe=xor4(e,kk&3)
-        out.append(pltpu.make_async_remote_copy(src_ref=src.at[pc*4+pe],dst_ref=dst.at[me],send_sem=send_sem.at[kk-1],recv_sem=recv_sem.at[kk-1],
-            device_id=(z2+pc,pe),device_id_type=pl.DeviceIdType.MESH))
-    return own,out
-
-def xor4(e,k):
-    lo=lax.rem(e,2); hi=lax.div(e,2)
-    if k&1: lo=1-lo
-    if k&2: hi=1-hi
-    return hi*2+lo
-
-def plane_barrier():
-    d=lax.axis_index("dp"); e=lax.axis_index("expert")
-    c=lax.rem(d,2); z2=d-c
-    b=pltpu.get_barrier_semaphore()
-    for kk in range(1,8):
-        pl.semaphore_signal(b,inc=1,device_id=(z2+lax.rem(c+(kk>>2),2),xor4(e,kk&3)),device_id_type=pl.DeviceIdType.MESH)
-    pl.semaphore_wait(b,7)
-
 def attn_fwd(tokens, prefix, again, wqkv, wo, fgain, cosw, sinw, rows=None, sout=None):
     T,D=tokens.shape
     ng=D//GW; nq=T//QC
@@ -56,7 +429,7 @@
     NS=E*CAP; CH=480
     def kernel(pre,tok,ag,fg,wq,wk,wv,wor,cw,sw,*rest):
         if fused:
-            rowr,so,qo,ko,vo,atto,lseo,stateo,ntwoo,xo,sino,normed,bias,q4,k4,vT,OT,acc,lsem,ssem,rsem=rest
+            rowr,so,qo,ko,vo,atto,lseo,stateo,ntwoo,xo,sia,sib,normed,bias,q4,k4,vT,OT,acc,*sems=rest
         else:
             qo,ko,vo,atto,lseo,stateo,ntwoo,normed,bias,q4,k4,vT,OT,acc=rest
         g=pl.program_id(0)
@@ -64,9 +437,7 @@
         def _():
             if fused:
                 plane_barrier()
-                own,others=plane_copies(so,sino,lsem.at[0],ssem,rsem)
-                own.start()
-                for cpy in others: cpy.start()
+                for cpy in plane_copies([(so.at[0],sia),(so.at[1],sib)],sems): cpy.start()
             for c in range(nq):
                 r=slice(c*QC,(c+1)*QC)
                 x=tok[r,:].astype(f32)
@@ -121,34 +492,37 @@
                     si=lax.broadcasted_iota(jnp.int32,(CH,T),0)+i*CH
                     d=jnp.where((si==rowr[0:1,:])|(si==rowr[1:2,:]),1.0,0.0).astype(bf16)
                     xo[i*CH:(i+1)*CH,:]=nn(d,ntwoo[...]).astype(bf16)
-                own,others=plane_copies(so,sino,lsem.at[0],ssem,rsem)
-                own.wait()
-                for cpy in others: cpy.wait()
+                for cpy in plane_copies([(so.at[0],sia),(so.at[1],sib)],sems): cpy.wait()
     full=lambda s: pl.BlockSpec(s,lambda g:(0,)*len(s))
     col=lambda off: pl.BlockSpec((D,GW),lambda g,off=off:(0,g+off))
     tcol=pl.BlockSpec((T,GW),lambda g:(0,g))
     return pl.pallas_call(kernel,grid=(ng,),
       in_specs=[pl.BlockSpec(memory_space=pltpu.SMEM),full((T,D)),full((1,D)),full((1,D)),col(0),col(ng),col(2*ng),pl.BlockSpec((GW,D),lambda g:(g,0)),full((T,128)),full((T,128))]+([full((8,T)),pl.BlockSpec(memory_space=pl.ANY)] if fused else []),
-      out_specs=[tcol,tcol,tcol,tcol,pl.BlockSpec((1,8,T),lambda g:(g,0,0)),full((T,D)),full((T,D))]+([full((NS,D)),pl.BlockSpec(memory_space=pl.ANY)] if fused else []),
-      out_shape=[jax.ShapeDtypeStruct((T,D),bf16)]*4+[jax.ShapeDtypeStruct((ng,8,T),f32),jax.ShapeDtypeStruct((T,D),f32),jax.ShapeDtypeStruct((T,D),bf16)]+([jax.ShapeDtypeStruct((NS,D),bf16),jax.ShapeDtypeStruct((8,2*CAP,D),bf16)] if fused else []),
-      scratch_shapes=[pltpu.VMEM((T,D),bf16),pltpu.VMEM((nq,T,QC),f32),pltpu.VMEM((T,GW),bf16),pltpu.VMEM((T,GW),bf16),pltpu.VMEM((GW,T),bf16),pltpu.VMEM((nq,GW,QC),f32),pltpu.VMEM((T,D),f32)]+([pltpu.SemaphoreType.DMA((1,)),pltpu.SemaphoreType.DMA((7,)),pltpu.SemaphoreType.DMA((7,))] if fused else []),
+      out_specs=[tcol,tcol,tcol,tcol,pl.BlockSpec((1,8,T),lambda g:(g,0,0)),full((T,D)),full((T,D))]+([full((NS,D))]+[pl.BlockSpec(memory_space=pl.ANY)]*2 if fused else []),
+      out_shape=[jax.ShapeDtypeStruct((T,D),bf16)]*4+[jax.ShapeDtypeStruct((ng,8,T),f32),jax.ShapeDtypeStruct((T,D),f32),jax.ShapeDtypeStruct((T,D),bf16)]+([jax.ShapeDtypeStruct((NS,D),bf16),*[jax.ShapeDtypeStruct((8,CAP,D),bf16)]*2] if fused else []),
+      scratch_shapes=[pltpu.VMEM((T,D),bf16),pltpu.VMEM((nq,T,QC),f32),pltpu.VMEM((T,GW),bf16),pltpu.VMEM((T,GW),bf16),pltpu.VMEM((GW,T),bf16),pltpu.VMEM((nq,GW,QC),f32),pltpu.VMEM((T,D),f32)]+(plane_sems(2) if fused else []),
       compiler_params=pltpu.CompilerParams(vmem_limit_bytes=56<<20,dimension_semantics=("arbitrary",),**(dict(collective_id=0,has_side_effects=True) if fused else {})),
       cost_estimate=pl.CostEstimate(flops=2*T*D*4*D+4*T*T*D,bytes_accessed=16<<20,transcendentals=12*T*T),
       name="attn_fwd")(prefix,tokens,again[None],fgain[None],wqkv,wqkv,wqkv,wo,cosw,sinw,*([rows,sout] if fused else []))
 
-def attn_bwd(sgrad, prefix, tokens, again, wqkv, wo, cosw, sinw, q, k, v, att, lse, place=None):
+def attn_bwd(sgrad, prefix, tokens, again, wqkv, wo, cosw, sinw, q, k, v, att, lse, tail=None):
     T,D=tokens.shape
     ng=D//GW; nq=T//QC
-    fast=place is not None
-    if not fast:
-        place=jnp.zeros((8,),jnp.int32)
-    SH=D//8
-    def kernel(pre,plc,sg,tok,ag,wq,wk,wv,wor,cw,sw,qr,kr,vr,attr,lser,tgo,ggo,*rest):
+    fast=tail is not None
+    def kernel(pre,sg,tok,ag,wq,wk,wv,wor,cw,sw,qr,kr,vr,attr,lser,*rest):
         if fast:
-            at0,at1,normed,normedT,bg,bias,dO,kT,PB,DS,dv,dk,dqT,drow,acc,GS=rest
+            ni,no=len(tail.in_specs),len(tail.out_specs)
+            tgo,ggo=rest[ni:ni+2]
+            tins,touts=rest[:ni],rest[ni+2:ni+2+no]
+            normed,normedT,bg,bias,dO,kT,PB,DS,dv,dk,dqT,drow,acc,GS,*tscr=rest[ni+2+no:]
+            tail.bind(tins,touts,tscr)
         else:
-            gq,gk,gv,gwo,normed,normedT,bg,bias,dO,kT,PB,DS,dv,dk,dqT,drow,acc=rest
+            tgo,ggo,gq,gk,gv,gwo,normed,normedT,bg,bias,dO,kT,PB,DS,dv,dk,dqT,drow,acc=rest
         g=pl.program_id(0)
+        if fast:
+            @pl.when(g==0)
+            def _():
+                tail.start()
         @pl.when(g==0)
         def _():
             for c in range(nq):
@@ -224,32 +598,27 @@
                 tgo[r,:]=(sg[r,:]+inv*(w-u*jnp.mean(w*u,axis=1,keepdims=True))).astype(bf16)
             ggo[...]=jnp.broadcast_to(gg,(8,D))
             if fast:
-                for i in range(4):
-                    for zr in range(4):
-                        for cp in range(2):
-                            src=pl.multiple_of(2*SH*plc[1+zr]+SH*((plc[0]+cp)&1),SH)
-                            (at0,at1)[cp][i,zr]=GS[i,pl.ds(src,SH),:]
-    full=lambda s: pl.BlockSpec(s,lambda g:(0,)*len(s))
+                tail.finish(GS,gg)
+    full=lambda s: pl.BlockSpec(s,lambda g:(0,)*len(s),pipeline_mode=pl.Buffered(1))
     col=lambda off: pl.BlockSpec((D,GW),lambda g,off=off:(0,g+off))
     tcol=pl.BlockSpec((T,GW),lambda g:(0,g))
     if fast:
-        outs=[full((4,4,SH,D))]*2
-        oshape=[jax.ShapeDtypeStruct((4,4,SH,D),bf16)]*2
-        extra=[pltpu.VMEM((4,D,D),bf16)]
+        outs=tail.out_specs; oshape=tail.oshape
+        extra=[pltpu.VMEM((4,D,D),bf16)]+tail.scratch
     else:
         outs=[tcol,tcol,tcol,pl.BlockSpec((GW,D),lambda g:(g,0))]
         oshape=[jax.ShapeDtypeStruct((D,D),bf16)]*4
         extra=[]
     rowb=pl.BlockSpec((GW,D),lambda g:(g,0))
     return pl.pallas_call(kernel,grid=(ng,),
-      in_specs=[pl.BlockSpec(memory_space=pltpu.SMEM)]*2+[full((T,D)),full((T,D)),full((1,D)),col(0),col(ng),col(2*ng),rowb,full((T,128)),full((T,128)),tcol,tcol,tcol,tcol,pl.BlockSpec((1,8,T),lambda g:(g,0,0))],
+      in_specs=[pl.BlockSpec(memory_space=pltpu.SMEM)]+[full((T,D)),full((T,D)),full((1,D)),col(0),col(ng),col(2*ng),rowb,full((T,128)),full((T,128)),tcol,tcol,tcol,tcol,pl.BlockSpec((1,8,T),lambda g:(g,0,0))]+(tail.in_specs if fast else []),
       out_specs=[full((T,D)),full((8,D))]+outs,
       out_shape=[jax.ShapeDtypeStruct((T,D),bf16),jax.ShapeDtypeStruct((8,D),f32)]+oshape,
       scratch_shapes=[pltpu.VMEM((T,D),bf16),pltpu.VMEM((D,T),bf16),pltpu.VMEM((T,D),bf16),pltpu.VMEM((nq,T,QC),f32),pltpu.VMEM((T,GW),bf16),pltpu.VMEM((GW,T),bf16),
         pltpu.VMEM((T,T),bf16),pltpu.VMEM((T,T),bf16),pltpu.VMEM((T,GW),f32),pltpu.VMEM((T,GW),f32),pltpu.VMEM((GW,T),f32),pltpu.VMEM((8,T),f32),pltpu.VMEM((T,D),f32)]+extra,
-      compiler_params=pltpu.CompilerParams(vmem_limit_bytes=60<<20,dimension_semantics=("arbitrary",)),
+      compiler_params=pltpu.CompilerParams(vmem_limit_bytes=63<<20,dimension_semantics=("arbitrary",),**(dict(collective_id=5,has_side_effects=True) if fast else {})),
       cost_estimate=pl.CostEstimate(flops=2*T*D*8*D+10*T*T*D,bytes_accessed=24<<20,transcendentals=12*T*T),
-      name="attn_bwd")(prefix,place,sgrad,tokens,again[None],wqkv,wqkv,wqkv,wo,cosw,sinw,q,k,v,att,lse)
+      name="attn_bwd")(prefix,sgrad,tokens,again[None],wqkv,wqkv,wqkv,wo,cosw,sinw,q,k,v,att,lse,*(tail.arrays if fast else ()))
 
 
 def make_ffn(parts, G, L, cap, D, FF, FB, chunk, out_dt):
@@ -323,23 +692,31 @@
     H[rows,:]=h; GB[rows,:]=gb; UB[rows,:]=ub
     return nn(h,wd),nt(gb,wg)+nt(ub,wu)
 
-def expert_ffn(place, xs, ss, wg, wu, wd, half, prev=(), FB=512, chunk=480):
+def expert_ffn(token, l2, xs, ss, wg, wu, wd, half, prev=(), carry=None, cid=None, FB=512, chunk=480):
     n=len(xs); RG,D=xs[0].shape; FF=wg.shape[2]; R=n*RG; nf=2; HB=nf*FB
-    SR=D//4; np_=len(prev)
-    def kernel(plc,*refs):
+    SR=D//4; np_=len(prev); nc=0 if carry is None else 1
+    def kernel(tk,*refs):
         xr=refs[:n]; sr=refs[n:2*n]; wgr,wur,wdr=refs[2*n:2*n+3]; o=2*n+3
         pv=refs[o:o+np_]; o+=np_
+        csrc=refs[o:o+nc]; o+=nc
         res=refs[o:o+n]; dgr=refs[o+n:o+2*n]; o+=2*n
-        gf,gi,go,dw,tok,XT,XN,H,GB,UB,AR,AD=refs[o:]
+        gf,gi,go,dw,tok=refs[o:o+5]; o+=5
+        cdst=refs[o:o+nc]; o+=nc
+        XT,XN,H,GB,UB,AR,AD=refs[o:o+7]; sems=refs[o+7:]
         f=pl.program_id(0)
         tok[...]=jnp.zeros_like(tok)
+        if nc:
+            @pl.when(f==0)
+            def _():
+                plane_barrier()
+                for cpy in plane_copies([(csrc[0],cdst[0])],sems): cpy.start()
         @pl.when(f==0)
         def _():
             for a in range(n):
                 for b in range(RG//chunk):
                     XN[...]=xr[a][b*chunk:(b+1)*chunk,:].astype(f32).T.astype(bf16)
                     for q in range(4):
-                        XT[a*(RG//chunk)+b,q*SR:(q+1)*SR,:]=XN[pl.ds(pl.multiple_of(plc[1+q]*SR,SR),SR),:]
+                        XT[a*(RG//chunk)+b,q*SR:(q+1)*SR,:]=XN[pl.ds(pl.multiple_of(shard_of(q)*SR,SR),SR),:]
         for a in range(n):
             @pl.loop(0,RG//chunk)
             def _(i):
@@ -368,29 +745,39 @@
             t=tn(H[a*RG:(a+1)*RG,:],sr[a][...])
             dv=t if dv is None else dv+t
         dw[...]=dv.astype(bf16)
+        if nc:
+            @pl.when(f==nf-1)
+            def _():
+                for cpy in plane_copies([(csrc[0],cdst[0])],sems): cpy.wait()
     one=pl.Buffered(1)
-    rowspec=pl.BlockSpec((RG,D),lambda f,p:(0,0),pipeline_mode=one)
-    wspec=pl.BlockSpec((1,D,FB),lambda f,p:(p[5],0,f+nf*half))
-    wdspec=pl.BlockSpec((1,FB,D),lambda f,p:(p[5],f+nf*half,0))
-    full=lambda r,c: pl.BlockSpec((r,c),lambda f,p:(0,0),pipeline_mode=one)
-    out=pl.pallas_call(kernel,
-      grid_spec=pltpu.PrefetchScalarGridSpec(num_scalar_prefetch=1,grid=(nf,),
-        in_specs=[rowspec]*(2*n)+[wspec,wspec,wdspec]+[rowspec]*np_,
-        out_specs=[rowspec]*(2*n)+[full(2*SR,2*HB),full(SR,2*HB),full(SR,2*HB),pl.BlockSpec((FB,D),lambda f,p:((1-f) if half else f,0)),full(8,128)],
-        scratch_shapes=[pltpu.VMEM((R//chunk,D,chunk),bf16),pltpu.VMEM((D,chunk),bf16)]+[pltpu.VMEM((R,FB),bf16)]*3+[pltpu.VMEM((R,D),f32)]*2),
-      out_shape=[jax.ShapeDtypeStruct((RG,D),bf16)]*(2*n)+[jax.ShapeDtypeStruct((2*SR,2*HB),bf16)]+[jax.ShapeDtypeStruct((SR,2*HB),bf16)]*2+[jax.ShapeDtypeStruct((HB,D),bf16),jax.ShapeDtypeStruct((8,128),f32)],
-      compiler_params=pltpu.CompilerParams(vmem_limit_bytes=62<<20,dimension_semantics=("arbitrary",)),
+    rowspec=pl.BlockSpec((RG,D),lambda f:(0,0),pipeline_mode=one)
+    wspec=pl.BlockSpec((1,D,FB),lambda f:(2*spot()[0]+l2,0,f+nf*half))
+    wdspec=pl.BlockSpec((1,FB,D),lambda f:(2*spot()[0]+l2,f+nf*half,0))
+    full=lambda r,c: pl.BlockSpec((r,c),lambda f:(0,0),pipeline_mode=one)
+    anyspec=pl.BlockSpec(memory_space=pl.ANY)
+    out=pl.pallas_call(kernel,grid=(nf,),
+        in_specs=[pl.BlockSpec(memory_space=pltpu.SMEM)]+[rowspec]*(2*n)+[wspec,wspec,wdspec]+[rowspec]*np_+[anyspec]*nc,
+        out_specs=[rowspec]*(2*n)+[full(2*SR,2*HB),full(SR,2*HB),full(SR,2*HB),pl.BlockSpec((FB,D),lambda f:((1-f) if half else f,0)),full(8,128)]+[anyspec]*nc,
+        scratch_shapes=[pltpu.VMEM((R//chunk,D,chunk),bf16),pltpu.VMEM((D,chunk),bf16)]+[pltpu.VMEM((R,FB),bf16)]*3+[pltpu.VMEM((R,D),f32)]*2+(plane_sems(1) if nc else []),
+      out_shape=[jax.ShapeDtypeStruct((RG,D),bf16)]*(2*n)+[jax.ShapeDtypeStruct((2*SR,2*HB),bf16)]+[jax.ShapeDtypeStruct((SR,2*HB),bf16)]*2+[jax.ShapeDtypeStruct((HB,D),bf16),jax.ShapeDtypeStruct((8,128),jnp.int32)]+[jax.ShapeDtypeStruct((8,RG//8,D),bf16)]*nc,
+      compiler_params=pltpu.CompilerParams(vmem_limit_bytes=62<<20,dimension_semantics=("arbitrary",),**(dict(collective_id=cid,has_side_effects=True) if nc else {})),
       cost_estimate=pl.CostEstimate(flops=9*R*D*FF,bytes_accessed=3*D*FF*2+4*R*D*2,transcendentals=R*FF//2),
-      name=f"expert_ffn{n}_{half}")(place,*xs,*ss,wg,wu,wd,*prev)
-    return out[:2*n],out[2*n:2*n+3],out[2*n+3],out[2*n+4]
-
-def shared_ffn(place, x, s, wg, wu, wd, FB=512):
+      name=f"expert_ffn{n}_{half}")(token,*xs,*ss,wg,wu,wd,*prev,*([carry] if nc else []))
+    return (out[:2*n],out[2*n:2*n+3],out[2*n+3],out[2*n+4][0,0:1],*out[2*n+5:])
+
+def shared_ffn(x, s, wg, wu, wd, xout, FB=512):
     T,D=x.shape; FF=wg.shape[1]; nf=FF//FB; chunk=T//2
     SG=D//8; SD=FB//8
     NR=2*SG*(FB//128)+SD*(D//128)
-    def kernel(plc,xr,sr,wgr,wur,wdr,res,dgr,o0,o1,tok,XT,H,GB,UB,VG,VD):
+    def kernel(xr,sr,wgr,wur,wdr,xo,res,dgr,o0,o1,tok,xia,xib,XT,H,GB,UB,VG,VD,*sems):
         f=pl.program_id(0)
         tok[...]=jnp.zeros_like(tok)
+        core=spot()[0]
+        pairs=[(xo.at[0],xia),(xo.at[1],xib)]
+        @pl.when(f==0)
+        def _():
+            plane_barrier()
+            for cpy in plane_copies(pairs,sems): cpy.start()
         @pl.when(f==0)
         def _():
             for b in range(2):
@@ -409,27 +796,30 @@
             VG[...]=nn(XT[...],Y[...]).astype(bf16)
             for zr in range(4):
                 for cp in range(2):
-                    src=pl.ds(pl.multiple_of(2*SG*plc[1+zr]+SG*((plc[0]+cp)&1),SG),SG)
+                    src=pl.ds(pl.multiple_of(2*SG*shard_of(zr)+SG*lax.rem(core+cp,2),SG),SG)
                     for b in range(FB//128):
                         off=(t*(FB//128)+b)*SG
                         (o0,o1)[cp][f,zr,off:off+SG,:]=VG[src,b*128:(b+1)*128]
         VD[...]=tn(H[...],sr[...]).astype(bf16)
-        zr=jnp.where(plc[1]==f,0,jnp.where(plc[2]==f,1,jnp.where(plc[3]==f,2,3)))
+        zr=jnp.where(spot()[1]<2,3-f,f)
         for cp in range(2):
             for e in range(4):
-                src=pl.ds(pl.multiple_of(((plc[0]+cp)&1)*4*SD+e*SD,SD),SD)
+                src=pl.ds(pl.multiple_of(lax.rem(core+cp,2)*4*SD+e*SD,SD),SD)
                 for b in range(D//128):
                     off=2*SG*(FB//128)+b*SD
                     (o0,o1)[cp][e,zr,off:off+SD,:]=VD[src,b*128:(b+1)*128]
+        @pl.when(f==nf-1)
+        def _():
+            for cpy in plane_copies(pairs,sems): cpy.wait()
     full=lambda sh: pl.BlockSpec(sh,lambda f:(0,)*len(sh))
     return pl.pallas_call(kernel,grid=(nf,),
-      in_specs=[pl.BlockSpec(memory_space=pltpu.SMEM),full((T,D)),full((T,D)),pl.BlockSpec((D,FB),lambda f:(0,f)),pl.BlockSpec((D,FB),lambda f:(0,f)),pl.BlockSpec((FB,D),lambda f:(f,0))],
-      out_specs=[full((T,D)),full((T,D)),full((4,4,NR,128)),full((4,4,NR,128)),full((8,128))],
-      out_shape=[jax.ShapeDtypeStruct((T,D),f32)]*2+[jax.ShapeDtypeStruct((4,4,NR,128),bf16)]*2+[jax.ShapeDtypeStruct((8,128),f32)],
-      scratch_shapes=[pltpu.VMEM((D,T),bf16)]+[pltpu.VMEM((T,FB),bf16)]*3+[pltpu.VMEM((D,FB),bf16),pltpu.VMEM((FB,D),bf16)],
-      compiler_params=pltpu.CompilerParams(vmem_limit_bytes=62<<20,dimension_semantics=("arbitrary",)),
+      in_specs=[full((T,D)),full((T,D)),pl.BlockSpec((D,FB),lambda f:(0,f)),pl.BlockSpec((D,FB),lambda f:(0,f)),pl.BlockSpec((FB,D),lambda f:(f,0)),pl.BlockSpec(memory_space=pl.ANY)],
+      out_specs=[full((T,D)),full((T,D)),full((4,4,NR,128)),full((4,4,NR,128)),full((8,128))]+[pl.BlockSpec(memory_space=pl.ANY)]*2,
+      out_shape=[jax.ShapeDtypeStruct((T,D),f32)]*2+[jax.ShapeDtypeStruct((4,4,NR,128),bf16)]*2+[jax.ShapeDtypeStruct((8,128),jnp.int32)]+[jax.ShapeDtypeStruct(xout.shape[1:],bf16)]*2,
+      scratch_shapes=[pltpu.VMEM((D,T),bf16)]+[pltpu.VMEM((T,FB),bf16)]*3+[pltpu.VMEM((D,FB),bf16),pltpu.VMEM((FB,D),bf16)]+plane_sems(2),
+      compiler_params=pltpu.CompilerParams(vmem_limit_bytes=62<<20,dimension_semantics=("arbitrary",),collective_id=1,has_side_effects=True),
       cost_estimate=pl.CostEstimate(flops=2*9*T*D*FF,bytes_accessed=6*D*FF*2+8*T*D*2,transcendentals=T*FF),
-      name="shared_ffn")(place,x,s,wg,wu,wd)
+      name="shared_ffn")(x,s,wg,wu,wd,xout)
 
 
 def route(order, expert_ids, gates, cot, core, G, L, parts, plane=False):
@@ -466,7 +856,7 @@
         e=ecat.astype(jnp.int32)
         l=lax.rem(e,L); j=lax.div(e,L)
         if plane:
-            base=((lax.div(l,2)*G+j)*2+lax.rem(l,2))*CAP
+            base=((lax.rem(l,2)*2+lax.div(l,2))*G+j)*CAP
         elif parts==2:
             cc=lax.rem(lax.div(l,LP)+core_ref[0],2)
             base=((cc*G+j)*LP+lax.rem(l,LP))*CAP
@@ -536,6 +926,39 @@
       compiler_params=pltpu.CompilerParams(vmem_limit_bytes=50<<20),
       cost_estimate=pl.CostEstimate(flops=4*S*parts*T*D,bytes_accessed=9<<20,transcendentals=0),name="combine")(cols,gates,*ret,state,shared)
 
+def mid_bwd_home(cols, own, ext, back_b, dsh, state, fgain, cot):
+    T,D=state.shape; S=8*CAP
+    def kernel(colr,hown,hext,bb,ds,st,fg,ct,sgo,fgo,ba,BV,cs,*hsems):
+        home_barrier()
+        home_run(hown,hext,ba,hsems,True)
+        fgo[...]=jnp.zeros_like(fgo)
+        home_run(hown,hext,ba,hsems,False)
+        cps=[pltpu.make_async_copy(ba.at[i],BV.at[i],cs.at[i]) for i in range(8)]
+        for cp in cps: cp.start()
+        for cp in cps: cp.wait()
+        @pl.loop(0,T//QC)
+        def _(i):
+            r=pl.ds(pl.multiple_of(i*QC,QC),QC)
+            n=ds[r,:]
+            si=lax.broadcasted_iota(jnp.int32,(QC,S),1)+S
+            d=jnp.where((si==colr[r,0:1])|(si==colr[r,1:2]),1.0,0.0).astype(bf16)
+            n=n+nn(d,bb[...])
+            for b in range(8):
+                si=lax.broadcasted_iota(jnp.int32,(QC,128),1)
+                si=jnp.where(si<CAP,si+b*CAP,-1)
+                d=jnp.where((si==colr[r,0:1])|(si==colr[r,1:2]),1.0,0.0).astype(bf16)[:,0:CAP]
+                n=n+nn(d,BV[b])
+            x=st[r,:]; inv=inv_rms(x); u=x*inv
+            fgo[...]+=jnp.broadcast_to(jnp.sum(n*u,axis=0,keepdims=True),(8,D))
+            w=n*fg[...]
+            sgo[r,:]=ct[r,:].astype(f32)+inv*(w-u*jnp.mean(w*u,axis=1,keepdims=True))
+    vm=pl.BlockSpec(memory_space=pltpu.VMEM); an=pl.BlockSpec(memory_space=pl.ANY)
+    return pl.pallas_call(kernel,in_specs=[vm,an,an]+[vm]*5,out_specs=[vm]*2+[an],
+      out_shape=[jax.ShapeDtypeStruct((T,D),f32),jax.ShapeDtypeStruct((8,D),f32),jax.ShapeDtypeStruct((8,CAP,D),bf16)],
+      scratch_shapes=[pltpu.VMEM((8,CAP,D),bf16),pltpu.SemaphoreType.DMA((8,))]+home_sems(),
+      compiler_params=pltpu.CompilerParams(vmem_limit_bytes=50<<20,collective_id=4,has_side_effects=True),
+      cost_estimate=pl.CostEstimate(flops=4*S*T*D,bytes_accessed=12<<20,transcendentals=0),name="mid_bwd")(cols,own,ext,back_b,dsh,state,fgain[None],cot)
+
 def mid_bwd(cols, back, dsh, state, fgain, cot):
     parts=len(back); T,D=state.shape; S=back[0].shape[0]
     def kernel(colr,*refs):
@@ -689,18 +1112,12 @@
                 output_weight, feedforward_gain, shared_gate, shared_up, shared_down, expert_gate, expert_up, expert_down):
     T, D = tokens.shape
     FF = expert_gate.shape[2]
-    i32 = jnp.int32
-    dpi = lax.axis_index("dp").astype(i32)
-    ei = lax.axis_index("expert").astype(i32)
+    dpi = lax.axis_index("dp").astype(jnp.int32)
+    ei = lax.axis_index("expert").astype(jnp.int32)
     core = lax.rem(dpi, 2)
     zi = lax.div(dpi, 2)
     outer = (zi == 0) | (zi == 3)
     low = zi < 2
-    pick = lambda a, b: jnp.where(low, a, b).astype(i32)
-    place = jnp.stack([core, pick(3, 0), pick(2, 1), pick(1, 2), pick(0, 3)])
-    place_a = jnp.concatenate([place, (2 * core)[None]])
-    place_b = jnp.concatenate([place, (2 * core + 1)[None]])
-    plane = [[(2 * z + c) * 4 + e for c in range(2) for e in range(4)] for z in range(4)]
 
     def swap(x):
         return lax.ppermute(x, "dp", [(i, i ^ 1) for i in range(8)])
@@ -714,127 +1131,72 @@
     def across(x):
         return lax.ppermute(x, "dp", [(2, 4), (3, 5), (4, 2), (5, 3)])
 
-    def a2a(x):
-        return lax.all_to_all(x.reshape(8, 2 * CAP, D), ("dp", "expert"), split_axis=0, concat_axis=0,
-                              axis_index_groups=plane, tiled=True)
-
-    def add(*xs):
+    def add(*xs, after=None):
         t = xs[0].astype(f32)
         for x in xs[1:]:
             t = t + x.astype(f32)
+        if after is not None:
+            t = t + after[0].astype(f32)
         return t.astype(bf16)
 
-    def tie(x, token):
-        return lax.optimization_barrier((x, token))[0]
-
-    def zdense(far, inner, out):
-        r = far.shape[0] // 2
-        m = across(add(far, inward(far)))
-        rin = inward(inner)
-        ro = outward(add(out, m[:r]))
-        return jnp.where(outer, add(out, ro), add(inner, m[r:], rin))
+    def mark(x):
+        y = lax.slice(x, (0,) * x.ndim, (1,) * x.ndim).reshape(1).astype(f32)
+        return jnp.minimum(y * y, 0.0).astype(jnp.int32)
 
     cosw, sinw = rope_wide(T)
     rows, cols, (s_out,) = route(slot_order, expert_ids, route_gates, cotangent, core[None], 4, 4, 1, True)
-    q, k, v, att, lse, state, ntwo, x_out, sab = attn_fwd(tokens, prefix_len, attention_gain, qkv_weight, output_weight,
-                                                     feedforward_gain, cosw, sinw, rows,
-                                                          s_out.reshape(8, 2 * CAP, D))
-    xab = a2a(x_out)
-    half_rows = lambda y, l: y.reshape(8, 2, CAP, D)[:, l].reshape(8 * CAP, D)
-    sa, sb = half_rows(sab, 0), half_rows(sab, 1)
-    sx = inward(sa)
-    shared_branch, dshared, sh0, sh1, t_sh = shared_ffn(place, ntwo, cotangent, shared_gate, shared_up, shared_down)
-    xa, xb = half_rows(xab, 0), half_rows(xab, 1)
+    q, k, v, att, lse, state, ntwo, x_out, sa, sb = attn_fwd(
+        tokens, prefix_len, attention_gain, qkv_weight, output_weight, feedforward_gain, cosw, sinw, rows,
+        s_out.reshape(2, 8, CAP, D))
+    flat = lambda y: y.reshape(8 * CAP, D)
+    sx = inward(flat(sa))
+    shared_branch, dshared, sh0, sh1, tok, xa, xb = shared_ffn(ntwo, cotangent, shared_gate, shared_up, shared_down,
+                                                               x_out.reshape(2, 8, CAP, D))
+    sa, sb, xa, xb = flat(sa), flat(sb), flat(xa), flat(xb)
     xx = inward(xa)
     ws = (expert_gate, expert_up, expert_down)
-    p0, gb0, wb0, t_b0 = expert_ffn(tie(place_b, t_sh), [xb], [sb], *ws, 0)
-    (rb, db), gb1, wb1, t_b1 = expert_ffn(place_b, [xb], [sb], *ws, 1, p0)
-    rf0 = inward(gb0[0])
-    p0, ga0, wa0, t_a0 = expert_ffn(tie(place_a, t_b1), [xa, xx], [sa, sx], *ws, 0)
-    bs0 = add(gb0[0], tie(rf0, t_a0))
-    (ra, rx, da, dx), ga1, wa1, t_a1 = expert_ffn(tie(place_a, bs0), [xa, xx], [sa, sx], *ws, 1, p0)
+    p0, gb0, wb0, tok = expert_ffn(tok[0, 0:1], 1, [xb], [sb], *ws, 0)
+    (rb, db), gb1, wb1, tok = expert_ffn(tok, 1, [xb], [sb], *ws, 1, p0)
 
     far_w = lambda w0, w1: jnp.where(low, w1, w0)
     near_w = lambda w0, w1: jnp.where(low, w0, w1)
     hw = FF // 4
-    bfar = [gb0[0], gb1[0], far_w(wb0, wb1)]
-    bin_ = [gb0[1], gb1[1], near_w(wb0[hw:], wb1[hw:])]
-    bout = [gb0[2], gb1[2], near_w(wb0[:hw], wb1[:hw])]
-    afar = [ga0[0], ga1[0], far_w(wa0, wa1)]
-    ain = [ga0[1], ga1[1], near_w(wa0[hw:], wa1[hw:])]
-    aout = [ga0[2], ga1[2], near_w(wa0[:hw], wa1[:hw])]
-
-    rf = [tie(inward(x), t_a1) for x in bfar[1:]]
-    bm = [across(bs0)] + [across(add(x, r)) for x, r in zip(bfar[1:], rf)]
-    am = [across(x) for x in afar]
-    rin = [inward(x) for x in bin_]
-
-    def both(b, a):
-        return jnp.concatenate([b.reshape(8, 1, CAP, D), a.reshape(8, 1, CAP, D)], axis=1)
-
-    da = jnp.where(outer, outward(dx), da)
-    dback = a2a(both(da, db)).reshape(16 * CAP, D)
-    sgrad, fgg = mid_bwd(cols, [dback], dshared, state, feedforward_gain, cotangent)
-    tokens_grad, agg, at0, at1 = attn_bwd(sgrad, prefix_len, tokens, attention_gain, qkv_weight, output_weight,
-                                          cosw, sinw, q, k, v, att, lse, place)
-    ra = jnp.where(outer, outward(rx), ra)
-    rback = a2a(both(ra, rb)).reshape(16 * CAP, D)
-    block_out = combine(tie(cols, agg), route_gates, [rback], state, shared_branch)
-
-    def last(m, inner, out, r=None):
-        h = m.shape[0] // 2
-        m = tie(m, agg)
-        ro = outward(add(out, m[:h]))
-        if r is None:
-            return jnp.where(outer, ro, add(inner, m[h:]))
-        return jnp.where(outer, add(out, ro), add(inner, m[h:], r))
-
-    eb = [last(m, i, o, r) for m, i, o, r in zip(bm, bin_, bout, rin)]
-    ea = [last(m, i, o) for m, i, o in zip(am, ain, aout)]
-
-    def dense(mine, other):
-        s = add(mine, swap(other))
-        s = lax.all_to_all(s, "expert", split_axis=0, concat_axis=0, tiled=True)
-        s = add(s[0], s[1], s[2], s[3])
-        s = zdense(s[0:2].reshape(-1, s.shape[2]), s[2], s[3])
-        p = [s] + [lax.ppermute(s, "expert", [(e, e ^ kk) for e in range(4)]) for kk in (1, 2, 3)]
-        odd = lax.rem(ei, 2) == 1
-        p = [jnp.where(odd, p[kk ^ 1], p[kk]) for kk in range(4)]
-        return [jnp.where(ei >= 2, p[kk ^ 2], p[kk]) for kk in range(4)]
-
-    shd = jnp.stack(dense(sh0, sh1))
-    nb = FF // 4 // 128
+    blocks = lambda y: y.reshape(8, CAP, D)
+    rf = [inward(gb0[0]), inward(gb1[0]), inward(far_w(wb0, wb1))]
+    p0, ga0, wa0, tok, db = expert_ffn(tok, 0, [xa, xx], [sa, sx], *ws, 0, carry=blocks(db), cid=2)
+    bs0 = add(gb0[0], rf[0], after=tok)
+    m_b0 = across(bs0)
+    m_a0 = across(ga0[0])
+    (ra, rx, da, dx), ga1, wa1, tok, rb = expert_ffn(tok + mark(bs0), 0, [xa, xx], [sa, sx], *ws, 1, p0, carry=blocks(rb), cid=3)
+    bs1 = add(gb1[0], rf[1], after=tok)
+    sgrad, fgg, _ = mid_bwd_home(cols + mark(bs1), blocks(da), blocks(dx), flat(db), dshared, state, feedforward_gain, cotangent)
+    tok = mark(fgg)
+    far_wb = far_w(wb0, wb1)
+    bs2 = add(far_wb, rf[2], after=tok)
+    near_wb = near_w(wb0, wb1)
+    rin = [inward(gb0[1]), inward(gb1[1]), inward(near_wb[hw:])]
+
+    s = add(sh0, swap(sh1))
+    s = lax.all_to_all(s, "expert", split_axis=0, concat_axis=0, tiled=True)
+    msh = add(s[0], s[1], s[2], s[3])
+    carried = {
+        "hown": blocks(ra), "hext": blocks(rx), "fgg": fgg, "msh": msh,
+        "m0": m_b0, "ni0": gb0[1], "no0": gb0[2], "rin0": rin[0],
+        "m1": m_a0, "ni1": ga0[1], "no1": ga0[2],
+        "far2": bs1, "ni2": gb1[1], "no2": gb1[2], "rin2": rin[1],
+        "far3": ga1[0], "ni3": ga1[1], "no3": ga1[2],
+        "far4": far_w(wa0, wa1), "nw4": near_w(wa0, wa1),
+        "far5": bs2, "nw5": near_wb, "rin5": rin[2],
+    }
+    tail = Tail(carried, T, D, FF)
+    tokens_grad, _, *rest = attn_bwd(sgrad, prefix_len + mark(bs2), tokens, attention_gain, qkv_weight, output_weight,
+                                     cosw, sinw, q, k, v, att, lse, tail)
+    o = dict(zip(tail.onames, rest))
+    block_out = combine(cols, route_gates, [flat(o["ra"]), flat(rb)], state, shared_branch)
     sg = D // 8
-    sd = FF // 32
-    cut = nb * sg
-
-    def columns(x):
-        return x.reshape(4, nb, sg, 128).transpose(2, 0, 1, 3).reshape(sg, FF).astype(f32)
-
-    d_gate = columns(shd[:, :cut])
-    d_up = columns(shd[:, cut:2 * cut])
-    d_down = shd[:, 2 * cut:].reshape(4, D // 128, sd, 128).transpose(0, 2, 1, 3).reshape(4 * sd, D).astype(f32)
-    dq, dk, dv, dwo = dense(at0, at1)
-
-    gains = jnp.concatenate([agg[0:1], fgg[0:1]], axis=0)
-    for kk in (1, 2, 4):
-        gains = gains + lax.ppermute(gains, "dp", [(i, i ^ kk) for i in range(8)])
-    for kk in (1, 2):
-        gains = gains + lax.ppermute(gains, "expert", [(i, i ^ kk) for i in range(4)])
-    gains = lax.dynamic_slice_in_dim(gains, dpi * sg, sg, 1)
-
-    def finish(a, b):
-        h = jnp.stack([a, b]).reshape(2, 2, a.shape[0] // 2, a.shape[1])
-        mine = lax.dynamic_index_in_dim(h, core, 1, keepdims=False)
-        other = swap(lax.dynamic_index_in_dim(h, 1 - core, 1, keepdims=False))
-        return jnp.concatenate([jnp.where(core == 0, mine, other), jnp.where(core == 0, other, mine)], axis=0).astype(f32)
-
-    full = [finish(a, b) for a, b in zip(ea, eb)]
-    hc = FF // 2
-    outs = [jnp.concatenate([full[0][:, :, :hc], full[1][:, :, :hc]], axis=2),
-            jnp.concatenate([full[0][:, :, hc:], full[1][:, :, hc:]], axis=2), full[2]]
-    return (block_out, tokens_grad, gains[0], jnp.concatenate([dq, dk, dv], axis=1).astype(f32), dwo.astype(f32), gains[1],
-            d_gate, d_up, d_down, *outs)
+    gains = lax.dynamic_slice_in_dim(o["gains"], dpi * sg, sg, 1)
+    return (block_out, tokens_grad, gains[0], o["dqkv"], o["dwo"], gains[1], o["dgate"], o["dup"], o["ddown"],
+            o["gate"], o["up"], o["down"])
 
 
 def shards(*args):

time: 729 us -> 647 us (0.89)
  Pallas kernels: 275 us -> 536 us
  waiting for transfers between devices: 199 us -> 5.8 us
  starting transfers between devices: 139 us -> 30.3 us
  other arithmetic: 76.9 us -> 26.8 us
    pallas_call x1, Pallas kernels: 45.8 us -> 220 us  [attn_bwd(): pl.pallas_call(kernel, grid=(ng,), in_specs=[pl.BlockSpec(memory_space=pl...]
    ppermute x21 -> x0, waiting for transfers between devices: 105 us -> none  [the longest x10 74.6 us: outward(): return lax.ppermute(x, 'dp', [(2, 0), (3, 1), (4, 6), (5, 7)])]
    pallas_call x6, Pallas kernels: 168 us -> 254 us  [the longest x4 162 us: expert_ffn(): pl.pallas_call(kernel, grid=(nf,), in_specs=[pl.BlockSpec(memory_space=pl...]
    ppermute x12 -> x8, waiting for transfers between devices: 53.9 us -> 5.79 us  [inward(): return lax.ppermute(x, 'dp', [(0, 2), (1, 3), (6, 4), (7, 5)])]
    ppermute x12 -> x8, starting transfers between devices: 67.4 us -> 21 us  [inward(): return lax.ppermute(x, 'dp', [(0, 2), (1, 3), (6, 4), (7, 5)])]
    all_to_all x5 -> x1, waiting for transfers between devices: 40.1 us -> 0.01 us  [shards_fast(): s = lax.all_to_all(s, 'expert', split_axis=0, concat_axis=0, tiled=True)]
    ppermute x21 -> x0, starting transfers between devices: 39.4 us -> none  [the longest x3 17 us: shards_fast(): gains = gains + lax.ppermute(gains, 'dp', [(i, i ^ kk) for i in range(8)])]
    select_n x15 -> x0, other arithmetic: 20.9 us -> none  [the longest x3 6 us: last(): return jnp.where(outer, add(out, ro), add(inner, m[h:], r))]
  transfers between devices with their start and end apart: 51 -> 12, of which waited for: 18 -> 1; matrix products, arithmetic and copies ran while one was open for 12% -> 5% of each run, Pallas kernels for 31% -> 40%
where the time goes in v3:
time: 647 us; the launch traced here: 641 us
  Pallas kernels  536 us (83%)
  local copies, waits for them, and re-layouts  33.7 us (5%)
  starting transfers between devices  30.3 us (5%)
  other arithmetic  26.8 us (4%)
  between operations  8.95 us (1%)
    pallas_call x1, Pallas kernels, attn_bwd(): pl.pallas_call(kernel, grid=(ng,), in_specs=[pl.BlockSpec(memory_space=pl...  220 us
    pallas_call x4, Pallas kernels, expert_ffn(): pl.pallas_call(kernel, grid=(nf,), in_specs=[pl.BlockSpec(memory_space=pl...  162 us
    pallas_call x1, Pallas kernels, mid_bwd_home(): pl.pallas_call(kernel, in_specs=[vm, an, an] + [vm] * 5, out_specs=[vm] *...  47.7 us
    pallas_call x1, Pallas kernels, shared_ffn(): pl.pallas_call(kernel, grid=(nf,), in_specs=[full((T, D)), full((T, D)),...  44 us
    pallas_call x1, Pallas kernels, attn_fwd(): pl.pallas_call(kernel, grid=(ng,), in_specs=[pl.BlockSpec(memory_space=pl...  42.8 us
    unnamed x59, local copies, waits for them, and re-layouts  21.7 us
    ppermute x8, starting transfers between devices, inward(): return lax.ppermute(x, 'dp', [(0, 2), (1, 3), (6, 4), (7, 5)])  21 us
    convert_element_type x4, other arithmetic, add(): return t.astype(bf16)  14.6 us
  transfers between devices with their start and end apart: 12, of which 1 were waited for; matrix products, arithmetic and copies ran while one was open for 5% of the time, Pallas kernels for 40%

profile of v3, /device:TPU:0, one launch (start us, length us, event | category | flops | bytes accessed | tf_op | source)
XLA Modules:
  0.0 641.3 jit_solution(767928993775808782)
XLA Ops:
  1.3 1.3 broadcast_in_dim.7.ag
  2.6 1.3 broadcast_in_dim.16.fg
  5.6 1.5 fusion.3
  7.1 1.6 pad_maximum_fusion
  8.7 9.9 %route.1 = (s32[8,768]{1,0:T(8,128)S(1)}, s32[768,8]{1,0:T(8,128)S(1)}, bf16[1920,768]{1,0:T(8,128)(2,1)}) custom-call(s32[1]{0:T(128)} %bitcast.core_ref, s32[1,1536]{1,0:T(1,128)S(1)} %copy-done.5, s32[768,2]{1,0:T(8,128)S(1)} %copy.28.ids, f32[768,2]{1,0:T(8,128)S(1)} %copy.29.gts.g, bf16[768,768]{1,0:T(8,128)(2,1)S(1)} %copy-done), custom_call_target="tpu_custom_call" | custom-call | flops 4680843264 | bytes 8388608 | tf_op jit(solution)/shard_map/route/pallas_call | solution.py:884
  19.2 42.8 %attn_fwd.1 = (bf16[768,768]{1,0:T(8,128)(2,1)}, bf16[768,768]{1,0:T(8,128)(2,1)}, bf16[768,768]{1,0:T(8,128)(2,1)}, bf16[768,768]{1,0:T(8,128)(2,1)}, f32[3,8,7...) custom-call(s32[1]{0:T(128)S(6)} %copy.40.pre, ...), custom_call_target="tpu_custom_call" | custom-call | flops 5435817984 | bytes 16777216 | tf_op jit(solution)/shard_map/attn_fwd/pallas_call | solution.py:499
  62.0 4.6 collective-permute-start.3
  66.7 44.0 %shared_ffn.1 = (f32[768,768]{1,0:T(8,128)}, f32[768,768]{1,0:T(8,128)}, bf16[4,4,1152,128]{3,2,1,0:T(8,128)(2,1)}, bf16[4,4,1152,128]{3,2,1,0:T(8,128)(2,1)}, s...) custom-call(bf16[768,768]{1,0:T(8,128)(2,1)} %get-tuple-element.82.xr, ...), custom_call_target="tpu_custom_call" | custom-call | flops 21743271936 | bytes 28311552 | tf_op jit(solution)/shard_map/shared_ffn/pallas_call | solution.py:815
  110.6 2.4 collective-permute-start.2
  113.3 1.2 slice.48
  114.5 22.0 %expert_ffn1_0.1 = (bf16[960,768]{1,0:T(8,128)(2,1)}, bf16[960,768]{1,0:T(8,128)(2,1)}, bf16[384,2048]{1,0:T(8,128)(2,1)}, bf16[192,2048]{1,0:T(8,128)(2,1)}, bf...) custom-call(s32[1]{0:T(128)} %bitcast.3.tk, bf16[960,768]{1,0:T(8,128)(2,1)} %bitcast.49, ...), custom_call_target="tpu_custom_call" | custom-call | flops 13589544960 | bytes 15335424 | tf_op jit(solution)/shard_map/expert_ffn1_0/pallas_call | solution.py:758
  136.5 2.2 collective-permute-start.7
  138.7 2.4 collective-permute-start.4
  141.1 1.2 slice.49
  142.3 23.1 %expert_ffn1_1.1 = (bf16[960,768]{1,0:T(8,128)(2,1)}, bf16[960,768]{1,0:T(8,128)(2,1)}, bf16[384,2048]{1,0:T(8,128)(2,1)}, bf16[192,2048]{1,0:T(8,128)(2,1)}, bf...) custom-call(s32[1]{0:T(128)} %bitcast.6.tk, bf16[960,768]{1,0:T(8,128)(2,1)} %bitcast.50, ...), custom_call_target="tpu_custom_call" | custom-call | flops 13589544960 | bytes 15335424 | tf_op jit(solution)/shard_map/expert_ffn1_1/pallas_call | solution.py:758
  165.5 1.2 slice.50
  166.7 3.2 broadcast_select_fusion
  169.9 1.2 copy-done.8
  171.1 2.2 collective-permute-start.10
  173.4 2.5 collective-permute-start
  175.8 44.0 %expert_ffn2_0.1 = (bf16[960,768]{1,0:T(8,128)(2,1)}, bf16[960,768]{1,0:T(8,128)(2,1)}, bf16[960,768]{1,0:T(8,128)(2,1)}, bf16[960,768]{1,0:T(8,128)(2,1)}, bf16...) custom-call(s32[1]{0:T(128)} %bitcast.7.tk, ...), custom_call_target="tpu_custom_call" | custom-call | flops 27179089920 | bytes 21233664 | tf_op jit(solution)/shard_map/expert_ffn2_0/pallas_call | solution.py:758
  219.8 1.2 slice.51
  221.6 2.4 collective-permute-start.1
  224.1 2.5 add_convert_fusion.3
  226.6 1.1 copy-done.14
  230.2 1.8 collective-permute-start.8
  232.0 7.1 %add_convert_fusion = bf16[4,4,1152,128]{3,2,1,0:T(8,128)(2,1)} fusion(bf16[4,4,1152,128]{3,2,1,0:T(8,128)(2,1)} %collective-permute-done.5, bf16[4,4,1152,128]{3,2,1,0:T(8,128)(2,1)} %get-tuple-element.119), kind=kLoop, calls=%fused_computation | loop fusion | flops 9437184 | bytes 14155776 | tf_op jit(solution)/shard_map/convert_element_type | solution.py:1140
  239.1 5.4 all-to-all-start
  244.5 73.4 %expert_ffn2_1.1 = (bf16[960,768]{1,0:T(8,128)(2,1)}, bf16[960,768]{1,0:T(8,128)(2,1)}, bf16[960,768]{1,0:T(8,128)(2,1)}, bf16[960,768]{1,0:T(8,128)(2,1)}, bf16...) custom-call(s32[1]{0:T(128)} %bitcast.12.tk, ...), custom_call_target="tpu_custom_call" | custom-call | flops 27179089920 | bytes 21233664 | tf_op jit(solution)/shard_map/expert_ffn2_1/pallas_call | solution.py:758
  317.9 1.2 slice.53
  319.8 1.8 collective-permute-start.6
  321.6 2.5 add_convert_fusion.2.rest_11_
  326.1 47.7 %mid_bwd.1 = (f32[768,768]{1,0:T(8,128)}, f32[8,768]{1,0:T(8,128)S(1)}, bf16[8,120,768]{2,1,0:T(8,128)(2,1)}) custom-call(s32[768,8]{1,0:T(8,128)S(1)} %broadcast_add_fusion.colr, bf16[8,120,768]{2,1,0:T(8,128)(2,1)} %bitcast.36, bf16[8,120,768]{2,1,0:T(8,128)(2,1)} %bitcast.37, bf16[960,768]{1,0:T(8,128)(2,1)} %bitcast.35, ...), custom_call_target="tpu_custom_call" | custom-call | flops 2264924160 | bytes 12582912 | tf_op jit(solution)/shard_map/mid_bwd/pallas_call | solution.py:956
  375.6 2.2 collective-permute-start.9
  377.9 2.5 add_convert_fusion.1.rest_20_
  382.9 1.9 broadcast_select_fusion.1
  384.8 4.0 fusion.rest_3_
  388.8 5.8 collective-permute-done.9.rest_14_
  394.5 219.9 %attn_bwd.1 = (bf16[768,768]{1,0:T(8,128)(2,1)}, f32[8,768]{1,0:T(8,128)}, f32[4,96,2048]{2,1,0:T(8,128)}, f32[4,96,2048]{2,1,0:T(8,128)}, f32[4,256,768]{2,1,0:...) custom-call(s32[1]{0:T(128)S(6)} %add.76.pre, ...), custom_call_target="tpu_custom_call" | custom-call | flops 11777605632 | bytes 25165824 | tf_op jit(solution)/shard_map/attn_bwd/pallas_call | solution.py:613
  615.8 1.4 copy-done.4
  617.1 1.4 copy-done.6
  618.5 9.0 %combine.1 = bf16[768,768]{1,0:T(8,128)(2,1)} custom-call(s32[768,8]{1,0:T(8,128)S(1)} %get-tuple-element.79.colr, f32[768,2]{1,0:T(8,128)S(1)} %copy.29.gts.g, bf16[960,768]{1,0:T(8,128)(2,1)S(1)} %bitcast.31, bf16[960,768]{1,0:T(8,128)(2,1)S(1)} %bitcast.32, f32[768,768]{1,0:T(8,128)} %get-tuple-element.109.st.refs_2_, f32[768,768]{1,0:T(8,128)} %get-tuple-element.135.refs_3_), custom_call_target="tpu_custom_call" | custom-call | flops 4529848320 | bytes 9437184 | tf_op jit(solution)/shard_map/combine/pallas_call | solution.py:925
  627.6 1.0 copy.41
  633.4 1.7 copy.47
  635.1 1.4 copy-done.12
  636.5 1.7 copy.48
  638.1 1.4 copy-done.11
  639.5 1.7 copy.49
  (70 shorter events, 11.8 us)
Async XLA Ops:
  5.6 3.1 copy-start
  5.6 3.1 copy-start.5
  18.6 0.6 copy-start.7
  62.0 109.1 %collective-permute-start.3 = (bf16[960,768]{1,0:T(8,128)(2,1)}, bf16[960,768]{1,0:T(8,128)(2,1)}, u32[]{:S(2)}, u32[]{:S(2)}) collective-permute-start(bf16[960,768]{1,0:T(8,128)(2,1)} %bitcast.38), channel_id=1, source_target_pairs={{0,8},{4,12},{24,16},{28,20},{1,9},{5,13},{25,17},{29,21},{2,10},{... | collective-permute-start | bytes 4423688 | tf_op jit(solution)/shard_map/ppermute | solution.py:1126
  110.6 62.8 %collective-permute-start.2 = (bf16[960,768]{1,0:T(8,128)(2,1)}, bf16[960,768]{1,0:T(8,128)(2,1)}, u32[]{:S(2)}, u32[]{:S(2)}) collective-permute-start(bf16[960,768]{1,0:T(8,128)(2,1)} %bitcast.41), channel_id=1, source_target_pairs={{0,8},{4,12},{24,16},{28,20},{1,9},{5,13},{25,17},{29,21},{2,10},{... | collective-permute-start | bytes 4423688 | tf_op jit(solution)/shard_map/ppermute | solution.py:1126
  113.0 117.1 %collective-permute-start.5 = (bf16[4,4,1152,128]{3,2,1,0:T(8,128)(2,1)}, bf16[4,4,1152,128]{3,2,1,0:T(8,128)(2,1)}, u32[]{:S(2)}, u32[]{:S(2)}) collective-permute-start(bf16[4,4,1152,128]{3,2,1,0:T(8,128)(2,1)} %get-tuple-element.120), channel_id=1, source_target_pairs={{0,4},{4,0},{8,12},{12,8},{16,20},{20,16},{24,28},{28,24},{1,5},{5... | collective-permute-start | bytes 14155784 | tf_op jit(solution)/shard_map/ppermute | solution.py:1123
  136.5 252.3 %collective-permute-start.7 = (bf16[192,2048]{1,0:T(8,128)(2,1)}, bf16[192,2048]{1,0:T(8,128)(2,1)}, u32[]{:S(2)}, u32[]{:S(2)}) collective-permute-start(bf16[192,2048]{1,0:T(8,128)(2,1)} %get-tuple-element.121.rest_5_), channel_id=1, source_target_pairs={{0,8},{4,12},{24,16},{28,20},{1,9},{5,13},{25,17},{29,21},{2,10},{... | collective-permute-start | bytes 2359304 | tf_op jit(solution)/shard_map/ppermute | solution.py:1126
  138.7 83.0 %collective-permute-start.4 = (bf16[384,2048]{1,0:T(8,128)(2,1)}, bf16[384,2048]{1,0:T(8,128)(2,1)}, u32[]{:S(2)}, u32[]{:S(2)}) collective-permute-start(bf16[384,2048]{1,0:T(8,128)(2,1)} %get-tuple-element.98), channel_id=1, source_target_pairs={{0,8},{4,12},{24,16},{28,20},{1,9},{5,13},{25,17},{29,21},{2,10},{... | collective-permute-start | bytes 4718600 | tf_op jit(solution)/shard_map/ppermute | solution.py:1126
  169.9 1.2 copy-start.8
  171.1 217.6 %collective-permute-start.10 = (bf16[512,768]{1,0:T(8,128)(2,1)S(1)}, bf16[512,768]{1,0:T(8,128)(2,1)}, u32[]{:S(2)}, u32[]{:S(2)}) collective-permute-start(bf16[512,768]{1,0:T(8,128)(2,1)S(1)} %slice.71), channel_id=1, source_target_pairs={{0,8},{4,12},{24,16},{28,20},{1,9},{5,13},{25,17},{29,21},{2,10},{... | collective-permute-start | bytes 2359304 | tf_op jit(solution)/shard_map/ppermute | solution.py:1126
  173.4 202.2 %collective-permute-start = (bf16[1024,768]{1,0:T(8,128)(2,1)}, bf16[1024,768]{1,0:T(8,128)(2,1)}, u32[]{:S(2)}, u32[]{:S(2)}) collective-permute-start(bf16[1024,768]{1,0:T(8,128)(2,1)} %get-tuple-element.147), channel_id=1, source_target_pairs={{0,8},{4,12},{24,16},{28,20},{1,9},{5,13},{25,17},{29,21},{2,10},{... | collective-permute-start | bytes 4718600 | tf_op jit(solution)/shard_map/ppermute | solution.py:1126
  221.6 98.1 %collective-permute-start.1 = (bf16[384,2048]{1,0:T(8,128)(2,1)}, bf16[384,2048]{1,0:T(8,128)(2,1)}, u32[]{:S(2)}, u32[]{:S(2)}) collective-permute-start(bf16[384,2048]{1,0:T(8,128)(2,1)} %get-tuple-element.92), channel_id=1, source_target_pairs={{0,8},{4,12},{24,16},{28,20},{1,9},{5,13},{25,17},{29,21},{2,10},{... | collective-permute-start | bytes 4718600 | tf_op jit(solution)/shard_map/ppermute | solution.py:1126
  226.5 1.1 copy-start.14
  230.2 164.4 %collective-permute-start.8 = (bf16[384,2048]{1,0:T(8,128)(2,1)}, bf16[384,2048]{1,0:T(8,128)(2,1)}, u32[]{:S(2)}, u32[]{:S(2)}) collective-permute-start(bf16[384,2048]{1,0:T(8,128)(2,1)} %get-tuple-element.123), channel_id=1, source_target_pairs={{8,16},{12,20},{16,8},{20,12},{9,17},{13,21},{17,9},{21,13},{10,18... | collective-permute-start | bytes 4718600 | tf_op jit(solution)/shard_map/ppermute | solution.py:1132
  239.1 145.7 %all-to-all-start = ((bf16[4,4,1152,128]{3,2,1,0:T(8,128)(2,1)}), bf16[4,4,1152,128]{3,2,1,0:T(8,128)(2,1)}, u32[]{:S(2)}, u32[]{:S(2)}) async-start(bf16[4,4,1152,128]{3,2,1,0:T(8,128)(2,1)} %add_convert_fusion), calls=%async_computation | async-start | bytes 9437184 | tf_op jit(solution)/shard_map/all_to_all | solution.py:1180
  319.8 74.8 %collective-permute-start.6 = (bf16[384,2048]{1,0:T(8,128)(2,1)}, bf16[384,2048]{1,0:T(8,128)(2,1)}, u32[]{:S(2)}, u32[]{:S(2)}) collective-permute-start(bf16[384,2048]{1,0:T(8,128)(2,1)} %copy-done.14), channel_id=1, source_target_pairs={{8,16},{12,20},{16,8},{20,12},{9,17},{13,21},{17,9},{21,13},{10,18... | collective-permute-start | bytes 4718600 | tf_op jit(solution)/shard_map/ppermute | solution.py:1132
  321.6 4.5 copy-start.1
  321.6 4.5 copy-start.3
  324.1 1.9 copy-start.9
  326.1 49.5 %copy-start.22 = (bf16[192,2048]{1,0:T(8,128)(2,1)S(1)}, bf16[192,2048]{1,0:T(8,128)(2,1)}, u32[]{:S(2)}) copy-start(bf16[192,2048]{1,0:T(8,128)(2,1)} %get-tuple-element.126.rest_12_) | copy-start | bytes 2359300
  373.8 6.6 %copy-start.2 = (f32[8,768]{1,0:T(8,128)}, f32[8,768]{1,0:T(8,128)S(1)}, u32[]{:S(2)}) copy-start(f32[8,768]{1,0:T(8,128)S(1)} %get-tuple-element.110.rest_2_) | copy-start | bytes 73732
  375.6 18.9 %collective-permute-start.9 = (bf16[192,2048]{1,0:T(8,128)(2,1)S(1)}, bf16[192,2048]{1,0:T(8,128)(2,1)}, u32[]{:S(2)}, u32[]{:S(2)}) collective-permute-start(bf16[192,2048]{1,0:T(8,128)(2,1)S(1)} %copy-done.22), channel_id=1, source_target_pairs={{0,8},{4,12},{24,16},{28,20},{1,9},{5,13},{25,17},{29,21},{2,10},{... | collective-permute-start | bytes 2359304 | tf_op jit(solution)/shard_map/ppermute | solution.py:1126
  377.9 5.0 copy-start.15
  377.9 5.1 copy-start.16
  380.4 1.2 copy-start.10
  615.8 1.4 copy-start.4
  617.1 1.4 copy-start.6
  618.5 9.0 %copy-start.17 = (bf16[768,768]{1,0:T(8,128)(2,1)S(1)}, bf16[768,768]{1,0:T(8,128)(2,1)}, u32[]{:S(2)}) copy-start(bf16[768,768]{1,0:T(8,128)(2,1)} %get-tuple-element.170) | copy-start | bytes 3538948
  627.6 1.6 copy-start.18
  627.6 2.5 copy-start.23
  629.1 1.6 copy-start.21
  629.2 2.5 copy-start.20
  630.1 2.5 copy-start.19
  630.8 2.6 copy-start.13
  633.4 3.0 copy-start.12
  636.5 3.0 copy-start.11

commit v4 on v3

--- a/solution.py
+++ b/solution.py
@@ -40,6 +40,34 @@
     for kk in range(1,8):
         pl.semaphore_signal(b,inc=1,device_id=peer(z,kk),device_id_type=MESH_ID)
     pl.semaphore_wait(b,7)
+
+def plane_z_barrier():
+    c,z,e=spot()
+    b=pltpu.get_barrier_semaphore()
+    for kk in range(1,8):
+        pl.semaphore_signal(b,inc=1,device_id=peer(z,kk),device_id_type=MESH_ID)
+    pl.semaphore_signal(b,inc=1,device_id=(2*side()+c,e),device_id_type=MESH_ID)
+    pl.semaphore_wait(b,8)
+
+def side():
+    c,z,e=spot()
+    return z+1-2*lax.rem(z,2)
+
+def inward_run(srcs, dst, sems, start):
+    c,z,e=spot()
+    end=(z==0)|(z==3)
+    def cp(src): return pltpu.make_async_remote_copy(src_ref=src,dst_ref=dst,send_sem=sems[0].at[0],recv_sem=sems[1].at[0],
+        device_id=(2*side()+c,e),device_id_type=MESH_ID)
+    if start:
+        @pl.when(z==0)
+        def _(): cp(srcs[0]).start()
+        @pl.when(z==3)
+        def _(): cp(srcs[1]).start()
+    else:
+        @pl.when(end)
+        def _(): cp(srcs[0]).wait_send()
+        @pl.when(jnp.logical_not(end))
+        def _(): cp(srcs[0]).wait_recv()
 
 def plane_copies(pairs, sems):
     local,send,recv=sems
@@ -103,11 +131,23 @@
             for kk in range(8):
                 remote(own,kk,zi,send).wait_recv()
 
-
-def addb(*refs):
-    t=refs[0].astype(f32)
-    for r in refs[1:]: t=t+r.astype(f32)
-    return t.astype(bf16)
+def row_sems():
+    return [pltpu.SemaphoreType.DMA((3,)),pltpu.SemaphoreType.DMA((3,))]
+
+def row_copies(src, dst, part, sems):
+    send,recv=sems
+    c,z,e=spot()
+    return [pltpu.make_async_remote_copy(src_ref=src.at[xor4(e,kk),part],dst_ref=dst.at[kk-1],send_sem=send.at[kk-1],recv_sem=recv.at[kk-1],
+        device_id=peer(z,kk),device_id_type=MESH_ID) for kk in (1,2,3)]
+
+
+def add_rows(dst, srcs, step=16):
+    @pl.loop(0,dst.shape[0]//step)
+    def _(i):
+        r=pl.ds(pl.multiple_of(i*step,step),step)
+        t=srcs[0][r,:].astype(f32)
+        for s in srcs[1:]: t=t+s[r,:].astype(f32)
+        dst[r,:]=t.astype(dst.dtype)
 
 class Tail:
     KIND=("g","g","g","g","w","w")
@@ -122,35 +162,36 @@
         self.NR=arrays["msh"].shape[1]
         an=pl.BlockSpec(memory_space=pl.ANY)
         S=jax.ShapeDtypeStruct
-        outs={"gate":S((4,SG,FF),f32),"up":S((4,SG,FF),f32),"down":S((4,FF//8,D),f32),
+        outs={"gate":S((4,SG,FF),bf16),"up":S((4,SG,FF),bf16),"down":S((4,FF//8,D),bf16),
               "dgate":S((SG,FF),f32),"dup":S((SG,FF),f32),"ddown":S((FF//8,D),f32),
               "dqkv":S((SG,3*D),f32),"dwo":S((SG,D),f32),"gains":S((8,D),f32),
-              "ra":S((8,CAP,D),bf16)}
-        for i in range(2,6):
+              "ra":S((8,CAP,D),bf16),"rb":S((8,CAP,D),bf16)}
+        for i in range(3,6):
             outs[f"m{i}"]=S((2*R2,FF) if self.KIND[i]=="g" else (2*HW,D),bf16)
+        for i in (0,2,5):
+            outs[f"rin{i}"]=S(self.shape(i),bf16)
         for i in range(6):
             outs[f"ro{i}"]=S(self.shape(i),bf16)
         self.onames=list(outs); self.oshape=[outs[n] for n in self.onames]
         self.in_specs=[an]*len(self.names); self.out_specs=[an]*len(self.onames)
         V=pltpu.VMEM; DM=pltpu.SemaphoreType.DMA
         scr={"ga":V((3,)+self.gs,bf16),"wa":V((3,)+self.ws,bf16),
-             "gto":V((2,)+self.gs,bf16),"wto":V((2,)+self.ws,bf16),
+             "gto":V((4,)+self.gs,bf16),"wto":V((2,)+self.ws,bf16),
              "gfin":V((2,)+self.gs,bf16),"wfin":V((2,)+self.ws,bf16),
-             "gfs":V((2,SG,FF),f32),"wfs":V((2,FF//8,D),f32),
              "gsw":V((4,SG,FF),bf16),"wsw":V((2,FF//8,D),bf16),
              "atr":V((4,4,SG,D),bf16),"sv":V((4,4,SG,D),bf16),"xr":V((3,4,SG,D),bf16),
              "za":V((4,SG,D),bf16),"zb":V((4,self.NR,128),bf16),
              "gn":V((8,8,D),f32),
-             "s_x":DM((4,)),"r_x":DM((4,)),"s_o":DM((6,)),"r_o":DM((6,)),"s_w":DM((6,)),"r_w":DM((6,)),
-             "ld":DM((3,)),"st":DM((8,)),"s_at":DM((16,)),"r_at":DM((16,)),"s_xr":DM((3,)),"r_xr":DM((3,)),
+             "s_x":DM((3,)),"r_x":DM((3,)),"s_o":DM((6,)),"r_o":DM((6,)),"s_w":DM((6,)),"r_w":DM((6,)),
+             "ld":DM((3,)),"st":DM((8,)),"so":DM((2,)),"s_r":DM((3,)),"r_r":DM((3,)),"s_at":DM((16,)),"r_at":DM((16,)),"s_xr":DM((3,)),"r_xr":DM((3,)),
              "s_gn":DM((7,)),"r_gn":DM((7,)),"st2":DM((4,))}
         for nm,sh in (("a",(SG,D)),("b",(self.NR,128))):
             scr.update({"zr"+nm:V((2,)+sh,bf16),"zs"+nm:V((2,)+sh,bf16),"zm"+nm:V((2,)+sh,bf16),"zi"+nm:V(sh,bf16),"zt"+nm:V(sh,bf16),
                 "zo"+nm:V(sh,bf16),"fi"+nm:V(sh,bf16),"ag"+nm:V((3,)+sh,bf16),
                 "s_z"+nm:DM((4,)),"r_z"+nm:DM((4,)),"s_ag"+nm:DM((3,)),"r_ag"+nm:DM((3,))})
         scr.update({"oa":V((2,SG,D),f32),"og":V((2,SG,FF//4),f32),"od":V((self.SD,D),f32)})
-        self.snames=list(scr)+[f"home{i}" for i in range(4)]
-        self.scratch=[scr[n] for n in scr]+home_sems()
+        self.snames=list(scr)+[f"home{i}" for i in range(4)]+[f"plane{i}" for i in range(3)]
+        self.scratch=[scr[n] for n in scr]+home_sems()+plane_sems(1)
     def shape(self,i): return self.gs if self.KIND[i]=="g" else self.ws
     def bind(self,ins,outs,scr):
         self.r=dict(zip(self.names,ins)); self.r.update(zip(self.onames,outs)); self.r.update(zip(self.snames,scr))
@@ -159,6 +200,7 @@
         self.inner=(z==1)|(z==2); self.outer=jnp.logical_not(self.inner); self.low=z<2
         self.zo=jnp.where(z<2,0,3); self.zi=jnp.where(z<2,1,2); self.zx=3-z
         self.home=[self.r[f"home{i}"] for i in range(4)]
+        self.plane=[self.r[f"plane{i}"] for i in range(3)]
     def rcopy(self,src,dst,s,r,dev):
         return pltpu.make_async_remote_copy(src_ref=src,dst_ref=dst,send_sem=s,recv_sem=r,device_id=dev,device_id_type=MESH_ID)
     def barrier(self):
@@ -174,81 +216,106 @@
         def _():
             for kk in range(8): sig(peer(self.zi,kk))
             pl.semaphore_wait(b,15)
-    def far_src(self,i):
-        return self.r[f"far{i}"]
-    def across(self,i):
-        return self.rcopy(self.far_src(i),self.r[f"m{i}"],self.r["s_x"].at[i-2],self.r["r_x"].at[i-2],peer(self.zx,0))
+    def across(self,i,src=None):
+        src=self.r["wa0"] if i==4 and src is None else self.r[f"far{i}"] if src is None else src
+        return self.rcopy(src,self.r[f"m{i}"],self.r["s_x"].at[i-3],self.r["r_x"].at[i-3],peer(self.zx,0))
+    def across_start(self):
+        @pl.when(self.inner)
+        def _():
+            self.across(3).start()
+            @pl.when(self.low)
+            def _(): self.across(4,self.r["wa1"]).start()
+            @pl.when(jnp.logical_not(self.low))
+            def _(): self.across(4,self.r["wa0"]).start()
+            self.across(5).start()
     def start(self):
         self.barrier()
         home_run(self.r["hown"],self.r["hext"],self.r["ra"],self.home,True)
         ld=pltpu.make_async_copy(self.r["msh"],self.r["zb"],self.r["st2"].at[0])
         ld.start(); ld.wait()
         self.z_inward("b")
-        @pl.when(self.inner)
-        def _():
-            for i in (2,3): self.across(i).start()
+        self.across_start()
+        for i in range(3): self.stage1(i)
+        self.rin_start()
+        for cp in plane_copies([(self.r["rbs"],self.r["rb"])],self.plane): cp.start()
     def load(self,pairs):
-        cs=[pltpu.make_async_copy(s,d,self.r["ld"].at[k]) for k,(s,d) in enumerate(pairs)]
-        for c in cs: c.start()
+        cs=[]
+        for k,(s,d) in enumerate(pairs):
+            both=[pltpu.make_async_copy(x,d,self.r["ld"].at[k]) for x in (s if isinstance(s,tuple) else (s,))]
+            if len(both)==2:
+                pl.when(self.low)(lambda: both[0].start())
+                pl.when(jnp.logical_not(self.low))(lambda: both[1].start())
+            else: both[0].start()
+            cs.append(both[0])
         for c in cs: c.wait()
     def near(self,i,which):
         if self.KIND[i]=="g":
             return self.r[f"n{which}{i}"]
         n=self.ws[0]
-        return self.r[f"nw{i}"].at[pl.ds(0 if which=="o" else n,n)]
+        x="a" if i==4 else "b"
+        return tuple(self.r[f"w{x}{h}"].at[pl.ds(0 if which=="o" else n,n)] for h in (0,1))
+    def rin(self,k,src=None):
+        i=(0,2,5)[k]
+        src=self.r[f"rin{i}"] if src is None else src
+        return self.rcopy(src,self.r[f"rin{i}"],self.r["s_r"].at[k],self.r["r_r"].at[k],peer(self.zi,0))
+    def rin_start(self):
+        @pl.when(self.outer)
+        def _():
+            for k,i in enumerate((0,2)): self.rin(k,self.near(i,"i")).start()
+            lo,hi=self.near(5,"i")
+            @pl.when(self.low)
+            def _(): self.rin(2,lo).start()
+            @pl.when(jnp.logical_not(self.low))
+            def _(): self.rin(2,hi).start()
+    def parts_of(self,i):
+        k="g" if self.KIND[i]=="g" else "w"
+        idx=i if k=="g" else i-4
+        return k,idx,self.shape(i)[0],self.L2[i]==1
+    def ro(self,i):
+        k,idx,n,b=self.parts_of(i)
+        return self.rcopy(self.r[k+"to"].at[idx],self.r[f"ro{i}"],self.r["s_o"].at[i],self.r["r_o"].at[i],peer(self.zo,0))
+    def stage1(self,i):
+        k,idx,n,b=self.parts_of(i)
+        buf=self.r[k+"a"]
+        @pl.when(self.inner)
+        def _():
+            if i>=3: self.across(i).wait()
+            self.load([(self.r[f"m{i}"].at[pl.ds(0,n)],buf.at[0]),(self.near(i,"o"),buf.at[1])])
+            add_rows(self.r[k+"to"].at[idx],[buf.at[0],buf.at[1]])
+            self.ro(i).start()
     def piece(self,i):
-        g=self.KIND[i]=="g"; k="g" if g else "w"
-        buf=self.r[k+"a"]; to=self.r[k+"to"]; fin=self.r[k+"fin"]; fs=self.r[k+"fs"]; sw=self.r[k+"sw"]
-        n=self.shape(i)[0]; hn=n//2; b=self.L2[i]==1
-        idx=i if g else i-4
-        slot=idx%2
-        o=self.rcopy(to.at[slot],self.r[f"ro{i}"],self.r["s_o"].at[i],self.r["r_o"].at[i],peer(self.zo,0))
+        k,idx,n,b=self.parts_of(i)
+        slot=idx%2; buf=self.r[k+"a"]; fin=self.r[k+"fin"]
         @pl.when(self.inner)
         def _():
-            if i>=2: self.across(i).wait()
-            m=self.r[f"m{i}"]
-            self.load([(m.at[pl.ds(0,n)],buf.at[0]),(self.near(i,"o"),buf.at[1])])
-            if g and idx>=2:
-                self.rcopy(to.at[slot],self.r[f"ro{i-2}"],self.r["s_o"].at[i-2],self.r["r_o"].at[i-2],peer(self.zo,0)).wait_send()
-            to[slot]=addb(buf[0],buf[1])
-            o.start()
-            self.load([(m.at[pl.ds(n,n)],buf.at[0]),(self.near(i,"i"),buf.at[1])]+([(self.r[f"rin{i}"],buf.at[2])] if b else []))
+            if b: self.rin((0,2,5).index(i)).wait_recv()
+            self.load([(self.r[f"m{i}"].at[pl.ds(n,n)],buf.at[0]),(self.near(i,"i"),buf.at[1])]+([(self.r[f"rin{i}"],buf.at[2])] if b else []))
+            add_rows(fin.at[slot],[buf.at[q] for q in range(3 if b else 2)])
         @pl.when(self.outer)
         def _():
-            self.rcopy(to.at[slot],self.r[f"ro{i}"],self.r["s_o"].at[i],self.r["r_o"].at[i],peer(self.zi,0)).wait_recv()
+            self.ro(i).wait_recv()
             self.load([(self.r[f"ro{i}"],buf.at[0])]+([(self.near(i,"o"),buf.at[1])] if b else []))
-        if g and idx>=2:
-            self.swap(i-2,fin,sw).wait_send()
-        @pl.when(self.inner)
-        def _():
-            fin[slot]=addb(buf[0],buf[1],buf[2]) if b else addb(buf[0],buf[1])
-        @pl.when(self.outer)
-        def _():
-            fin[slot]=addb(buf[0],buf[1]) if b else buf[0]
-        self.swap(i,fin,sw).start()
-        fs[slot]=fin[slot,pl.ds(pl.multiple_of(self.c*hn,hn),hn),:].astype(f32)
-        for cp in self.store(i,fs,slot,self.c): cp.start()
-    def swap(self,i,fin,sw):
-        g=self.KIND[i]=="g"; n=self.shape(i)[0]; hn=n//2; idx=i if g else i-4
-        return self.rcopy(fin.at[idx%2,pl.ds(pl.multiple_of((1-self.c)*hn,hn),hn)],sw.at[idx],self.r["s_w"].at[i],self.r["r_w"].at[i],peer(self.z,4))
-    def store(self,i,fs,slot,core):
-        ex=2*core+self.L2[i]; base=0 if self.KIND[i]=="g" else 4
-        if self.KIND[i]=="g":
+            add_rows(fin.at[slot],[buf.at[q] for q in range(2 if b else 1)])
+        self.swap(i).start()
+        hn=n//2
+        for cp in self.store(i,fin.at[slot,pl.ds(pl.multiple_of(self.c*hn,hn),hn)],self.c,False): cp.start()
+    def swap(self,i):
+        k,idx,n,b=self.parts_of(i); hn=n//2
+        return self.rcopy(self.r[k+"fin"].at[idx%2,pl.ds(pl.multiple_of((1-self.c)*hn,hn),hn)],self.r[k+"sw"].at[idx],self.r["s_w"].at[i],self.r["r_w"].at[i],peer(self.z,4))
+    def store(self,i,src,core,theirs):
+        ex=2*core+self.L2[i]; k,idx,n,b=self.parts_of(i); slot=idx%2
+        if k=="g":
             hc=self.FF//2; h=self.H[i]
-            return [pltpu.make_async_copy(fs.at[slot,:,pl.ds(t*hc,hc)],self.r[nm].at[ex,:,pl.ds(h*hc,hc)],self.r["st"].at[base+2*slot+t])
+            return [pltpu.make_async_copy(src.at[:,pl.ds(t*hc,hc)],self.r[nm].at[ex,:,pl.ds(h*hc,hc)],self.r["so"].at[t] if theirs else self.r["st"].at[2*slot+t])
                     for t,nm in enumerate(("gate","up"))]
-        return [pltpu.make_async_copy(fs.at[slot],self.r["down"].at[ex],self.r["st"].at[base+slot])]
-    def store_wait(self,i,fs):
-        idx=i if self.KIND[i]=="g" else i-4
-        for cp in self.store(i,fs,idx%2,self.c): cp.wait()
+        return [pltpu.make_async_copy(src,self.r["down"].at[ex],self.r["so"].at[0] if theirs else self.r["st"].at[4+slot])]
     def other_half(self,i):
-        g=self.KIND[i]=="g"; k="g" if g else "w"
-        fin=self.r[k+"fin"]; sw=self.r[k+"sw"]; fs=self.r[k+"fs"]; idx=i if g else i-4; slot=idx%2
-        self.store_wait(i,fs)
-        self.swap(i,fin,sw).wait_recv()
-        fs[slot]=sw[idx].astype(f32)
-        for cp in self.store(i,fs,slot,1-self.c): cp.start()
-        for cp in self.store(i,fs,slot,1-self.c): cp.wait()
+        k,idx,n,b=self.parts_of(i); hn=n//2
+        for cp in self.store(i,self.r[k+"fin"].at[idx%2,pl.ds(pl.multiple_of(self.c*hn,hn),hn)],self.c,False): cp.wait()
+        self.swap(i).wait()
+        cps=self.store(i,self.r[k+"sw"].at[idx],1-self.c,True)
+        for cp in cps: cp.start()
+        for cp in cps: cp.wait()
     def zsem(self,nm,k): return self.r["s_z"+nm].at[k],self.r["r_z"+nm].at[k]
     def zc(self,nm,k):
         r=self.r; M=r["z"+nm]
@@ -265,7 +332,7 @@
         @pl.when(self.inner)
         def _():
             self.zrecv(nm,0)
-            r["zs"+nm][...]=addb(r["z"+nm][0:2],r["zr"+nm][...])
+            for k in (0,1): add_rows(r["zs"+nm].at[k],[r["z"+nm].at[k],r["zr"+nm].at[k]])
             self.zc(nm,2).start()
     def zrecv(self,nm,k):
         r=self.r; M=r["z"+nm]
@@ -279,15 +346,15 @@
         @pl.when(self.inner)
         def _():
             self.zrecv(nm,2)
-            r["zt"+nm][...]=addb(M[3],r["zm"+nm][0])
+            add_rows(r["zt"+nm],[M.at[3],r["zm"+nm].at[0]])
             self.zc(nm,3).start()
             self.zrecv(nm,1)
-            r["fi"+nm][...]=addb(M[2],r["zm"+nm][1],r["zi"+nm][...])
+            add_rows(r["fi"+nm],[M.at[2],r["zm"+nm].at[1],r["zi"+nm]])
             self.zc(nm,2).wait_send()
         @pl.when(self.outer)
         def _():
             self.zrecv(nm,3)
-            r["fi"+nm][...]=addb(M[3],r["zo"+nm][...])
+            add_rows(r["fi"+nm],[M.at[3],r["zo"+nm]])
             self.zc(nm,0).wait_send(); self.zc(nm,1).wait_send()
         for kk in (1,2,3): self.agc(nm,kk).start()
     def agc(self,nm,kk):
@@ -298,10 +365,10 @@
         for kk in range(4):
             if kk: self.agc(nm,kk).wait()
             a=xor4(self.e,kk)
-            v=(r["fi"+nm][...] if kk==0 else r["ag"+nm][kk-1]).astype(f32)
+            src=r["fi"+nm] if kk==0 else r["ag"+nm].at[kk-1]
             if nm=="a":
                 oa=r["oa"].at[kk%2]
-                oa[...]=v
+                add_rows(oa,[src])
                 cols=pl.ds(pl.multiple_of(jnp.minimum(a,2)*self.D,self.D),self.D)
                 @pl.when(a<3)
                 def _():
@@ -313,10 +380,10 @@
                 SG,SD,Q=self.SG,self.SD,self.FF//4; nb=Q//128
                 for t in range(2):
                     for b in range(nb):
-                        r["og"][t,:,b*128:(b+1)*128]=v[(t*nb+b)*SG:(t*nb+b+1)*SG,:]
+                        r["og"][t,:,b*128:(b+1)*128]=src[(t*nb+b)*SG:(t*nb+b+1)*SG,:].astype(f32)
                 off=2*nb*SG
                 for b in range(self.D//128):
-                    r["od"][:,b*128:(b+1)*128]=v[off+b*SD:off+(b+1)*SD,:]
+                    r["od"][:,b*128:(b+1)*128]=src[off+b*SD:off+(b+1)*SD,:].astype(f32)
                 cols=pl.ds(pl.multiple_of(a*Q,Q),Q)
                 cps=[pltpu.make_async_copy(r["og"].at[0],r["dgate"].at[:,cols],r["st2"].at[0]),
                      pltpu.make_async_copy(r["og"].at[1],r["dup"].at[:,cols],r["st2"].at[1]),
@@ -332,6 +399,9 @@
         return self.rcopy(self.r["sv"].at[xor4(self.e,kk)],self.r["xr"].at[kk-1],self.r["s_xr"].at[kk-1],self.r["r_xr"].at[kk-1],peer(self.z,kk))
     def gcopy(self,k,dev):
         return self.rcopy(self.r["gn"].at[0] ,self.r["gn"].at[k+1],self.r["s_gn"].at[k],self.r["r_gn"].at[k],dev)
+    def middle(self):
+        self.z_across("b")
+        self.stage1(3)
     def finish(self,GS,gg):
         r=self.r; gn=r["gn"]
         sw=self.at_swap(GS)
@@ -340,29 +410,27 @@
         ld=pltpu.make_async_copy(r["fgg"],gn.at[7],r["st2"].at[1]); ld.start(); ld.wait()
         gn[0]=jnp.where(row==0,gg,jnp.where(row==1,gn[7],0.0))
         self.gcopy(0,peer(self.z,4)).start()
-        @pl.when(self.inner)
-        def _(): self.across(4).start()
-        self.z_across("b")
         self.piece(0)
-        self.piece(1)
+        for cp in sw: cp.wait()
+        for i in range(4):
+            for zr in range(4):
+                add_rows(r["sv"].at[i,zr],[GS.at[i,self.rows_of(self.c,zr)],r["atr"].at[i,zr]])
+        for kk in (1,2,3): self.at_xy(kk).start()
         self.gcopy(0,peer(self.z,4)).wait()
         gn[0]=gn[0]+gn[1]
         for kk in (1,2,3): self.gcopy(kk,peer(self.z,kk)).start()
-        for cp in sw: cp.wait()
-        for i in range(4):
-            for zr in range(4):
-                r["sv"][i,zr]=addb(GS[i,self.rows_of(self.c,zr),:],r["atr"][i,zr])
-        for kk in (1,2,3): self.at_xy(kk).start()
         self.z_last("b")
+        self.piece(1)
+        self.stage1(4)
         self.other_half(0)
+        self.piece(2)
         self.other_half(1)
-        self.piece(2)
         for kk in (1,2,3): self.gcopy(kk,peer(self.z,kk)).wait()
         gn[0]=(gn[0]+gn[2])+(gn[3]+gn[4])
         @pl.when(self.outer)
         def _(): self.gcopy(4,peer(self.zi,0)).start()
         for kk in (1,2,3): self.at_xy(kk).wait()
-        r["za"][...]=addb(r["sv"][self.e],r["xr"][0],r["xr"][1],r["xr"][2])
+        for zr in range(4): add_rows(r["za"].at[zr],[r["sv"].at[self.e,zr]]+[r["xr"].at[k,zr] for k in range(3)])
         self.z_inward("a")
         self.z_out("b")
         @pl.when(self.inner)
@@ -370,11 +438,11 @@
             self.gcopy(4,peer(self.zo,0)).wait_recv()
             gn[0]=gn[0]+gn[5]
             self.gcopy(5,peer(self.zx,0)).start()
+        self.z_across("a")
+        self.stage1(5)
         self.piece(3)
-        self.z_across("a")
         @pl.when(self.inner)
         def _():
-            self.across(5).start()
             self.gcopy(5,peer(self.zx,0)).wait()
             gn[0]=gn[0]+gn[6]
             self.gcopy(6,peer(self.zo,0)).start()
@@ -383,26 +451,25 @@
             self.gcopy(4,peer(self.zi,0)).wait_send()
             self.gcopy(6,peer(self.zi,0)).wait_recv()
             gn[0]=gn[7]
+        gcp=pltpu.make_async_copy(gn.at[0],r["gains"],r["st2"].at[3]); gcp.start()
         self.other_half(2)
+        self.z_last("a")
         self.piece(4)
-        self.z_last("a")
         self.other_half(3)
         self.z_out("a")
         self.piece(5)
+        self.other_half(4); self.other_half(5)
+        gcp.wait()
         @pl.when(self.inner)
-        def _(): self.gcopy(6,peer(self.zo,0)).wait_send()
-        gcp=pltpu.make_async_copy(gn.at[0],r["gains"],r["st2"].at[1]); gcp.start()
-        self.other_half(4); self.other_half(5)
-        for i in (2,3): self.swap(i,r["gfin"],r["gsw"]).wait_send()
-        for i in (4,5): self.swap(i,r["wfin"],r["wsw"]).wait_send()
-        @pl.when(self.inner)
-        def _():
-            for i in (2,3,4,5):
-                k="g" if self.KIND[i]=="g" else "w"; idx=i if k=="g" else i-4
-                self.rcopy(r[k+"to"].at[idx%2],r[f"ro{i}"],r["s_o"].at[i],r["r_o"].at[i],peer(self.zo,0)).wait_send()
+        def _():
+            self.gcopy(6,peer(self.zo,0)).wait_send()
+            for i in range(6): self.ro(i).wait_send()
             self.zc("a",3).wait_send(); self.zc("b",3).wait_send()
-        gcp.wait()
+        @pl.when(self.outer)
+        def _():
+            for k in range(3): self.rin(k).wait_send()
         home_run(r["hown"],r["hext"],r["ra"],self.home,False)
+        for cp in plane_copies([(r["rbs"],r["rb"])],self.plane): cp.wait()
 
 f32=jnp.float32; bf16=jnp.bfloat16
 def nn(a,b): return lax.dot_general(a,b,(((1,),(0,)),((),())),preferred_element_type=f32)
@@ -523,6 +590,9 @@
             @pl.when(g==0)
             def _():
                 tail.start()
+            @pl.when(g==ng-1)
+            def _():
+                tail.middle()
         @pl.when(g==0)
         def _():
             for c in range(nq):
@@ -692,24 +762,37 @@
     H[rows,:]=h; GB[rows,:]=gb; UB[rows,:]=ub
     return nn(h,wd),nt(gb,wg)+nt(ub,wu)
 
-def expert_ffn(token, l2, xs, ss, wg, wu, wd, half, prev=(), carry=None, cid=None, FB=512, chunk=480):
-    n=len(xs); RG,D=xs[0].shape; FF=wg.shape[2]; R=n*RG; nf=2; HB=nf*FB
-    SR=D//4; np_=len(prev); nc=0 if carry is None else 1
-    def kernel(tk,*refs):
+def expert_ffn(deps, l2, xs, ss, wg, wu, wd, f0, nf, prev=(), carry=None, dense=None, inw=None, cid=None, FB=512, chunk=480):
+    n=len(xs); RG,D=xs[0].shape; FF=wg.shape[2]; R=n*RG; HB=2*FB; ng=nf//2
+    SR=D//4; np_=len(prev); nc=0 if carry is None else 1; nd=0 if dense is None else 1
+    part=pl.ds(dense[1],dense[2]) if nd else None
+    nx=len(deps); nz=0 if inw is None else 2
+    def kernel(*refs):
+        refs=refs[nx:]
         xr=refs[:n]; sr=refs[n:2*n]; wgr,wur,wdr=refs[2*n:2*n+3]; o=2*n+3
         pv=refs[o:o+np_]; o+=np_
         csrc=refs[o:o+nc]; o+=nc
+        dsrc=refs[o:o+nd]; o+=nd
+        zsrc=refs[o:o+nz]; o+=nz
         res=refs[o:o+n]; dgr=refs[o+n:o+2*n]; o+=2*n
-        gf,gi,go,dw,tok=refs[o:o+5]; o+=5
+        gus=[refs[o+3*q:o+3*q+3] for q in range(ng)]; o+=3*ng
+        dws=refs[o:o+ng]; o+=ng
         cdst=refs[o:o+nc]; o+=nc
+        ddst=refs[o:o+nd]; o+=nd
+        zdst=refs[o:o+nz//2]; o+=nz//2
         XT,XN,H,GB,UB,AR,AD=refs[o:o+7]; sems=refs[o+7:]
         f=pl.program_id(0)
-        tok[...]=jnp.zeros_like(tok)
-        if nc:
+        def copies():
+            return (plane_copies([(csrc[0],cdst[0])],sems[2*nd+nz:]) if nc else [])+(row_copies(dsrc[0],ddst[0],part,sems[nz:nz+2]) if nd else [])
+        if nc or nd or nz:
             @pl.when(f==0)
             def _():
-                plane_barrier()
-                for cpy in plane_copies([(csrc[0],cdst[0])],sems): cpy.start()
+                if nz:
+                    plane_z_barrier()
+                    inward_run(zsrc,zdst[0],sems[:2],True)
+                else:
+                    plane_barrier()
+                for cpy in copies(): cpy.start()
         @pl.when(f==0)
         def _():
             for a in range(n):
@@ -729,7 +812,11 @@
                         AR[rows,:]=r+pv[a][src,:].astype(f32); AD[rows,:]=d+pv[n+a][src,:].astype(f32)
                     else:
                         AR[rows,:]=r; AD[rows,:]=d
-                @pl.when(f>0)
+                if nf>2:
+                    @pl.when((f>0)&(f<nf-1))
+                    def _():
+                        AR[rows,:]+=r; AD[rows,:]+=d
+                @pl.when(f==nf-1)
                 def _():
                     res[a][src,:]=(AR[rows,:]+r).astype(bf16); dgr[a][src,:]=(AD[rows,:]+d).astype(bf16)
         for t,Y in enumerate((GB,UB)):
@@ -738,46 +825,58 @@
                 p=nn(XT[b],Y[b*chunk:(b+1)*chunk,:])
                 gv=p if gv is None else gv+p
             gv=gv.astype(bf16)
-            cols=pl.ds(pl.multiple_of(t*HB+f*FB,FB),FB)
-            gf[:,cols]=gv[0:2*SR]; gi[:,cols]=gv[2*SR:3*SR]; go[:,cols]=gv[3*SR:4*SR]
+            cols=pl.ds(pl.multiple_of(t*HB+lax.rem(f,2)*FB,FB),FB)
+            for q in range(ng):
+                def put(gf=gus[q][0],gi=gus[q][1],go=gus[q][2],gv=gv,cols=cols):
+                    gf[:,cols]=gv[0:2*SR]; gi[:,cols]=gv[2*SR:3*SR]; go[:,cols]=gv[3*SR:4*SR]
+                if ng==1: put()
+                else: pl.when(lax.div(f,2)==q)(put)
         dv=None
         for a in range(n):
             t=tn(H[a*RG:(a+1)*RG,:],sr[a][...])
             dv=t if dv is None else dv+t
-        dw[...]=dv.astype(bf16)
-        if nc:
+        dv=dv.astype(bf16)
+        for q in range(ng):
+            def put(dw=dws[q],dv=dv): dw[...]=dv
+            if ng==1: put()
+            else: pl.when(lax.div(f,2)==q)(put)
+        if nc or nd or nz:
             @pl.when(f==nf-1)
             def _():
-                for cpy in plane_copies([(csrc[0],cdst[0])],sems): cpy.wait()
+                for cpy in copies(): cpy.wait()
+                if nz: inward_run(zsrc,zdst[0],sems[:2],False)
     one=pl.Buffered(1)
     rowspec=pl.BlockSpec((RG,D),lambda f:(0,0),pipeline_mode=one)
-    wspec=pl.BlockSpec((1,D,FB),lambda f:(2*spot()[0]+l2,0,f+nf*half))
-    wdspec=pl.BlockSpec((1,FB,D),lambda f:(2*spot()[0]+l2,f+nf*half,0))
+    wspec=pl.BlockSpec((1,D,FB),lambda f:(2*spot()[0]+l2,0,f+f0))
+    wdspec=pl.BlockSpec((1,FB,D),lambda f:(2*spot()[0]+l2,f+f0,0))
     full=lambda r,c: pl.BlockSpec((r,c),lambda f:(0,0),pipeline_mode=one)
     anyspec=pl.BlockSpec(memory_space=pl.ANY)
+    wspecs=[pl.BlockSpec((FB,D),lambda f: ((1-f) if f0 else f,0))] if ng==1 else [
+        pl.BlockSpec((FB,D),lambda f: (jnp.minimum(f,1),0)),pl.BlockSpec((FB,D),lambda f: (jnp.minimum(3-f,1),0))]
     out=pl.pallas_call(kernel,grid=(nf,),
-        in_specs=[pl.BlockSpec(memory_space=pltpu.SMEM)]+[rowspec]*(2*n)+[wspec,wspec,wdspec]+[rowspec]*np_+[anyspec]*nc,
-        out_specs=[rowspec]*(2*n)+[full(2*SR,2*HB),full(SR,2*HB),full(SR,2*HB),pl.BlockSpec((FB,D),lambda f:((1-f) if half else f,0)),full(8,128)]+[anyspec]*nc,
-        scratch_shapes=[pltpu.VMEM((R//chunk,D,chunk),bf16),pltpu.VMEM((D,chunk),bf16)]+[pltpu.VMEM((R,FB),bf16)]*3+[pltpu.VMEM((R,D),f32)]*2+(plane_sems(1) if nc else []),
-      out_shape=[jax.ShapeDtypeStruct((RG,D),bf16)]*(2*n)+[jax.ShapeDtypeStruct((2*SR,2*HB),bf16)]+[jax.ShapeDtypeStruct((SR,2*HB),bf16)]*2+[jax.ShapeDtypeStruct((HB,D),bf16),jax.ShapeDtypeStruct((8,128),jnp.int32)]+[jax.ShapeDtypeStruct((8,RG//8,D),bf16)]*nc,
-      compiler_params=pltpu.CompilerParams(vmem_limit_bytes=62<<20,dimension_semantics=("arbitrary",),**(dict(collective_id=cid,has_side_effects=True) if nc else {})),
-      cost_estimate=pl.CostEstimate(flops=9*R*D*FF,bytes_accessed=3*D*FF*2+4*R*D*2,transcendentals=R*FF//2),
-      name=f"expert_ffn{n}_{half}")(token,*xs,*ss,wg,wu,wd,*prev,*([carry] if nc else []))
-    return (out[:2*n],out[2*n:2*n+3],out[2*n+3],out[2*n+4][0,0:1],*out[2*n+5:])
-
-def shared_ffn(x, s, wg, wu, wd, xout, FB=512):
+        in_specs=[anyspec]*nx+[rowspec]*(2*n)+[wspec,wspec,wdspec]+[rowspec]*np_+[anyspec]*(nc+nd+nz),
+        out_specs=[rowspec]*(2*n)+[full(2*SR,2*HB),full(SR,2*HB),full(SR,2*HB)]*ng+wspecs+[anyspec]*(nc+nd+nz//2),
+        scratch_shapes=[pltpu.VMEM((R//chunk,D,chunk),bf16),pltpu.VMEM((D,chunk),bf16)]+[pltpu.VMEM((R,FB),bf16)]*3+[pltpu.VMEM((R,D),f32)]*2+([pltpu.SemaphoreType.DMA((1,)),pltpu.SemaphoreType.DMA((1,))] if nz else [])+(row_sems() if nd else [])+(plane_sems(1) if nc else []),
+      out_shape=[jax.ShapeDtypeStruct((RG,D),bf16)]*(2*n)+([jax.ShapeDtypeStruct((2*SR,2*HB),bf16)]+[jax.ShapeDtypeStruct((SR,2*HB),bf16)]*2)*ng+[jax.ShapeDtypeStruct((HB,D),bf16)]*ng+[jax.ShapeDtypeStruct((8,RG//8,D),bf16)]*nc+([jax.ShapeDtypeStruct((3,dense[2])+dense[0].shape[2:],bf16)] if nd else [])+([jax.ShapeDtypeStruct(inw[0].shape,bf16)] if nz else []),
+      compiler_params=pltpu.CompilerParams(vmem_limit_bytes=62<<20,dimension_semantics=("arbitrary",),**(dict(collective_id=cid,has_side_effects=True) if nc or nd or nz else {})),
+      cost_estimate=pl.CostEstimate(flops=9*R*D*FF*ng,bytes_accessed=3*D*FF*2*ng+4*R*D*2,transcendentals=R*FF*ng//2),
+      name=f"expert_ffn{n}_{f0}")(*deps,*xs,*ss,wg,wu,wd,*prev,*([carry] if nc else []),*([dense[0]] if nd else []),*(inw if nz else ()))
+    o=2*n
+    return (out[:o],*[out[o+3*q:o+3*q+3] for q in range(ng)],*out[o+3*ng:])
+
+def shared_ffn(x, s, wg, wu, wd, xout, sa, FB=512):
     T,D=x.shape; FF=wg.shape[1]; nf=FF//FB; chunk=T//2
     SG=D//8; SD=FB//8
     NR=2*SG*(FB//128)+SD*(D//128)
-    def kernel(xr,sr,wgr,wur,wdr,xo,res,dgr,o0,o1,tok,xia,xib,XT,H,GB,UB,VG,VD,*sems):
+    def kernel(xr,sr,wgr,wur,wdr,xo,zs,res,dgr,o0,o1,xia,xib,zd,XT,H,GB,UB,VG,VD,zs0,zs1,*sems):
         f=pl.program_id(0)
-        tok[...]=jnp.zeros_like(tok)
         core=spot()[0]
         pairs=[(xo.at[0],xia),(xo.at[1],xib)]
         @pl.when(f==0)
         def _():
-            plane_barrier()
+            plane_z_barrier()
             for cpy in plane_copies(pairs,sems): cpy.start()
+            inward_run((zs,zs),zd,(zs0,zs1),True)
         @pl.when(f==0)
         def _():
             for b in range(2):
@@ -811,15 +910,16 @@
         @pl.when(f==nf-1)
         def _():
             for cpy in plane_copies(pairs,sems): cpy.wait()
+            inward_run((zs,zs),zd,(zs0,zs1),False)
     full=lambda sh: pl.BlockSpec(sh,lambda f:(0,)*len(sh))
     return pl.pallas_call(kernel,grid=(nf,),
-      in_specs=[full((T,D)),full((T,D)),pl.BlockSpec((D,FB),lambda f:(0,f)),pl.BlockSpec((D,FB),lambda f:(0,f)),pl.BlockSpec((FB,D),lambda f:(f,0)),pl.BlockSpec(memory_space=pl.ANY)],
-      out_specs=[full((T,D)),full((T,D)),full((4,4,NR,128)),full((4,4,NR,128)),full((8,128))]+[pl.BlockSpec(memory_space=pl.ANY)]*2,
-      out_shape=[jax.ShapeDtypeStruct((T,D),f32)]*2+[jax.ShapeDtypeStruct((4,4,NR,128),bf16)]*2+[jax.ShapeDtypeStruct((8,128),jnp.int32)]+[jax.ShapeDtypeStruct(xout.shape[1:],bf16)]*2,
-      scratch_shapes=[pltpu.VMEM((D,T),bf16)]+[pltpu.VMEM((T,FB),bf16)]*3+[pltpu.VMEM((D,FB),bf16),pltpu.VMEM((FB,D),bf16)]+plane_sems(2),
+      in_specs=[full((T,D)),full((T,D)),pl.BlockSpec((D,FB),lambda f:(0,f)),pl.BlockSpec((D,FB),lambda f:(0,f)),pl.BlockSpec((FB,D),lambda f:(f,0))]+[pl.BlockSpec(memory_space=pl.ANY)]*2,
+      out_specs=[full((T,D)),full((T,D)),full((4,4,NR,128)),full((4,4,NR,128))]+[pl.BlockSpec(memory_space=pl.ANY)]*3,
+      out_shape=[jax.ShapeDtypeStruct((T,D),f32)]*2+[jax.ShapeDtypeStruct((4,4,NR,128),bf16)]*2+[jax.ShapeDtypeStruct(xout.shape[1:],bf16)]*3,
+      scratch_shapes=[pltpu.VMEM((D,T),bf16)]+[pltpu.VMEM((T,FB),bf16)]*3+[pltpu.VMEM((D,FB),bf16),pltpu.VMEM((FB,D),bf16)]+[pltpu.SemaphoreType.DMA((1,))]*2+plane_sems(2),
       compiler_params=pltpu.CompilerParams(vmem_limit_bytes=62<<20,dimension_semantics=("arbitrary",),collective_id=1,has_side_effects=True),
       cost_estimate=pl.CostEstimate(flops=2*9*T*D*FF,bytes_accessed=6*D*FF*2+8*T*D*2,transcendentals=T*FF),
-      name="shared_ffn")(x,s,wg,wu,wd,xout)
+      name="shared_ffn")(x,s,wg,wu,wd,xout,sa)
 
 
 def route(order, expert_ids, gates, cot, core, G, L, parts, plane=False):
@@ -926,11 +1026,14 @@
       compiler_params=pltpu.CompilerParams(vmem_limit_bytes=50<<20),
       cost_estimate=pl.CostEstimate(flops=4*S*parts*T*D,bytes_accessed=9<<20,transcendentals=0),name="combine")(cols,gates,*ret,state,shared)
 
-def mid_bwd_home(cols, own, ext, back_b, dsh, state, fgain, cot):
-    T,D=state.shape; S=8*CAP
-    def kernel(colr,hown,hext,bb,ds,st,fg,ct,sgo,fgo,ba,BV,cs,*hsems):
+def mid_bwd_home(deps, inw, cols, own, ext, back_b, dsh, state, fgain, cot):
+    T,D=state.shape; S=8*CAP; nx=len(deps)
+    def kernel(*refs):
+        body(*refs[nx:])
+    def body(z0,z1,colr,hown,hext,bb,ds,st,fg,ct,sgo,fgo,ba,zd,BV,cs,zs0,zs1,*hsems):
         home_barrier()
         home_run(hown,hext,ba,hsems,True)
+        inward_run((z0,z1),zd,(zs0,zs1),True)
         fgo[...]=jnp.zeros_like(fgo)
         home_run(hown,hext,ba,hsems,False)
         cps=[pltpu.make_async_copy(ba.at[i],BV.at[i],cs.at[i]) for i in range(8)]
@@ -952,12 +1055,13 @@
             fgo[...]+=jnp.broadcast_to(jnp.sum(n*u,axis=0,keepdims=True),(8,D))
             w=n*fg[...]
             sgo[r,:]=ct[r,:].astype(f32)+inv*(w-u*jnp.mean(w*u,axis=1,keepdims=True))
+        inward_run((z0,z1),zd,(zs0,zs1),False)
     vm=pl.BlockSpec(memory_space=pltpu.VMEM); an=pl.BlockSpec(memory_space=pl.ANY)
-    return pl.pallas_call(kernel,in_specs=[vm,an,an]+[vm]*5,out_specs=[vm]*2+[an],
-      out_shape=[jax.ShapeDtypeStruct((T,D),f32),jax.ShapeDtypeStruct((8,D),f32),jax.ShapeDtypeStruct((8,CAP,D),bf16)],
-      scratch_shapes=[pltpu.VMEM((8,CAP,D),bf16),pltpu.SemaphoreType.DMA((8,))]+home_sems(),
+    return pl.pallas_call(kernel,in_specs=[an]*(nx+2)+[vm,an,an]+[vm]*5,out_specs=[vm]*2+[an]*2,
+      out_shape=[jax.ShapeDtypeStruct((T,D),f32),jax.ShapeDtypeStruct((8,D),f32),jax.ShapeDtypeStruct((8,CAP,D),bf16),jax.ShapeDtypeStruct(inw[0].shape,bf16)],
+      scratch_shapes=[pltpu.VMEM((8,CAP,D),bf16),pltpu.SemaphoreType.DMA((8,))]+[pltpu.SemaphoreType.DMA((1,))]*2+home_sems(),
       compiler_params=pltpu.CompilerParams(vmem_limit_bytes=50<<20,collective_id=4,has_side_effects=True),
-      cost_estimate=pl.CostEstimate(flops=4*S*T*D,bytes_accessed=12<<20,transcendentals=0),name="mid_bwd")(cols,own,ext,back_b,dsh,state,fgain[None],cot)
+      cost_estimate=pl.CostEstimate(flops=4*S*T*D,bytes_accessed=12<<20,transcendentals=0),name="mid_bwd")(*deps,*inw,cols,own,ext,back_b,dsh,state,fgain[None],cot)
 
 def mid_bwd(cols, back, dsh, state, fgain, cot):
     parts=len(back); T,D=state.shape; S=back[0].shape[0]
@@ -1122,26 +1226,14 @@
     def swap(x):
         return lax.ppermute(x, "dp", [(i, i ^ 1) for i in range(8)])
 
-    def inward(x):
-        return lax.ppermute(x, "dp", [(0, 2), (1, 3), (6, 4), (7, 5)])
-
-    def outward(x):
-        return lax.ppermute(x, "dp", [(2, 0), (3, 1), (4, 6), (5, 7)])
-
     def across(x):
         return lax.ppermute(x, "dp", [(2, 4), (3, 5), (4, 2), (5, 3)])
 
-    def add(*xs, after=None):
+    def add(*xs):
         t = xs[0].astype(f32)
         for x in xs[1:]:
             t = t + x.astype(f32)
-        if after is not None:
-            t = t + after[0].astype(f32)
         return t.astype(bf16)
-
-    def mark(x):
-        y = lax.slice(x, (0,) * x.ndim, (1,) * x.ndim).reshape(1).astype(f32)
-        return jnp.minimum(y * y, 0.0).astype(jnp.int32)
 
     cosw, sinw = rope_wide(T)
     rows, cols, (s_out,) = route(slot_order, expert_ids, route_gates, cotangent, core[None], 4, 4, 1, True)
@@ -1149,54 +1241,45 @@
         tokens, prefix_len, attention_gain, qkv_weight, output_weight, feedforward_gain, cosw, sinw, rows,
         s_out.reshape(2, 8, CAP, D))
     flat = lambda y: y.reshape(8 * CAP, D)
-    sx = inward(flat(sa))
-    shared_branch, dshared, sh0, sh1, tok, xa, xb = shared_ffn(ntwo, cotangent, shared_gate, shared_up, shared_down,
-                                                               x_out.reshape(2, 8, CAP, D))
-    sa, sb, xa, xb = flat(sa), flat(sb), flat(xa), flat(xb)
-    xx = inward(xa)
+    shared_branch, dshared, sh0, sh1, xa, xb, sx = shared_ffn(ntwo, cotangent, shared_gate, shared_up, shared_down,
+                                                              x_out.reshape(2, 8, CAP, D), sa)
     ws = (expert_gate, expert_up, expert_down)
-    p0, gb0, wb0, tok = expert_ffn(tok[0, 0:1], 1, [xb], [sb], *ws, 0)
-    (rb, db), gb1, wb1, tok = expert_ffn(tok, 1, [xb], [sb], *ws, 1, p0)
-
-    far_w = lambda w0, w1: jnp.where(low, w1, w0)
-    near_w = lambda w0, w1: jnp.where(low, w0, w1)
-    hw = FF // 4
     blocks = lambda y: y.reshape(8, CAP, D)
-    rf = [inward(gb0[0]), inward(gb1[0]), inward(far_w(wb0, wb1))]
-    p0, ga0, wa0, tok, db = expert_ffn(tok, 0, [xa, xx], [sa, sx], *ws, 0, carry=blocks(db), cid=2)
-    bs0 = add(gb0[0], rf[0], after=tok)
+    dsum = add(sh0, swap(sh1))
+    (rb, db), gb0, gb1, wb0, wb1, xx = expert_ffn([], 1, [flat(xb)], [flat(sb)], *ws, 0, 4, inw=(xa, xa), cid=6)
+    sa, sx, xa, xx = flat(sa), flat(sx), flat(xa), flat(xx)
+    p0, ga0, wa0, db, r0, rf0 = expert_ffn([], 0, [xa, xx], [sa, sx], *ws, 0, 2, carry=blocks(db), dense=(dsum, 0, 1),
+                                           inw=(gb0[0], gb0[0]), cid=2)
+    bs0 = add(gb0[0], rf0)
     m_b0 = across(bs0)
     m_a0 = across(ga0[0])
-    (ra, rx, da, dx), ga1, wa1, tok, rb = expert_ffn(tok + mark(bs0), 0, [xa, xx], [sa, sx], *ws, 1, p0, carry=blocks(rb), cid=3)
-    bs1 = add(gb1[0], rf[1], after=tok)
-    sgrad, fgg, _ = mid_bwd_home(cols + mark(bs1), blocks(da), blocks(dx), flat(db), dshared, state, feedforward_gain, cotangent)
-    tok = mark(fgg)
-    far_wb = far_w(wb0, wb1)
-    bs2 = add(far_wb, rf[2], after=tok)
-    near_wb = near_w(wb0, wb1)
-    rin = [inward(gb0[1]), inward(gb1[1]), inward(near_wb[hw:])]
-
-    s = add(sh0, swap(sh1))
-    s = lax.all_to_all(s, "expert", split_axis=0, concat_axis=0, tiled=True)
-    msh = add(s[0], s[1], s[2], s[3])
+    (ra, rx, da, dx), ga1, wa1, r1, rf1 = expert_ffn([bs0], 0, [xa, xx], [sa, sx], *ws, 2, 2, p0, dense=(dsum, 1, 3),
+                                                     inw=(gb1[0], gb1[0]), cid=3)
+    bs1 = add(gb1[0], rf1)
+    m_b1 = across(bs1)
+    sgrad, fgg, _, rf2 = mid_bwd_home([bs1], (wb1, wb0), cols, blocks(da), blocks(dx), flat(db), dshared, state,
+                                      feedforward_gain, cotangent)
+    bs2 = add(jnp.where(low, wb1, wb0), rf2)
+    mine = lax.dynamic_index_in_dim(dsum, ei, 0, keepdims=False)
+    msh = jnp.concatenate([add(mine[:1], r0[0], r0[1], r0[2]), add(mine[1:], r1[0], r1[1], r1[2])])
     carried = {
-        "hown": blocks(ra), "hext": blocks(rx), "fgg": fgg, "msh": msh,
-        "m0": m_b0, "ni0": gb0[1], "no0": gb0[2], "rin0": rin[0],
+        "hown": blocks(ra), "hext": blocks(rx), "rbs": blocks(rb), "fgg": fgg, "msh": msh,
+        "m0": m_b0, "ni0": gb0[1], "no0": gb0[2],
         "m1": m_a0, "ni1": ga0[1], "no1": ga0[2],
-        "far2": bs1, "ni2": gb1[1], "no2": gb1[2], "rin2": rin[1],
+        "m2": m_b1, "ni2": gb1[1], "no2": gb1[2],
         "far3": ga1[0], "ni3": ga1[1], "no3": ga1[2],
-        "far4": far_w(wa0, wa1), "nw4": near_w(wa0, wa1),
-        "far5": bs2, "nw5": near_wb, "rin5": rin[2],
+        "wa0": wa0, "wa1": wa1, "wb0": wb0, "wb1": wb1,
+        "far5": bs2,
     }
     tail = Tail(carried, T, D, FF)
-    tokens_grad, _, *rest = attn_bwd(sgrad, prefix_len + mark(bs2), tokens, attention_gain, qkv_weight, output_weight,
+    tokens_grad, _, *rest = attn_bwd(sgrad, prefix_len, tokens, attention_gain, qkv_weight, output_weight,
                                      cosw, sinw, q, k, v, att, lse, tail)
     o = dict(zip(tail.onames, rest))
-    block_out = combine(cols, route_gates, [flat(o["ra"]), flat(rb)], state, shared_branch)
+    block_out = combine(cols, route_gates, [flat(o["ra"]), flat(o["rb"])], state, shared_branch)
     sg = D // 8
     gains = lax.dynamic_slice_in_dim(o["gains"], dpi * sg, sg, 1)
     return (block_out, tokens_grad, gains[0], o["dqkv"], o["dwo"], gains[1], o["dgate"], o["dup"], o["ddown"],
-            o["gate"], o["up"], o["down"])
+            o["gate"].astype(f32), o["up"].astype(f32), o["down"].astype(f32))
 
 
 def shards(*args):

time: 647 us -> 548 us (0.85)
  Pallas kernels: 536 us -> 494 us
  starting transfers between devices: 30.3 us -> 4.95 us
  local copies, waits for them, and re-layouts: 33.7 us -> 12.8 us
  between operations: 8.95 us -> 1.82 us
    pallas_call x1, Pallas kernels: 220 us -> 193 us  [attn_bwd(): pl.pallas_call(kernel, grid=(ng,), in_specs=[pl.BlockSpec(memory_space=pl...]
    ppermute x8 -> x0, starting transfers between devices: 21 us -> none  [inward(): return lax.ppermute(x, 'dp', [(0, 2), (1, 3), (6, 4), (7, 5)])]
    pallas_call x5 -> x4, Pallas kernels: 210 us -> 195 us  [the longest x3 144 us: expert_ffn(): pl.pallas_call(kernel, grid=(nf,), in_specs=[anyspec] * nx + [rowspec] *...]
    unnamed x59 -> x60, local copies, waits for them, and re-layouts: 21.7 us -> 10.2 us
    slice x10 -> x0, local copies, waits for them, and re-layouts: 8.18 us -> none  [the longest x4 4.77 us: expert_ffn(): out[2 * n + 4][0, 0:1]]
    convert_element_type x0 -> x3, other arithmetic: none -> 7.53 us  [the longest x1 3.57 us: shards_fast(): o['gate'].astype(f32)]
  transfers between devices with their start and end apart: 12 -> 4, of which waited for: 1 -> 0; matrix products, arithmetic and copies ran while one was open for 5% -> 2% of each run, Pallas kernels for 40% -> 28%
where the time goes in v4:
time: 548 us; the launch traced here: 543 us
  Pallas kernels  494 us (90%)
  other arithmetic  29.9 us (5%)
  local copies, waits for them, and re-layouts  12.8 us (2%)
    pallas_call x1, Pallas kernels, attn_bwd(): pl.pallas_call(kernel, grid=(ng,), in_specs=[pl.BlockSpec(memory_space=pl...  193 us
    pallas_call x3, Pallas kernels, expert_ffn(): pl.pallas_call(kernel, grid=(nf,), in_specs=[anyspec] * nx + [rowspec] *...  144 us
    pallas_call x1, Pallas kernels, mid_bwd_home(): pl.pallas_call(kernel, in_specs=[an] * (nx + 2) + [vm, an, an] + [vm] * 5...  51 us
    pallas_call x1, Pallas kernels, shared_ffn(): pl.pallas_call(kernel, grid=(nf,), in_specs=[full((T, D)), full((T, D)),...  44.4 us
    pallas_call x1, Pallas kernels, attn_fwd(): pl.pallas_call(kernel, grid=(ng,), in_specs=[pl.BlockSpec(memory_space=pl...  42.7 us
    convert_element_type x4, other arithmetic, add(): return t.astype(bf16)  15.3 us
  transfers between devices with their start and end apart: 4, of which 0 were waited for; matrix products, arithmetic and copies ran while one was open for 2% of the time, Pallas kernels for 28%

profile of v4, /device:TPU:0, one launch (start us, length us, event | category | flops | bytes accessed | tf_op | source)
XLA Modules:
  0.0 543.3 jit_solution(17087957927083583582)
XLA Ops:
  0.7 0.9 copy.29.gts.g
  1.6 0.9 copy.28.ids
  2.4 0.0 copy-start
  2.5 0.0 copy-start.6
  2.5 1.5 fusion.4
  4.0 0.6 broadcast_in_dim.14.ag
  4.5 0.6 broadcast_in_dim.15.fg.refs_9_
  5.8 1.6 pad_maximum_fusion.1
  7.3 9.8 %route.1 = (s32[8,768]{1,0:T(8,128)S(1)}, s32[768,8]{1,0:T(8,128)S(1)}, bf16[1920,768]{1,0:T(8,128)(2,1)}) custom-call(s32[1]{0:T(128)} %bitcast.core_ref, s32[1,1536]{1,0:T(1,128)S(1)} %copy-done.6, s32[768,2]{1,0:T(8,128)S(1)} %copy.28.ids, f32[768,2]{1,0:T(8,128)S(1)} %copy.29.gts.g, bf16[768,768]{1,0:T(8,128)(2,1)S(1)} %copy-done), custom_call_target="tpu_custom_call" | custom-call | flops 4680843264 | bytes 8388608 | tf_op jit(solution)/shard_map/route/pallas_call | solution.py:984
  17.2 0.6 copy-done.7
  17.8 42.7 %attn_fwd.1 = (bf16[768,768]{1,0:T(8,128)(2,1)}, bf16[768,768]{1,0:T(8,128)(2,1)}, bf16[768,768]{1,0:T(8,128)(2,1)}, bf16[768,768]{1,0:T(8,128)(2,1)}, f32[3,8,7...) custom-call(s32[1]{0:T(128)S(6)} %copy.37.pre, ...), custom_call_target="tpu_custom_call" | custom-call | flops 5435817984 | bytes 16777216 | tf_op jit(solution)/shard_map/attn_fwd/pallas_call | solution.py:566
  60.5 44.4 %shared_ffn.1 = (f32[768,768]{1,0:T(8,128)}, f32[768,768]{1,0:T(8,128)}, bf16[4,4,1152,128]{3,2,1,0:T(8,128)(2,1)}, bf16[4,4,1152,128]{3,2,1,0:T(8,128)(2,1)}, b...) custom-call(bf16[768,768]{1,0:T(8,128)(2,1)} %get-tuple-element.82.xr, ...), custom_call_target="tpu_custom_call" | custom-call | flops 21743271936 | bytes 28311552 | tf_op jit(solution)/shard_map/shared_ffn/pallas_call | solution.py:915
  104.9 0.5 collective-permute-start
  105.4 46.9 %expert_ffn1_0.1 = (bf16[960,768]{1,0:T(8,128)(2,1)}, bf16[960,768]{1,0:T(8,128)(2,1)}, bf16[384,2048]{1,0:T(8,128)(2,1)}, bf16[192,2048]{1,0:T(8,128)(2,1)}, bf...) custom-call(bf16[960,768]{1,0:T(8,128)(2,1)} %bitcast.43, ...), custom_call_target="tpu_custom_call" | custom-call | flops 27179089920 | bytes 24772608 | tf_op jit(solution)/shard_map/expert_ffn1_0/pallas_call | solution.py:856
  152.3 0.0 collective-permute-done
  152.3 7.1 %add_convert_fusion.refs_8_.refs_12_ = bf16[4,4,1152,128]{3,2,1,0:T(8,128)(2,1)} fusion(bf16[4,4,1152,128]{3,2,1,0:T(8,128)(2,1)} %collective-permute-done, bf16[4,4,1152,128]{3,2,1,0:T(8,128)(2,1)} %get-tuple-element.93), kind=kLoop, calls=%fused_computation | loop fusion | flops 9437184 | bytes 14155776 | tf_op jit(solution)/shard_map/convert_element_type | solution.py:1236
  159.4 43.7 %expert_ffn2_0.1 = (bf16[960,768]{1,0:T(8,128)(2,1)}, bf16[960,768]{1,0:T(8,128)(2,1)}, bf16[960,768]{1,0:T(8,128)(2,1)}, bf16[960,768]{1,0:T(8,128)(2,1)}, bf16...) custom-call(bf16[960,768]{1,0:T(8,128)(2,1)} %bitcast.38, ...), custom_call_target="tpu_custom_call" | custom-call | flops 27179089920 | bytes 21233664 | tf_op jit(solution)/shard_map/expert_ffn2_0/pallas_call | solution.py:856
  203.2 3.7 add_convert_fusion.3.refs_0_
  206.9 1.8 collective-permute-start.1
  208.7 53.8 %expert_ffn2_2.1 = (bf16[960,768]{1,0:T(8,128)(2,1)}, bf16[960,768]{1,0:T(8,128)(2,1)}, bf16[960,768]{1,0:T(8,128)(2,1)}, bf16[960,768]{1,0:T(8,128)(2,1)}, bf16...) custom-call(bf16[384,2048]{1,0:T(8,128)(2,1)} %add_convert_fusion.3., ...), custom_call_target="tpu_custom_call" | custom-call | flops 27179089920 | bytes 21233664 | tf_op jit(solution)/shard_map/expert_ffn2_2/pallas_call | solution.py:856
  262.5 0.0 copy-start.1
  262.5 0.0 copy-start.3
  262.5 2.7 add_convert_fusion.2.refs_0_
  265.2 0.0 copy-start.10
  265.2 0.8 collective-permute-start.3
  266.0 1.8 collective-permute-start.2
  267.9 51.0 %mid_bwd.1 = (f32[768,768]{1,0:T(8,128)}, f32[8,768]{1,0:T(8,128)S(1)}, bf16[8,120,768]{2,1,0:T(8,128)(2,1)}, bf16[1024,768]{1,0:T(8,128)(2,1)}) custom-call(bf16[384,2048]{1,0:T(8,128)(2,1)} %copy-done.10, bf16[1024,768]{1,0:T(8,128)(2,1)} %get-tuple-element.101.refs_1_.rest_20_, bf16[1024,768]{1,0:T(8,128)(2,1)} %get-tuple-element.102.refs_2_.rest_19_, ...), custom_call_target="tpu_custom_call" | custom-call | flops 2264924160 | bytes 12582912 | tf_op jit(solution)/shard_map/mid_bwd/pallas_call | solution.py:1060
  318.9 0.0 copy-start.2
  318.9 1.1 fusion.3
  320.1 1.8 fusion
  321.9 1.1 pad_maximum_fusion.rest_4_
  323.0 0.8 copy-done.8
  323.8 1.8 add_convert_fusion.1.rest_21_
  325.6 1.1 copy-done.12
  326.7 192.5 %attn_bwd.1 = (bf16[768,768]{1,0:T(8,128)(2,1)}, f32[8,768]{1,0:T(8,128)}, bf16[4,96,2048]{2,1,0:T(8,128)(2,1)}, bf16[4,96,2048]{2,1,0:T(8,128)(2,1)}, bf16[4,25...) custom-call(s32[1]{0:T(128)S(6)} %copy.37.pre, ...), custom_call_target="tpu_custom_call" | custom-call | flops 11777605632 | bytes 25165824 | tf_op jit(solution)/shard_map/attn_bwd/pallas_call | solution.py:683
  519.3 3.6 convert_element_type.139
  522.8 2.0 convert_element_type.140
  524.9 1.9 convert_element_type.141
  526.8 0.9 constant_dynamic-slice_fusion
  527.7 0.5 slice_bitcast_fusion
  528.2 9.0 %combine.1 = bf16[768,768]{1,0:T(8,128)(2,1)} custom-call(s32[768,8]{1,0:T(8,128)S(1)} %get-tuple-element.79.refs_3_.colr, f32[768,2]{1,0:T(8,128)S(1)} %copy.29.gts.g, bf16[960,768]{1,0:T(8,128)(2,1)S(1)} %bitcast.26, bf16[960,768]{1,0:T(8,128)(2,1)S(1)} %bitcast.27, f32[768,768]{1,0:T(8,128)} %get-tuple-element.107.refs_8_.refs_2_, ...), custom_call_target="tpu_custom_call" | custom-call | flops 4529848320 | bytes 9437184 | tf_op jit(solution)/shard_map/combine/pallas_call | solution.py:1025
  537.2 1.0 copy.38
  538.2 0.6 copy-done.17
  538.8 0.9 copy.39
  539.7 0.7 copy.40
  540.5 0.9 copy.41
  541.3 0.9 copy.42
  542.2 0.9 copy.43
  (46 shorter events, 0.1 us)
Async XLA Ops:
  0.6 3.3 copy-start.23
  0.7 3.9 copy-start.24
  2.4 4.9 copy-start
  2.5 4.9 copy-start.6
  17.2 0.6 copy-start.7
  104.9 47.4 %collective-permute-start = (bf16[4,4,1152,128]{3,2,1,0:T(8,128)(2,1)}, bf16[4,4,1152,128]{3,2,1,0:T(8,128)(2,1)}, u32[]{:S(2)}, u32[]{:S(2)}) collective-permute-start(bf16[4,4,1152,128]{3,2,1,0:T(8,128)(2,1)} %get-tuple-element.94), channel_id=1, source_target_pairs={{0,4},{4,0},{8,12},{12,8},{16,20},{20,16},{24,28},{28,24},{1,5},{5... | collective-permute-start | bytes 14155784 | tf_op jit(solution)/shard_map/ppermute | solution.py:1227
  206.9 119.8 %collective-permute-start.1 = (bf16[384,2048]{1,0:T(8,128)(2,1)}, bf16[384,2048]{1,0:T(8,128)(2,1)}, u32[]{:S(2)}, u32[]{:S(2)}) collective-permute-start(bf16[384,2048]{1,0:T(8,128)(2,1)} %add_convert_fusion.3.refs_0_), channel_id=1, source_target_pairs={{8,16},{12,20},{16,8},{20,12},{9,17},{13,21},{17,9},{21,13},{10,18... | collective-permute-start | bytes 4718600 | tf_op jit(solution)/shard_map/ppermute | solution.py:1230
  262.5 3.5 copy-start.25
  262.5 5.4 copy-start.1
  262.5 5.4 copy-start.3
  265.2 2.6 copy-start.10
  265.2 60.3 %collective-permute-start.3 = (bf16[384,2048]{1,0:T(8,128)(2,1)S(1)}, bf16[384,2048]{1,0:T(8,128)(2,1)S(1)}, u32[]{:S(2)}, u32[]{:S(2)}) collective-permute-start(bf16[384,2048]{1,0:T(8,128)(2,1)S(1)} %add_convert_fusion.2.refs_0_), channel_id=1, source_target_pairs={{8,16},{12,20},{16,8},{20,12},{9,17},{13,21},{17,9},{21,13},{10,18... | collective-permute-start | bytes 4718600 | tf_op jit(solution)/shard_map/ppermute | solution.py:1230
  266.0 60.7 %collective-permute-start.2 = (bf16[384,2048]{1,0:T(8,128)(2,1)S(1)}, bf16[384,2048]{1,0:T(8,128)(2,1)}, u32[]{:S(2)}, u32[]{:S(2)}) collective-permute-start(bf16[384,2048]{1,0:T(8,128)(2,1)S(1)} %copy-done.25), channel_id=1, source_target_pairs={{8,16},{12,20},{16,8},{20,12},{9,17},{13,21},{17,9},{21,13},{10,18... | collective-permute-start | bytes 4718600 | tf_op jit(solution)/shard_map/ppermute | solution.py:1230
  267.9 51.0 %copy-start.18 = (bf16[3,1,1152,128]{3,2,1,0:T(8,128)(2,1)S(1)}, bf16[3,1,1152,128]{3,2,1,0:T(8,128)(2,1)}, u32[]{:S(2)}) copy-start(bf16[3,1,1152,128]{3,2,1,0:T(8,128)(2,1)} %get-tuple-element.118) | copy-start | bytes 2654212
  267.9 52.2 %copy-start.11 = (bf16[3,3,1152,128]{3,2,1,0:T(8,128)(2,1)S(1)}, bf16[3,3,1152,128]{3,2,1,0:T(8,128)(2,1)}, u32[]{:S(2)}) copy-start(bf16[3,3,1152,128]{3,2,1,0:T(8,128)(2,1)} %get-tuple-element.119) | copy-start | bytes 7962628
  318.9 3.0 copy-start.2
  320.1 2.9 copy-start.9
  320.1 2.9 copy-start.15
  321.9 1.9 copy-start.8
  325.6 1.1 copy-start.12
  519.2 3.6 copy-start.14
  522.8 2.0 copy-start.13
  524.9 3.3 copy-start.4
  524.9 3.3 copy-start.5
  528.2 9.0 %copy-start.16 = (bf16[768,768]{1,0:T(8,128)(2,1)S(1)}, bf16[768,768]{1,0:T(8,128)(2,1)}, u32[]{:S(2)}) copy-start(bf16[768,768]{1,0:T(8,128)(2,1)} %get-tuple-element.166) | copy-start | bytes 3538948
  537.2 1.6 copy-start.17
  537.2 2.5 copy-start.22
  538.8 1.6 copy-start.21
  538.8 2.5 copy-start.20
  540.5 1.8 copy-start.19

commit v5 on v4

--- a/solution.py
+++ b/solution.py
@@ -1,5 +1,6 @@
 import jax
 import jax.numpy as jnp
+import numpy as np
 from jax import lax
 from jax.experimental import pallas as pl
 from jax.experimental.pallas import tpu as pltpu
@@ -80,9 +81,6 @@
             out.append(pltpu.make_async_remote_copy(src_ref=src.at[block_of(kk)],dst_ref=dst.at[me],send_sem=send.at[i,kk-1],
                 recv_sem=recv.at[i,kk-1],device_id=peer(z,kk),device_id_type=MESH_ID))
     return out
-
-def home_sems():
-    return [pltpu.SemaphoreType.DMA((1,)),pltpu.SemaphoreType.DMA((8,)),pltpu.SemaphoreType.DMA((8,)),pltpu.SemaphoreType.DMA((8,))]
 
 def home_barrier():
     c,z,e=spot()
@@ -100,36 +98,40 @@
     def _():
         for kk in range(8):
             pl.semaphore_signal(b,inc=1,device_id=peer(zi,kk),device_id_type=MESH_ID)
-        pl.semaphore_wait(b,8)
-
-def home_run(own, ext, dst, sems, start):
-    local,send,send2,recv=sems
+            if kk:
+                pl.semaphore_signal(b,inc=1,device_id=peer(z,kk),device_id_type=MESH_ID)
+        pl.semaphore_wait(b,15)
+
+def is_inner():
     c,z,e=spot()
-    inner=(z==1)|(z==2)
-    zo=jnp.where(z<2,0,3); zi=jnp.where(z<2,1,2)
+    return (z==1)|(z==2)
+
+def ext_sems():
+    return [pltpu.SemaphoreType.DMA((8,)),pltpu.SemaphoreType.DMA((8,))]
+
+def ext_run(src, dst, sems, start):
+    send,recv=sems
     me=block_of(0)
-    def remote(src,kk,zz,s):
-        return pltpu.make_async_remote_copy(src_ref=src.at[block_of(kk)],dst_ref=dst.at[me],send_sem=s.at[kk],recv_sem=recv.at[kk],
+    c,z,e=spot()
+    def remote(kk,zz):
+        return pltpu.make_async_remote_copy(src_ref=src.at[block_of(kk)],dst_ref=dst.at[me],send_sem=send.at[kk],recv_sem=recv.at[kk],
             device_id=peer(zz,kk),device_id_type=MESH_ID)
-    @pl.when(inner)
+    @pl.when(is_inner())
     def _():
-        lc=pltpu.make_async_copy(own.at[me],dst.at[me],local.at[0])
-        if start:
-            lc.start()
-            for kk in range(8):
-                remote(ext,kk,zo,send2).start()
-                if kk: remote(own,kk,z,send).start()
-        else:
-            lc.wait()
-            for kk in range(8):
-                remote(ext,kk,zo,send2).wait_send()
-                if kk:
-                    remote(own,kk,z,send).wait()
+        for kk in range(8):
+            if start: remote(kk,side()).start()
+            else: remote(kk,side()).wait_send()
     if not start:
-        @pl.when(jnp.logical_not(inner))
-        def _():
-            for kk in range(8):
-                remote(own,kk,zi,send).wait_recv()
+        @pl.when(jnp.logical_not(is_inner()))
+        def _():
+            for kk in range(8): remote(kk,side()).wait_recv()
+
+def own_run(src, dst, sems, start):
+    @pl.when(is_inner())
+    def _():
+        for cp in plane_copies([(src,dst)],sems):
+            if start: cp.start()
+            else: cp.wait()
 
 def row_sems():
     return [pltpu.SemaphoreType.DMA((3,)),pltpu.SemaphoreType.DMA((3,))]
@@ -141,7 +143,9 @@
         device_id=peer(z,kk),device_id_type=MESH_ID) for kk in (1,2,3)]
 
 
-def add_rows(dst, srcs, step=16):
+def add_rows(dst, srcs):
+    rows,cols=dst.shape
+    step=max(s for s in range(16,rows+1,16) if rows%s==0 and s*cols<=40000)
     @pl.loop(0,dst.shape[0]//step)
     def _(i):
         r=pl.ds(pl.multiple_of(i*step,step),step)
@@ -151,8 +155,10 @@
 
 class Tail:
     KIND=("g","g","g","g","w","w")
-    L2=(1,0,1,0,0,1)
-    H=(0,0,1,1,0,0)
+    L2=(1,1,0,0,0,1)
+    H=(0,1,0,1,0,0)
+    RIN=(0,1,5)
+    MID=((3,"o"),(4,"o"),(5,"o"),(2,"i"),(3,"i"),(4,"i"),(5,"i"))
     def __init__(self, arrays, T, D, FF):
         self.names=list(arrays); self.arrays=[arrays[n] for n in self.names]
         self.T,self.D,self.FF=T,D,FF
@@ -166,32 +172,32 @@
               "dgate":S((SG,FF),f32),"dup":S((SG,FF),f32),"ddown":S((FF//8,D),f32),
               "dqkv":S((SG,3*D),f32),"dwo":S((SG,D),f32),"gains":S((8,D),f32),
               "ra":S((8,CAP,D),bf16),"rb":S((8,CAP,D),bf16)}
-        for i in range(3,6):
-            outs[f"m{i}"]=S((2*R2,FF) if self.KIND[i]=="g" else (2*HW,D),bf16)
-        for i in (0,2,5):
+        for i,w in self.MID:
+            outs[f"m{i}{w}"]=S(self.shape(i),bf16)
+        for i in self.RIN:
             outs[f"rin{i}"]=S(self.shape(i),bf16)
         for i in range(6):
             outs[f"ro{i}"]=S(self.shape(i),bf16)
         self.onames=list(outs); self.oshape=[outs[n] for n in self.onames]
         self.in_specs=[an]*len(self.names); self.out_specs=[an]*len(self.onames)
         V=pltpu.VMEM; DM=pltpu.SemaphoreType.DMA
-        scr={"ga":V((3,)+self.gs,bf16),"wa":V((3,)+self.ws,bf16),
-             "gto":V((4,)+self.gs,bf16),"wto":V((2,)+self.ws,bf16),
-             "gfin":V((2,)+self.gs,bf16),"wfin":V((2,)+self.ws,bf16),
+        scr={"ga":V((2,3)+self.gs,bf16),"wa":V((2,3)+self.ws,bf16),
+             "gto":V((3,)+self.gs,bf16),"wto":V((1,)+self.ws,bf16),
+             "gfin":V((2,)+self.gs,bf16),"wfin":V((1,)+self.ws,bf16),
              "gsw":V((4,SG,FF),bf16),"wsw":V((2,FF//8,D),bf16),
              "atr":V((4,4,SG,D),bf16),"sv":V((4,4,SG,D),bf16),"xr":V((3,4,SG,D),bf16),
              "za":V((4,SG,D),bf16),"zb":V((4,self.NR,128),bf16),
              "gn":V((8,8,D),f32),
-             "s_x":DM((3,)),"r_x":DM((3,)),"s_o":DM((6,)),"r_o":DM((6,)),"s_w":DM((6,)),"r_w":DM((6,)),
-             "ld":DM((3,)),"st":DM((8,)),"so":DM((2,)),"s_r":DM((3,)),"r_r":DM((3,)),"s_at":DM((16,)),"r_at":DM((16,)),"s_xr":DM((3,)),"r_xr":DM((3,)),
-             "s_gn":DM((7,)),"r_gn":DM((7,)),"st2":DM((4,))}
+             "s_x":DM((7,)),"r_x":DM((7,)),"lra":DM((1,)),"s_o":DM((6,)),"r_o":DM((6,)),"s_w":DM((6,)),"r_w":DM((6,)),
+             "ld":DM((2,2,3)),"st":DM((8,)),"so":DM((6,2)),"s_r":DM((3,)),"r_r":DM((3,)),"s_at":DM((16,)),"r_at":DM((16,)),"s_xr":DM((3,)),"r_xr":DM((3,)),
+             "s_gn":DM((7,)),"r_gn":DM((7,)),"st2":DM((4,)),"sz":DM((2,3))}
         for nm,sh in (("a",(SG,D)),("b",(self.NR,128))):
             scr.update({"zr"+nm:V((2,)+sh,bf16),"zs"+nm:V((2,)+sh,bf16),"zm"+nm:V((2,)+sh,bf16),"zi"+nm:V(sh,bf16),"zt"+nm:V(sh,bf16),
                 "zo"+nm:V(sh,bf16),"fi"+nm:V(sh,bf16),"ag"+nm:V((3,)+sh,bf16),
                 "s_z"+nm:DM((4,)),"r_z"+nm:DM((4,)),"s_ag"+nm:DM((3,)),"r_ag"+nm:DM((3,))})
-        scr.update({"oa":V((2,SG,D),f32),"og":V((2,SG,FF//4),f32),"od":V((self.SD,D),f32)})
-        self.snames=list(scr)+[f"home{i}" for i in range(4)]+[f"plane{i}" for i in range(3)]
-        self.scratch=[scr[n] for n in scr]+home_sems()+plane_sems(1)
+        scr.update({"oa":V((2,SG,D),f32),"og":V((2,2,SG,FF//4),f32),"od":V((2,self.SD,D),f32)})
+        self.snames=list(scr)+[f"own{i}" for i in range(3)]+[f"plane{i}" for i in range(3)]
+        self.scratch=[scr[n] for n in scr]+plane_sems(1)+plane_sems(1)
     def shape(self,i): return self.gs if self.KIND[i]=="g" else self.ws
     def bind(self,ins,outs,scr):
         self.r=dict(zip(self.names,ins)); self.r.update(zip(self.onames,outs)); self.r.update(zip(self.snames,scr))
@@ -199,7 +205,7 @@
         self.c,self.z,self.e=c,z,e
         self.inner=(z==1)|(z==2); self.outer=jnp.logical_not(self.inner); self.low=z<2
         self.zo=jnp.where(z<2,0,3); self.zi=jnp.where(z<2,1,2); self.zx=3-z
-        self.home=[self.r[f"home{i}"] for i in range(4)]
+        self.own=[self.r[f"own{i}"] for i in range(3)]
         self.plane=[self.r[f"plane{i}"] for i in range(3)]
     def rcopy(self,src,dst,s,r,dev):
         return pltpu.make_async_remote_copy(src_ref=src,dst_ref=dst,send_sem=s,recv_sem=r,device_id=dev,device_id_type=MESH_ID)
@@ -216,38 +222,48 @@
         def _():
             for kk in range(8): sig(peer(self.zi,kk))
             pl.semaphore_wait(b,15)
-    def across(self,i,src=None):
-        src=self.r["wa0"] if i==4 and src is None else self.r[f"far{i}"] if src is None else src
-        return self.rcopy(src,self.r[f"m{i}"],self.r["s_x"].at[i-3],self.r["r_x"].at[i-3],peer(self.zx,0))
-    def across_start(self):
+    def across(self,q,high=False):
+        i,w=self.MID[q]; n=self.shape(i)[0]
+        src={2:self.r["far2"],3:self.r["far3"],4:self.r["wa0" if high else "wa1"],5:self.r["far5"]}[i]
+        return self.rcopy(src.at[pl.ds(0 if w=="o" else n,n)],self.r[f"m{i}{w}"],self.r["s_x"].at[q],self.r["r_x"].at[q],peer(self.zx,0))
+    def across_start(self,qs):
         @pl.when(self.inner)
         def _():
-            self.across(3).start()
-            @pl.when(self.low)
-            def _(): self.across(4,self.r["wa1"]).start()
-            @pl.when(jnp.logical_not(self.low))
-            def _(): self.across(4,self.r["wa0"]).start()
-            self.across(5).start()
+            for q in qs:
+                if self.MID[q][0]==4:
+                    @pl.when(self.low)
+                    def _(q=q): self.across(q).start()
+                    @pl.when(jnp.logical_not(self.low))
+                    def _(q=q): self.across(q,True).start()
+                else: self.across(q).start()
+    def rows_home(self,start):
+        own_run(self.r["hown"],self.r["ra"],self.own,start)
+        @pl.when(self.outer)
+        def _():
+            cp=pltpu.make_async_copy(self.r["rxl"],self.r["ra"],self.r["lra"].at[0])
+            if start: cp.start()
+            else: cp.wait()
     def start(self):
         self.barrier()
-        home_run(self.r["hown"],self.r["hext"],self.r["ra"],self.home,True)
+        self.across_start((0,1,2))
+        self.stage1(0,1)
         ld=pltpu.make_async_copy(self.r["msh"],self.r["zb"],self.r["st2"].at[0])
         ld.start(); ld.wait()
         self.z_inward("b")
-        self.across_start()
-        for i in range(3): self.stage1(i)
         self.rin_start()
         for cp in plane_copies([(self.r["rbs"],self.r["rb"])],self.plane): cp.start()
-    def load(self,pairs):
-        cs=[]
-        for k,(s,d) in enumerate(pairs):
-            both=[pltpu.make_async_copy(x,d,self.r["ld"].at[k]) for x in (s if isinstance(s,tuple) else (s,))]
-            if len(both)==2:
-                pl.when(self.low)(lambda: both[0].start())
-                pl.when(jnp.logical_not(self.low))(lambda: both[1].start())
-            else: both[0].start()
-            cs.append(both[0])
-        for c in cs: c.wait()
+        self.rows_home(True)
+        self.stage1(2)
+    def load(self,pairs,kind,slot,go):
+        buf=self.r[kind+"a"]; ki=0 if kind=="g" else 1
+        for k,s in enumerate(pairs):
+            def cp(x,k=k): return pltpu.make_async_copy(x,buf.at[slot,k],self.r["ld"].at[ki,slot,k])
+            two=isinstance(s,tuple)
+            if not go: cp(s[0] if two else s).wait()
+            elif two:
+                pl.when(self.low)(lambda cp=cp,s=s: cp(s[0]).start())
+                pl.when(jnp.logical_not(self.low))(lambda cp=cp,s=s: cp(s[1]).start())
+            else: cp(s).start()
     def near(self,i,which):
         if self.KIND[i]=="g":
             return self.r[f"n{which}{i}"]
@@ -255,13 +271,13 @@
         x="a" if i==4 else "b"
         return tuple(self.r[f"w{x}{h}"].at[pl.ds(0 if which=="o" else n,n)] for h in (0,1))
     def rin(self,k,src=None):
-        i=(0,2,5)[k]
+        i=self.RIN[k]
         src=self.r[f"rin{i}"] if src is None else src
         return self.rcopy(src,self.r[f"rin{i}"],self.r["s_r"].at[k],self.r["r_r"].at[k],peer(self.zi,0))
     def rin_start(self):
         @pl.when(self.outer)
         def _():
-            for k,i in enumerate((0,2)): self.rin(k,self.near(i,"i")).start()
+            for k,i in enumerate((0,1)): self.rin(k,self.near(i,"i")).start()
             lo,hi=self.near(5,"i")
             @pl.when(self.low)
             def _(): self.rin(2,lo).start()
@@ -273,49 +289,80 @@
         return k,idx,self.shape(i)[0],self.L2[i]==1
     def ro(self,i):
         k,idx,n,b=self.parts_of(i)
-        return self.rcopy(self.r[k+"to"].at[idx],self.r[f"ro{i}"],self.r["s_o"].at[i],self.r["r_o"].at[i],peer(self.zo,0))
-    def stage1(self,i):
+        return self.rcopy(self.r[k+"to"].at[idx%3 if k=="g" else 0],self.r[f"ro{i}"],self.r["s_o"].at[i],self.r["r_o"].at[i],peer(self.zo,0))
+    def view(self,i,w):
+        if i<2:
+            n=self.shape(i)[0]
+            return self.r[f"m{i}"].at[pl.ds(0 if w=="o" else n,n)]
+        return self.r[f"m{i}{w}"]
+    def outward_load(self,i,go=True):
         k,idx,n,b=self.parts_of(i)
-        buf=self.r[k+"a"]
+        if go and (i,"o") in self.MID: self.across(self.MID.index((i,"o"))).wait()
+        self.load([self.view(i,"o"),self.near(i,"o")],k,idx%2,go)
+    def outward_load_start(self,i):
         @pl.when(self.inner)
-        def _():
-            if i>=3: self.across(i).wait()
-            self.load([(self.r[f"m{i}"].at[pl.ds(0,n)],buf.at[0]),(self.near(i,"o"),buf.at[1])])
-            add_rows(self.r[k+"to"].at[idx],[buf.at[0],buf.at[1]])
+        def _(): self.outward_load(i)
+    def outward_send(self,i):
+        k,idx,n,b=self.parts_of(i); buf=self.r[k+"a"]
+        @pl.when(self.inner)
+        def _():
+            self.outward_load(i,False)
+            if i==3: self.ro(0).wait_send()
+            if i==5: self.ro(4).wait_send()
+            add_rows(self.r[k+"to"].at[idx%3 if k=="g" else 0],[buf.at[idx%2,0],buf.at[idx%2,1]])
             self.ro(i).start()
+    def stage1(self,*pieces):
+        for p,i in enumerate(pieces):
+            self.outward_load_start(i)
+            if p: self.outward_send(pieces[p-1])
+        self.outward_send(pieces[-1])
+    def sources(self,i):
+        b=self.L2[i]==1
+        return ([self.view(i,"i"),self.near(i,"i")]+([self.r[f"rin{i}"]] if b else []),
+                [self.r[f"ro{i}"]]+([self.near(i,"o")] if b else []))
+    def piece_load(self,i):
+        k,idx,n,b=self.parts_of(i); s=self.sources(i)
+        @pl.when(self.inner)
+        def _():
+            if (i,"i") in self.MID: self.across(self.MID.index((i,"i"))).wait()
+            if b: self.rin(self.RIN.index(i)).wait_recv()
+            self.load(s[0],k,idx%2,True)
+        @pl.when(self.outer)
+        def _():
+            self.ro(i).wait_recv()
+            self.load(s[1],k,idx%2,True)
+    def fin_of(self,i):
+        k,idx,n,b=self.parts_of(i)
+        return self.r[k+"fin"].at[idx%2 if k=="g" else 0]
     def piece(self,i):
         k,idx,n,b=self.parts_of(i)
-        slot=idx%2; buf=self.r[k+"a"]; fin=self.r[k+"fin"]
-        @pl.when(self.inner)
-        def _():
-            if b: self.rin((0,2,5).index(i)).wait_recv()
-            self.load([(self.r[f"m{i}"].at[pl.ds(n,n)],buf.at[0]),(self.near(i,"i"),buf.at[1])]+([(self.r[f"rin{i}"],buf.at[2])] if b else []))
-            add_rows(fin.at[slot],[buf.at[q] for q in range(3 if b else 2)])
-        @pl.when(self.outer)
-        def _():
-            self.ro(i).wait_recv()
-            self.load([(self.r[f"ro{i}"],buf.at[0])]+([(self.near(i,"o"),buf.at[1])] if b else []))
-            add_rows(fin.at[slot],[buf.at[q] for q in range(2 if b else 1)])
+        slot=idx%2; buf=self.r[k+"a"]; fin=self.fin_of(i); s=self.sources(i); hn=n//2
+        for who,src in ((self.inner,s[0]),(self.outer,s[1])):
+            @pl.when(who)
+            def _(src=src):
+                self.load(src,k,slot,False)
+                add_rows(fin,[buf.at[slot,q] for q in range(len(src))])
         self.swap(i).start()
-        hn=n//2
-        for cp in self.store(i,fin.at[slot,pl.ds(pl.multiple_of(self.c*hn,hn),hn)],self.c,False): cp.start()
+        for cp in self.store(i,fin.at[pl.ds(pl.multiple_of(self.c*hn,hn),hn)],self.c,False): cp.start()
     def swap(self,i):
         k,idx,n,b=self.parts_of(i); hn=n//2
-        return self.rcopy(self.r[k+"fin"].at[idx%2,pl.ds(pl.multiple_of((1-self.c)*hn,hn),hn)],self.r[k+"sw"].at[idx],self.r["s_w"].at[i],self.r["r_w"].at[i],peer(self.z,4))
+        return self.rcopy(self.fin_of(i).at[pl.ds(pl.multiple_of((1-self.c)*hn,hn),hn)],self.r[k+"sw"].at[idx],self.r["s_w"].at[i],self.r["r_w"].at[i],peer(self.z,4))
     def store(self,i,src,core,theirs):
         ex=2*core+self.L2[i]; k,idx,n,b=self.parts_of(i); slot=idx%2
         if k=="g":
             hc=self.FF//2; h=self.H[i]
-            return [pltpu.make_async_copy(src.at[:,pl.ds(t*hc,hc)],self.r[nm].at[ex,:,pl.ds(h*hc,hc)],self.r["so"].at[t] if theirs else self.r["st"].at[2*slot+t])
+            return [pltpu.make_async_copy(src.at[:,pl.ds(t*hc,hc)],self.r[nm].at[ex,:,pl.ds(h*hc,hc)],self.r["so"].at[i,t] if theirs else self.r["st"].at[2*slot+t])
                     for t,nm in enumerate(("gate","up"))]
-        return [pltpu.make_async_copy(src,self.r["down"].at[ex],self.r["so"].at[0] if theirs else self.r["st"].at[4+slot])]
+        return [pltpu.make_async_copy(src,self.r["down"].at[ex],self.r["so"].at[i,0] if theirs else self.r["st"].at[4+slot])]
     def other_half(self,i):
         k,idx,n,b=self.parts_of(i); hn=n//2
-        for cp in self.store(i,self.r[k+"fin"].at[idx%2,pl.ds(pl.multiple_of(self.c*hn,hn),hn)],self.c,False): cp.wait()
+        for cp in self.store(i,self.fin_of(i).at[pl.ds(pl.multiple_of(self.c*hn,hn),hn)],self.c,False): cp.wait()
         self.swap(i).wait()
-        cps=self.store(i,self.r[k+"sw"].at[idx],1-self.c,True)
-        for cp in cps: cp.start()
-        for cp in cps: cp.wait()
+        for cp in self.store(i,self.r[k+"sw"].at[idx],1-self.c,True): cp.start()
+    def stores_end(self):
+        for i in range(6):
+            k,idx,n,b=self.parts_of(i)
+            for cp in self.store(i,self.r[k+"sw"].at[idx],1-self.c,True): cp.wait()
     def zsem(self,nm,k): return self.r["s_z"+nm].at[k],self.r["r_z"+nm].at[k]
     def zc(self,nm,k):
         r=self.r; M=r["z"+nm]
@@ -361,35 +408,40 @@
         r=self.r
         return self.rcopy(r["fi"+nm],r["ag"+nm].at[kk-1],r["s_ag"+nm].at[kk-1],r["r_ag"+nm].at[kk-1],peer(self.z,kk))
     def z_out(self,nm):
-        r=self.r
+        r=self.r; SG,SD,Q=self.SG,self.SD,self.FF//4; nb=Q//128
+        def stores(kk):
+            a=xor4(self.e,kk); s=kk%2
+            cols=pl.ds(pl.multiple_of(a*Q,Q),Q)
+            return [pltpu.make_async_copy(r["og"].at[s,0],r["dgate"].at[:,cols],r["sz"].at[s,0]),
+                    pltpu.make_async_copy(r["og"].at[s,1],r["dup"].at[:,cols],r["sz"].at[s,1]),
+                    pltpu.make_async_copy(r["od"].at[s],r["ddown"].at[pl.ds(pl.multiple_of(a*SD,SD),SD),:],r["sz"].at[s,2])]
+        def store_a(kk,go):
+            a=xor4(self.e,kk); s=kk%2
+            cols=pl.ds(pl.multiple_of(jnp.minimum(a,2)*self.D,self.D),self.D)
+            one=pltpu.make_async_copy(r["oa"].at[s],r["dqkv"].at[:,cols],r["sz"].at[s,0])
+            if not go: one.wait(); return
+            pl.when(a<3)(lambda: one.start())
+            pl.when(a==3)(lambda: pltpu.make_async_copy(r["oa"].at[s],r["dwo"],r["sz"].at[s,0]).start())
+        def done(kk):
+            if nm=="a": store_a(kk,False)
+            else:
+                for cp in stores(kk): cp.wait()
         for kk in range(4):
             if kk: self.agc(nm,kk).wait()
-            a=xor4(self.e,kk)
+            if kk>=2: done(kk-2)
             src=r["fi"+nm] if kk==0 else r["ag"+nm].at[kk-1]
             if nm=="a":
-                oa=r["oa"].at[kk%2]
-                add_rows(oa,[src])
-                cols=pl.ds(pl.multiple_of(jnp.minimum(a,2)*self.D,self.D),self.D)
-                @pl.when(a<3)
-                def _():
-                    cp=pltpu.make_async_copy(oa,r["dqkv"].at[:,cols],r["st2"].at[0]); cp.start(); cp.wait()
-                @pl.when(a==3)
-                def _():
-                    cp=pltpu.make_async_copy(oa,r["dwo"],r["st2"].at[0]); cp.start(); cp.wait()
+                add_rows(r["oa"].at[kk%2],[src])
+                store_a(kk,True)
             else:
-                SG,SD,Q=self.SG,self.SD,self.FF//4; nb=Q//128
                 for t in range(2):
                     for b in range(nb):
-                        r["og"][t,:,b*128:(b+1)*128]=src[(t*nb+b)*SG:(t*nb+b+1)*SG,:].astype(f32)
+                        r["og"][kk%2,t,:,b*128:(b+1)*128]=src[(t*nb+b)*SG:(t*nb+b+1)*SG,:].astype(f32)
                 off=2*nb*SG
                 for b in range(self.D//128):
-                    r["od"][:,b*128:(b+1)*128]=src[off+b*SD:off+(b+1)*SD,:].astype(f32)
-                cols=pl.ds(pl.multiple_of(a*Q,Q),Q)
-                cps=[pltpu.make_async_copy(r["og"].at[0],r["dgate"].at[:,cols],r["st2"].at[0]),
-                     pltpu.make_async_copy(r["og"].at[1],r["dup"].at[:,cols],r["st2"].at[1]),
-                     pltpu.make_async_copy(r["od"],r["ddown"].at[pl.ds(pl.multiple_of(a*SD,SD),SD),:],r["st2"].at[2])]
-                for cp in cps: cp.start()
-                for cp in cps: cp.wait()
+                    r["od"][kk%2,:,b*128:(b+1)*128]=src[off+b*SD:off+(b+1)*SD,:].astype(f32)
+                for cp in stores(kk): cp.start()
+        done(2); done(3)
     def rows_of(self,core,zr):
         return pl.ds(pl.multiple_of(2*self.SG*shard_of(zr)+self.SG*core,self.SG),self.SG)
     def at_swap(self,GS):
@@ -401,7 +453,8 @@
         return self.rcopy(self.r["gn"].at[0] ,self.r["gn"].at[k+1],self.r["s_gn"].at[k],self.r["r_gn"].at[k],dev)
     def middle(self):
         self.z_across("b")
-        self.stage1(3)
+        self.across_start((3,4,5,6))
+        self.stage1(3,4)
     def finish(self,GS,gg):
         r=self.r; gn=r["gn"]
         sw=self.at_swap(GS)
@@ -410,65 +463,73 @@
         ld=pltpu.make_async_copy(r["fgg"],gn.at[7],r["st2"].at[1]); ld.start(); ld.wait()
         gn[0]=jnp.where(row==0,gg,jnp.where(row==1,gn[7],0.0))
         self.gcopy(0,peer(self.z,4)).start()
+        self.piece_load(0)
+        self.piece_load(1)
+        self.outward_load_start(5)
         self.piece(0)
         for cp in sw: cp.wait()
         for i in range(4):
             for zr in range(4):
                 add_rows(r["sv"].at[i,zr],[GS.at[i,self.rows_of(self.c,zr)],r["atr"].at[i,zr]])
         for kk in (1,2,3): self.at_xy(kk).start()
+        self.outward_send(5)
         self.gcopy(0,peer(self.z,4)).wait()
         gn[0]=gn[0]+gn[1]
         for kk in (1,2,3): self.gcopy(kk,peer(self.z,kk)).start()
         self.z_last("b")
         self.piece(1)
-        self.stage1(4)
         self.other_half(0)
+        self.piece_load(2)
+        self.other_half(1)
         self.piece(2)
-        self.other_half(1)
+        self.piece_load(3)
         for kk in (1,2,3): self.gcopy(kk,peer(self.z,kk)).wait()
         gn[0]=(gn[0]+gn[2])+(gn[3]+gn[4])
         @pl.when(self.outer)
         def _(): self.gcopy(4,peer(self.zi,0)).start()
+        self.z_out("b")
         for kk in (1,2,3): self.at_xy(kk).wait()
         for zr in range(4): add_rows(r["za"].at[zr],[r["sv"].at[self.e,zr]]+[r["xr"].at[k,zr] for k in range(3)])
         self.z_inward("a")
-        self.z_out("b")
         @pl.when(self.inner)
         def _():
             self.gcopy(4,peer(self.zo,0)).wait_recv()
             gn[0]=gn[0]+gn[5]
             self.gcopy(5,peer(self.zx,0)).start()
+        self.piece(3)
         self.z_across("a")
-        self.stage1(5)
-        self.piece(3)
+        self.other_half(2)
+        self.piece_load(4)
         @pl.when(self.inner)
         def _():
             self.gcopy(5,peer(self.zx,0)).wait()
             gn[0]=gn[0]+gn[6]
             self.gcopy(6,peer(self.zo,0)).start()
+        self.other_half(3)
+        self.z_last("a")
+        self.piece(4)
+        self.piece_load(5)
         @pl.when(self.outer)
         def _():
             self.gcopy(4,peer(self.zi,0)).wait_send()
             self.gcopy(6,peer(self.zi,0)).wait_recv()
             gn[0]=gn[7]
         gcp=pltpu.make_async_copy(gn.at[0],r["gains"],r["st2"].at[3]); gcp.start()
-        self.other_half(2)
-        self.z_last("a")
-        self.piece(4)
-        self.other_half(3)
+        self.other_half(4)
+        self.piece(5)
         self.z_out("a")
-        self.piece(5)
-        self.other_half(4); self.other_half(5)
+        self.other_half(5)
+        self.stores_end()
         gcp.wait()
         @pl.when(self.inner)
         def _():
             self.gcopy(6,peer(self.zo,0)).wait_send()
-            for i in range(6): self.ro(i).wait_send()
+            for i in (1,2,3,5): self.ro(i).wait_send()
             self.zc("a",3).wait_send(); self.zc("b",3).wait_send()
         @pl.when(self.outer)
         def _():
             for k in range(3): self.rin(k).wait_send()
-        home_run(r["hown"],r["hext"],r["ra"],self.home,False)
+        self.rows_home(False)
         for cp in plane_copies([(r["rbs"],r["rb"])],self.plane): cp.wait()
 
 f32=jnp.float32; bf16=jnp.bfloat16
@@ -581,10 +642,10 @@
             ni,no=len(tail.in_specs),len(tail.out_specs)
             tgo,ggo=rest[ni:ni+2]
             tins,touts=rest[:ni],rest[ni+2:ni+2+no]
-            normed,normedT,bg,bias,dO,kT,PB,DS,dv,dk,dqT,drow,acc,GS,*tscr=rest[ni+2+no:]
+            normedT,bg,bias,dO,kT,PB,DS,dv,dk,dqT,drow,acc,GS,*tscr=rest[ni+2+no:]
             tail.bind(tins,touts,tscr)
         else:
-            tgo,ggo,gq,gk,gv,gwo,normed,normedT,bg,bias,dO,kT,PB,DS,dv,dk,dqT,drow,acc=rest
+            tgo,ggo,gq,gk,gv,gwo,normedT,bg,bias,dO,kT,PB,DS,dv,dk,dqT,drow,acc=rest
         g=pl.program_id(0)
         if fast:
             @pl.when(g==0)
@@ -603,7 +664,7 @@
                 bg[r,:]=sg[r,:].astype(bf16)
                 j=lax.broadcasted_iota(jnp.int32,(T,QC),0)
                 i=lax.broadcasted_iota(jnp.int32,(T,QC),1)+c*QC
-                bias[c]=jnp.where((j<=i)|(j<pre[0]),0.0,-1e30)
+                bias[c]=jnp.where((j<=i)|(j<pre[0]),0.0,-1e30).astype(bf16)
         hmask=(lax.broadcasted_iota(jnp.int32,(8,GW),0)==lane_head((8,GW))).astype(f32)
         for c in range(nq):
             r=slice(c*QC,(c+1)*QC)
@@ -627,7 +688,7 @@
                 r=slice(c*QC,(c+1)*QC)
                 qm=jnp.where(lh==h,qr[r,:],zero)
                 dOm=jnp.where(lh==h,dO[r,:],zero)
-                st=nt(kr[...],qm)+bias[c]
+                st=nt(kr[...],qm)+bias[c].astype(f32)
                 p=jnp.exp(st-lser[0,pl.ds(h,1),r])
                 PB[:,r]=p.astype(bf16)
                 dp=nt(vr[...],dOm)
@@ -684,7 +745,7 @@
       in_specs=[pl.BlockSpec(memory_space=pltpu.SMEM)]+[full((T,D)),full((T,D)),full((1,D)),col(0),col(ng),col(2*ng),rowb,full((T,128)),full((T,128)),tcol,tcol,tcol,tcol,pl.BlockSpec((1,8,T),lambda g:(g,0,0))]+(tail.in_specs if fast else []),
       out_specs=[full((T,D)),full((8,D))]+outs,
       out_shape=[jax.ShapeDtypeStruct((T,D),bf16),jax.ShapeDtypeStruct((8,D),f32)]+oshape,
-      scratch_shapes=[pltpu.VMEM((T,D),bf16),pltpu.VMEM((D,T),bf16),pltpu.VMEM((T,D),bf16),pltpu.VMEM((nq,T,QC),f32),pltpu.VMEM((T,GW),bf16),pltpu.VMEM((GW,T),bf16),
+      scratch_shapes=[pltpu.VMEM((D,T),bf16),pltpu.VMEM((T,D),bf16),pltpu.VMEM((nq,T,QC),bf16),pltpu.VMEM((T,GW),bf16),pltpu.VMEM((GW,T),bf16),
         pltpu.VMEM((T,T),bf16),pltpu.VMEM((T,T),bf16),pltpu.VMEM((T,GW),f32),pltpu.VMEM((T,GW),f32),pltpu.VMEM((GW,T),f32),pltpu.VMEM((8,T),f32),pltpu.VMEM((T,D),f32)]+extra,
       compiler_params=pltpu.CompilerParams(vmem_limit_bytes=63<<20,dimension_semantics=("arbitrary",),**(dict(collective_id=5,has_side_effects=True) if fast else {})),
       cost_estimate=pl.CostEstimate(flops=2*T*D*8*D+10*T*T*D,bytes_accessed=24<<20,transcendentals=12*T*T),
@@ -762,11 +823,11 @@
     H[rows,:]=h; GB[rows,:]=gb; UB[rows,:]=ub
     return nn(h,wd),nt(gb,wg)+nt(ub,wu)
 
-def expert_ffn(deps, l2, xs, ss, wg, wu, wd, f0, nf, prev=(), carry=None, dense=None, inw=None, cid=None, FB=512, chunk=480):
+def expert_ffn(deps, l2, xs, ss, wg, wu, wd, f0, nf, prev=(), carry=None, dense=None, inw=None, ext=None, gprev=None, cid=None, FB=512, chunk=480):
     n=len(xs); RG,D=xs[0].shape; FF=wg.shape[2]; R=n*RG; HB=2*FB; ng=nf//2
     SR=D//4; np_=len(prev); nc=0 if carry is None else 1; nd=0 if dense is None else 1
     part=pl.ds(dense[1],dense[2]) if nd else None
-    nx=len(deps); nz=0 if inw is None else 2
+    nx=len(deps); nz=0 if inw is None else 2; ne=0 if ext is None else 1; ngp=0 if gprev is None else 6*ng+ng
     def kernel(*refs):
         refs=refs[nx:]
         xr=refs[:n]; sr=refs[n:2*n]; wgr,wur,wdr=refs[2*n:2*n+3]; o=2*n+3
@@ -774,24 +835,29 @@
         csrc=refs[o:o+nc]; o+=nc
         dsrc=refs[o:o+nd]; o+=nd
         zsrc=refs[o:o+nz]; o+=nz
+        esrc=refs[o:o+ne]; o+=ne
+        gp=refs[o:o+ngp]; o+=ngp
         res=refs[o:o+n]; dgr=refs[o+n:o+2*n]; o+=2*n
         gus=[refs[o+3*q:o+3*q+3] for q in range(ng)]; o+=3*ng
         dws=refs[o:o+ng]; o+=ng
         cdst=refs[o:o+nc]; o+=nc
         ddst=refs[o:o+nd]; o+=nd
         zdst=refs[o:o+nz//2]; o+=nz//2
+        edst=refs[o:o+ne]; o+=ne
         XT,XN,H,GB,UB,AR,AD=refs[o:o+7]; sems=refs[o+7:]
         f=pl.program_id(0)
         def copies():
-            return (plane_copies([(csrc[0],cdst[0])],sems[2*nd+nz:]) if nc else [])+(row_copies(dsrc[0],ddst[0],part,sems[nz:nz+2]) if nd else [])
+            return (plane_copies([(csrc[0],cdst[0])],sems[2*nd+nz+2*ne:]) if nc else [])+(row_copies(dsrc[0],ddst[0],part,sems[nz+2*ne:nz+2*ne+2]) if nd else [])
         if nc or nd or nz:
             @pl.when(f==0)
             def _():
                 if nz:
-                    plane_z_barrier()
+                    if ne: home_barrier()
+                    else: plane_z_barrier()
                     inward_run(zsrc,zdst[0],sems[:2],True)
                 else:
                     plane_barrier()
+                if ne: ext_run(esrc[0],edst[0],sems[nz:nz+2],True)
                 for cpy in copies(): cpy.start()
         @pl.when(f==0)
         def _():
@@ -824,20 +890,22 @@
             for b in range(R//chunk):
                 p=nn(XT[b],Y[b*chunk:(b+1)*chunk,:])
                 gv=p if gv is None else gv+p
-            gv=gv.astype(bf16)
             cols=pl.ds(pl.multiple_of(t*HB+lax.rem(f,2)*FB,FB),FB)
             for q in range(ng):
-                def put(gf=gus[q][0],gi=gus[q][1],go=gus[q][2],gv=gv,cols=cols):
-                    gf[:,cols]=gv[0:2*SR]; gi[:,cols]=gv[2*SR:3*SR]; go[:,cols]=gv[3*SR:4*SR]
+                def put(q=q,t=t,gv=gv,cols=cols):
+                    for s,(ref,lo,hi) in enumerate(zip(gus[q],(0,2*SR,3*SR),(2*SR,3*SR,4*SR))):
+                        v=gv[lo:hi]
+                        if ngp: v=v+gp[6*q+3*t+s][...].astype(f32)
+                        ref[:,cols]=v.astype(bf16)
                 if ng==1: put()
                 else: pl.when(lax.div(f,2)==q)(put)
         dv=None
         for a in range(n):
             t=tn(H[a*RG:(a+1)*RG,:],sr[a][...])
             dv=t if dv is None else dv+t
-        dv=dv.astype(bf16)
         for q in range(ng):
-            def put(dw=dws[q],dv=dv): dw[...]=dv
+            def put(q=q,dv=dv):
+                dws[q][...]=((dv+gp[6*ng+q][...].astype(f32)) if ngp else dv).astype(bf16)
             if ng==1: put()
             else: pl.when(lax.div(f,2)==q)(put)
         if nc or nd or nz:
@@ -845,6 +913,7 @@
             def _():
                 for cpy in copies(): cpy.wait()
                 if nz: inward_run(zsrc,zdst[0],sems[:2],False)
+                if ne: ext_run(esrc[0],edst[0],sems[nz:nz+2],False)
     one=pl.Buffered(1)
     rowspec=pl.BlockSpec((RG,D),lambda f:(0,0),pipeline_mode=one)
     wspec=pl.BlockSpec((1,D,FB),lambda f:(2*spot()[0]+l2,0,f+f0))
@@ -853,14 +922,22 @@
     anyspec=pl.BlockSpec(memory_space=pl.ANY)
     wspecs=[pl.BlockSpec((FB,D),lambda f: ((1-f) if f0 else f,0))] if ng==1 else [
         pl.BlockSpec((FB,D),lambda f: (jnp.minimum(f,1),0)),pl.BlockSpec((FB,D),lambda f: (jnp.minimum(3-f,1),0))]
+    gpspecs=[]; gpargs=[]
+    if ngp:
+        for q in range(ng):
+            for t in range(2):
+                for s,rr in enumerate((2*SR,SR,SR)):
+                    gpspecs.append(pl.BlockSpec((rr,FB),lambda f,q=q,t=t: (0,2*t+jnp.clip(f-2*q,0,1))))
+                    gpargs.append(gprev[q][s])
+        gpspecs+=wspecs; gpargs+=list(gprev[ng:])
     out=pl.pallas_call(kernel,grid=(nf,),
-        in_specs=[anyspec]*nx+[rowspec]*(2*n)+[wspec,wspec,wdspec]+[rowspec]*np_+[anyspec]*(nc+nd+nz),
-        out_specs=[rowspec]*(2*n)+[full(2*SR,2*HB),full(SR,2*HB),full(SR,2*HB)]*ng+wspecs+[anyspec]*(nc+nd+nz//2),
-        scratch_shapes=[pltpu.VMEM((R//chunk,D,chunk),bf16),pltpu.VMEM((D,chunk),bf16)]+[pltpu.VMEM((R,FB),bf16)]*3+[pltpu.VMEM((R,D),f32)]*2+([pltpu.SemaphoreType.DMA((1,)),pltpu.SemaphoreType.DMA((1,))] if nz else [])+(row_sems() if nd else [])+(plane_sems(1) if nc else []),
-      out_shape=[jax.ShapeDtypeStruct((RG,D),bf16)]*(2*n)+([jax.ShapeDtypeStruct((2*SR,2*HB),bf16)]+[jax.ShapeDtypeStruct((SR,2*HB),bf16)]*2)*ng+[jax.ShapeDtypeStruct((HB,D),bf16)]*ng+[jax.ShapeDtypeStruct((8,RG//8,D),bf16)]*nc+([jax.ShapeDtypeStruct((3,dense[2])+dense[0].shape[2:],bf16)] if nd else [])+([jax.ShapeDtypeStruct(inw[0].shape,bf16)] if nz else []),
+        in_specs=[anyspec]*nx+[rowspec]*(2*n)+[wspec,wspec,wdspec]+[rowspec]*np_+[anyspec]*(nc+nd+nz+ne)+gpspecs,
+        out_specs=[rowspec]*(2*n)+[full(2*SR,2*HB),full(SR,2*HB),full(SR,2*HB)]*ng+wspecs+[anyspec]*(nc+nd+nz//2+ne),
+        scratch_shapes=[pltpu.VMEM((R//chunk,D,chunk),bf16),pltpu.VMEM((D,chunk),bf16)]+[pltpu.VMEM((R,FB),bf16)]*3+[pltpu.VMEM((R,D),f32)]*2+([pltpu.SemaphoreType.DMA((1,)),pltpu.SemaphoreType.DMA((1,))] if nz else [])+(ext_sems() if ne else [])+(row_sems() if nd else [])+(plane_sems(1) if nc else []),
+      out_shape=[jax.ShapeDtypeStruct((RG,D),bf16)]*(2*n)+([jax.ShapeDtypeStruct((2*SR,2*HB),bf16)]+[jax.ShapeDtypeStruct((SR,2*HB),bf16)]*2)*ng+[jax.ShapeDtypeStruct((HB,D),bf16)]*ng+[jax.ShapeDtypeStruct((8,RG//8,D),bf16)]*nc+([jax.ShapeDtypeStruct((3,dense[2])+dense[0].shape[2:],bf16)] if nd else [])+([jax.ShapeDtypeStruct(inw[0].shape,bf16)] if nz else [])+([jax.ShapeDtypeStruct(ext.shape,bf16)] if ne else []),
       compiler_params=pltpu.CompilerParams(vmem_limit_bytes=62<<20,dimension_semantics=("arbitrary",),**(dict(collective_id=cid,has_side_effects=True) if nc or nd or nz else {})),
       cost_estimate=pl.CostEstimate(flops=9*R*D*FF*ng,bytes_accessed=3*D*FF*2*ng+4*R*D*2,transcendentals=R*FF*ng//2),
-      name=f"expert_ffn{n}_{f0}")(*deps,*xs,*ss,wg,wu,wd,*prev,*([carry] if nc else []),*([dense[0]] if nd else []),*(inw if nz else ()))
+      name=f"expert_ffn{n}_{f0}")(*deps,*xs,*ss,wg,wu,wd,*prev,*([carry] if nc else []),*([dense[0]] if nd else []),*(inw if nz else ()),*([ext] if ne else []),*gpargs)
     o=2*n
     return (out[:o],*[out[o+3*q:o+3*q+3] for q in range(ng)],*out[o+3*ng:])
 
@@ -1026,26 +1103,35 @@
       compiler_params=pltpu.CompilerParams(vmem_limit_bytes=50<<20),
       cost_estimate=pl.CostEstimate(flops=4*S*parts*T*D,bytes_accessed=9<<20,transcendentals=0),name="combine")(cols,gates,*ret,state,shared)
 
-def mid_bwd_home(deps, inw, cols, own, ext, back_b, dsh, state, fgain, cot):
+def mid_bwd_home(deps, inw, dsum, rext, cols, own, ext, back_b, dsh, state, fgain, cot):
     T,D=state.shape; S=8*CAP; nx=len(deps)
     def kernel(*refs):
         body(*refs[nx:])
-    def body(z0,z1,colr,hown,hext,bb,ds,st,fg,ct,sgo,fgo,ba,zd,BV,cs,zs0,zs1,*hsems):
+    def body(z0,z1,dsrc,rsrc,colr,hown,hext,bb,ds,st,fg,ct,sgo,fgo,ba,zd,dd,rd,BV,cs,zs0,zs1,rs0,rs1,es0,es1,*osems):
         home_barrier()
-        home_run(hown,hext,ba,hsems,True)
+        own_run(hown,ba,osems,True)
+        ext_run(rsrc,rd,(es0,es1),True)
         inward_run((z0,z1),zd,(zs0,zs1),True)
+        rows=lambda: row_copies(dsrc,dd,pl.ds(3,1),(rs0,rs1))
+        for cp in rows(): cp.start()
         fgo[...]=jnp.zeros_like(fgo)
-        home_run(hown,hext,ba,hsems,False)
-        cps=[pltpu.make_async_copy(ba.at[i],BV.at[i],cs.at[i]) for i in range(8)]
-        for cp in cps: cp.start()
-        for cp in cps: cp.wait()
         @pl.loop(0,T//QC)
         def _(i):
             r=pl.ds(pl.multiple_of(i*QC,QC),QC)
-            n=ds[r,:]
             si=lax.broadcasted_iota(jnp.int32,(QC,S),1)+S
             d=jnp.where((si==colr[r,0:1])|(si==colr[r,1:2]),1.0,0.0).astype(bf16)
-            n=n+nn(d,bb[...])
+            sgo[r,:]=ds[r,:]+nn(d,bb[...])
+        own_run(hown,ba,osems,False)
+        def fetch(src):
+            cps=[pltpu.make_async_copy(src.at[i],BV.at[i],cs.at[i]) for i in range(8)]
+            for cp in cps: cp.start()
+            for cp in cps: cp.wait()
+        pl.when(is_inner())(lambda: fetch(ba))
+        pl.when(jnp.logical_not(is_inner()))(lambda: fetch(hext))
+        @pl.loop(0,T//QC)
+        def _(i):
+            r=pl.ds(pl.multiple_of(i*QC,QC),QC)
+            n=sgo[r,:]
             for b in range(8):
                 si=lax.broadcasted_iota(jnp.int32,(QC,128),1)
                 si=jnp.where(si<CAP,si+b*CAP,-1)
@@ -1056,12 +1142,15 @@
             w=n*fg[...]
             sgo[r,:]=ct[r,:].astype(f32)+inv*(w-u*jnp.mean(w*u,axis=1,keepdims=True))
         inward_run((z0,z1),zd,(zs0,zs1),False)
+        for cp in rows(): cp.wait()
+        ext_run(rsrc,rd,(es0,es1),False)
     vm=pl.BlockSpec(memory_space=pltpu.VMEM); an=pl.BlockSpec(memory_space=pl.ANY)
-    return pl.pallas_call(kernel,in_specs=[an]*(nx+2)+[vm,an,an]+[vm]*5,out_specs=[vm]*2+[an]*2,
-      out_shape=[jax.ShapeDtypeStruct((T,D),f32),jax.ShapeDtypeStruct((8,D),f32),jax.ShapeDtypeStruct((8,CAP,D),bf16),jax.ShapeDtypeStruct(inw[0].shape,bf16)],
-      scratch_shapes=[pltpu.VMEM((8,CAP,D),bf16),pltpu.SemaphoreType.DMA((8,))]+[pltpu.SemaphoreType.DMA((1,))]*2+home_sems(),
+    SD=jax.ShapeDtypeStruct
+    return pl.pallas_call(kernel,in_specs=[an]*(nx+4)+[vm,an,an]+[vm]*5,out_specs=[vm]*2+[an]*4,
+      out_shape=[SD((T,D),f32),SD((8,D),f32),SD((8,CAP,D),bf16),SD(inw[0].shape,bf16),SD((3,1)+dsum.shape[2:],bf16),SD((8,CAP,D),bf16)],
+      scratch_shapes=[pltpu.VMEM((8,CAP,D),bf16),pltpu.SemaphoreType.DMA((8,))]+[pltpu.SemaphoreType.DMA((1,))]*2+row_sems()+ext_sems()+plane_sems(1),
       compiler_params=pltpu.CompilerParams(vmem_limit_bytes=50<<20,collective_id=4,has_side_effects=True),
-      cost_estimate=pl.CostEstimate(flops=4*S*T*D,bytes_accessed=12<<20,transcendentals=0),name="mid_bwd")(*deps,*inw,cols,own,ext,back_b,dsh,state,fgain[None],cot)
+      cost_estimate=pl.CostEstimate(flops=4*S*T*D,bytes_accessed=12<<20,transcendentals=0),name="mid_bwd")(*deps,*inw,dsum,rext,cols,own,ext,back_b,dsh,state,fgain[None],cot)
 
 def mid_bwd(cols, back, dsh, state, fgain, cot):
     parts=len(back); T,D=state.shape; S=back[0].shape[0]
@@ -1090,12 +1179,12 @@
 
 
 def rope_wide(length):
-    positions = jnp.arange(length, dtype=f32)
-    frequency = 10000.0 ** (-jnp.arange(HEAD_DIM // 2, dtype=f32) * 2.0 / HEAD_DIM)
-    angles = positions[:, None] * frequency[None, :]
-    c = jnp.cos(angles)
-    s = jnp.sin(angles)
-    return jnp.concatenate([c, c, c, c], axis=1), jnp.concatenate([-s, s, -s, s], axis=1)
+    positions = np.arange(length, dtype=np.float32)
+    frequency = (10000.0 ** (-np.arange(HEAD_DIM // 2) * 2.0 / HEAD_DIM)).astype(np.float32)
+    angles = (positions[:, None] * frequency[None, :]).astype(np.float64)
+    c = np.cos(angles).astype(np.float32)
+    s = np.sin(angles).astype(np.float32)
+    return np.concatenate([c, c, c, c], axis=1), np.concatenate([-s, s, -s, s], axis=1)
 
 
 def shards_any(tokens, cotangent, expert_ids, route_gates, slot_order, prefix_len, attention_gain, qkv_weight,
@@ -1248,25 +1337,27 @@
     dsum = add(sh0, swap(sh1))
     (rb, db), gb0, gb1, wb0, wb1, xx = expert_ffn([], 1, [flat(xb)], [flat(sb)], *ws, 0, 4, inw=(xa, xa), cid=6)
     sa, sx, xa, xx = flat(sa), flat(sx), flat(xa), flat(xx)
-    p0, ga0, wa0, db, r0, rf0 = expert_ffn([], 0, [xa, xx], [sa, sx], *ws, 0, 2, carry=blocks(db), dense=(dsum, 0, 1),
-                                           inw=(gb0[0], gb0[0]), cid=2)
+    (rx, dx), gx0, gx1, wx0, wx1, db, r0, rf0 = expert_ffn([], 0, [xx], [sx], *ws, 0, 4, carry=blocks(db), dense=(dsum, 0, 1),
+                                                           inw=(gb0[0], gb0[0]), cid=2)
     bs0 = add(gb0[0], rf0)
     m_b0 = across(bs0)
-    m_a0 = across(ga0[0])
-    (ra, rx, da, dx), ga1, wa1, r1, rf1 = expert_ffn([bs0], 0, [xa, xx], [sa, sx], *ws, 2, 2, p0, dense=(dsum, 1, 3),
-                                                     inw=(gb1[0], gb1[0]), cid=3)
+    (ra, da), ga0, ga1, wa0, wa1, r1, rf1, dxl = expert_ffn([bs0], 0, [xa], [sa], *ws, 0, 4, dense=(dsum, 1, 2),
+                                                            inw=(gb1[0], gb1[0]), ext=blocks(dx),
+                                                            gprev=(gx0, gx1, wx0, wx1), cid=3)
     bs1 = add(gb1[0], rf1)
     m_b1 = across(bs1)
-    sgrad, fgg, _, rf2 = mid_bwd_home([bs1], (wb1, wb0), cols, blocks(da), blocks(dx), flat(db), dshared, state,
-                                      feedforward_gain, cotangent)
+    m_a0o = across(ga0[0][:D // 4])
+    sgrad, fgg, _, rf2, r2, rxl = mid_bwd_home([bs1], (wb1, wb0), dsum, blocks(rx), cols, blocks(da), dxl, flat(db), dshared,
+                                               state, feedforward_gain, cotangent)
     bs2 = add(jnp.where(low, wb1, wb0), rf2)
     mine = lax.dynamic_index_in_dim(dsum, ei, 0, keepdims=False)
-    msh = jnp.concatenate([add(mine[:1], r0[0], r0[1], r0[2]), add(mine[1:], r1[0], r1[1], r1[2])])
+    got = jnp.concatenate([r0, r1, r2], axis=1)
+    msh = add(mine, got[0], got[1], got[2])
     carried = {
-        "hown": blocks(ra), "hext": blocks(rx), "rbs": blocks(rb), "fgg": fgg, "msh": msh,
+        "hown": blocks(ra), "rxl": rxl, "rbs": blocks(rb), "fgg": fgg, "msh": msh,
         "m0": m_b0, "ni0": gb0[1], "no0": gb0[2],
-        "m1": m_a0, "ni1": ga0[1], "no1": ga0[2],
-        "m2": m_b1, "ni2": gb1[1], "no2": gb1[2],
+        "m1": m_b1, "m2o": m_a0o, "ni1": gb1[1], "no1": gb1[2],
+        "far2": ga0[0], "ni2": ga0[1], "no2": ga0[2],
         "far3": ga1[0], "ni3": ga1[1], "no3": ga1[2],
         "wa0": wa0, "wa1": wa1, "wb0": wb0, "wb1": wb1,
         "far5": bs2,

time: 548 us -> 523 us (0.954)
  Pallas kernels: 494 us -> 463 us
    pallas_call x1, Pallas kernels: 193 us -> 161 us  [attn_bwd(): pl.pallas_call(kernel, grid=(ng,), in_specs=[pl.BlockSpec(memory_space=pl...]
    pallas_call x3, Pallas kernels: 144 us -> 153 us  [expert_ffn(): pl.pallas_call(kernel, grid=(nf,), in_specs=[anyspec] * nx + [rowspec] *...]
    pallas_call x1, Pallas kernels: 51 us -> 42.7 us  [mid_bwd_home(): pl.pallas_call(kernel, in_specs=[an] * (nx + 4) + [vm, an, an] + [vm] * 5...]
    unnamed x60 -> x54, local copies, waits for them, and re-layouts: 10.2 us -> 12.4 us
  transfers between devices with their start and end apart: 4 -> 4, of which waited for: 0 -> 0; matrix products, arithmetic and copies ran while one was open for 2% -> 2% of each run, Pallas kernels for 28% -> 29%
where the time goes in v5:
time: 523 us; the launch traced here: 514 us
  Pallas kernels  463 us (89%)
  other arithmetic  27.1 us (5%)
  local copies, waits for them, and re-layouts  16.5 us (3%)
  starting transfers between devices  5.85 us (1%)
    pallas_call x1, Pallas kernels, attn_bwd(): pl.pallas_call(kernel, grid=(ng,), in_specs=[pl.BlockSpec(memory_space=pl...  161 us
    pallas_call x3, Pallas kernels, expert_ffn(): pl.pallas_call(kernel, grid=(nf,), in_specs=[anyspec] * nx + [rowspec] *...  153 us
    pallas_call x1, Pallas kernels, shared_ffn(): pl.pallas_call(kernel, grid=(nf,), in_specs=[full((T, D)), full((T, D)),...  44.4 us
    pallas_call x1, Pallas kernels, mid_bwd_home(): pl.pallas_call(kernel, in_specs=[an] * (nx + 4) + [vm, an, an] + [vm] * 5...  42.7 us
    pallas_call x1, Pallas kernels, attn_fwd(): pl.pallas_call(kernel, grid=(ng,), in_specs=[pl.BlockSpec(memory_space=pl...  42.7 us
    convert_element_type x4, other arithmetic, add(): return t.astype(bf16)  16.7 us
    unnamed x54, local copies, waits for them, and re-layouts  12.4 us
  transfers between devices with their start and end apart: 4, of which 0 were waited for; matrix products, arithmetic and copies ran while one was open for 2% of the time, Pallas kernels for 29%

profile of v5, /device:TPU:0, one launch (start us, length us, event | category | flops | bytes accessed | tf_op | source)
XLA Modules:
  0.0 514.0 jit_solution(8965765075007851062)
XLA Ops:
  0.6 0.9 copy.31.gts.g
  1.5 0.9 copy.30.ids
  2.4 1.3 broadcast_in_dim.12.ag
  3.7 1.3 broadcast_in_dim.13.fg.refs_11_
  5.6 0.0 copy-start
  5.6 1.3 copy-done
  6.9 0.7 copy-done.6
  7.6 9.7 %route.1 = (s32[8,768]{1,0:T(8,128)S(1)}, s32[768,8]{1,0:T(8,128)S(1)}, bf16[1920,768]{1,0:T(8,128)(2,1)}) custom-call(s32[1]{0:T(128)} %bitcast.core_ref, s32[1,1536]{1,0:T(1,128)S(1)} %copy-done.6, s32[768,2]{1,0:T(8,128)S(1)} %copy.30.ids, f32[768,2]{1,0:T(8,128)S(1)} %copy.31.gts.g, bf16[768,768]{1,0:T(8,128)(2,1)S(1)} %copy-done), custom_call_target="tpu_custom_call" | custom-call | flops 4680843264 | bytes 8388608 | tf_op jit(solution)/shard_map/route/pallas_call | solution.py:1061
  17.2 0.6 copy-done.7
  17.8 42.7 %attn_fwd.1 = (bf16[768,768]{1,0:T(8,128)(2,1)}, bf16[768,768]{1,0:T(8,128)(2,1)}, bf16[768,768]{1,0:T(8,128)(2,1)}, bf16[768,768]{1,0:T(8,128)(2,1)}, f32[3,8,7...) custom-call(s32[1]{0:T(128)S(6)} %copy.41.pre, ...), custom_call_target="tpu_custom_call" | custom-call | flops 5435817984 | bytes 16777216 | tf_op jit(solution)/shard_map/attn_fwd/pallas_call | solution.py:627
  60.5 44.4 %shared_ffn.1 = (f32[768,768]{1,0:T(8,128)}, f32[768,768]{1,0:T(8,128)}, bf16[4,4,1152,128]{3,2,1,0:T(8,128)(2,1)}, bf16[4,4,1152,128]{3,2,1,0:T(8,128)(2,1)}, b...) custom-call(bf16[768,768]{1,0:T(8,128)(2,1)} %get-tuple-element.89.xr, ...), custom_call_target="tpu_custom_call" | custom-call | flops 21743271936 | bytes 28311552 | tf_op jit(solution)/shard_map/shared_ffn/pallas_call | solution.py:992
  104.9 0.5 collective-permute-start
  105.4 46.9 %expert_ffn1_0.3 = (bf16[960,768]{1,0:T(8,128)(2,1)}, bf16[960,768]{1,0:T(8,128)(2,1)}, bf16[384,2048]{1,0:T(8,128)(2,1)}, bf16[192,2048]{1,0:T(8,128)(2,1)}, bf...) custom-call(bf16[960,768]{1,0:T(8,128)(2,1)} %bitcast.37, ...), custom_call_target="tpu_custom_call" | custom-call | flops 27179089920 | bytes 24772608 | tf_op jit(solution)/shard_map/expert_ffn1_0/pallas_call | solution.py:933
  152.4 7.1 %add_convert_fusion.refs_6_.refs_3_ = bf16[4,4,1152,128]{3,2,1,0:T(8,128)(2,1)} fusion(bf16[4,4,1152,128]{3,2,1,0:T(8,128)(2,1)} %collective-permute-done, bf16[4,4,1152,128]{3,2,1,0:T(8,128)(2,1)} %get-tuple-element.100), kind=kLoop, calls=%fused_computation | loop fusion | flops 9437184 | bytes 14155776 | tf_op jit(solution)/shard_map/convert_element_type | solution.py:1325
  159.5 47.0 %expert_ffn1_0.4 = (bf16[960,768]{1,0:T(8,128)(2,1)}, bf16[960,768]{1,0:T(8,128)(2,1)}, bf16[384,2048]{1,0:T(8,128)(2,1)}, bf16[192,2048]{1,0:T(8,128)(2,1)}, bf...) custom-call(bf16[960,768]{1,0:T(8,128)(2,1)} %bitcast.40, ...), custom_call_target="tpu_custom_call" | custom-call | flops 27179089920 | bytes 24772608 | tf_op jit(solution)/shard_map/expert_ffn1_0/pallas_call | solution.py:933
  206.5 3.7 add_convert_fusion.3.refs_0_
  210.2 1.8 collective-permute-start.1
  212.0 59.4 %expert_ffn1_0.5 = (bf16[960,768]{1,0:T(8,128)(2,1)}, bf16[960,768]{1,0:T(8,128)(2,1)}, bf16[384,2048]{1,0:T(8,128)(2,1)}, bf16[192,2048]{1,0:T(8,128)(2,1)}, bf...) custom-call(bf16[384,2048]{1,0:T(8,128)(2,1)} %add_convert_fusion.3., ...), custom_call_target="tpu_custom_call" | custom-call | flops 27179089920 | bytes 24772608 | tf_op jit(solution)/shard_map/expert_ffn1_0/pallas_call | solution.py:933
  271.5 2.6 add_convert_fusion.2.refs_0_
  274.1 0.0 copy-start.10
  274.1 0.0 copy-start.3
  274.2 0.1 constant_dynamic-update-slice_fusion.2
  274.2 1.9 collective-permute-start.2
  276.1 0.2 copy-done.11
  276.4 0.1 slice.21
  276.4 1.6 collective-permute-start.3
  278.0 42.7 %mid_bwd.1 = (f32[768,768]{1,0:T(8,128)}, f32[8,768]{1,0:T(8,128)S(1)}, bf16[8,120,768]{2,1,0:T(8,128)(2,1)}, bf16[1024,768]{1,0:T(8,128)(2,1)}, bf16[3,1,1152,1...) custom-call(bf16[384,2048]{1,0:T(8,128)(2,1)} %copy-done.10, bf16[1024,768]{1,0:T(8,128)(2,1)} %get-tuple-element.113.refs_1_.rest_21_, ...), custom_call_target="tpu_custom_call" | custom-call | flops 2264924160 | bytes 12582912 | tf_op jit(solution)/shard_map/mid_bwd/pallas_call | solution.py:1149
  320.8 0.2 constant_dynamic-update-slice_fusion.1
  321.0 0.4 copy-done.2
  321.4 0.8 copy-done.8
  322.2 0.5 copy-done.9
  322.7 3.2 add_convert_fusion.1.rest_22_
  325.9 0.1 constant_dynamic-update-slice_fusion
  326.0 2.9 fusion.rest_4_
  328.9 160.8 %attn_bwd.1 = (bf16[768,768]{1,0:T(8,128)(2,1)}, f32[8,768]{1,0:T(8,128)}, bf16[4,96,2048]{2,1,0:T(8,128)(2,1)}, bf16[4,96,2048]{2,1,0:T(8,128)(2,1)}, bf16[4,25...) custom-call(s32[1]{0:T(128)S(6)} %copy.41.pre, ...), custom_call_target="tpu_custom_call" | custom-call | flops 11777605632 | bytes 25165824 | tf_op jit(solution)/shard_map/attn_bwd/pallas_call | solution.py:744
  489.8 3.6 convert_element_type.78
  493.3 2.0 convert_element_type.79
  495.4 1.9 convert_element_type.80
  497.3 0.9 constant_dynamic-slice_fusion
  498.2 0.5 slice_bitcast_fusion
  498.7 9.0 %combine.1 = bf16[768,768]{1,0:T(8,128)(2,1)} custom-call(s32[768,8]{1,0:T(8,128)S(1)} %get-tuple-element.86.refs_5_.colr, f32[768,2]{1,0:T(8,128)S(1)} %copy.31.gts.g, bf16[960,768]{1,0:T(8,128)(2,1)S(1)} %bitcast.24, bf16[960,768]{1,0:T(8,128)(2,1)S(1)} %bitcast.25, f32[768,768]{1,0:T(8,128)} %get-tuple-element.120.refs_10_.refs_2_, ...), custom_call_target="tpu_custom_call" | custom-call | flops 4529848320 | bytes 9437184 | tf_op jit(solution)/shard_map/combine/pallas_call | solution.py:1102
  507.7 1.0 copy.42
  508.8 0.6 copy-done.16
  509.3 0.9 copy.43
  510.3 0.7 copy.44
  511.0 0.9 copy.45
  511.9 0.9 copy.46
  512.7 0.9 copy.47
  (37 shorter events, 0.1 us)
Async XLA Ops:
  5.6 1.3 copy-start
  6.9 0.7 copy-start.6
  17.2 0.6 copy-start.7
  104.9 47.4 %collective-permute-start = (bf16[4,4,1152,128]{3,2,1,0:T(8,128)(2,1)}, bf16[4,4,1152,128]{3,2,1,0:T(8,128)(2,1)}, u32[]{:S(2)}, u32[]{:S(2)}) collective-permute-start(bf16[4,4,1152,128]{3,2,1,0:T(8,128)(2,1)} %get-tuple-element.101), channel_id=1, source_target_pairs={{0,4},{4,0},{8,12},{12,8},{16,20},{20,16},{24,28},{28,24},{1,5},{5... | collective-permute-start | bytes 14155784 | tf_op jit(solution)/shard_map/ppermute | solution.py:1316
  210.2 118.7 %collective-permute-start.1 = (bf16[384,2048]{1,0:T(8,128)(2,1)}, bf16[384,2048]{1,0:T(8,128)(2,1)}, u32[]{:S(2)}, u32[]{:S(2)}) collective-permute-start(bf16[384,2048]{1,0:T(8,128)(2,1)} %add_convert_fusion.3.refs_0_), channel_id=1, source_target_pairs={{8,16},{12,20},{16,8},{20,12},{9,17},{13,21},{17,9},{21,13},{10,18... | collective-permute-start | bytes 4718600 | tf_op jit(solution)/shard_map/ppermute | solution.py:1319
  271.5 2.7 copy-start.17
  274.1 2.3 copy-start.10
  274.1 2.3 copy-start.11
  274.1 3.9 copy-start.1
  274.1 3.9 copy-start.3
  274.2 54.7 %collective-permute-start.2 = (bf16[384,2048]{1,0:T(8,128)(2,1)S(1)}, bf16[384,2048]{1,0:T(8,128)(2,1)}, u32[]{:S(2)}, u32[]{:S(2)}) collective-permute-start(bf16[384,2048]{1,0:T(8,128)(2,1)S(1)} %add_convert_fusion.2.refs_0_), channel_id=1, source_target_pairs={{8,16},{12,20},{16,8},{20,12},{9,17},{13,21},{17,9},{21,13},{10,18... | collective-permute-start | bytes 4718600 | tf_op jit(solution)/shard_map/ppermute | solution.py:1319
  276.4 52.5 %collective-permute-start.3 = (bf16[192,2048]{1,0:T(8,128)(2,1)S(1)}, bf16[192,2048]{1,0:T(8,128)(2,1)}, u32[]{:S(2)}, u32[]{:S(2)}) collective-permute-start(bf16[192,2048]{1,0:T(8,128)(2,1)S(1)} %slice.21), channel_id=1, source_target_pairs={{8,16},{12,20},{16,8},{20,12},{9,17},{13,21},{17,9},{21,13},{10,18... | collective-permute-start | bytes 2359304 | tf_op jit(solution)/shard_map/ppermute | solution.py:1319
  278.0 42.8 %copy-start.12 = (bf16[3,2,1152,128]{3,2,1,0:T(8,128)(2,1)S(1)}, bf16[3,2,1152,128]{3,2,1,0:T(8,128)(2,1)}, u32[]{:S(2)}) copy-start(bf16[3,2,1152,128]{3,2,1,0:T(8,128)(2,1)} %get-tuple-element.132) | copy-start | bytes 5308420
  320.8 0.7 copy-start.2
  320.8 1.4 copy-start.8
  320.8 1.9 copy-start.9
  489.8 3.6 copy-start.14
  493.3 2.0 copy-start.13
  495.4 3.3 copy-start.4
  495.4 3.3 copy-start.5
  498.7 9.0 %copy-start.15 = (bf16[768,768]{1,0:T(8,128)(2,1)S(1)}, bf16[768,768]{1,0:T(8,128)(2,1)}, u32[]{:S(2)}) copy-start(bf16[768,768]{1,0:T(8,128)(2,1)} %get-tuple-element.175) | copy-start | bytes 3538948
  507.7 1.6 copy-start.16
  507.7 2.5 copy-start.21
  509.3 1.6 copy-start.20
  509.3 2.5 copy-start.19
  511.0 1.8 copy-start.18

commit v6 on v5

--- a/solution.py
+++ b/solution.py
@@ -6,6 +6,10 @@
 from jax.experimental.pallas import tpu as pltpu
 from jax.sharding import PartitionSpec as P
 
+EX = "expert"
+DX = "dp"
+ARB = "arbitrary"
+
 
 MESH_ID = pl.DeviceIdType.MESH
 
@@ -16,7 +20,7 @@
     return hi*2+lo
 
 def spot():
-    d=lax.axis_index("dp"); e=lax.axis_index("expert")
+    d=lax.axis_index(DX); e=lax.axis_index(EX)
     c=lax.rem(d,2)
     return c,lax.div(d,2),e
 
@@ -171,7 +175,7 @@
         outs={"gate":S((4,SG,FF),bf16),"up":S((4,SG,FF),bf16),"down":S((4,FF//8,D),bf16),
               "dgate":S((SG,FF),f32),"dup":S((SG,FF),f32),"ddown":S((FF//8,D),f32),
               "dqkv":S((SG,3*D),f32),"dwo":S((SG,D),f32),"gains":S((8,D),f32),
-              "ra":S((8,CAP,D),bf16),"rb":S((8,CAP,D),bf16)}
+              "ra":S((8,CAP,D),bf16),"rb":S((8,CAP,D),bf16),"block":S((T,D),bf16)}
         for i,w in self.MID:
             outs[f"m{i}{w}"]=S(self.shape(i),bf16)
         for i in self.RIN:
@@ -179,7 +183,7 @@
         for i in range(6):
             outs[f"ro{i}"]=S(self.shape(i),bf16)
         self.onames=list(outs); self.oshape=[outs[n] for n in self.onames]
-        self.in_specs=[an]*len(self.names); self.out_specs=[an]*len(self.onames)
+        self.in_specs=[pl.BlockSpec(memory_space=pltpu.VMEM) if n in ("cols","gates") else an for n in self.names]; self.out_specs=[an]*len(self.onames)
         V=pltpu.VMEM; DM=pltpu.SemaphoreType.DMA
         scr={"ga":V((2,3)+self.gs,bf16),"wa":V((2,3)+self.ws,bf16),
              "gto":V((3,)+self.gs,bf16),"wto":V((1,)+self.ws,bf16),
@@ -188,14 +192,14 @@
              "atr":V((4,4,SG,D),bf16),"sv":V((4,4,SG,D),bf16),"xr":V((3,4,SG,D),bf16),
              "za":V((4,SG,D),bf16),"zb":V((4,self.NR,128),bf16),
              "gn":V((8,8,D),f32),
-             "s_x":DM((7,)),"r_x":DM((7,)),"lra":DM((1,)),"s_o":DM((6,)),"r_o":DM((6,)),"s_w":DM((6,)),"r_w":DM((6,)),
+             "s_x":DM((7,)),"r_x":DM((7,)),"lra":DM((1,)),"cb":DM((18,)),"s_o":DM((6,)),"r_o":DM((6,)),"s_w":DM((6,)),"r_w":DM((6,)),
              "ld":DM((2,2,3)),"st":DM((8,)),"so":DM((6,2)),"s_r":DM((3,)),"r_r":DM((3,)),"s_at":DM((16,)),"r_at":DM((16,)),"s_xr":DM((3,)),"r_xr":DM((3,)),
              "s_gn":DM((7,)),"r_gn":DM((7,)),"st2":DM((4,)),"sz":DM((2,3))}
         for nm,sh in (("a",(SG,D)),("b",(self.NR,128))):
             scr.update({"zr"+nm:V((2,)+sh,bf16),"zs"+nm:V((2,)+sh,bf16),"zm"+nm:V((2,)+sh,bf16),"zi"+nm:V(sh,bf16),"zt"+nm:V(sh,bf16),
                 "zo"+nm:V(sh,bf16),"fi"+nm:V(sh,bf16),"ag"+nm:V((3,)+sh,bf16),
                 "s_z"+nm:DM((4,)),"r_z"+nm:DM((4,)),"s_ag"+nm:DM((3,)),"r_ag"+nm:DM((3,))})
-        scr.update({"oa":V((2,SG,D),f32),"og":V((2,2,SG,FF//4),f32),"od":V((2,self.SD,D),f32)})
+        scr.update({"og":V((2,2,SG,FF//4),f32),"od":V((2,self.SD,D),f32)})
         self.snames=list(scr)+[f"own{i}" for i in range(3)]+[f"plane{i}" for i in range(3)]
         self.scratch=[scr[n] for n in scr]+plane_sems(1)+plane_sems(1)
     def shape(self,i): return self.gs if self.KIND[i]=="g" else self.ws
@@ -418,10 +422,10 @@
         def store_a(kk,go):
             a=xor4(self.e,kk); s=kk%2
             cols=pl.ds(pl.multiple_of(jnp.minimum(a,2)*self.D,self.D),self.D)
-            one=pltpu.make_async_copy(r["oa"].at[s],r["dqkv"].at[:,cols],r["sz"].at[s,0])
+            one=pltpu.make_async_copy(self.oa.at[pl.ds(kk*self.SG,self.SG)],r["dqkv"].at[:,cols],r["sz"].at[s,0])
             if not go: one.wait(); return
             pl.when(a<3)(lambda: one.start())
-            pl.when(a==3)(lambda: pltpu.make_async_copy(r["oa"].at[s],r["dwo"],r["sz"].at[s,0]).start())
+            pl.when(a==3)(lambda: pltpu.make_async_copy(self.oa.at[pl.ds(kk*self.SG,self.SG)],r["dwo"],r["sz"].at[s,0]).start())
         def done(kk):
             if nm=="a": store_a(kk,False)
             else:
@@ -431,7 +435,7 @@
             if kk>=2: done(kk-2)
             src=r["fi"+nm] if kk==0 else r["ag"+nm].at[kk-1]
             if nm=="a":
-                add_rows(r["oa"].at[kk%2],[src])
+                add_rows(self.oa.at[pl.ds(kk*self.SG,self.SG)],[src])
                 store_a(kk,True)
             else:
                 for t in range(2):
@@ -449,13 +453,40 @@
                 for i in range(4) for zr in range(4)]
     def at_xy(self,kk):
         return self.rcopy(self.r["sv"].at[xor4(self.e,kk)],self.r["xr"].at[kk-1],self.r["s_xr"].at[kk-1],self.r["r_xr"].at[kk-1],peer(self.z,kk))
+    def combine(self,GS,acc,chunk_in,chunks_out):
+        r=self.r; T=self.T; Q=chunk_in.shape[0]; self.oa=acc
+        self.rows_home(False)
+        for cp in plane_copies([(r["rbs"],r["rb"])],self.plane): cp.wait()
+        B=T//128
+        cps=[pltpu.make_async_copy((r["ra"] if b<8 else r["rb"]).at[b%8],GS.at[b//B,pl.ds((b%B)*128,CAP)],r["cb"].at[b]) for b in range(16)]
+        cps.append(pltpu.make_async_copy(r["state"],acc,r["cb"].at[16]))
+        for cp in cps: cp.start()
+        for cp in cps: cp.wait()
+        for c in range(T//Q):
+            rows=slice(c*Q,(c+1)*Q)
+            cp=pltpu.make_async_copy(r["shared"].at[pl.ds(c*Q,Q)],chunk_in,r["cb"].at[17]); cp.start(); cp.wait()
+            out=acc[rows,:]+chunk_in[...]
+            for k in range(2):
+                s=r["cols"][rows,k:k+1]
+                s=s+8*((s*34953)>>22)
+                pk=None
+                for g in range(3):
+                    w=min(T,16*128-g*T)
+                    d=jnp.where(lax.broadcasted_iota(jnp.int32,(Q,w),1)+g*T==s,1.0,0.0).astype(bf16)
+                    q=lax.dot_general(d,GS[g,0:w,:],(((1,),(0,)),((),())),preferred_element_type=f32)
+                    pk=q if pk is None else pk+q
+                out=out+r["gates"][rows,k:k+1]*pk
+            chunks_out[rows,:]=out.astype(bf16)
+        pltpu.make_async_copy(chunks_out,r["block"],r["cb"].at[17]).start()
+    def combine_end(self,chunks_out):
+        pltpu.make_async_copy(chunks_out,self.r["block"],self.r["cb"].at[17]).wait()
     def gcopy(self,k,dev):
         return self.rcopy(self.r["gn"].at[0] ,self.r["gn"].at[k+1],self.r["s_gn"].at[k],self.r["r_gn"].at[k],dev)
     def middle(self):
         self.z_across("b")
         self.across_start((3,4,5,6))
         self.stage1(3,4)
-    def finish(self,GS,gg):
+    def finish(self,GS,gg,acc,chunk_in,chunks_out):
         r=self.r; gn=r["gn"]
         sw=self.at_swap(GS)
         for cp in sw: cp.start()
@@ -473,6 +504,7 @@
                 add_rows(r["sv"].at[i,zr],[GS.at[i,self.rows_of(self.c,zr)],r["atr"].at[i,zr]])
         for kk in (1,2,3): self.at_xy(kk).start()
         self.outward_send(5)
+        self.combine(GS,acc,chunk_in,chunks_out)
         self.gcopy(0,peer(self.z,4)).wait()
         gn[0]=gn[0]+gn[1]
         for kk in (1,2,3): self.gcopy(kk,peer(self.z,kk)).start()
@@ -529,8 +561,7 @@
         @pl.when(self.outer)
         def _():
             for k in range(3): self.rin(k).wait_send()
-        self.rows_home(False)
-        for cp in plane_copies([(r["rbs"],r["rb"])],self.plane): cp.wait()
+        self.combine_end(chunks_out)
 
 f32=jnp.float32; bf16=jnp.bfloat16
 def nn(a,b): return lax.dot_general(a,b,(((1,),(0,)),((),())),preferred_element_type=f32)
@@ -629,7 +660,7 @@
       out_specs=[tcol,tcol,tcol,tcol,pl.BlockSpec((1,8,T),lambda g:(g,0,0)),full((T,D)),full((T,D))]+([full((NS,D))]+[pl.BlockSpec(memory_space=pl.ANY)]*2 if fused else []),
       out_shape=[jax.ShapeDtypeStruct((T,D),bf16)]*4+[jax.ShapeDtypeStruct((ng,8,T),f32),jax.ShapeDtypeStruct((T,D),f32),jax.ShapeDtypeStruct((T,D),bf16)]+([jax.ShapeDtypeStruct((NS,D),bf16),*[jax.ShapeDtypeStruct((8,CAP,D),bf16)]*2] if fused else []),
       scratch_shapes=[pltpu.VMEM((T,D),bf16),pltpu.VMEM((nq,T,QC),f32),pltpu.VMEM((T,GW),bf16),pltpu.VMEM((T,GW),bf16),pltpu.VMEM((GW,T),bf16),pltpu.VMEM((nq,GW,QC),f32),pltpu.VMEM((T,D),f32)]+(plane_sems(2) if fused else []),
-      compiler_params=pltpu.CompilerParams(vmem_limit_bytes=56<<20,dimension_semantics=("arbitrary",),**(dict(collective_id=0,has_side_effects=True) if fused else {})),
+      compiler_params=pltpu.CompilerParams(vmem_limit_bytes=56<<20,dimension_semantics=(ARB,),**(dict(collective_id=0,has_side_effects=True) if fused else {})),
       cost_estimate=pl.CostEstimate(flops=2*T*D*4*D+4*T*T*D,bytes_accessed=16<<20,transcendentals=12*T*T),
       name="attn_fwd")(prefix,tokens,again[None],fgain[None],wqkv,wqkv,wqkv,wo,cosw,sinw,*([rows,sout] if fused else []))
 
@@ -729,7 +760,7 @@
                 tgo[r,:]=(sg[r,:]+inv*(w-u*jnp.mean(w*u,axis=1,keepdims=True))).astype(bf16)
             ggo[...]=jnp.broadcast_to(gg,(8,D))
             if fast:
-                tail.finish(GS,gg)
+                tail.finish(GS,gg,acc,dqT,PB)
     full=lambda s: pl.BlockSpec(s,lambda g:(0,)*len(s),pipeline_mode=pl.Buffered(1))
     col=lambda off: pl.BlockSpec((D,GW),lambda g,off=off:(0,g+off))
     tcol=pl.BlockSpec((T,GW),lambda g:(0,g))
@@ -747,7 +778,7 @@
       out_shape=[jax.ShapeDtypeStruct((T,D),bf16),jax.ShapeDtypeStruct((8,D),f32)]+oshape,
       scratch_shapes=[pltpu.VMEM((D,T),bf16),pltpu.VMEM((T,D),bf16),pltpu.VMEM((nq,T,QC),bf16),pltpu.VMEM((T,GW),bf16),pltpu.VMEM((GW,T),bf16),
         pltpu.VMEM((T,T),bf16),pltpu.VMEM((T,T),bf16),pltpu.VMEM((T,GW),f32),pltpu.VMEM((T,GW),f32),pltpu.VMEM((GW,T),f32),pltpu.VMEM((8,T),f32),pltpu.VMEM((T,D),f32)]+extra,
-      compiler_params=pltpu.CompilerParams(vmem_limit_bytes=63<<20,dimension_semantics=("arbitrary",),**(dict(collective_id=5,has_side_effects=True) if fast else {})),
+      compiler_params=pltpu.CompilerParams(vmem_limit_bytes=63<<20,dimension_semantics=(ARB,),**(dict(collective_id=5,has_side_effects=True) if fast else {})),
       cost_estimate=pl.CostEstimate(flops=2*T*D*8*D+10*T*T*D,bytes_accessed=24<<20,transcendentals=12*T*T),
       name="attn_bwd")(prefix,sgrad,tokens,again[None],wqkv,wqkv,wqkv,wo,cosw,sinw,q,k,v,att,lse,*(tail.arrays if fast else ()))
 
@@ -807,7 +838,7 @@
       in_specs=[rowspec]*(2*parts)+[wspec,wspec,wdspec],
       out_specs=[rowspec]*(2*parts)+[wspec,wspec,wdspec],
       scratch_shapes=[pltpu.VMEM((R,D),bf16)]*2+[pltpu.VMEM((R,FB),bf16)]*3+[pltpu.VMEM((R,D),f32)]*2,
-      compiler_params=pltpu.CompilerParams(vmem_limit_bytes=60<<20,dimension_semantics=("arbitrary","arbitrary")),
+      compiler_params=pltpu.CompilerParams(vmem_limit_bytes=60<<20,dimension_semantics=(ARB,ARB)),
       cost_estimate=pl.CostEstimate(flops=2*9*R*D*FF*L,bytes_accessed=L*(6*D*FF*2+4*R*D*2),transcendentals=R*FF*L),
       name="ffn")
     return call
@@ -935,7 +966,7 @@
         out_specs=[rowspec]*(2*n)+[full(2*SR,2*HB),full(SR,2*HB),full(SR,2*HB)]*ng+wspecs+[anyspec]*(nc+nd+nz//2+ne),
         scratch_shapes=[pltpu.VMEM((R//chunk,D,chunk),bf16),pltpu.VMEM((D,chunk),bf16)]+[pltpu.VMEM((R,FB),bf16)]*3+[pltpu.VMEM((R,D),f32)]*2+([pltpu.SemaphoreType.DMA((1,)),pltpu.SemaphoreType.DMA((1,))] if nz else [])+(ext_sems() if ne else [])+(row_sems() if nd else [])+(plane_sems(1) if nc else []),
       out_shape=[jax.ShapeDtypeStruct((RG,D),bf16)]*(2*n)+([jax.ShapeDtypeStruct((2*SR,2*HB),bf16)]+[jax.ShapeDtypeStruct((SR,2*HB),bf16)]*2)*ng+[jax.ShapeDtypeStruct((HB,D),bf16)]*ng+[jax.ShapeDtypeStruct((8,RG//8,D),bf16)]*nc+([jax.ShapeDtypeStruct((3,dense[2])+dense[0].shape[2:],bf16)] if nd else [])+([jax.ShapeDtypeStruct(inw[0].shape,bf16)] if nz else [])+([jax.ShapeDtypeStruct(ext.shape,bf16)] if ne else []),
-      compiler_params=pltpu.CompilerParams(vmem_limit_bytes=62<<20,dimension_semantics=("arbitrary",),**(dict(collective_id=cid,has_side_effects=True) if nc or nd or nz else {})),
+      compiler_params=pltpu.CompilerParams(vmem_limit_bytes=62<<20,dimension_semantics=(ARB,),**(dict(collective_id=cid,has_side_effects=True) if nc or nd or nz else {})),
       cost_estimate=pl.CostEstimate(flops=9*R*D*FF*ng,bytes_accessed=3*D*FF*2*ng+4*R*D*2,transcendentals=R*FF*ng//2),
       name=f"expert_ffn{n}_{f0}")(*deps,*xs,*ss,wg,wu,wd,*prev,*([carry] if nc else []),*([dense[0]] if nd else []),*(inw if nz else ()),*([ext] if ne else []),*gpargs)
     o=2*n
@@ -994,7 +1025,7 @@
       out_specs=[full((T,D)),full((T,D)),full((4,4,NR,128)),full((4,4,NR,128))]+[pl.BlockSpec(memory_space=pl.ANY)]*3,
       out_shape=[jax.ShapeDtypeStruct((T,D),f32)]*2+[jax.ShapeDtypeStruct((4,4,NR,128),bf16)]*2+[jax.ShapeDtypeStruct(xout.shape[1:],bf16)]*3,
       scratch_shapes=[pltpu.VMEM((D,T),bf16)]+[pltpu.VMEM((T,FB),bf16)]*3+[pltpu.VMEM((D,FB),bf16),pltpu.VMEM((FB,D),bf16)]+[pltpu.SemaphoreType.DMA((1,))]*2+plane_sems(2),
-      compiler_params=pltpu.CompilerParams(vmem_limit_bytes=62<<20,dimension_semantics=("arbitrary",),collective_id=1,has_side_effects=True),
+      compiler_params=pltpu.CompilerParams(vmem_limit_bytes=62<<20,dimension_semantics=(ARB,),collective_id=1,has_side_effects=True),
       cost_estimate=pl.CostEstimate(flops=2*9*T*D*FF,bytes_accessed=6*D*FF*2+8*T*D*2,transcendentals=T*FF),
       name="shared_ffn")(x,s,wg,wu,wd,xout,sa)
 
@@ -1191,21 +1222,21 @@
            output_weight, feedforward_gain, shared_gate, shared_up, shared_down, expert_gate, expert_up, expert_down):
     T, D = tokens.shape
     L, _, FF = expert_gate.shape
-    G = lax.axis_size("expert")
-    DP = lax.axis_size("dp")
+    G = lax.axis_size(EX)
+    DP = lax.axis_size(DX)
     Z = DP // 2
     parts = 2 if L % 2 == 0 else 1
     LP = L // parts
-    dpi = lax.axis_index("dp")
+    dpi = lax.axis_index(DX)
     core = lax.rem(dpi, 2)
     swap_perm = [(i, i ^ 1) for i in range(DP)]
     zgroups = [[2 * z + c for z in range(Z)] for c in range(2)]
 
     def swap(x):
-        return lax.ppermute(x, "dp", swap_perm)
+        return lax.ppermute(x, DX, swap_perm)
 
     def a2a(x):
-        return lax.all_to_all(x, "expert", split_axis=0, concat_axis=0, tiled=True)
+        return lax.all_to_all(x, EX, split_axis=0, concat_axis=0, tiled=True)
 
     def to_experts(arrs):
         arrs = [a.reshape(G, LP, CAP, D) for a in arrs]
@@ -1248,10 +1279,10 @@
     egr = []
     for l in range(LP):
         if parts == 2:
-            egr.append([lax.psum_scatter(g[0], "dp", scatter_dimension=0, tiled=True, axis_index_groups=zgroups)
+            egr.append([lax.psum_scatter(g[0], DX, scatter_dimension=0, tiled=True, axis_index_groups=zgroups)
                         for g in eg[l]])
         else:
-            egr.append([lax.psum_scatter(g[0], "dp", scatter_dimension=0, tiled=True) for g in eg[l]])
+            egr.append([lax.psum_scatter(g[0], DX, scatter_dimension=0, tiled=True) for g in eg[l]])
 
     back = from_experts(dgr)
     ret = from_experts(res)
@@ -1268,14 +1299,14 @@
         s = (mine.astype(f32) + swap(other).astype(f32)).astype(bf16)
         quarter = s.reshape(Z, G, r // G, g.shape[1])
         quarter = jnp.swapaxes(quarter, 0, 1)
-        got = lax.all_to_all(quarter, "expert", split_axis=0, concat_axis=0, tiled=True)
+        got = lax.all_to_all(quarter, EX, split_axis=0, concat_axis=0, tiled=True)
         s = jnp.sum(got.astype(f32), axis=0).astype(bf16)
-        zs = lax.psum_scatter(s, "dp", scatter_dimension=0, tiled=True, axis_index_groups=zgroups)
-        return lax.all_gather(zs[0], "expert", axis=0, tiled=True).astype(f32)
+        zs = lax.psum_scatter(s, DX, scatter_dimension=0, tiled=True, axis_index_groups=zgroups)
+        return lax.all_gather(zs[0], EX, axis=0, tiled=True).astype(f32)
 
     def dense_simple(g):
-        p = lax.psum_scatter(g, "dp", scatter_dimension=0, tiled=True)
-        return lax.psum(p, "expert").astype(f32)
+        p = lax.psum_scatter(g, DX, scatter_dimension=0, tiled=True)
+        return lax.psum(p, EX).astype(f32)
 
     if (qkv_weight.shape[0] // DP) % (8 * G) == 0 and parts == 2:
         dn = dense
@@ -1283,7 +1314,7 @@
         dn = dense_simple
     dsh = [dn(g) for g in dense_shared]
     dq, dk, dv, dwo = [dn(g) for g in (gq, gk, gv, gwo)]
-    gains = lax.psum(jnp.stack([agg[0], fgg[0]]), ("dp", "expert"))
+    gains = lax.psum(jnp.stack([agg[0], fgg[0]]), (DX, EX))
     gs = D // DP
     gains = lax.dynamic_slice_in_dim(gains, dpi * gs, gs, 1)
 
@@ -1305,18 +1336,18 @@
                 output_weight, feedforward_gain, shared_gate, shared_up, shared_down, expert_gate, expert_up, expert_down):
     T, D = tokens.shape
     FF = expert_gate.shape[2]
-    dpi = lax.axis_index("dp").astype(jnp.int32)
-    ei = lax.axis_index("expert").astype(jnp.int32)
+    dpi = lax.axis_index(DX).astype(jnp.int32)
+    ei = lax.axis_index(EX).astype(jnp.int32)
     core = lax.rem(dpi, 2)
     zi = lax.div(dpi, 2)
     outer = (zi == 0) | (zi == 3)
     low = zi < 2
 
     def swap(x):
-        return lax.ppermute(x, "dp", [(i, i ^ 1) for i in range(8)])
+        return lax.ppermute(x, DX, [(i, i ^ 1) for i in range(8)])
 
     def across(x):
-        return lax.ppermute(x, "dp", [(2, 4), (3, 5), (4, 2), (5, 3)])
+        return lax.ppermute(x, DX, [(2, 4), (3, 5), (4, 2), (5, 3)])
 
     def add(*xs):
         t = xs[0].astype(f32)
@@ -1354,7 +1385,7 @@
     got = jnp.concatenate([r0, r1, r2], axis=1)
     msh = add(mine, got[0], got[1], got[2])
     carried = {
-        "hown": blocks(ra), "rxl": rxl, "rbs": blocks(rb), "fgg": fgg, "msh": msh,
+        "cols": cols, "gates": route_gates, "state": state, "shared": shared_branch, "hown": blocks(ra), "rxl": rxl, "rbs": blocks(rb), "fgg": fgg, "msh": msh,
         "m0": m_b0, "ni0": gb0[1], "no0": gb0[2],
         "m1": m_b1, "m2o": m_a0o, "ni1": gb1[1], "no1": gb1[2],
         "far2": ga0[0], "ni2": ga0[1], "no2": ga0[2],
@@ -1366,28 +1397,27 @@
     tokens_grad, _, *rest = attn_bwd(sgrad, prefix_len, tokens, attention_gain, qkv_weight, output_weight,
                                      cosw, sinw, q, k, v, att, lse, tail)
     o = dict(zip(tail.onames, rest))
-    block_out = combine(cols, route_gates, [flat(o["ra"]), flat(o["rb"])], state, shared_branch)
     sg = D // 8
     gains = lax.dynamic_slice_in_dim(o["gains"], dpi * sg, sg, 1)
-    return (block_out, tokens_grad, gains[0], o["dqkv"], o["dwo"], gains[1], o["dgate"], o["dup"], o["ddown"],
+    return (o["block"], tokens_grad, gains[0], o["dqkv"], o["dwo"], gains[1], o["dgate"], o["dup"], o["ddown"],
             o["gate"].astype(f32), o["up"].astype(f32), o["down"].astype(f32))
 
 
 def shards(*args):
     local = args[13].shape[0]
-    if lax.axis_size("dp") == 8 and lax.axis_size("expert") == 4 and local == 4:
+    if lax.axis_size(DX) == 8 and lax.axis_size(EX) == 4 and local == 4:
         return shards_fast(*args)
     return shards_any(*args)
 
 
 def solution(mesh):
-    row = P(("dp", "expert"), None)
+    row = P((DX, EX), None)
     return jax.shard_map(
         shards,
         mesh=mesh,
-        in_specs=(row, row, row, row, row, P(("dp", "expert")), P(), P(), P(), P(), P(), P(), P(),
-                  P("expert", None, None), P("expert", None, None), P("expert", None, None)),
-        out_specs=(row, row, P("dp"), P("dp", None), P("dp", None), P("dp"), P("dp", None), P("dp", None),
-                   P("dp", None), P("expert", "dp", None), P("expert", "dp", None), P("expert", "dp", None)),
+        in_specs=(row, row, row, row, row, P((DX, EX)), P(), P(), P(), P(), P(), P(), P(),
+                  P(EX, None, None), P(EX, None, None), P(EX, None, None)),
+        out_specs=(row, row, P(DX), P(DX, None), P(DX, None), P(DX), P(DX, None), P(DX, None),
+                   P(DX, None), P(EX, DX, None), P(EX, DX, None), P(EX, DX, None)),
         check_vma=False,
     )

time: 523 us -> 515 us (0.985)
  Pallas kernels: 463 us -> 454 us
    pallas_call x1 -> x0, Pallas kernels: 9.04 us -> none  [combine(): pl.pallas_call(kernel, in_specs=[vm] * (4 + parts), out_specs=vm, out_sha...]
    unnamed x54 -> x61, local copies, waits for them, and re-layouts: 12.4 us -> 15.4 us
where the time goes in v6:
time: 515 us; the launch traced here: 507 us
  Pallas kernels  454 us (88%)
  other arithmetic  27.1 us (5%)
  local copies, waits for them, and re-layouts  19.4 us (4%)
    pallas_call x1, Pallas kernels, attn_bwd(): pl.pallas_call(kernel, grid=(ng,), in_specs=[pl.BlockSpec(memory_space=pl...  161 us
    pallas_call x3, Pallas kernels, expert_ffn(): pl.pallas_call(kernel, grid=(nf,), in_specs=[anyspec] * nx + [rowspec] *...  154 us
    pallas_call x1, Pallas kernels, shared_ffn(): pl.pallas_call(kernel, grid=(nf,), in_specs=[full((T, D)), full((T, D)),...  44.4 us
    pallas_call x1, Pallas kernels, attn_fwd(): pl.pallas_call(kernel, grid=(ng,), in_specs=[pl.BlockSpec(memory_space=pl...  42.8 us
    pallas_call x1, Pallas kernels, mid_bwd_home(): pl.pallas_call(kernel, in_specs=[an] * (nx + 4) + [vm, an, an] + [vm] * 5...  42.7 us
    convert_element_type x4, other arithmetic, add(): return t.astype(bf16)  16.6 us
    unnamed x61, local copies, waits for them, and re-layouts  15.4 us
  transfers between devices with their start and end apart: 4, of which 0 were waited for; matrix products, arithmetic and copies ran while one was open for 2% of the time, Pallas kernels for 29%

profile of v6, /device:TPU:0, one launch (start us, length us, event | category | flops | bytes accessed | tf_op | source)
XLA Modules:
  0.0 506.7 jit_solution(901159984228231902)
XLA Ops:
  1.3 1.3 broadcast_in_dim.11.ag
  2.6 1.3 broadcast_in_dim.12.fg.refs_11_
  3.8 0.9 copy.31.gts.rest_1_
  4.7 0.9 copy.30.ids
  5.6 1.3 copy-done.2
  6.9 0.7 copy-done.6
  7.6 9.7 %route.1 = (s32[8,768]{1,0:T(8,128)S(1)}, s32[768,8]{1,0:T(8,128)S(1)}, bf16[1920,768]{1,0:T(8,128)(2,1)}) custom-call(s32[1]{0:T(128)} %bitcast.core_ref, s32[1,1536]{1,0:T(1,128)S(1)} %copy-done.6, s32[768,2]{1,0:T(8,128)S(1)} %copy.30.ids, f32[768,2]{1,0:T(8,128)S(1)} %copy.31.gts.rest_1_, bf16[768,768]{1,0:T(8,128)(2,1)S(1)} %copy-done.2), custom_call_target="tpu_custom_call" | custom-call | flops 4680843264 | bytes 8388608 | tf_op jit(solution)/shard_map/route/pallas_call | solution.py:1092
  17.3 0.6 copy-done.7
  17.9 42.8 %attn_fwd.1 = (bf16[768,768]{1,0:T(8,128)(2,1)}, bf16[768,768]{1,0:T(8,128)(2,1)}, bf16[768,768]{1,0:T(8,128)(2,1)}, bf16[768,768]{1,0:T(8,128)(2,1)}, f32[3,8,7...) custom-call(s32[1]{0:T(128)S(6)} %copy.42.pre, ...), custom_call_target="tpu_custom_call" | custom-call | flops 5435817984 | bytes 16777216 | tf_op jit(solution)/shard_map/attn_fwd/pallas_call | solution.py:658
  60.7 44.4 %shared_ffn.1 = (f32[768,768]{1,0:T(8,128)}, f32[768,768]{1,0:T(8,128)}, bf16[4,4,1152,128]{3,2,1,0:T(8,128)(2,1)}, bf16[4,4,1152,128]{3,2,1,0:T(8,128)(2,1)}, b...) custom-call(bf16[768,768]{1,0:T(8,128)(2,1)} %get-tuple-element.87.xr, ...), custom_call_target="tpu_custom_call" | custom-call | flops 21743271936 | bytes 28311552 | tf_op jit(solution)/shard_map/shared_ffn/pallas_call | solution.py:1023
  105.1 0.5 collective-permute-start
  105.6 46.9 %expert_ffn1_0.3 = (bf16[960,768]{1,0:T(8,128)(2,1)}, bf16[960,768]{1,0:T(8,128)(2,1)}, bf16[384,2048]{1,0:T(8,128)(2,1)}, bf16[192,2048]{1,0:T(8,128)(2,1)}, bf...) custom-call(bf16[960,768]{1,0:T(8,128)(2,1)} %bitcast.33, ...), custom_call_target="tpu_custom_call" | custom-call | flops 27179089920 | bytes 24772608 | tf_op jit(solution)/shard_map/expert_ffn1_0/pallas_call | solution.py:964
  152.6 7.1 %add_convert_fusion.refs_6_.refs_3_ = bf16[4,4,1152,128]{3,2,1,0:T(8,128)(2,1)} fusion(bf16[4,4,1152,128]{3,2,1,0:T(8,128)(2,1)} %collective-permute-done, bf16[4,4,1152,128]{3,2,1,0:T(8,128)(2,1)} %get-tuple-element.98), kind=kLoop, calls=%fused_computation | loop fusion | flops 9437184 | bytes 14155776 | tf_op jit(solution)/shard_map/convert_element_type | solution.py:1356
  159.7 47.3 %expert_ffn1_0.4 = (bf16[960,768]{1,0:T(8,128)(2,1)}, bf16[960,768]{1,0:T(8,128)(2,1)}, bf16[384,2048]{1,0:T(8,128)(2,1)}, bf16[192,2048]{1,0:T(8,128)(2,1)}, bf...) custom-call(bf16[960,768]{1,0:T(8,128)(2,1)} %bitcast.36, ...), custom_call_target="tpu_custom_call" | custom-call | flops 27179089920 | bytes 24772608 | tf_op jit(solution)/shard_map/expert_ffn1_0/pallas_call | solution.py:964
  207.0 3.7 add_convert_fusion.3.refs_0_
  210.7 1.8 collective-permute-start.1
  212.5 59.4 %expert_ffn1_0.5 = (bf16[960,768]{1,0:T(8,128)(2,1)}, bf16[960,768]{1,0:T(8,128)(2,1)}, bf16[384,2048]{1,0:T(8,128)(2,1)}, bf16[192,2048]{1,0:T(8,128)(2,1)}, bf...) custom-call(bf16[384,2048]{1,0:T(8,128)(2,1)} %add_convert_fusion.3., ...), custom_call_target="tpu_custom_call" | custom-call | flops 27179089920 | bytes 24772608 | tf_op jit(solution)/shard_map/expert_ffn1_0/pallas_call | solution.py:964
  272.0 2.6 add_convert_fusion.2.refs_0_
  274.6 0.1 slice.21
  274.7 0.8 collective-permute-start.3
  275.5 0.9 collective-permute-start.2
  276.5 0.1 constant_dynamic-update-slice_fusion.2
  276.5 0.2 copy-done.3
  276.7 42.7 %mid_bwd.1 = (f32[768,768]{1,0:T(8,128)}, f32[8,768]{1,0:T(8,128)S(1)}, bf16[8,120,768]{2,1,0:T(8,128)(2,1)}, bf16[1024,768]{1,0:T(8,128)(2,1)}, bf16[3,1,1152,1...) custom-call(bf16[384,2048]{1,0:T(8,128)(2,1)} %copy-done.10, bf16[1024,768]{1,0:T(8,128)(2,1)} %get-tuple-element.111.refs_1_.rest_25_, ...), custom_call_target="tpu_custom_call" | custom-call | flops 2264924160 | bytes 12582912 | tf_op jit(solution)/shard_map/mid_bwd/pallas_call | solution.py:1180
  319.4 0.2 constant_dynamic-update-slice_fusion.1
  319.7 0.4 copy-done.4
  320.0 0.8 copy-done.8
  320.8 0.5 copy-done.9
  321.3 3.2 add_convert_fusion.1.rest_26_
  324.5 0.1 constant_dynamic-update-slice_fusion
  324.6 2.9 fusion.rest_8_
  327.6 1.2 copy-done.13
  328.7 0.2 copy-done.23
  328.9 161.0 %attn_bwd.1 = (bf16[768,768]{1,0:T(8,128)(2,1)}, f32[8,768]{1,0:T(8,128)}, bf16[4,96,2048]{2,1,0:T(8,128)(2,1)}, bf16[4,96,2048]{2,1,0:T(8,128)(2,1)}, bf16[4,25...) custom-call(s32[1]{0:T(128)S(6)} %copy.42.pre, ...), custom_call_target="tpu_custom_call" | custom-call | flops 11777605632 | bytes 25165824 | tf_op jit(solution)/shard_map/attn_bwd/pallas_call | solution.py:775
  489.9 0.8 constant_dynamic-slice_fusion
  490.7 0.5 slice_bitcast_fusion
  491.2 3.6 convert_element_type.78
  494.8 2.0 convert_element_type.79
  496.8 1.9 convert_element_type.80
  498.8 1.0 copy.43
  499.8 0.7 copy-done.16
  500.5 1.0 copy.44
  501.5 0.6 copy-done.18
  502.1 0.9 copy.45
  503.0 0.7 copy.46
  503.7 0.9 copy.47
  504.6 0.9 copy.48
  505.5 0.9 copy.49
  (43 shorter events, 0.1 us)
Async XLA Ops:
  4.7 12.6 %copy-start = (f32[768,2]{1,0:T(8,128)}, f32[768,2]{1,0:T(8,128)S(1)}, u32[]{:S(2)}) copy-start(f32[768,2]{1,0:T(8,128)S(1)} %copy.31.gts.rest_1_) | copy-start | bytes 18436
  5.6 1.3 copy-start.2
  6.9 0.7 copy-start.6
  17.3 0.6 copy-start.7
  17.9 258.6 %copy-start.1 = (s32[768,8]{1,0:T(8,128)}, s32[768,8]{1,0:T(8,128)S(1)}, u32[]{:S(2)}) copy-start(s32[768,8]{1,0:T(8,128)S(1)} %get-tuple-element.114.refs_5_.rest_0_) | copy-start | bytes 73732
  105.1 47.4 %collective-permute-start = (bf16[4,4,1152,128]{3,2,1,0:T(8,128)(2,1)}, bf16[4,4,1152,128]{3,2,1,0:T(8,128)(2,1)}, u32[]{:S(2)}, u32[]{:S(2)}) collective-permute-start(bf16[4,4,1152,128]{3,2,1,0:T(8,128)(2,1)} %get-tuple-element.99), channel_id=1, source_target_pairs={{0,4},{4,0},{8,12},{12,8},{16,20},{20,16},{24,28},{28,24},{1,5},{5... | collective-permute-start | bytes 14155784 | tf_op jit(solution)/shard_map/ppermute | solution.py:1347
  210.7 116.8 %collective-permute-start.1 = (bf16[384,2048]{1,0:T(8,128)(2,1)}, bf16[384,2048]{1,0:T(8,128)(2,1)}, u32[]{:S(2)}, u32[]{:S(2)}) collective-permute-start(bf16[384,2048]{1,0:T(8,128)(2,1)} %add_convert_fusion.3.refs_0_), channel_id=1, source_target_pairs={{8,16},{12,20},{16,8},{20,12},{9,17},{13,21},{17,9},{21,13},{10,18... | collective-permute-start | bytes 4718600 | tf_op jit(solution)/shard_map/ppermute | solution.py:1350
  272.0 2.6 copy-start.11
  274.6 1.9 copy-start.10
  274.6 1.9 copy-start.19
  274.6 2.1 copy-start.3
  274.6 2.1 copy-start.5
  274.7 52.8 %collective-permute-start.3 = (bf16[192,2048]{1,0:T(8,128)(2,1)S(1)}, bf16[192,2048]{1,0:T(8,128)(2,1)S(1)}, u32[]{:S(2)}, u32[]{:S(2)}) collective-permute-start(bf16[192,2048]{1,0:T(8,128)(2,1)S(1)} %slice.21), channel_id=1, source_target_pairs={{8,16},{12,20},{16,8},{20,12},{9,17},{13,21},{17,9},{21,13},{10,18... | collective-permute-start | bytes 2359304 | tf_op jit(solution)/shard_map/ppermute | solution.py:1350
  275.5 52.0 %collective-permute-start.2 = (bf16[384,2048]{1,0:T(8,128)(2,1)S(1)}, bf16[384,2048]{1,0:T(8,128)(2,1)S(1)}, u32[]{:S(2)}, u32[]{:S(2)}) collective-permute-start(bf16[384,2048]{1,0:T(8,128)(2,1)S(1)} %add_convert_fusion.2.refs_0_), channel_id=1, source_target_pairs={{8,16},{12,20},{16,8},{20,12},{9,17},{13,21},{17,9},{21,13},{10,18... | collective-permute-start | bytes 4718600 | tf_op jit(solution)/shard_map/ppermute | solution.py:1350
  276.7 42.7 %copy-start.12 = (bf16[3,2,1152,128]{3,2,1,0:T(8,128)(2,1)S(1)}, bf16[3,2,1152,128]{3,2,1,0:T(8,128)(2,1)}, u32[]{:S(2)}) copy-start(bf16[3,2,1152,128]{3,2,1,0:T(8,128)(2,1)} %get-tuple-element.132) | copy-start | bytes 5308420
  319.4 0.7 copy-start.4
  319.4 1.4 copy-start.8
  319.4 1.9 copy-start.9
  327.5 1.4 copy-start.23
  327.5 1.2 copy-start.13
  491.2 3.6 copy-start.15
  494.8 2.0 copy-start.14
  496.8 1.9 copy-start.17
  498.8 1.7 copy-start.16
  500.5 1.6 copy-start.18
  500.5 2.5 copy-start.24
  502.1 1.6 copy-start.22
  502.1 2.5 copy-start.21
  503.7 1.8 copy-start.20

commit v7 on v6

--- a/solution.py
+++ b/solution.py
@@ -578,6 +578,9 @@
     return jnp.where(first,pltpu.roll(x,w-HD//2,1),pltpu.roll(x,HD//2,1))
 def wide(t):
     return jnp.concatenate([t,t],axis=1)
+def as_rows(g):
+    return g if g.ndim==2 else g[None]
+
 def inv_rms(v):
     return lax.rsqrt(jnp.mean(v*v,axis=1,keepdims=True)+EPS)
 
@@ -600,7 +603,7 @@
             for c in range(nq):
                 r=slice(c*QC,(c+1)*QC)
                 x=tok[r,:].astype(f32)
-                normed[r,:]=(x*inv_rms(x)*ag[...]).astype(bf16)
+                normed[r,:]=(x*inv_rms(x)*ag[0:1,:]).astype(bf16)
                 j=lax.broadcasted_iota(jnp.int32,(T,QC),0)
                 i=lax.broadcasted_iota(jnp.int32,(T,QC),1)+c*QC
                 bias[c]=jnp.where((j<=i)|(j<pre[0]),0.0,-1e30)
@@ -645,7 +648,7 @@
                 r=slice(c*QC,(c+1)*QC)
                 st=acc[r,:]
                 stateo[r,:]=st
-                ntwoo[r,:]=(st*inv_rms(st)*fg[...]).astype(bf16)
+                ntwoo[r,:]=(st*inv_rms(st)*fg[fg.shape[0]-1:,:]).astype(bf16)
             if fused:
                 for i in range(NS//CH):
                     si=lax.broadcasted_iota(jnp.int32,(CH,T),0)+i*CH
@@ -656,13 +659,13 @@
     col=lambda off: pl.BlockSpec((D,GW),lambda g,off=off:(0,g+off))
     tcol=pl.BlockSpec((T,GW),lambda g:(0,g))
     return pl.pallas_call(kernel,grid=(ng,),
-      in_specs=[pl.BlockSpec(memory_space=pltpu.SMEM),full((T,D)),full((1,D)),full((1,D)),col(0),col(ng),col(2*ng),pl.BlockSpec((GW,D),lambda g:(g,0)),full((T,128)),full((T,128))]+([full((8,T)),pl.BlockSpec(memory_space=pl.ANY)] if fused else []),
+      in_specs=[pl.BlockSpec(memory_space=pltpu.SMEM),full((T,D)),full(as_rows(again).shape),full(as_rows(fgain).shape),col(0),col(ng),col(2*ng),pl.BlockSpec((GW,D),lambda g:(g,0)),full((T,128)),full((T,128))]+([full((8,T)),pl.BlockSpec(memory_space=pl.ANY)] if fused else []),
       out_specs=[tcol,tcol,tcol,tcol,pl.BlockSpec((1,8,T),lambda g:(g,0,0)),full((T,D)),full((T,D))]+([full((NS,D))]+[pl.BlockSpec(memory_space=pl.ANY)]*2 if fused else []),
       out_shape=[jax.ShapeDtypeStruct((T,D),bf16)]*4+[jax.ShapeDtypeStruct((ng,8,T),f32),jax.ShapeDtypeStruct((T,D),f32),jax.ShapeDtypeStruct((T,D),bf16)]+([jax.ShapeDtypeStruct((NS,D),bf16),*[jax.ShapeDtypeStruct((8,CAP,D),bf16)]*2] if fused else []),
       scratch_shapes=[pltpu.VMEM((T,D),bf16),pltpu.VMEM((nq,T,QC),f32),pltpu.VMEM((T,GW),bf16),pltpu.VMEM((T,GW),bf16),pltpu.VMEM((GW,T),bf16),pltpu.VMEM((nq,GW,QC),f32),pltpu.VMEM((T,D),f32)]+(plane_sems(2) if fused else []),
       compiler_params=pltpu.CompilerParams(vmem_limit_bytes=56<<20,dimension_semantics=(ARB,),**(dict(collective_id=0,has_side_effects=True) if fused else {})),
       cost_estimate=pl.CostEstimate(flops=2*T*D*4*D+4*T*T*D,bytes_accessed=16<<20,transcendentals=12*T*T),
-      name="attn_fwd")(prefix,tokens,again[None],fgain[None],wqkv,wqkv,wqkv,wo,cosw,sinw,*([rows,sout] if fused else []))
+      name="attn_fwd")(prefix,tokens,as_rows(again),as_rows(fgain),wqkv,wqkv,wqkv,wo,cosw,sinw,*([rows,sout] if fused else []))
 
 def attn_bwd(sgrad, prefix, tokens, again, wqkv, wo, cosw, sinw, q, k, v, att, lse, tail=None):
     T,D=tokens.shape
@@ -690,7 +693,7 @@
             for c in range(nq):
                 r=slice(c*QC,(c+1)*QC)
                 x=tok[r,:].astype(f32)
-                n=x*inv_rms(x)*ag[...]
+                n=x*inv_rms(x)*ag[0:1,:]
                 normedT[:,r]=n.T.astype(bf16)
                 bg[r,:]=sg[r,:].astype(bf16)
                 j=lax.broadcasted_iota(jnp.int32,(T,QC),0)
@@ -756,7 +759,7 @@
                 inv=inv_rms(x); u=x*inv
                 ngd=acc[r,:]
                 gg=gg+jnp.sum(ngd*u,axis=0,keepdims=True)
-                w=ngd*ag[...]
+                w=ngd*ag[0:1,:]
                 tgo[r,:]=(sg[r,:]+inv*(w-u*jnp.mean(w*u,axis=1,keepdims=True))).astype(bf16)
             ggo[...]=jnp.broadcast_to(gg,(8,D))
             if fast:
@@ -773,14 +776,14 @@
         extra=[]
     rowb=pl.BlockSpec((GW,D),lambda g:(g,0))
     return pl.pallas_call(kernel,grid=(ng,),
-      in_specs=[pl.BlockSpec(memory_space=pltpu.SMEM)]+[full((T,D)),full((T,D)),full((1,D)),col(0),col(ng),col(2*ng),rowb,full((T,128)),full((T,128)),tcol,tcol,tcol,tcol,pl.BlockSpec((1,8,T),lambda g:(g,0,0))]+(tail.in_specs if fast else []),
+      in_specs=[pl.BlockSpec(memory_space=pltpu.SMEM)]+[full((T,D)),full((T,D)),full(as_rows(again).shape),col(0),col(ng),col(2*ng),rowb,full((T,128)),full((T,128)),tcol,tcol,tcol,tcol,pl.BlockSpec((1,8,T),lambda g:(g,0,0))]+(tail.in_specs if fast else []),
       out_specs=[full((T,D)),full((8,D))]+outs,
       out_shape=[jax.ShapeDtypeStruct((T,D),bf16),jax.ShapeDtypeStruct((8,D),f32)]+oshape,
       scratch_shapes=[pltpu.VMEM((D,T),bf16),pltpu.VMEM((T,D),bf16),pltpu.VMEM((nq,T,QC),bf16),pltpu.VMEM((T,GW),bf16),pltpu.VMEM((GW,T),bf16),
         pltpu.VMEM((T,T),bf16),pltpu.VMEM((T,T),bf16),pltpu.VMEM((T,GW),f32),pltpu.VMEM((T,GW),f32),pltpu.VMEM((GW,T),f32),pltpu.VMEM((8,T),f32),pltpu.VMEM((T,D),f32)]+extra,
       compiler_params=pltpu.CompilerParams(vmem_limit_bytes=63<<20,dimension_semantics=(ARB,),**(dict(collective_id=5,has_side_effects=True) if fast else {})),
       cost_estimate=pl.CostEstimate(flops=2*T*D*8*D+10*T*T*D,bytes_accessed=24<<20,transcendentals=12*T*T),
-      name="attn_bwd")(prefix,sgrad,tokens,again[None],wqkv,wqkv,wqkv,wo,cosw,sinw,q,k,v,att,lse,*(tail.arrays if fast else ()))
+      name="attn_bwd")(prefix,sgrad,tokens,as_rows(again),wqkv,wqkv,wqkv,wo,cosw,sinw,q,k,v,att,lse,*(tail.arrays if fast else ()))
 
 
 def make_ffn(parts, G, L, cap, D, FF, FB, chunk, out_dt):
@@ -1170,7 +1173,7 @@
                 n=n+nn(d,BV[b])
             x=st[r,:]; inv=inv_rms(x); u=x*inv
             fgo[...]+=jnp.broadcast_to(jnp.sum(n*u,axis=0,keepdims=True),(8,D))
-            w=n*fg[...]
+            w=n*fg[fg.shape[0]-1:,:]
             sgo[r,:]=ct[r,:].astype(f32)+inv*(w-u*jnp.mean(w*u,axis=1,keepdims=True))
         inward_run((z0,z1),zd,(zs0,zs1),False)
         for cp in rows(): cp.wait()
@@ -1181,7 +1184,7 @@
       out_shape=[SD((T,D),f32),SD((8,D),f32),SD((8,CAP,D),bf16),SD(inw[0].shape,bf16),SD((3,1)+dsum.shape[2:],bf16),SD((8,CAP,D),bf16)],
       scratch_shapes=[pltpu.VMEM((8,CAP,D),bf16),pltpu.SemaphoreType.DMA((8,))]+[pltpu.SemaphoreType.DMA((1,))]*2+row_sems()+ext_sems()+plane_sems(1),
       compiler_params=pltpu.CompilerParams(vmem_limit_bytes=50<<20,collective_id=4,has_side_effects=True),
-      cost_estimate=pl.CostEstimate(flops=4*S*T*D,bytes_accessed=12<<20,transcendentals=0),name="mid_bwd")(*deps,*inw,dsum,rext,cols,own,ext,back_b,dsh,state,fgain[None],cot)
+      cost_estimate=pl.CostEstimate(flops=4*S*T*D,bytes_accessed=12<<20,transcendentals=0),name="mid_bwd")(*deps,*inw,dsum,rext,cols,own,ext,back_b,dsh,state,as_rows(fgain),cot)
 
 def mid_bwd(cols, back, dsh, state, fgain, cot):
     parts=len(back); T,D=state.shape; S=back[0].shape[0]
@@ -1334,6 +1337,7 @@
 
 def shards_fast(tokens, cotangent, expert_ids, route_gates, slot_order, prefix_len, attention_gain, qkv_weight,
                 output_weight, feedforward_gain, shared_gate, shared_up, shared_down, expert_gate, expert_up, expert_down):
+    attention_gain = feedforward_gain = jnp.stack([attention_gain, feedforward_gain])
     T, D = tokens.shape
     FF = expert_gate.shape[2]
     dpi = lax.axis_index(DX).astype(jnp.int32)

time: 515 us -> 516 us (level)
    unnamed x61 -> x55, local copies, waits for them, and re-layouts: 15.4 us -> 14.4 us
where the time goes in v7:
time: 516 us; the launch traced here: 507 us
  Pallas kernels  454 us (88%)
  other arithmetic  27.7 us (5%)
  local copies, waits for them, and re-layouts  18.1 us (4%)
  starting transfers between devices  5.89 us (1%)
    pallas_call x1, Pallas kernels, attn_bwd(): pl.pallas_call(kernel, grid=(ng,), in_specs=[pl.BlockSpec(memory_space=pl...  161 us
    pallas_call x3, Pallas kernels, expert_ffn(): pl.pallas_call(kernel, grid=(nf,), in_specs=[anyspec] * nx + [rowspec] *...  153 us
    pallas_call x1, Pallas kernels, shared_ffn(): pl.pallas_call(kernel, grid=(nf,), in_specs=[full((T, D)), full((T, D)),...  44.4 us
    pallas_call x1, Pallas kernels, attn_fwd(): pl.pallas_call(kernel, grid=(ng,), in_specs=[pl.BlockSpec(memory_space=pl...  42.8 us
    pallas_call x1, Pallas kernels, mid_bwd_home(): pl.pallas_call(kernel, in_specs=[an] * (nx + 4) + [vm, an, an] + [vm] * 5...  42.6 us
    convert_element_type x4, other arithmetic, add(): return t.astype(bf16)  16.6 us
    unnamed x55, local copies, waits for them, and re-layouts  14.4 us
  transfers between devices with their start and end apart: 4, of which 0 were waited for; matrix products, arithmetic and copies ran while one was open for 2% of the time, Pallas kernels for 29%

profile of v7, /device:TPU:0, one launch (start us, length us, event | category | flops | bytes accessed | tf_op | source)
XLA Modules:
  0.0 507.5 jit_solution(13516013347969507131)
XLA Ops:
  1.3 0.7 stack.9
  2.0 0.7 stack.10
  2.7 0.9 copy.31.gts.rest_1_
  3.5 0.0 copy-start
  3.6 0.9 copy.30.ids
  4.5 0.6 pad_maximum_fusion.ag.fg.refs_11_
  5.1 1.3 copy-done.2
  6.3 0.7 copy-done.6
  7.0 9.7 %route.1 = (s32[8,768]{1,0:T(8,128)S(1)}, s32[768,8]{1,0:T(8,128)S(1)}, bf16[1920,768]{1,0:T(8,128)(2,1)}) custom-call(s32[1]{0:T(128)} %bitcast.core_ref, s32[1,1536]{1,0:T(1,128)S(1)} %copy-done.6, s32[768,2]{1,0:T(8,128)S(1)} %copy.30.ids, f32[768,2]{1,0:T(8,128)S(1)} %copy.31.gts.rest_1_, bf16[768,768]{1,0:T(8,128)(2,1)S(1)} %copy-done.2), custom_call_target="tpu_custom_call" | custom-call | flops 4680843264 | bytes 8388608 | tf_op jit(solution)/shard_map/route/pallas_call | solution.py:1095
  16.7 0.6 copy-done.7
  17.3 42.8 %attn_fwd.1 = (bf16[768,768]{1,0:T(8,128)(2,1)}, bf16[768,768]{1,0:T(8,128)(2,1)}, bf16[768,768]{1,0:T(8,128)(2,1)}, bf16[768,768]{1,0:T(8,128)(2,1)}, f32[3,8,7...) custom-call(s32[1]{0:T(128)S(6)} %copy.42.pre, ...), custom_call_target="tpu_custom_call" | custom-call | flops 5435817984 | bytes 16777216 | tf_op jit(solution)/shard_map/attn_fwd/pallas_call | solution.py:661
  60.2 44.4 %shared_ffn.1 = (f32[768,768]{1,0:T(8,128)}, f32[768,768]{1,0:T(8,128)}, bf16[4,4,1152,128]{3,2,1,0:T(8,128)(2,1)}, bf16[4,4,1152,128]{3,2,1,0:T(8,128)(2,1)}, b...) custom-call(bf16[768,768]{1,0:T(8,128)(2,1)} %get-tuple-element.87.xr, ...), custom_call_target="tpu_custom_call" | custom-call | flops 21743271936 | bytes 28311552 | tf_op jit(solution)/shard_map/shared_ffn/pallas_call | solution.py:1026
  104.5 0.5 collective-permute-start
  105.1 46.8 %expert_ffn1_0.3 = (bf16[960,768]{1,0:T(8,128)(2,1)}, bf16[960,768]{1,0:T(8,128)(2,1)}, bf16[384,2048]{1,0:T(8,128)(2,1)}, bf16[192,2048]{1,0:T(8,128)(2,1)}, bf...) custom-call(bf16[960,768]{1,0:T(8,128)(2,1)} %bitcast.33, ...), custom_call_target="tpu_custom_call" | custom-call | flops 27179089920 | bytes 24772608 | tf_op jit(solution)/shard_map/expert_ffn1_0/pallas_call | solution.py:967
  151.9 7.1 %add_convert_fusion.refs_6_.refs_3_ = bf16[4,4,1152,128]{3,2,1,0:T(8,128)(2,1)} fusion(bf16[4,4,1152,128]{3,2,1,0:T(8,128)(2,1)} %collective-permute-done, bf16[4,4,1152,128]{3,2,1,0:T(8,128)(2,1)} %get-tuple-element.98), kind=kLoop, calls=%fused_computation | loop fusion | flops 9437184 | bytes 14155776 | tf_op jit(solution)/shard_map/convert_element_type | solution.py:1360
  159.1 47.0 %expert_ffn1_0.4 = (bf16[960,768]{1,0:T(8,128)(2,1)}, bf16[960,768]{1,0:T(8,128)(2,1)}, bf16[384,2048]{1,0:T(8,128)(2,1)}, bf16[192,2048]{1,0:T(8,128)(2,1)}, bf...) custom-call(bf16[960,768]{1,0:T(8,128)(2,1)} %bitcast.36, ...), custom_call_target="tpu_custom_call" | custom-call | flops 27179089920 | bytes 24772608 | tf_op jit(solution)/shard_map/expert_ffn1_0/pallas_call | solution.py:967
  206.1 3.7 add_convert_fusion.3.refs_0_
  209.8 1.8 collective-permute-start.1
  211.6 59.4 %expert_ffn1_0.5 = (bf16[960,768]{1,0:T(8,128)(2,1)}, bf16[960,768]{1,0:T(8,128)(2,1)}, bf16[384,2048]{1,0:T(8,128)(2,1)}, bf16[192,2048]{1,0:T(8,128)(2,1)}, bf...) custom-call(bf16[384,2048]{1,0:T(8,128)(2,1)} %add_convert_fusion.3., ...), custom_call_target="tpu_custom_call" | custom-call | flops 27179089920 | bytes 24772608 | tf_op jit(solution)/shard_map/expert_ffn1_0/pallas_call | solution.py:967
  271.0 2.7 add_convert_fusion.2.refs_0_
  273.7 0.0 copy-start.10
  273.7 0.0 copy-start.4
  273.7 1.0 slice.21
  274.7 1.7 collective-permute-start.3
  276.4 1.8 collective-permute-start.2
  278.2 0.1 constant_dynamic-update-slice_fusion.2
  278.3 42.6 %mid_bwd.1 = (f32[768,768]{1,0:T(8,128)}, f32[8,768]{1,0:T(8,128)S(1)}, bf16[8,120,768]{2,1,0:T(8,128)(2,1)}, bf16[1024,768]{1,0:T(8,128)(2,1)}, bf16[3,1,1152,1...) custom-call(bf16[384,2048]{1,0:T(8,128)(2,1)} %copy-done.10, bf16[1024,768]{1,0:T(8,128)(2,1)} %get-tuple-element.111.refs_1_.rest_25_, ...), custom_call_target="tpu_custom_call" | custom-call | flops 2264924160 | bytes 12582912 | tf_op jit(solution)/shard_map/mid_bwd/pallas_call | solution.py:1183
  321.0 1.9 constant_dynamic-update-slice_fusion.1
  322.9 0.1 copy-done.8
  322.9 0.5 copy-done.9
  323.4 3.1 add_convert_fusion.1.rest_26_
  326.5 0.1 constant_dynamic-update-slice_fusion
  326.6 2.9 fusion.rest_8_
  329.6 161.1 %attn_bwd.1 = (bf16[768,768]{1,0:T(8,128)(2,1)}, f32[8,768]{1,0:T(8,128)}, bf16[4,96,2048]{2,1,0:T(8,128)(2,1)}, bf16[4,96,2048]{2,1,0:T(8,128)(2,1)}, bf16[4,25...) custom-call(s32[1]{0:T(128)S(6)} %copy.42.pre, ...), custom_call_target="tpu_custom_call" | custom-call | flops 11777605632 | bytes 25165824 | tf_op jit(solution)/shard_map/attn_bwd/pallas_call | solution.py:778
  490.7 0.8 constant_dynamic-slice_fusion
  491.5 0.5 slice_bitcast_fusion
  492.0 3.6 convert_element_type.78
  495.6 2.0 convert_element_type.79
  497.6 1.9 convert_element_type.80
  499.5 1.0 copy.43
  500.6 0.7 copy-done.14
  501.2 1.0 copy.44
  502.3 0.6 copy-done.16
  502.8 0.9 copy.45
  503.8 0.7 copy.46
  504.5 0.9 copy.47
  505.4 0.9 copy.48
  506.2 0.9 copy.49
  (38 shorter events, 0.1 us)
Async XLA Ops:
  3.5 13.2 %copy-start = (f32[768,2]{1,0:T(8,128)}, f32[768,2]{1,0:T(8,128)S(1)}, u32[]{:S(2)}) copy-start(f32[768,2]{1,0:T(8,128)S(1)} %copy.31.gts.rest_1_) | copy-start | bytes 18436
  5.1 1.3 copy-start.2
  6.3 0.7 copy-start.6
  16.7 0.6 copy-start.7
  17.3 261.0 %copy-start.1 = (s32[768,8]{1,0:T(8,128)}, s32[768,8]{1,0:T(8,128)S(1)}, u32[]{:S(2)}) copy-start(s32[768,8]{1,0:T(8,128)S(1)} %get-tuple-element.114.refs_5_.rest_0_) | copy-start | bytes 73732
  104.5 47.4 %collective-permute-start = (bf16[4,4,1152,128]{3,2,1,0:T(8,128)(2,1)}, bf16[4,4,1152,128]{3,2,1,0:T(8,128)(2,1)}, u32[]{:S(2)}, u32[]{:S(2)}) collective-permute-start(bf16[4,4,1152,128]{3,2,1,0:T(8,128)(2,1)} %get-tuple-element.99), channel_id=1, source_target_pairs={{0,4},{4,0},{8,12},{12,8},{16,20},{20,16},{24,28},{28,24},{1,5},{5... | collective-permute-start | bytes 14155784 | tf_op jit(solution)/shard_map/ppermute | solution.py:1351
  209.8 119.8 %collective-permute-start.1 = (bf16[384,2048]{1,0:T(8,128)(2,1)}, bf16[384,2048]{1,0:T(8,128)(2,1)}, u32[]{:S(2)}, u32[]{:S(2)}) collective-permute-start(bf16[384,2048]{1,0:T(8,128)(2,1)} %add_convert_fusion.3.refs_0_), channel_id=1, source_target_pairs={{8,16},{12,20},{16,8},{20,12},{9,17},{13,21},{17,9},{21,13},{10,18... | collective-permute-start | bytes 4718600 | tf_op jit(solution)/shard_map/ppermute | solution.py:1354
  271.0 2.7 copy-start.11
  273.7 4.6 copy-start.10
  273.7 4.5 copy-start.17
  273.7 4.6 copy-start.3
  273.7 4.6 copy-start.4
  274.7 54.9 %collective-permute-start.3 = (bf16[192,2048]{1,0:T(8,128)(2,1)}, bf16[192,2048]{1,0:T(8,128)(2,1)}, u32[]{:S(2)}, u32[]{:S(2)}) collective-permute-start(bf16[192,2048]{1,0:T(8,128)(2,1)} %slice.21), channel_id=1, source_target_pairs={{8,16},{12,20},{16,8},{20,12},{9,17},{13,21},{17,9},{21,13},{10,18... | collective-permute-start | bytes 2359304 | tf_op jit(solution)/shard_map/ppermute | solution.py:1354
  276.4 53.2 %collective-permute-start.2 = (bf16[384,2048]{1,0:T(8,128)(2,1)S(1)}, bf16[384,2048]{1,0:T(8,128)(2,1)}, u32[]{:S(2)}, u32[]{:S(2)}) collective-permute-start(bf16[384,2048]{1,0:T(8,128)(2,1)S(1)} %add_convert_fusion.2.refs_0_), channel_id=1, source_target_pairs={{8,16},{12,20},{16,8},{20,12},{9,17},{13,21},{17,9},{21,13},{10,18... | collective-permute-start | bytes 4718600 | tf_op jit(solution)/shard_map/ppermute | solution.py:1354
  321.0 1.9 copy-start.5
  321.0 1.9 copy-start.8
  321.0 2.4 copy-start.9
  492.0 3.6 copy-start.13
  495.6 2.0 copy-start.12
  497.6 1.9 copy-start.15
  499.5 1.7 copy-start.14
  501.2 1.6 copy-start.16
  501.2 2.5 copy-start.21
  502.8 1.6 copy-start.20
  502.8 2.5 copy-start.19
  504.5 1.8 copy-start.18
